TPU v7x, 32 devices: a whole 2x2x4 slice. The times are simulated.
32 devices in a mesh: dp: 16 (over z, y, x), seq: 2 (over core).
Axes of the slice: x: 2, y: 2, z: 4, core: 2. Of those that a mesh axis runs over, the one named last changes fastest.
Arguments:
- chains_in: bfloat16 [128, 160, 768], P(('dp', 'seq')), may hold values from -6 to 6
- lengths: int32 [128], P(('dp', 'seq')), may hold values from 95 to 160
- d_out: bfloat16 [128, 160, 768], P(('dp', 'seq')), may hold values from -6 to 6
- w_query: bfloat16 [768, 768], replicated, may hold values from -0.21875 to 0.21875
- b_query: float32 [768], replicated, may hold values from -3 to 3
- w_key: bfloat16 [768, 768], replicated, may hold values from -0.21875 to 0.21875
- w_value: bfloat16 [768, 768], replicated, may hold values from -0.21875 to 0.21875
- b_value: float32 [768], replicated, may hold values from -3 to 3
- w_output: bfloat16 [768, 768], replicated, may hold values from -2.5 to 2.5
- b_output: float32 [768], replicated, may hold values from -3 to 3
- gain_one: float32 [768], replicated, may hold values from 0.25 to 1.75
- shift_one: float32 [768], replicated, may hold values from -2 to 2
- w_inner: bfloat16 [768, 3072], replicated, may hold values from -0.21875 to 0.21875
- b_inner: float32 [3072], replicated, may hold values from -3 to 3
- w_outer: bfloat16 [3072, 768], replicated, may hold values from -0.109375 to 0.109375
- b_outer: float32 [768], replicated, may hold values from -3 to 3
- gain_two: float32 [768], replicated, may hold values from 0.25 to 1.75
- shift_two: float32 [768], replicated, may hold values from -2 to 2
Outputs:
- layer_out: bfloat16 [128, 160, 768], P(('dp', 'seq'))
- d_x: float32 [128, 160, 768], P(('dp', 'seq'))
- d_w_query: float32 [768, 768], replicated
- d_b_query: float32 [768], replicated
- d_w_key: float32 [768, 768], replicated
- d_w_value: float32 [768, 768], replicated
- d_b_value: float32 [768], replicated
- d_w_output: float32 [768, 768], replicated
- d_b_output: float32 [768], replicated
- d_gain_one: float32 [768], replicated
- d_shift_one: float32 [768], replicated
- d_w_inner: float32 [768, 3072], replicated
- d_b_inner: float32 [3072], replicated
- d_w_outer: float32 [3072, 768], replicated
- d_b_outer: float32 [768], replicated
- d_gain_two: float32 [768], replicated
- d_shift_two: float32 [768], replicated
Inputs may be any that keep to these rules, and one draw needn't show every extreme that they name: `lengths`: every chain fills more than half of its 160 positions.
All inputs are finite; a program needn't handle non-finite values.
Results may differ from a plain program's by a relative error of at most 0.015.
Values may be sent and summed in bfloat16 or wider, within the bound.
No kernel may reach another device: no remote copies, remote signals or barrier semaphores. Data moves between devices by JAX's collectives and lax.ppermute only.
A program may use at most 256 MiB of HBM per device.

v0:
```python
import jax
import jax.numpy as jnp
from jax import lax
from jax.sharding import PartitionSpec as P

H = 12


EPS = 1e-12


def norm_forward(h, gain, shift):
    centre = h - jnp.mean(h, -1, keepdims=True)
    scale = lax.rsqrt(jnp.mean(centre * centre, -1, keepdims=True) + EPS)
    unit = centre * scale
    return (unit * gain + shift, unit, scale)


def norm_backward(grad, unit, scale, gain):
    d_gain = jnp.sum(grad * unit, 0)
    d_shift = jnp.sum(grad, 0)
    inner = grad * gain
    d_h = scale * (
        inner
        - jnp.mean(inner, -1, keepdims=True)
        - unit * jnp.mean(inner * unit, -1, keepdims=True)
    )
    return (d_h, d_gain, d_shift)


def over_rows(left, right):
    return lax.dot_general(
        left, right, (((0,), (0,)), ((), ())), preferred_element_type=jnp.float32
    )


def times_trans(left, weight):
    return lax.dot_general(
        left, weight, (((1,), (1,)), ((), ())), preferred_element_type=jnp.float32
    )


def attn_scores(query, keys, live_keys):
    seqs, count, width = query.shape
    total = keys.shape[1]
    size = width // H
    q_heads = query.reshape(seqs, count, H, size)
    k_heads = keys.reshape(seqs, total, H, size)
    scores = (
        jnp.einsum("bqhe,bkhe->bhqk", q_heads, k_heads, preferred_element_type=jnp.float32) * 0.125
    )
    return jnp.where(live_keys[:, None, None, :], scores, -1000000000.0)


def packed(grads, count):
    flat = jnp.concatenate([g.reshape(-1) for g in grads])
    extra = -flat.shape[0] % count
    return flat.reshape(count, -1)


def unpacked(flat, grads):
    flat = flat.reshape(-1)
    pieces = []
    start = 0
    for grad in grads:
        number = grad.size
        pieces.append(flat[start : start + number].reshape(grad.shape))
        start = start + number
    return tuple(pieces)


def body(
    chains_in,
    lengths,
    d_out,
    w_query,
    b_query,
    w_key,
    w_value,
    b_value,
    w_output,
    b_output,
    gain_one,
    shift_one,
    w_inner,
    b_inner,
    w_outer,
    b_outer,
    gain_two,
    shift_two,
):
    f32 = jnp.float32
    low_type = jnp.bfloat16
    seqs, length, width = chains_in.shape
    rows = seqs * length
    size = width // H
    parts = lax.axis_size("dp")
    count = lax.axis_size("dp") * lax.axis_size("seq")
    place = jnp.arange(length, dtype=jnp.int32)
    live_rows = place[None, :] < lengths[:, None]
    flat_x = chains_in.reshape(rows, width)
    query = (
        (jnp.dot(flat_x, w_query, preferred_element_type=f32) + b_query)
        .astype(low_type)
        .reshape(seqs, length, width)
    )
    keys = (
        jnp.dot(flat_x, w_key, preferred_element_type=f32)
        .astype(low_type)
        .reshape(seqs, length, width)
    )
    values = (
        (jnp.dot(flat_x, w_value, preferred_element_type=f32) + b_value)
        .astype(low_type)
        .reshape(seqs, length, width)
    )
    scores = attn_scores(query, keys, live_rows)
    top = jnp.max(scores, -1, keepdims=True)
    expo = jnp.exp(scores - top)
    summed = jnp.sum(expo, -1, keepdims=True)
    prob_b = (expo / summed).astype(low_type)
    lse = top + jnp.log(summed)
    v_heads = values.reshape(seqs, length, H, size)
    mixed = (
        jnp.einsum("bhqk,bkhe->bqhe", prob_b, v_heads, preferred_element_type=f32)
        .reshape(rows, width)
        .astype(low_type)
    )
    h_one = flat_x.astype(f32) + jnp.dot(mixed, w_output, preferred_element_type=f32) + b_output
    first, unit_one, scale_one = norm_forward(h_one, gain_one, shift_one)
    live_flat = live_rows.reshape(rows)
    iota = jnp.arange(rows, dtype=jnp.int32)
    order = jnp.argsort(jnp.where(live_flat, iota, iota + rows))
    dealt = order.reshape(rows // parts, parts).T.reshape(rows)
    restore = jnp.zeros((rows,), jnp.int32).at[dealt].set(iota)
    sent = jnp.take(first.astype(low_type), dealt, axis=0).reshape(parts, rows // parts, width)
    fin = lax.all_to_all(sent, "dp", split_axis=0, concat_axis=0, tiled=True).reshape(rows, width)
    pre = jnp.dot(fin, w_inner, preferred_element_type=f32) + b_inner
    hidden = jax.nn.gelu(pre, approximate=False).astype(low_type)
    ffn_flat = (jnp.dot(hidden, w_outer, preferred_element_type=f32) + b_outer).astype(low_type)
    returned = lax.all_to_all(
        ffn_flat.reshape(parts, rows // parts, width), "dp", split_axis=0, concat_axis=0, tiled=True
    ).reshape(rows, width)
    ffn_home = jnp.take(returned, restore, axis=0)
    h_two = first + ffn_home.astype(f32)
    second, unit_two, scale_two = norm_forward(h_two, gain_two, shift_two)
    keep = live_flat[:, None].astype(f32)
    layer_out = (second * keep).astype(low_type).reshape(seqs, length, width)
    grad_out = d_out.reshape(rows, width).astype(f32) * keep
    d_h_two, d_gain_two, d_shift_two = norm_backward(grad_out, unit_two, scale_two, gain_two)
    grad_sent = jnp.take(d_h_two.astype(low_type), dealt, axis=0).reshape(
        parts, rows // parts, width
    )
    d_ffn = lax.all_to_all(grad_sent, "dp", split_axis=0, concat_axis=0, tiled=True).reshape(
        rows, width
    )
    d_w_outer = over_rows(hidden, d_ffn)
    d_b_outer = jnp.sum(d_ffn.astype(f32), 0)
    d_hidden = times_trans(d_ffn, w_outer)
    gelu_pull = jax.vjp(lambda z: jax.nn.gelu(z, approximate=False), pre)[1]
    d_pre = gelu_pull(d_hidden)[0].astype(low_type)
    d_w_inner = over_rows(fin, d_pre)
    d_b_inner = jnp.sum(d_pre.astype(f32), 0)
    d_fin = times_trans(d_pre, w_inner).astype(low_type)
    d_back = lax.all_to_all(
        d_fin.reshape(parts, rows // parts, width), "dp", split_axis=0, concat_axis=0, tiled=True
    ).reshape(rows, width)
    d_home = jnp.take(d_back, restore, axis=0)
    d_first = d_h_two + d_home.astype(f32)
    ffn_grads = (d_w_inner, d_b_inner, d_w_outer, d_b_outer, d_gain_two, d_shift_two)
    d_h_one, d_gain_one, d_shift_one = norm_backward(d_first, unit_one, scale_one, gain_one)
    d_attn = d_h_one.astype(low_type)
    d_w_output = over_rows(mixed, d_attn)
    d_b_output = jnp.sum(d_attn.astype(f32), 0)
    d_mixed = times_trans(d_attn, w_output).astype(low_type).reshape(seqs, length, H, size)
    scores = attn_scores(query, keys, live_rows)
    prob = jnp.exp(scores - lse)
    prob_b = prob.astype(low_type)
    d_prob = jnp.einsum("bqhe,bkhe->bhqk", d_mixed, v_heads, preferred_element_type=f32)
    delta = jnp.sum(prob * d_prob, -1, keepdims=True)
    d_scores = (prob * (d_prob - delta)).astype(low_type)
    k_heads = keys.reshape(seqs, length, H, size)
    q_heads = query.reshape(seqs, length, H, size)
    d_query = (
        (jnp.einsum("bhqk,bkhe->bqhe", d_scores, k_heads, preferred_element_type=f32) * 0.125)
        .astype(low_type)
        .reshape(rows, width)
    )
    d_key = (
        (jnp.einsum("bhqk,bqhe->bkhe", d_scores, q_heads, preferred_element_type=f32) * 0.125)
        .astype(low_type)
        .reshape(rows, width)
    )
    d_value = (
        jnp.einsum("bhqk,bqhe->bkhe", prob_b, d_mixed, preferred_element_type=f32)
        .astype(low_type)
        .reshape(rows, width)
    )
    d_w_query = over_rows(flat_x, d_query)
    d_b_query = jnp.sum(d_query.astype(f32), 0)
    d_w_key = over_rows(flat_x, d_key)
    d_w_value = over_rows(flat_x, d_value)
    d_b_value = jnp.sum(d_value.astype(f32), 0)
    d_x = (
        d_h_one
        + times_trans(d_query, w_query)
        + times_trans(d_key, w_key)
        + times_trans(d_value, w_value)
    )
    d_x = d_x.reshape(seqs, length, width)
    attn_grads = (
        d_w_query,
        d_b_query,
        d_w_key,
        d_w_value,
        d_b_value,
        d_w_output,
        d_b_output,
        d_gain_one,
        d_shift_one,
    )
    local_grads = attn_grads + ffn_grads
    all_part = lax.psum_scatter(
        packed(local_grads, count), ("dp", "seq"), scatter_dimension=0, tiled=True
    )
    every = unpacked(
        lax.all_gather(all_part.astype(jnp.bfloat16), ("dp", "seq"), axis=0, tiled=True).astype(
            all_part.dtype
        ),
        local_grads,
    )
    return (
        layer_out,
        d_x,
        every[0],
        every[1],
        every[2],
        every[3],
        every[4],
        every[5],
        every[6],
        every[7],
        every[8],
        every[9],
        every[10],
        every[11],
        every[12],
        every[13],
        every[14],
    )


def solution(mesh):
    return jax.shard_map(
        body,
        mesh=mesh,
        in_specs=(
            P(("dp", "seq"), None, None),
            P(("dp", "seq")),
            P(("dp", "seq"), None, None),
            P(),
            P(),
            P(),
            P(),
            P(),
            P(),
            P(),
            P(),
            P(),
            P(),
            P(),
            P(),
            P(),
            P(),
            P(),
        ),
        out_specs=(
            P(("dp", "seq"), None, None),
            P(("dp", "seq"), None, None),
            P(),
            P(),
            P(),
            P(),
            P(),
            P(),
            P(),
            P(),
            P(),
            P(),
            P(),
            P(),
            P(),
            P(),
            P(),
        ),
        check_vma=False,
    )
```

profile of v0, /device:TPU:0, one launch (start us, length us, event | category | flops | bytes accessed | tf_op | source)
XLA Modules:
  0.0 1660.4 jit_solution(12550708858252004042)
XLA Ops:
  62.6 33.5 %all_to_all.20 = bf16[16,40,768]{2,1,0:T(8,128)(2,1)S(1)} all-to-all(bf16[16,40,768]{2,1,0:T(8,128)(2,1)S(1)} %bitcast.101), channel_id=1, replica_groups=mesh['dp'=16,'seq'=2] {'dp'}, dimensions={0} | all-to-all | bytes 1966080 | tf_op jit(solution)/shard_map/all_to_all | solution.py:137
  96.1 22.7 %multiply_convert_fusion.1 = (bf16[640,3072]{1,0:T(8,128)(2,1)S(1)}, f32[640,3072]{1,0:T(8,128)}, f32[640,3072]{1,0:T(8,128)}) fusion(f32[3072]{0:T(1024)S(1)} %copy-done.28, bf16[640,768]{1,0:T(8,128)(2,1)S(1)} %bitcast.102, bf16[768,3072]{1,0:T(8,128)(2,1)} %param.32), kind=kOutput, calls=%fused_computation.13 | convolution fusion | flops 3149660160 | bytes 25374720 | tf_op jit(solution)/shard_map/dot_general | solution.py:138
  131.8 17.5 %all-to-all-done.1 = bf16[16,40,768]{2,1,0:T(8,128)(2,1)S(1)} async-done(((bf16[16,40,768]{2,1,0:T(8,128)(2,1)}), bf16[16,40,768]{2,1,0:T(8,128)(2,1)S(1)}, u32[]{:S(2)}, u32[]{:S(2)}) %all-to-all-start.1) | async-done | bytes 983072 | tf_op jit(solution)/shard_map/all_to_all | solution.py:141
  162.0 29.2 %all_to_all.21 = bf16[16,40,768]{2,1,0:T(8,128)(2,1)S(1)} all-to-all(bf16[16,40,768]{2,1,0:T(8,128)(2,1)S(1)} %bitcast.100), channel_id=1, replica_groups=mesh['dp'=16,'seq'=2] {'dp'}, dimensions={0} | all-to-all | bytes 1966080 | tf_op jit(solution)/shard_map/all_to_all | solution.py:154
  191.2 10.7 convert_reduce_fusion.1
  202.0 8.1 convolution_convert_fusion
  226.0 6.7 fusion.46
  232.8 10.7 reshape.307
  262.4 7.2 convert_reduce_fusion.2
  343.2 21.2 %dynamic-update-slice.2 = f32[7087104]{0:T(1024)} dynamic-update-slice(f32[7087104]{0:T(1024)} %constant_dynamic-update-slice_fusion.8, f32[589824]{0:T(1024)} %reshape.303, s32[]{} %constant.107) | dynamic-update-slice | bytes 4718596
  364.4 21.2 %dynamic-update-slice.3 = f32[7087104]{0:T(1024)} dynamic-update-slice(f32[7087104]{0:T(1024)} %dynamic-update-slice.2, f32[589824]{0:T(1024)} %reshape.304, s32[]{} %constant.108) | dynamic-update-slice | bytes 4718596
  386.9 21.2 %dynamic-update-slice.5 = f32[7087104]{0:T(1024)} dynamic-update-slice(f32[7087104]{0:T(1024)} %constant_dynamic-update-slice_fusion.7, f32[589824]{0:T(1024)} %reshape.305, s32[]{} %constant.110) | dynamic-update-slice | bytes 4718596
  411.9 80.6 %dynamic-update-slice.9 = f32[7087104]{0:T(1024)} dynamic-update-slice(f32[7087104]{0:T(1024)} %constant_dynamic-update-slice_fusion.4, f32[2359296]{0:T(1024)} %bitcast.99, s32[]{} %constant.114) | dynamic-update-slice | bytes 18874372
  493.9 80.7 %dynamic-update-slice.11 = f32[7087104]{0:T(1024)} dynamic-update-slice(f32[7087104]{0:T(1024)} %constant_dynamic-update-slice_fusion.3, f32[2359296]{0:T(1024)} %reshape.307, s32[]{} %constant.116) | dynamic-update-slice | bytes 18874372
  578.5 37.6 %reshape.308 = f32[32,221472]{1,0:T(8,128)} reshape(f32[7087104]{0:T(1024)} %constant_dynamic-update-slice_fusion) | data formatting | bytes 56696832 | tf_op jit(solution)/shard_map/reshape | solution.py:58
  616.1 456.3 %all-reduce.2 = bf16[32,221472]{1,0:T(8,128)(2,1)} all-reduce(f32[32,221472]{1,0:T(8,128)} %reshape.308), channel_id=2, replica_groups=mesh['dp'=16,'seq'=2] {'dp','seq'}, use_global_device_ids=true, to_apply=%region_22.24.clone | all-reduce | flops 7087104 | bytes 42522624
  1081.8 162.3 %all-gather.3.cloned.1.call-done = bf16[32,1,221472]{2,1,0:T(2,128)(2,1)} async-done(((bf16[1,1,221472]{2,1,0:T(2,128)(2,1)}), bf16[32,1,221472]{2,1,0:T(2,128)(2,1)}) %all-gather.3.cloned.1.call-update) | async-done | bytes 14174224 | tf_op jit(solution)/shard_map/all_gather | solution.py:227
  1244.1 303.5 %convert_reduce_fusion = f32[32,221472]{1,0:T(8,128)} fusion(bf16[32,1,221472]{2,1,0:T(2,128)(2,1)} %all-gather.3.cloned.1.call-done), kind=kLoop, calls=%fused_computation.5 | loop fusion | flops 7087104 | bytes 42522624 | tf_op jit(solution)/shard_map/convert_element_type | solution.py:227
  1547.5 36.7 %reshape.378 = f32[7087104]{0:T(1024)} reshape(f32[32,221472]{1,0:T(8,128)} %convert_reduce_fusion) | data formatting | bytes 56696832
  1586.9 8.4 slice.85
  1595.3 31.3 %slice.52 = f32[9228,768]{1,0:T(8,128)} reshape(f32[7087104]{0:T(1024)} %reshape.378) | data formatting | bytes 56696832 | tf_op jit(solution)/shard_map/slice | solution.py:67
  1626.6 8.0 slice.87
  1634.7 7.7 fusion.41
  1642.3 11.0 reshape.310
  (189 shorter events, 211.3 us)
Async XLA Ops:
  7.2 47.5 %copy-start = (bf16[768,768]{1,0:T(8,128)(2,1)S(1)}, bf16[768,768]{1,0:T(8,128)(2,1)}, u32[]{:S(2)}) copy-start(bf16[768,768]{1,0:T(8,128)(2,1)} %param.28) | copy-start | bytes 3538948
  7.2 8.2 copy-start.18
  7.2 8.2 copy-start.29
  17.4 8.7 copy-start.30
  59.0 37.1 %copy-start.28 = (f32[3072]{0:T(1024)S(1)}, f32[3072]{0:T(1024)}, u32[]{:S(2)}) copy-start(f32[3072]{0:T(1024)} %param.33) | copy-start | bytes 36868
  62.5 56.4 %slice-start.2 = ((s8[4718592]{0:T(1024)(128)(4,1)}), s8[4194304]{0:T(1024)(128)(4,1)S(1)}, s32[]{:S(2)}) async-start(s8[4718592]{0:T(1024)(128)(4,1)} %bitcast.111), calls=%async_computation.7 | async-start | bytes 8388608
  96.1 22.8 %copy-start.14 = (bf16[16,40,768]{2,1,0:T(8,128)(2,1)}, bf16[16,40,768]{2,1,0:T(8,128)(2,1)S(1)}, u32[]{:S(2)}) copy-start(bf16[16,40,768]{2,1,0:T(8,128)(2,1)S(1)} %all_to_all.20) | copy-start | bytes 2949124
  96.1 22.8 %slice-start.3 = ((s8[4718592]{0:T(1024)(128)(4,1)}), s8[524288]{0:T(1024)(128)(4,1)S(1)}, s32[]{:S(2)}) async-start(s8[4718592]{0:T(1024)(128)(4,1)} %bitcast.111), calls=%async_computation.8 | async-start | bytes 1048576
  96.1 22.8 %copy-start.32 = (f32[768]{0:T(1024)S(1)}, f32[768]{0:T(1024)}, u32[]{:S(2)}) copy-start(f32[768]{0:T(1024)} %param.35) | copy-start | bytes 9220
  118.9 8.1 copy-start.8
  118.9 8.1 copy-start.23
  123.1 26.2 %all-to-all-start.1 = ((bf16[16,40,768]{2,1,0:T(8,128)(2,1)}), bf16[16,40,768]{2,1,0:T(8,128)(2,1)S(1)}, u32[]{:S(2)}, u32[]{:S(2)}) async-start(bf16[16,40,768]{2,1,0:T(8,128)(2,1)} %bitcast.108), calls=%async_computation.1 | async-start | bytes 1966080 | tf_op jit(solution)/shard_map/all_to_all | solution.py:141
  191.2 10.8 copy-start.16
  202.0 8.1 copy-start.12
  202.0 12.0 copy-start.15
  210.1 33.6 %all-to-all-start.3 = ((bf16[16,40,768]{2,1,0:T(8,128)(2,1)}), bf16[16,40,768]{2,1,0:T(8,128)(2,1)S(1)}, u32[]{:S(2)}, u32[]{:S(2)}) async-start(bf16[16,40,768]{2,1,0:T(8,128)(2,1)} %bitcast.109), calls=%async_computation.3 | async-start | bytes 1966080 | tf_op jit(solution)/shard_map/all_to_all | solution.py:165
  213.9 1030.2 %all-gather.3.cloned.1.call-start = ((), (), s32[]{:S(2)}) async-start(), calls=%async_computation.4 | async-start | bytes 29246976 | tf_op jit(solution)/shard_map/all_gather | solution.py:227
  220.0 6.0 copy-start.17
  220.0 6.0 copy-start.34
  262.4 7.2 copy-start.10
  262.4 7.2 copy-start.11
  262.4 12.9 slice-start
  269.6 5.7 slice-start.1
  1642.3 11.0 copy-start.1
  (18 other events, 56.6 us)
Sparse Core Ops, SparseCore 0:
  1075.8 168.2 all-gather.2
where the time goes:
time: 1690 us; the launch traced here: 1660 us
  blocking collectives  519 us (31%)
  local copies, waits for them, and re-layouts  499 us (30%)
  other arithmetic  325 us (19%)
  waiting for transfers between devices  180 us (11%)
  matrix products  114 us (7%)
    unnamed x1, blocking collectives  456 us
    convert_element_type x1, other arithmetic, body(): lax.all_gather(all_part.astype(jnp.bfloat16), ('dp', 'seq'), axis=0, tile...  303 us
    unnamed x95, local copies, waits for them, and re-layouts  287 us
    all_gather x1, waiting for transfers between devices, body(): lax.all_gather(all_part.astype(jnp.bfloat16), ('dp', 'seq'), axis=0, tile...  162 us
    slice x6, local copies, waits for them, and re-layouts, unpacked(): pieces.append(flat[start:start + number].reshape(grad.shape))  58.1 us
    reshape x1, local copies, waits for them, and re-layouts, packed(): return flat.reshape(count, -1)  37.6 us
  transfers between devices with their start and end apart: 3, of which 2 were waited for; matrix products, arithmetic and copies ran while one was open for 2% of the time, Pallas kernels for 0%

commit v1 on v0

--- a/solution.py
+++ b/solution.py
@@ -129,31 +129,17 @@
     h_one = flat_x.astype(f32) + jnp.dot(mixed, w_output, preferred_element_type=f32) + b_output
     first, unit_one, scale_one = norm_forward(h_one, gain_one, shift_one)
     live_flat = live_rows.reshape(rows)
-    iota = jnp.arange(rows, dtype=jnp.int32)
-    order = jnp.argsort(jnp.where(live_flat, iota, iota + rows))
-    dealt = order.reshape(rows // parts, parts).T.reshape(rows)
-    restore = jnp.zeros((rows,), jnp.int32).at[dealt].set(iota)
-    sent = jnp.take(first.astype(low_type), dealt, axis=0).reshape(parts, rows // parts, width)
-    fin = lax.all_to_all(sent, "dp", split_axis=0, concat_axis=0, tiled=True).reshape(rows, width)
+    fin = first.astype(low_type)
     pre = jnp.dot(fin, w_inner, preferred_element_type=f32) + b_inner
     hidden = jax.nn.gelu(pre, approximate=False).astype(low_type)
-    ffn_flat = (jnp.dot(hidden, w_outer, preferred_element_type=f32) + b_outer).astype(low_type)
-    returned = lax.all_to_all(
-        ffn_flat.reshape(parts, rows // parts, width), "dp", split_axis=0, concat_axis=0, tiled=True
-    ).reshape(rows, width)
-    ffn_home = jnp.take(returned, restore, axis=0)
+    ffn_home = (jnp.dot(hidden, w_outer, preferred_element_type=f32) + b_outer).astype(low_type)
     h_two = first + ffn_home.astype(f32)
     second, unit_two, scale_two = norm_forward(h_two, gain_two, shift_two)
     keep = live_flat[:, None].astype(f32)
     layer_out = (second * keep).astype(low_type).reshape(seqs, length, width)
     grad_out = d_out.reshape(rows, width).astype(f32) * keep
     d_h_two, d_gain_two, d_shift_two = norm_backward(grad_out, unit_two, scale_two, gain_two)
-    grad_sent = jnp.take(d_h_two.astype(low_type), dealt, axis=0).reshape(
-        parts, rows // parts, width
-    )
-    d_ffn = lax.all_to_all(grad_sent, "dp", split_axis=0, concat_axis=0, tiled=True).reshape(
-        rows, width
-    )
+    d_ffn = d_h_two.astype(low_type)
     d_w_outer = over_rows(hidden, d_ffn)
     d_b_outer = jnp.sum(d_ffn.astype(f32), 0)
     d_hidden = times_trans(d_ffn, w_outer)
@@ -162,10 +148,7 @@
     d_w_inner = over_rows(fin, d_pre)
     d_b_inner = jnp.sum(d_pre.astype(f32), 0)
     d_fin = times_trans(d_pre, w_inner).astype(low_type)
-    d_back = lax.all_to_all(
-        d_fin.reshape(parts, rows // parts, width), "dp", split_axis=0, concat_axis=0, tiled=True
-    ).reshape(rows, width)
-    d_home = jnp.take(d_back, restore, axis=0)
+    d_home = d_fin
     d_first = d_h_two + d_home.astype(f32)
     ffn_grads = (d_w_inner, d_b_inner, d_w_outer, d_b_outer, d_gain_two, d_shift_two)
     d_h_one, d_gain_one, d_shift_one = norm_backward(d_first, unit_one, scale_one, gain_one)
@@ -220,15 +203,20 @@
         d_shift_one,
     )
     local_grads = attn_grads + ffn_grads
-    all_part = lax.psum_scatter(
-        packed(local_grads, count), ("dp", "seq"), scatter_dimension=0, tiled=True
-    )
-    every = unpacked(
-        lax.all_gather(all_part.astype(jnp.bfloat16), ("dp", "seq"), axis=0, tiled=True).astype(
-            all_part.dtype
-        ),
-        local_grads,
-    )
+    big = [g for g in local_grads if g.ndim == 2]
+    small = [g for g in local_grads if g.ndim == 1]
+    sums = lax.psum(jnp.concatenate(small), ("dp", "seq"))
+    small_sums = unpacked(sums, small)
+    big_sums = []
+    for grad in big:
+        part = lax.psum_scatter(
+            grad.astype(low_type), ("dp", "seq"), scatter_dimension=0, tiled=True
+        )
+        big_sums.append(lax.all_gather(part, ("dp", "seq"), axis=0, tiled=True).astype(f32))
+    every = []
+    for grad in local_grads:
+        every.append(big_sums.pop(0) if grad.ndim == 2 else small_sums[0])
+        small_sums = small_sums if grad.ndim == 2 else small_sums[1:]
     return (
         layer_out,
         d_x,

time: 1690 us -> 1150 us (0.68); the launches traced: 1660 us -> 1140 us
  waiting for transfers between devices: 180 us -> 864 us
  blocking collectives: 519 us -> 40.6 us
  local copies, waits for them, and re-layouts: 499 us -> 60.8 us
  other arithmetic: 325 us -> 38.7 us
    reduce_scatter x0 -> x6, waiting for transfers between devices: none -> 577 us  [body(): lax.psum_scatter(grad.astype(low_type), ('dp', 'seq'), scatter_dimension=...]
    unnamed x1 -> x0, blocking collectives: 456 us -> none
    convert_element_type x3 -> x6, other arithmetic: 306 us -> 25.6 us  [body(): lax.all_gather(part, ('dp', 'seq'), axis=0, tiled=True).astype(f32)]
    unnamed x95 -> x73, local copies, waits for them, and re-layouts: 287 us -> 14.4 us
    all_gather x1 -> x6, waiting for transfers between devices: 162 us -> 287 us  [body(): lax.all_gather(part, ('dp', 'seq'), axis=0, tiled=True).astype(f32)]
    reshape x10 -> x0, local copies, waits for them, and re-layouts: 72.5 us -> none  [the longest x1 37.6 us: packed(): return flat.reshape(count, -1)]
    all_to_all x2 -> x0, blocking collectives: 62.7 us -> none  [the longest x1 33.5 us: body(): lax.all_to_all(sent, 'dp', split_axis=0, concat_axis=0, tiled=True)]
    slice x6 -> x2, local copies, waits for them, and re-layouts: 58.1 us -> 1.23 us  [unpacked(): pieces.append(flat[start:start + number].reshape(grad.shape))]
  transfers between devices with their start and end apart: 3 -> 12, of which waited for: 2 -> 12; matrix products, arithmetic and copies ran while one was open for 2% -> 7% of each run, Pallas kernels for 0% -> 0%
where the time goes in v1:
time: 1150 us; the launch traced here: 1140 us
  waiting for transfers between devices  864 us (75%)
  matrix products  120 us (10%)
  local copies, waits for them, and re-layouts  60.8 us (5%)
  blocking collectives  40.6 us (4%)
  other arithmetic  38.7 us (3%)
  between operations  15.3 us (1%)
    reduce_scatter x6, waiting for transfers between devices, body(): lax.psum_scatter(grad.astype(low_type), ('dp', 'seq'), scatter_dimension=...  577 us
    all_gather x6, waiting for transfers between devices, body(): lax.all_gather(part, ('dp', 'seq'), axis=0, tiled=True).astype(f32)  287 us
    psum x1, blocking collectives, body(): sums = lax.psum(jnp.concatenate(small), ('dp', 'seq'))  40.6 us
    dot_general x6, matrix products, over_rows(): lax.dot_general(left, right, (((0,), (0,)), ((), ())), preferred_element_...  32.1 us
    convert_element_type x6, other arithmetic, body(): lax.all_gather(part, ('dp', 'seq'), axis=0, tiled=True).astype(f32)  25.6 us
    dot_general x1, matrix products, body(): pre = jnp.dot(fin, w_inner, preferred_element_type=f32) + b_inner  23.9 us
    dot_general x6, matrix products, times_trans(): lax.dot_general(left, weight, (((1,), (1,)), ((), ())), preferred_element...  23.5 us
  transfers between devices with their start and end apart: 12, of which 12 were waited for; matrix products, arithmetic and copies ran while one was open for 7% of the time, Pallas kernels for 0%

profile of v1, /device:TPU:0, one launch (start us, length us, event | category | flops | bytes accessed | tf_op | source)
XLA Modules:
  0.0 1139.7 jit_solution(12008616428699110538)
XLA Ops:
  55.6 23.9 %multiply_convert_fusion.1 = (bf16[640,3072]{1,0:T(8,128)(2,1)S(1)}, f32[640,3072]{1,0:T(8,128)}, f32[640,3072]{1,0:T(8,128)}) fusion(f32[3072]{0:T(1024)S(1)} %copy-done.22, bf16[768,3072]{1,0:T(8,128)(2,1)} %param.30, f32[640,768]{1,0:T(8,128)} %copy-done.8, f32[768]{0:T(1024)S(1)} %copy-done.26, f32[768]{0:T(1024)S(1)} %copy-done.19, ...), kind=kOutput, calls=%fused_computation.7 | convolution fusion | flops 3152117760 | bytes 26369024 | tf_op jit(solution)/shard_map/dot_general | solution.py:133
  79.5 7.2 fusion.47
  93.5 11.6 %convert_reduce_fusion = (f32[3072]{0:T(1024)S(1)}, bf16[640,3072]{1,0:T(8,128)(2,1)S(1)}) fusion(f32[640,3072]{1,0:T(8,128)} %get-tuple-element.64, bf16[3072,768]{1,0:T(8,128)(2,1)} %param.32, f32[640,768]{1,0:T(8,128)S(1)} %get-tuple-element.60, f32[640,3072]{1,0:T(8,128)} %get-tuple-element.80, f32[3072]{0:T(1024)S(1)} %copy-done.22), kind=kOutput, calls=%fused_computation.2 | convolution fusion | flops 3053810688 | bytes 26370048 | tf_op jit(solution)/shard_map/dot_general | solution.py:38
  117.0 4.6 copy.82
  121.6 7.5 multiply_reduce_fusion
  129.1 4.9 multiply_convert_fusion
  157.8 5.5 convert_reduce_fusion.1
  176.2 9.1 convolution_convert_fusion.1
  185.3 8.8 convolution_convert_fusion
  194.3 49.8 %reduce-scatter.19.cloned.1.call-done = bf16[24,768]{1,0:T(8,128)(2,1)} async-done(((bf16[768,768]{1,0:T(8,128)(2,1)}), bf16[24,768]{1,0:T(8,128)(2,1)}) %reduce-scatter.19.cloned.1.call-update) | async-done | bytes 36880 | tf_op jit(solution)/shard_map/reduce_scatter | solution.py:212
  244.2 100.9 %reduce-scatter.21.cloned.1.call-done = bf16[24,768]{1,0:T(8,128)(2,1)} async-done(((bf16[768,768]{1,0:T(8,128)(2,1)}), bf16[24,768]{1,0:T(8,128)(2,1)}) %reduce-scatter.21.cloned.1.call-update) | async-done | bytes 36880 | tf_op jit(solution)/shard_map/reduce_scatter | solution.py:212
  345.1 100.4 %reduce-scatter.23.cloned.1.call-done = bf16[24,768]{1,0:T(8,128)(2,1)} async-done(((bf16[768,768]{1,0:T(8,128)(2,1)}), bf16[24,768]{1,0:T(8,128)(2,1)}) %reduce-scatter.23.cloned.1.call-update) | async-done | bytes 36880 | tf_op jit(solution)/shard_map/reduce_scatter | solution.py:212
  445.6 100.8 %reduce-scatter.13.cloned.1.call-done = bf16[24,768]{1,0:T(8,128)(2,1)} async-done(((bf16[768,768]{1,0:T(8,128)(2,1)}), bf16[24,768]{1,0:T(8,128)(2,1)}) %reduce-scatter.13.cloned.1.call-update) | async-done | bytes 36880 | tf_op jit(solution)/shard_map/reduce_scatter | solution.py:212
  546.4 111.9 %reduce-scatter.15.cloned.1.call-done = bf16[24,3072]{1,0:T(8,128)(2,1)} async-done(((bf16[768,3072]{1,0:T(8,128)(2,1)}), bf16[24,3072]{1,0:T(8,128)(2,1)}) %reduce-scatter.15.cloned.1.call-update) | async-done | bytes 147472 | tf_op jit(solution)/shard_map/reduce_scatter | solution.py:212
  658.4 112.9 %reduce-scatter.17.cloned.1.call-done = bf16[96,768]{1,0:T(8,128)(2,1)} async-done(((bf16[3072,768]{1,0:T(8,128)(2,1)}), bf16[96,768]{1,0:T(8,128)(2,1)}) %reduce-scatter.17.cloned.1.call-update) | async-done | bytes 147472 | tf_op jit(solution)/shard_map/reduce_scatter | solution.py:212
  771.5 40.6 %psum.7 = f32[9216]{0:T(1024)S(1)} all-reduce(f32[9216]{0:T(1024)S(1)} %constant_dynamic-update-slice_fusion), channel_id=1, replica_groups=mesh['dp'=16,'seq'=2] {'dp','seq'}, use_global_device_ids=true, to_apply=%region_21.22 | all-reduce | flops 9216 | bytes 73728 | tf_op jit(solution)/shard_map/psum | solution.py:208
  820.0 7.2 all-gather.7.cloned.1.call-done
  830.1 53.1 %all-gather.9.cloned.1.call-done = bf16[768,768]{1,0:T(8,128)(2,1)} async-done(((bf16[24,768]{1,0:T(8,128)(2,1)}), bf16[768,768]{1,0:T(8,128)(2,1)}) %all-gather.9.cloned.1.call-update) | async-done | bytes 1179664 | tf_op jit(solution)/shard_map/all_gather | solution.py:215
  886.0 53.1 %all-gather.11.cloned.1.call-done = bf16[768,768]{1,0:T(8,128)(2,1)} async-done(((bf16[24,768]{1,0:T(8,128)(2,1)}), bf16[768,768]{1,0:T(8,128)(2,1)}) %all-gather.11.cloned.1.call-update) | async-done | bytes 1179664 | tf_op jit(solution)/shard_map/all_gather | solution.py:215
  941.9 52.9 %all-gather.13.cloned.1.call-done = bf16[768,768]{1,0:T(8,128)(2,1)} async-done(((bf16[24,768]{1,0:T(8,128)(2,1)}), bf16[768,768]{1,0:T(8,128)(2,1)}) %all-gather.13.cloned.1.call-update) | async-done | bytes 1179664 | tf_op jit(solution)/shard_map/all_gather | solution.py:215
  997.7 62.7 %all-gather.15.cloned.1.call-done = bf16[768,3072]{1,0:T(8,128)(2,1)} async-done(((bf16[24,3072]{1,0:T(8,128)(2,1)}), bf16[768,3072]{1,0:T(8,128)(2,1)}) %all-gather.15.cloned.1.call-update) | async-done | bytes 4718608 | tf_op jit(solution)/shard_map/all_gather | solution.py:215
  1060.4 7.4 convert_element_type.217
  1067.7 57.9 %all-gather.17.cloned.1.call-done = bf16[3072,768]{1,0:T(8,128)(2,1)} async-done(((bf16[96,768]{1,0:T(8,128)(2,1)}), bf16[3072,768]{1,0:T(8,128)(2,1)}) %all-gather.17.cloned.1.call-update) | async-done | bytes 4718608 | tf_op jit(solution)/shard_map/all_gather | solution.py:215
  1125.6 6.8 convert_element_type.219
  (158 shorter events, 123.0 us)
Async XLA Ops:
  7.2 43.9 %copy-start = (bf16[768,768]{1,0:T(8,128)(2,1)S(1)}, bf16[768,768]{1,0:T(8,128)(2,1)}, u32[]{:S(2)}) copy-start(bf16[768,768]{1,0:T(8,128)(2,1)} %param.26) | copy-start | bytes 3538948
  7.2 236.9 %reduce-scatter.19.cloned.1.call-start = ((), (), s32[]{:S(2)}) async-start(), calls=%async_computation.15 | async-start | bytes 1216512 | tf_op jit(solution)/shard_map/reduce_scatter | solution.py:212
  12.5 4.6 copy-start.20
  12.5 4.6 copy-start.23
  44.6 6.5 copy-start.24
  55.5 24.0 %copy-start.9 = (f32[640,768]{1,0:T(8,128)S(1)}, f32[640,768]{1,0:T(8,128)}, u32[]{:S(2)}) copy-start(f32[640,768]{1,0:T(8,128)} %copy-done.8) | copy-start | bytes 5898244
  55.5 24.0 %copy-start.25 = (f32[768]{0:T(1024)S(1)}, f32[768]{0:T(1024)}, u32[]{:S(2)}) copy-start(f32[768]{0:T(1024)} %param.33) | copy-start | bytes 9220
  79.5 7.2 copy-start.27
  79.5 7.6 copy-start.17
  90.2 15.0 %slice-start = ((s8[4718592]{0:T(1024)(128)(4,1)}), s8[4194304]{0:T(1024)(128)(4,1)S(1)}, s32[]{:S(2)}) async-start(s8[4718592]{0:T(1024)(128)(4,1)} %bitcast.81), calls=%async_computation.18 | async-start | bytes 8388608
  93.5 11.7 %copy-start.14 = (f32[640,768]{1,0:T(8,128)}, f32[640,768]{1,0:T(8,128)S(1)}, u32[]{:S(2)}) copy-start(f32[640,768]{1,0:T(8,128)S(1)} %get-tuple-element.60) | copy-start | bytes 5898244
  93.5 11.7 %copy-start.10 = (f32[640,768]{1,0:T(8,128)S(1)}, f32[640,768]{1,0:T(8,128)}, u32[]{:S(2)}) copy-start(f32[640,768]{1,0:T(8,128)} %copy-done.8) | copy-start | bytes 5898244
  93.5 11.7 %slice-start.1 = ((s8[4718592]{0:T(1024)(128)(4,1)}), s8[524288]{0:T(1024)(128)(4,1)S(1)}, s32[]{:S(2)}) async-start(s8[4718592]{0:T(1024)(128)(4,1)} %bitcast.81), calls=%async_computation.19 | async-start | bytes 1048576
  145.0 200.0 %reduce-scatter.21.cloned.1.call-start = ((), (), s32[]{:S(2)}) async-start(), calls=%async_computation.16 | async-start | bytes 1216512 | tf_op jit(solution)/shard_map/reduce_scatter | solution.py:212
  157.7 287.8 %reduce-scatter.23.cloned.1.call-start = ((), (), s32[]{:S(2)}) async-start(), calls=%async_computation.17 | async-start | bytes 1216512 | tf_op jit(solution)/shard_map/reduce_scatter | solution.py:212
  172.7 373.6 %reduce-scatter.13.cloned.1.call-start = ((), (), s32[]{:S(2)}) async-start(), calls=%async_computation.9 | async-start | bytes 1216512 | tf_op jit(solution)/shard_map/reduce_scatter | solution.py:212
  176.1 482.2 %reduce-scatter.15.cloned.1.call-start = ((), (), s32[]{:S(2)}) async-start(), calls=%async_computation.11 | async-start | bytes 4866048 | tf_op jit(solution)/shard_map/reduce_scatter | solution.py:212
  185.3 585.9 %reduce-scatter.17.cloned.1.call-start = ((), (), s32[]{:S(2)}) async-start(), calls=%async_computation.13 | async-start | bytes 4866048 | tf_op jit(solution)/shard_map/reduce_scatter | solution.py:212
  194.2 633.1 %all-gather.7.cloned.1.call-start = ((), (), s32[]{:S(2)}) async-start(), calls=%async_computation.6 | async-start | bytes 1216512 | tf_op jit(solution)/shard_map/all_gather | solution.py:215
  244.1 639.1 %all-gather.9.cloned.1.call-start = ((), (), s32[]{:S(2)}) async-start(), calls=%async_computation.7 | async-start | bytes 1216512 | tf_op jit(solution)/shard_map/all_gather | solution.py:215
  345.0 594.0 %all-gather.11.cloned.1.call-start = ((), (), s32[]{:S(2)}) async-start(), calls=%async_computation.8 | async-start | bytes 1216512 | tf_op jit(solution)/shard_map/all_gather | solution.py:215
  445.5 549.3 %all-gather.13.cloned.1.call-start = ((), (), s32[]{:S(2)}) async-start(), calls=%async_computation.10 | async-start | bytes 1216512 | tf_op jit(solution)/shard_map/all_gather | solution.py:215
  546.3 514.0 %all-gather.15.cloned.1.call-start = ((), (), s32[]{:S(2)}) async-start(), calls=%async_computation.12 | async-start | bytes 4866048 | tf_op jit(solution)/shard_map/all_gather | solution.py:215
  658.3 467.3 %all-gather.17.cloned.1.call-start = ((), (), s32[]{:S(2)}) async-start(), calls=%async_computation.14 | async-start | bytes 4866048 | tf_op jit(solution)/shard_map/all_gather | solution.py:215
  (19 other events, 53.4 us)
Sparse Core Ops, SparseCore 0:
  145.2 98.8 reduce-scatter.18
  249.7 95.2 reduce-scatter.20
  350.1 95.3 reduce-scatter.22
  451.0 95.2 reduce-scatter.12
  552.2 106.0 reduce-scatter.14
  665.1 106.0 reduce-scatter.16
  774.1 53.1 all-gather.6
  830.2 52.9 all-gather.8
  886.1 52.9 all-gather.10
  941.8 52.9 all-gather.12
  997.7 62.5 all-gather.14
  1063.1 62.4 all-gather.16

commit v2 on v1

v2 whole, which is shorter than its diff:
```python
import functools
import jax
import jax.numpy as jnp
from jax import lax
from jax.experimental import pallas as pl
from jax.experimental.pallas import tpu as pltpu
from jax.sharding import PartitionSpec as P
H=12; EPS=1e-12
f32=jnp.float32; bf16=jnp.bfloat16
VM=60*1024*1024
def cp(**k): return pltpu.CompilerParams(vmem_limit_bytes=VM, **k)
def nt(a,b): return lax.dot_general(a,b,(((1,),(1,)),((),())),preferred_element_type=f32)
def tn(a,b): return lax.dot_general(a,b,(((0,),(0,)),((),())),preferred_element_type=f32)
def nn(a,b): return jnp.dot(a,b,preferred_element_type=f32)

def attn_fwd_kernel(lens, x, wq, bq, wk, wv, bv, wo, bo, q_o, k_o, v_o, mixed_o, xhat_o, rstd_o, lse_o, h_s):
    rows, width = x.shape
    seqs = lens.shape[0]
    length = rows // seqs
    size = width // H
    def proj(n, _):
        c = pl.ds(pl.multiple_of(n*256,256),256)
        q_o[:, c] = ((nn(x[...], wq[:, c]) + bq[:, c]).astype(bf16).astype(f32)*0.125).astype(bf16)
        k_o[:, c] = nn(x[...], wk[:, c]).astype(bf16)
        v_o[:, c] = (nn(x[...], wv[:, c]) + bv[:, c]).astype(bf16)
        return 0
    lax.fori_loop(0, width//256, proj, 0)
    lane = lax.broadcasted_iota(jnp.int32, (length,128), 1)
    low = lane < size
    pos = lax.broadcasted_iota(jnp.int32, (length,1), 0)
    def chain(s, _):
        r = pl.ds(pl.multiple_of(s*length, 32), length)
        live = pos < lens[s]
        for p in range(H//2):
            c = slice(128*p,128*p+128)
            qp=q_o[r,c]; kp=k_o[r,c]; vp=v_o[r,c]
            outs=[]
            for h in range(2):
                sel = low if h==0 else ~low
                kh = jnp.where(sel,kp,jnp.zeros_like(kp))
                st = nt(kh,qp)
                st = jnp.where(live, st, -1e9)
                m = jnp.max(st,0,keepdims=True)
                e = jnp.exp(st-m)
                l = jnp.sum(e,0,keepdims=True)
                pt = (e*(1.0/l)).astype(bf16)
                lse_o[s, pl.ds(2*p+h,1), :] = m+jnp.log(l)
                outs.append(tn(pt,vp))
            mixed_o[r,c] = jnp.where(low,outs[0],outs[1]).astype(bf16)
        return 0
    lax.fori_loop(0, seqs, chain, 0)
    def outp(n,_):
        c = pl.ds(pl.multiple_of(n*256,256),256)
        h_s[:, c] = nn(mixed_o[...], wo[:, c]) + bo[:, c] + x[:, c].astype(f32)
        return 0
    lax.fori_loop(0, width//256, outp, 0)
    def norm(n,_):
        r = pl.ds(pl.multiple_of(n*128,128),128)
        h = h_s[r,:]
        cen = h - jnp.mean(h,-1,keepdims=True)
        rs = lax.rsqrt(jnp.mean(cen*cen,-1,keepdims=True)+EPS)
        xhat_o[r,:] = cen*rs
        rstd_o[r,:] = rs
        return 0
    lax.fori_loop(0, rows//128, norm, 0)

def attn_fwd(lens,x,wq,bq,wk,wv,bv,wo,bo):
    rows,width=x.shape; seqs=lens.shape[0]
    sd=jax.ShapeDtypeStruct
    vm=pl.BlockSpec(memory_space=pltpu.VMEM); sm=pl.BlockSpec(memory_space=pltpu.SMEM)
    return pl.pallas_call(attn_fwd_kernel, in_specs=[sm]+[vm]*8, out_specs=[vm]*7,
        out_shape=[sd((rows,width),bf16)]*4+[sd((rows,width),f32),sd((rows,1),f32),sd((seqs,H,rows//seqs),f32)],
        scratch_shapes=[pltpu.VMEM((rows,width),f32)], compiler_params=cp(), name="attn_fwd")(lens,x,wq,bq,wk,wv,bv,wo,bo)

GP=0.21
GC=(0.08371157579811618,0.08506885551666664,0.06919218864603045,0.12487264645005582,-0.09392498947908608,0.3494006440217003,-0.3302530091485681,0.2835883509790708,-0.07165625592844904)
def gelu_parts(u):
    a = jnp.abs(u)
    t = 1.0/(1.0+GP*a)
    e = jnp.exp(-0.5*u*u)
    q = jnp.full_like(t,GC[-1])
    for c in GC[-2::-1]: q = q*t+c
    tail = q*t*e
    cdf = jnp.where(u>0, 1.0-tail, tail)
    return u*cdf, cdf + u*e*0.3989422804014327

FB=512
def ffn_fwd_kernel(lens, xhat, g1, s1, wi, bi, wo, bo, g2, s2, dout, fin_o, hid_o, gp_o, lo_o, dffn_o, dh2_o, dg2_o, ds2_o, dbo_o, acc):
    n = pl.program_id(0)
    rows,width=xhat.shape
    seqs=lens.shape[0]; length=rows//seqs
    @pl.when(n==0)
    def _():
        fin_o[...] = (xhat[...]*g1[...]+s1[...]).astype(bf16)
    RB=128
    for i in range(rows//RB):
        r=slice(i*RB,(i+1)*RB)
        u = nn(fin_o[r,:],wi[...])+bi[...]
        hid,gp=gelu_parts(u)
        hb=hid.astype(bf16)
        hid_o[r,:]=hb; gp_o[r,:]=gp.astype(bf16)
    part = nn(hid_o[...],wo[...])
    @pl.when(n==0)
    def _(): acc[...]=part
    @pl.when(n>0)
    def _(): acc[...]=acc[...]+part
    @pl.when(n==pl.num_programs(0)-1)
    def _():
        dg2_o[...]=jnp.zeros_like(dg2_o); ds2_o[...]=jnp.zeros_like(ds2_o); dbo_o[...]=jnp.zeros_like(dbo_o)
        B=32
        pos=lax.broadcasted_iota(jnp.int32,(B,1),0)
        def blk(i,_):
            r=pl.ds(pl.multiple_of(i*B,B),B)
            s=i//(length//B); off=(i%(length//B))*B
            keep=jnp.where(pos+off<lens[s],1.0,0.0).astype(f32)
            x1=xhat[r,:]*g1[...]+s1[...]
            ffn=(acc[r,:]+bo[...]).astype(bf16).astype(f32)
            h=x1+ffn
            cen=h-jnp.mean(h,-1,keepdims=True)
            rs=lax.rsqrt(jnp.mean(cen*cen,-1,keepdims=True)+EPS)
            unit=cen*rs
            lo_o[r,:]=((unit*g2[...]+s2[...])*keep).astype(bf16)
            g=dout[r,:].astype(f32)*keep
            e=g*g2[...]
            dh=rs*(e-jnp.mean(e,-1,keepdims=True)-unit*jnp.mean(e*unit,-1,keepdims=True))
            dh2_o[r,:]=dh
            db=dh.astype(bf16)
            dffn_o[r,:]=db
            dg2_o[...]+=jnp.sum(g*unit,0,keepdims=True)
            ds2_o[...]+=jnp.sum(g,0,keepdims=True)
            dbo_o[...]+=jnp.sum(db.astype(f32),0,keepdims=True)
            return 0
        lax.fori_loop(0,rows//B,blk,0)

def ffn_fwd(lens,xhat,g1,s1,wi,bi,wo,bo,g2,s2,dout):
    rows,width=xhat.shape; ff=wi.shape[1]
    sd=jax.ShapeDtypeStruct
    full=lambda a: pl.BlockSpec(a.shape, lambda n,*_: (0,)*len(a.shape))
    col=lambda r: pl.BlockSpec((r,FB),lambda n,*_:(0,n))
    outs=[sd((rows,width),bf16),sd((rows,ff),bf16),sd((rows,ff),bf16),sd((rows,width),bf16),sd((rows,width),bf16),sd((rows,width),f32)]+[sd((1,width),f32)]*3
    return pl.pallas_call(ffn_fwd_kernel, grid_spec=pltpu.PrefetchScalarGridSpec(num_scalar_prefetch=1,grid=(ff//FB,),
        in_specs=[full(xhat),full(g1),full(s1),col(width),col(1),pl.BlockSpec((FB,width),lambda n,*_:(n,0)),full(bo),full(g2),full(s2),full(dout)],
        out_specs=[full(outs[0]),col(rows),col(rows)]+[full(o) for o in outs[3:]],
        scratch_shapes=[pltpu.VMEM((rows,width),f32)]),
        out_shape=outs, compiler_params=cp(), name="ffn_fwd")(lens,xhat,g1,s1,wi,bi,wo,bo,g2,s2,dout)

def ffn_bwd_kernel(dffn, wo, gp, wi, dh2, xhat, rstd, g1, wout, dpre_o, dbi_o, dh1_o, dob_o, dmix_o, dg1_o, ds1_o, dbo_o, acc):
    n=pl.program_id(0)
    rows,width=dffn.shape
    RB=128
    for i in range(rows//RB):
        r=slice(i*RB,(i+1)*RB)
        d=nt(dffn[r,:],wo[...])*gp[r,:].astype(f32)
        db=d.astype(bf16)
        dpre_o[r,:]=db
    dbi_o[...]=jnp.sum(dpre_o[...].astype(f32),0,keepdims=True)
    part=nt(dpre_o[...],wi[...])
    @pl.when(n==0)
    def _(): acc[...]=part
    @pl.when(n>0)
    def _(): acc[...]=acc[...]+part
    @pl.when(n==pl.num_programs(0)-1)
    def _():
        dg1_o[...]=jnp.zeros_like(dg1_o); ds1_o[...]=jnp.zeros_like(ds1_o); dbo_o[...]=jnp.zeros_like(dbo_o)
        B=32
        def blk(i,_):
            r=pl.ds(pl.multiple_of(i*B,B),B)
            g=dh2[r,:]+acc[r,:].astype(bf16).astype(f32)
            unit=xhat[r,:]
            e=g*g1[...]
            dh=rstd[r,:]*(e-jnp.mean(e,-1,keepdims=True)-unit*jnp.mean(e*unit,-1,keepdims=True))
            dh1_o[r,:]=dh
            db=dh.astype(bf16)
            dob_o[r,:]=db
            dg1_o[...]+=jnp.sum(g*unit,0,keepdims=True)
            ds1_o[...]+=jnp.sum(g,0,keepdims=True)
            dbo_o[...]+=jnp.sum(db.astype(f32),0,keepdims=True)
            return 0
        lax.fori_loop(0,rows//B,blk,0)
        def mx(k,_):
            c=pl.ds(pl.multiple_of(k*256,256),256)
            dmix_o[:,c]=nt(dob_o[...],wout[c,:]).astype(bf16)
            return 0
        lax.fori_loop(0,width//256,mx,0)

def ffn_bwd(dffn,wo,gp,wi,dh2,xhat,rstd,g1,wout):
    rows,width=dffn.shape; ff=wi.shape[1]
    sd=jax.ShapeDtypeStruct
    full=lambda a: pl.BlockSpec(a.shape, lambda n: (0,)*len(a.shape))
    col=lambda r: pl.BlockSpec((r,FB),lambda n:(0,n))
    outs=[sd((rows,ff),bf16),sd((1,ff),f32),sd((rows,width),f32),sd((rows,width),bf16),sd((rows,width),bf16)]+[sd((1,width),f32)]*3
    return pl.pallas_call(ffn_bwd_kernel, grid=(ff//FB,),
        in_specs=[full(dffn),pl.BlockSpec((FB,width),lambda n:(n,0)),col(rows),col(width),full(dh2),full(xhat),full(rstd),full(g1),full(wout)],
        out_specs=[col(rows),col(1)]+[full(o) for o in outs[2:]],
        scratch_shapes=[pltpu.VMEM((rows,width),f32)],
        out_shape=outs, compiler_params=cp(), name="ffn_bwd")(dffn,wo,gp,wi,dh2,xhat,rstd,g1,wout)

def attn_bwd_kernel(lens, q, k, v, dm, lse, dob, d_o, dbq_o, dbv_o):
    rows,width=q.shape; seqs=lens.shape[0]; length=rows//seqs; size=width//H
    lane=lax.broadcasted_iota(jnp.int32,(length,128),1); low=lane<size
    pos=lax.broadcasted_iota(jnp.int32,(length,1),0)
    dbq_o[...]=jnp.zeros_like(dbq_o); dbv_o[...]=jnp.zeros_like(dbv_o)
    d_o[:,3*width:]=dob[...]
    def chain(s,_):
        r=pl.ds(pl.multiple_of(s*length,32),length)
        live=pos<lens[s]
        for p in range(H//2):
            c=slice(128*p,128*p+128)
            qp=q[r,c]; kp=k[r,c]; vp=v[r,c]; dp=dm[r,c]
            dq=[];dk=[];dv=[]
            for h in range(2):
                sel=low if h==0 else ~low
                kh=jnp.where(sel,kp,jnp.zeros_like(kp)); vh=jnp.where(sel,vp,jnp.zeros_like(vp))
                st=nt(kh,qp)
                st=jnp.where(live,st,-1e9)
                pt=jnp.exp(st-lse[s,pl.ds(2*p+h,1),:])
                dpt=nt(vh,dp)
                delta=jnp.sum(pt*dpt,0,keepdims=True)
                ds=(pt*(dpt-delta)).astype(bf16)
                dv.append(nn(pt.astype(bf16),dp))
                dk.append(nn(ds,qp))
                dq.append(tn(ds,kp))
            dqb=(jnp.where(low,dq[0],dq[1])*0.125).astype(bf16)
            dvb=jnp.where(low,dv[0],dv[1]).astype(bf16)
            d_o[r,128*p:128*p+128]=dqb
            d_o[r,width+128*p:width+128*p+128]=jnp.where(low,dk[0],dk[1]).astype(bf16)
            d_o[r,2*width+128*p:2*width+128*p+128]=dvb
            dbq_o[:,c]+=jnp.sum(dqb.astype(f32),0,keepdims=True)
            dbv_o[:,c]+=jnp.sum(dvb.astype(f32),0,keepdims=True)
        return 0
    lax.fori_loop(0,seqs,chain,0)

def attn_bwd(lens,q,k,v,dm,lse,dob):
    rows,width=q.shape
    sd=jax.ShapeDtypeStruct
    vm=pl.BlockSpec(memory_space=pltpu.VMEM); sm=pl.BlockSpec(memory_space=pltpu.SMEM)
    return pl.pallas_call(attn_bwd_kernel,in_specs=[sm]+[vm]*6,out_specs=[vm]*3,
        out_shape=[sd((rows,4*width),bf16),sd((1,width),f32),sd((1,width),f32)],compiler_params=cp(),name="attn_bwd")(lens,q,k,v,dm,lse,dob)

def dx_kernel(dh1,d,wq,wk,wv,o):
    width=dh1.shape[1]
    def blk(n,_):
        c=pl.ds(pl.multiple_of(n*256,256),256)
        o[:,c]=dh1[:,c]+nt(d[:,0:width],wq[c,:])+nt(d[:,width:2*width],wk[c,:])+nt(d[:,2*width:3*width],wv[c,:])
        return 0
    lax.fori_loop(0,width//256,blk,0)
def dx_call(dh1,d,wq,wk,wv):
    vm=pl.BlockSpec(memory_space=pltpu.VMEM)
    return pl.pallas_call(dx_kernel,in_specs=[vm]*5,out_specs=vm,out_shape=jax.ShapeDtypeStruct(dh1.shape,f32),compiler_params=cp(),name="dx")(dh1,d,wq,wk,wv)

CHUNK = 384
COLORS = 3


def bit(value, name):
    return (value >> "xya".index(name)) & 1


def lhs_of(kind, me, step, refs):
    if kind == "attn":
        return jnp.where((step ^ me[1]) >= 6, refs[1][...], refs[0][...])
    return refs[0][...]


def send_kernel(kind, me, *refs):
    step = pl.program_id(0)
    rhs, out = refs[-2:]
    grad = tn(lhs_of(kind, me, step, refs), rhs[...]).astype(bf16)
    part = grad.shape[0] // 2
    for t in range(2):
        out[0, t ^ me[2]] = grad[t * part : (t + 1) * part]


def keep_kernel(kind, orders, me, *refs):
    step = pl.program_id(0)
    n_in = 4 if kind == "attn" else 3
    rhs, got = refs[n_in - 2 : n_in]
    outs = refs[n_in:]
    grad = tn(lhs_of(kind, me, step, refs), rhs[...])
    part = grad.shape[0] // 2
    piece = part // len(orders)
    for t in range(2):
        rel = t ^ me[2]
        total = (grad[t * part : (t + 1) * part] + got[0, rel].astype(f32)).astype(bf16)
        for n, order in enumerate(orders):
            where = bit(step, order[1]) * 4 + bit(step, order[2]) * 2 + rel
            first = bit(step, order[0])
            value = total[n * piece : (n + 1) * piece]

            @pl.when(first == 0)
            def _():
                outs[2 * n][where] = value

            @pl.when(first == 1)
            def _():
                outs[2 * n + 1][where] = value


def grad_specs(kind, rows, flip):
    chunk = lambda s, me: (0, s ^ me[1])
    half = lambda s, me: (0, me[0] ^ flip)
    block = (rows, CHUNK)
    if kind == "outer":
        return [pl.BlockSpec(block, chunk), pl.BlockSpec(block, half)]
    if kind == "inner":
        return [pl.BlockSpec(block, half), pl.BlockSpec(block, chunk)]
    return [pl.BlockSpec(block, half), pl.BlockSpec(block, half), pl.BlockSpec(block, chunk)]


def grad_send(kind, me, args):
    rows = args[0].shape[0]
    part = CHUNK // 2
    return pl.pallas_call(
        functools.partial(send_kernel, kind),
        grid_spec=pltpu.PrefetchScalarGridSpec(
            num_scalar_prefetch=1,
            grid=(8,),
            in_specs=grad_specs(kind, rows, 1),
            out_specs=pl.BlockSpec((1, 2, part, CHUNK), lambda s, me: (s, 0, 0, 0)),
        ),
        out_shape=jax.ShapeDtypeStruct((8, 2, part, CHUNK), bf16),
        compiler_params=cp(),
        name="send_" + kind,
    )(me, *args)


def grad_keep(kind, me, args, got, orders):
    rows = args[0].shape[0]
    part = CHUNK // 2
    shape = (8, part // len(orders), CHUNK)
    return pl.pallas_call(
        functools.partial(keep_kernel, kind, orders),
        grid_spec=pltpu.PrefetchScalarGridSpec(
            num_scalar_prefetch=1,
            grid=(8,),
            in_specs=grad_specs(kind, rows, 0)
            + [pl.BlockSpec((1, 2, part, CHUNK), lambda s, me: (s, 0, 0, 0))],
            out_specs=[pl.BlockSpec(shape, lambda s, me: (0, 0, 0))] * (2 * len(orders)),
        ),
        out_shape=[jax.ShapeDtypeStruct(shape, bf16)] * (2 * len(orders)),
        compiler_params=cp(),
        name="keep_" + kind,
    )(me, *args, got)


def unpack_kernel(kind, orders, me, *refs):
    chunk = pl.program_id(0)
    step = chunk ^ me[1]
    ins = refs[: 4 * len(orders)]
    outs = refs[4 * len(orders) :]
    part = CHUNK // 2
    piece = part // len(orders)

    def fill(out):
        for n, order in enumerate(orders):
            own0, got0, own1, got1 = ins[4 * n : 4 * n + 4]
            first = bit(step, order[0]) == 1
            for t in range(2):
                where = bit(step, order[1]) * 4 + bit(step, order[2]) * 2 + (t ^ me[2])
                near = jnp.where(first, got0[where], own0[where])
                far = jnp.where(first, got1[where], own1[where])
                for half in range(2):
                    value = jnp.where(half == me[0], near, far).astype(f32)
                    row = t * part + n * piece
                    if kind == "outer":
                        out[row : row + piece, half * CHUNK : (half + 1) * CHUNK] = value
                    else:
                        row = row + half * CHUNK
                        out[row : row + piece, :] = value

    if kind == "attn":
        for mat in range(4):

            @pl.when(chunk // 2 == mat)
            def _():
                fill(outs[mat])
    else:
        fill(outs[0])


def unpack(kind, me, pieces, orders):
    width = 2 * CHUNK
    shape = (8, CHUNK // 2 // len(orders), CHUNK)
    if kind == "outer":
        out_specs = [pl.BlockSpec((CHUNK, width), lambda c, me: (c, 0))]
        out_shape = [jax.ShapeDtypeStruct((8 * CHUNK, width), f32)]
    elif kind == "inner":
        out_specs = [pl.BlockSpec((width, CHUNK), lambda c, me: (0, c))]
        out_shape = [jax.ShapeDtypeStruct((width, 8 * CHUNK), f32)]
    else:
        out_specs = [
            pl.BlockSpec((width, CHUNK), lambda c, me, m=m: (0, jnp.clip(c - 2 * m, 0, 1)))
            for m in range(4)
        ]
        out_shape = [jax.ShapeDtypeStruct((width, width), f32)] * 4
    return pl.pallas_call(
        functools.partial(unpack_kernel, kind, orders),
        grid_spec=pltpu.PrefetchScalarGridSpec(
            num_scalar_prefetch=1,
            grid=(8,),
            in_specs=[pl.BlockSpec(shape, lambda c, me: (0, 0, 0))] * (4 * len(orders)),
            out_specs=out_specs,
        ),
        out_shape=out_shape,
        compiler_params=cp(),
        name="unpack_" + kind,
    )(me, *pieces)


AXES = ("dp", "seq")
DP_BIT = {"x": 0, "y": 1, "a": 2, "b": 3}


def swap(value, name):
    dp = lax.axis_size("dp")
    seq = lax.axis_size("seq")
    flip = 1 if name == "c" else seq << (name if isinstance(name, int) else DP_BIT[name])
    return lax.ppermute(value, AXES, [(i, i ^ flip) for i in range(dp * seq)])


def scatter_sum(keep, send, order):
    for n, name in enumerate(order):
        got = swap(send, name)
        if n + 1 < len(order):
            half = keep.shape[0] // 2
            keep, send = keep[:half] + got[:half], keep[half:] + got[half:]
        else:
            keep = keep + got
    own = keep
    for extra in range(4, lax.axis_size("dp").bit_length() - 1):
        own = own + swap(own, extra)
    return own


def gather(own, order):
    for n, name in enumerate(reversed(order)):
        got = swap(own, name)
        if n + 1 < len(order):
            own = jnp.concatenate([own, got])
    return own, got


ORDERS = {
    "outer": ("xyab", "yxab", "axyb"),
    "inner": ("xyab", "yxab", "ayxb"),
    "attn": ("xyab", "yxab", "axyb"),
}


def reduce_group(kind, me, args):
    orders = ORDERS[kind]
    got = swap(grad_send(kind, me, args), "c")
    blocks = grad_keep(kind, me, args, got, orders)
    pieces = []
    for n, order in enumerate(orders):
        own = scatter_sum(blocks[2 * n], blocks[2 * n + 1], order)
        own0, got0 = gather(own, order)
        pieces += [own0, got0, swap(own0, "c"), swap(got0, "c")]
    return unpack(kind, me, pieces, orders)


def body(chains_in, lengths, d_out, w_query, b_query, w_key, w_value, b_value, w_output, b_output, gain_one, shift_one,
         w_inner, b_inner, w_outer, b_outer, gain_two, shift_two):
    seqs, length, width = chains_in.shape
    rows = seqs * length
    place = lax.axis_index("dp") * 2 + lax.axis_index("seq")
    me = (place >> jnp.array([0, 1, 4], jnp.int32)) & jnp.array([1, 7, 1], jnp.int32)
    x = chains_in.reshape(rows, width)
    row = lambda v: v.reshape(1, -1)
    q, k, v, mixed, xhat, rstd, lse = attn_fwd(
        lengths, x, w_query, row(b_query), w_key, w_value, row(b_value), w_output, row(b_output)
    )
    fin, hid, slope, out, dffn, dh2, dg2, ds2, dbo2 = ffn_fwd(
        lengths, xhat, row(gain_one), row(shift_one), w_inner, row(b_inner), w_outer, row(b_outer),
        row(gain_two), row(shift_two), d_out.reshape(rows, width),
    )
    (d_w_outer,) = reduce_group("outer", me, (hid, dffn))
    dpre, dbi, dh1, dob, dmix, dg1, ds1, dbo1 = ffn_bwd(
        dffn, w_outer, slope, w_inner, dh2, xhat, rstd, row(gain_one), w_output
    )
    (d_w_inner,) = reduce_group("inner", me, (fin, dpre))
    d, dbq, dbv = attn_bwd(lengths, q, k, v, dmix, lse, dob)
    d_w_query, d_w_key, d_w_value, d_w_output = reduce_group("attn", me, (x, mixed, d))
    small = [dbq[0], dbv[0], dbo1[0], dg1[0], ds1[0], dbi[0], dbo2[0], dg2[0], ds2[0]]
    sums = lax.psum(jnp.concatenate(small), AXES)
    cuts = []
    start = 0
    for value in small:
        cuts.append(sums[start : start + value.size])
        start += value.size
    d_x = dx_call(dh1, d, w_query, w_key, w_value)
    return (
        out.reshape(seqs, length, width), d_x.reshape(seqs, length, width),
        d_w_query, cuts[0], d_w_key, d_w_value, cuts[1], d_w_output, cuts[2], cuts[3], cuts[4],
        d_w_inner, cuts[5], d_w_outer, cuts[6], cuts[7], cuts[8],
    )


def solution(mesh):
    rows = P(AXES, None, None)
    return jax.shard_map(
        body, mesh=mesh, in_specs=(rows, P(AXES), rows) + (P(),) * 15, out_specs=(rows, rows) + (P(),) * 15, check_vma=False
    )
```

time: 1150 us -> 406 us (0.35)
  waiting for transfers between devices: 864 us -> 63.4 us
  Pallas kernels: 0 us -> 175 us
  matrix products: 120 us -> 0 us
  starting transfers between devices: 0.48 us -> 87 us
  local copies, waits for them, and re-layouts: 60.8 us -> 27.1 us
  other arithmetic: 38.7 us -> 10.6 us
  between operations: 15.3 us -> 1.6 us
    reduce_scatter x6 -> x0, waiting for transfers between devices: 577 us -> none  [body(): lax.psum_scatter(grad.astype(low_type), ('dp', 'seq'), scatter_dimension=...]
    all_gather x6 -> x0, waiting for transfers between devices: 287 us -> none  [body(): lax.all_gather(part, ('dp', 'seq'), axis=0, tiled=True).astype(f32)]
    pallas_call x0 -> x14, Pallas kernels: none -> 175 us  [the longest x3 29.8 us: grad_keep(): pl.pallas_call(functools.partial(keep_kernel, kind, orders), grid_spec=pl...]
    dot_general x24 -> x0, matrix products: 120 us -> none  [the longest x6 32.1 us: over_rows(): lax.dot_general(left, right, (((0,), (0,)), ((), ())), preferred_element_...]
    ppermute x0 -> x93, starting transfers between devices: none -> 87 us  [swap(): return lax.ppermute(value, AXES, [(i, i ^ flip) for i in range(dp * seq)])]
    ppermute x0 -> x93, waiting for transfers between devices: none -> 63.4 us  [swap(): return lax.ppermute(value, AXES, [(i, i ^ flip) for i in range(dp * seq)])]
    convert_element_type x8 -> x0, other arithmetic: 30.6 us -> none  [the longest x6 25.6 us: body(): lax.all_gather(part, ('dp', 'seq'), axis=0, tiled=True).astype(f32)]
    another operation x6 -> x0, local copies, waits for them, and re-layouts: 20.5 us -> none  [the longest x2 7.19 us: body(): v_heads = values.reshape(seqs, length, H, size)]
  transfers between devices with their start and end apart: 12 -> 93, of which waited for: 12 -> 34; matrix products, arithmetic and copies ran while one was open for 7% -> 6% of each run, Pallas kernels for 0% -> 22%
where the time goes in v2:
time: 406 us; the launch traced here: 404 us
  Pallas kernels  175 us (43%)
  starting transfers between devices  87 us (21%)
  waiting for transfers between devices  63.4 us (16%)
  blocking collectives  39.3 us (10%)
  local copies, waits for them, and re-layouts  27.1 us (7%)
  other arithmetic  10.6 us (3%)
    ppermute x93, starting transfers between devices, swap(): return lax.ppermute(value, AXES, [(i, i ^ flip) for i in range(dp * seq)])  87 us
    ppermute x93, waiting for transfers between devices, swap(): return lax.ppermute(value, AXES, [(i, i ^ flip) for i in range(dp * seq)])  63.4 us
    psum x1, blocking collectives, body(): sums = lax.psum(jnp.concatenate(small), AXES)  39.3 us
    pallas_call x3, Pallas kernels, grad_keep(): pl.pallas_call(functools.partial(keep_kernel, kind, orders), grid_spec=pl...  29.8 us
    pallas_call x1, Pallas kernels, ffn_fwd(): pl.pallas_call(ffn_fwd_kernel, grid_spec=pltpu.PrefetchScalarGridSpec(num...  27.9 us
    pallas_call x3, Pallas kernels, grad_send(): pl.pallas_call(functools.partial(send_kernel, kind), grid_spec=pltpu.Pref...  26.2 us
    pallas_call x3, Pallas kernels, unpack(): pl.pallas_call(functools.partial(unpack_kernel, kind, orders), grid_spec=...  24.8 us
    pallas_call x1, Pallas kernels, ffn_bwd(): pl.pallas_call(ffn_bwd_kernel, grid=(ff // FB,), in_specs=[full(dffn), pl...  23.3 us
  transfers between devices with their start and end apart: 93, of which 34 were waited for; matrix products, arithmetic and copies ran while one was open for 6% of the time, Pallas kernels for 22%

profile of v2, /device:TPU:0, one launch (start us, length us, event | category | flops | bytes accessed | tf_op | source)
XLA Modules:
  0.0 403.6 jit_solution(9812332445924963968)
XLA Ops:
  12.0 16.0 %attn_fwd.1 = (bf16[640,768]{1,0:T(8,128)(2,1)}, bf16[640,768]{1,0:T(8,128)(2,1)}, bf16[640,768]{1,0:T(8,128)(2,1)}, bf16[640,768]{1,0:T(8,128)(2,1)}, f32[640,7...) custom-call(s32[4]{0:T(128)} %lens.5, bf16[640,768]{1,0:T(8,128)(2,1)} %bitcast.6, bf16[768,768]{1,0:T(8,128)(2,1)} %wq.3, ...), custom_call_target="tpu_custom_call" | custom-call | tf_op jit(solution)/shard_map/attn_fwd/pallas_call | solution.py:71
  28.0 27.9 %ffn_fwd.1 = (bf16[640,768]{1,0:T(8,128)(2,1)}, bf16[640,3072]{1,0:T(8,128)(2,1)}, bf16[640,3072]{1,0:T(8,128)(2,1)}, bf16[640,768]{1,0:T(8,128)(2,1)}, bf16[640...) custom-call(s32[4]{0:T(128)} %lens.5, ...), custom_call_target="tpu_custom_call" | custom-call | tf_op jit(solution)/shard_map/ffn_fwd/pallas_call | solution.py:141
  55.9 23.3 %ffn_bwd.1 = (bf16[640,3072]{1,0:T(8,128)(2,1)}, f32[1,3072]{1,0:T(1,128)}, f32[640,768]{1,0:T(8,128)}, bf16[640,768]{1,0:T(8,128)(2,1)}, bf16[640,768]{1,0:T(8,...) custom-call(bf16[640,768]{1,0:T(8,128)(2,1)} %get-tuple-element.68.dffn.refs_1_, ...), custom_call_target="tpu_custom_call" | custom-call | tf_op jit(solution)/shard_map/ffn_bwd/pallas_call | solution.py:192
  79.2 8.7 %send_inner.1 = bf16[8,2,192,384]{3,2,1,0:T(8,128)(2,1)} custom-call(s32[3]{0:T(128)} %shift-right-arithmetic_and_fusion.me, bf16[640,768]{1,0:T(8,128)(2,1)} %get-tuple-element.100.refs_0_, bf16[640,3072]{1,0:T(8,128)(2,1)} %get-tuple-element.101.refs_1_), custom_call_target="tpu_custom_call" | custom-call | tf_op jit(solution)/shard_map/send_inner/pallas_call | solution.py:313
  88.4 18.7 %attn_bwd.1 = (bf16[640,3072]{1,0:T(8,128)(2,1)}, f32[1,768]{1,0:T(1,128)}, f32[1,768]{1,0:T(1,128)}) custom-call(s32[4]{0:T(128)} %lens.5, bf16[640,768]{1,0:T(8,128)(2,1)} %get-tuple-element.73.q, bf16[640,768]{1,0:T(8,128)(2,1)} %get-tuple-element.74.k, bf16[640,768]{1,0:T(8,128)(2,1)} %get-tuple-element.75.v, bf16[640,768]{1,0:T(8,128)(2,1)} %get-tuple-element.76.dm, ...), custom_call_target="tpu_custom_call" | custom-call | tf_op jit(solution)/shard_map/attn_bwd/pallas_call | solution.py:237
  107.0 8.9 %send_attn.1 = bf16[8,2,192,384]{3,2,1,0:T(8,128)(2,1)} custom-call(s32[3]{0:T(128)} %shift-right-arithmetic_and_fusion.me, bf16[640,768]{1,0:T(8,128)(2,1)} %bitcast.7, bf16[640,768]{1,0:T(8,128)(2,1)} %get-tuple-element.80.refs_1_, bf16[640,3072]{1,0:T(8,128)(2,1)} %get-tuple-element.79.d.refs_2_), custom_call_target="tpu_custom_call" | custom-call | tf_op jit(solution)/shard_map/send_attn/pallas_call | solution.py:313
  115.9 8.7 %send_outer.1 = bf16[8,2,192,384]{3,2,1,0:T(8,128)(2,1)} custom-call(s32[3]{0:T(128)} %shift-right-arithmetic_and_fusion.me, bf16[640,3072]{1,0:T(8,128)(2,1)} %get-tuple-element.108.refs_0_, bf16[640,768]{1,0:T(8,128)(2,1)} %get-tuple-element.68.dffn.refs_1_), custom_call_target="tpu_custom_call" | custom-call | tf_op jit(solution)/shard_map/send_outer/pallas_call | solution.py:313
  125.1 9.8 %keep_inner.1 = (bf16[8,64,384]{2,1,0:T(8,128)(2,1)}, bf16[8,64,384]{2,1,0:T(8,128)(2,1)}, bf16[8,64,384]{2,1,0:T(8,128)(2,1)}, bf16[8,64,384]{2,1,0:T(8,128)(2,...) custom-call(s32[3]{0:T(128)} %shift-right-arithmetic_and_fusion.me, ...), custom_call_target="tpu_custom_call" | custom-call | tf_op jit(solution)/shard_map/keep_inner/pallas_call | solution.py:331
  140.5 10.1 %keep_attn.1 = (bf16[8,64,384]{2,1,0:T(8,128)(2,1)}, bf16[8,64,384]{2,1,0:T(8,128)(2,1)}, bf16[8,64,384]{2,1,0:T(8,128)(2,1)}, bf16[8,64,384]{2,1,0:T(8,128)(2,1...) custom-call(s32[3]{0:T(128)} %shift-right-arithmetic_and_fusion.me, bf16[640,768]{1,0:T(8,128)(2,1)} %bitcast.8, ...), custom_call_target="tpu_custom_call" | custom-call | tf_op jit(solution)/shard_map/keep_attn/pallas_call | solution.py:331
  152.5 9.8 %keep_outer.1 = (bf16[8,64,384]{2,1,0:T(8,128)(2,1)}, bf16[8,64,384]{2,1,0:T(8,128)(2,1)}, bf16[8,64,384]{2,1,0:T(8,128)(2,1)}, bf16[8,64,384]{2,1,0:T(8,128)(2,...) custom-call(s32[3]{0:T(128)} %shift-right-arithmetic_and_fusion.me, ...), custom_call_target="tpu_custom_call" | custom-call | tf_op jit(solution)/shard_map/keep_outer/pallas_call | solution.py:331
  171.0 3.8 collective-permute-done.21
  188.1 3.6 collective-permute-done.2
  214.8 3.1 collective-permute-done.45
  239.4 4.0 collective-permute-start.37
  272.2 10.3 %collective-permute-done.79 = bf16[4,64,384]{2,1,0:T(8,128)(2,1)S(1)} collective-permute-done((bf16[4,64,384]{2,1,0:T(8,128)(2,1)S(1)}, bf16[4,64,384]{2,1,0:T(8,128)(2,1)S(1)}, u32[]{:S(2)}, u32[]{:S(2)}) %collective-permute-start.79) | collective-permute-done | bytes 196640 | tf_op jit(solution)/shard_map/ppermute | solution.py:418
  287.3 3.5 collective-permute-done.49.refs_5_
  291.7 4.8 %collective-permute-done.59.refs_9_ = bf16[8,64,384]{2,1,0:T(8,128)(2,1)S(1)} collective-permute-done((bf16[8,64,384]{2,1,0:T(8,128)(2,1)S(1)}, bf16[8,64,384]{2,1,0:T(8,128)(2,1)S(1)}, u32[]{:S(2)}, u32[]{:S(2)}) %collective-permute-start.59) | collective-permute-done | bytes 393248 | tf_op jit(solution)/shard_map/ppermute | solution.py:418
  300.9 3.6 collective-permute-done.28.refs_9_
  305.2 3.0 collective-permute-done.70.refs_1_
  328.9 7.9 %dx.1 = f32[640,768]{1,0:T(8,128)} custom-call(f32[640,768]{1,0:T(8,128)} %get-tuple-element.72.dh1, bf16[640,3072]{1,0:T(8,128)(2,1)} %get-tuple-element.79.d.refs_2_, bf16[768,768]{1,0:T(8,128)(2,1)} %wq.3, bf16[768,768]{1,0:T(8,128)(2,1)} %wk.3, bf16[768,768]{1,0:T(8,128)(2,1)} %wv.3), custom_call_target="tpu_custom_call" | custom-call | tf_op jit(solution)/shard_map/dx/pallas_call | solution.py:249
  338.1 39.3 %psum.7 = f32[9216]{0:T(1024)S(1)} all-reduce(f32[9216]{0:T(1024)} %constant_dynamic-update-slice_fusion), channel_id=1, replica_groups=mesh['dp'=16,'seq'=2] {'dp','seq'}, use_global_device_ids=true, to_apply=%region_0.0 | all-reduce | flops 9216 | bytes 73728 | tf_op jit(solution)/shard_map/psum | solution.py:485
  378.7 7.8 %unpack_outer.1 = f32[3072,768]{1,0:T(8,128)} custom-call(s32[3]{0:T(128)} %shift-right-arithmetic_and_fusion.me, bf16[8,64,384]{2,1,0:T(8,128)(2,1)} %copy-done.4, bf16[8,64,384]{2,1,0:T(8,128)(2,1)} %copy-done.16, bf16[8,64,384]{2,1,0:T(8,128)(2,1)} %copy-done.15, bf16[8,64,384]{2,1,0:T(8,128)(2,1)} %collective-permute-done.72.refs_3_, ...), custom_call_target="tpu_custom_call" | custom-call | tf_op jit(solution)/shard_map/unpack_outer/pallas_call | solution.py:396
  386.6 7.8 %unpack_inner.1 = f32[768,3072]{1,0:T(8,128)} custom-call(s32[3]{0:T(128)} %shift-right-arithmetic_and_fusion.me, bf16[8,64,384]{2,1,0:T(8,128)(2,1)} %copy-done.1, bf16[8,64,384]{2,1,0:T(8,128)(2,1)} %collective-permute-done.39.refs_1_, bf16[8,64,384]{2,1,0:T(8,128)(2,1)} %copy-done.10, bf16[8,64,384]{2,1,0:T(8,128)(2,1)} %collective-permute-done.41.refs_3_, ...), custom_call_target="tpu_custom_call" | custom-call | tf_op jit(solution)/shard_map/unpack_inner/pallas_call | solution.py:396
  394.4 9.1 %unpack_attn.1 = (f32[768,768]{1,0:T(8,128)}, f32[768,768]{1,0:T(8,128)}, f32[768,768]{1,0:T(8,128)}, f32[768,768]{1,0:T(8,128)}) custom-call(s32[3]{0:T(128)} %shift-right-arithmetic_and_fusion.me, bf16[8,64,384]{2,1,0:T(8,128)(2,1)} %copy-done.7, bf16[8,64,384]{2,1,0:T(8,128)(2,1)} %copy-done.20, bf16[8,64,384]{2,1,0:T(8,128)(2,1)} %copy-done.19, ...), custom_call_target="tpu_custom_call" | custom-call | tf_op jit(solution)/shard_map/unpack_attn/pallas_call | solution.py:396
  (341 shorter events, 148.4 us)
Async XLA Ops:
  87.9 37.2 %collective-permute-start.31 = (bf16[8,2,192,384]{3,2,1,0:T(8,128)(2,1)}, bf16[8,2,192,384]{3,2,1,0:T(8,128)(2,1)}, u32[]{:S(2)}, u32[]{:S(2)}) collective-permute-start(bf16[8,2,192,384]{3,2,1,0:T(8,128)(2,1)} %send_inner.1), channel_id=1, source_target_pairs={{0,1},{1,0},{2,3},{3,2},{4,5},{5,4},{6,7},{7,6},{8,9},{9,8},{10,11... | collective-permute-start | bytes 7077896 | tf_op jit(solution)/shard_map/ppermute | solution.py:418
  115.9 24.6 %collective-permute-start = (bf16[8,2,192,384]{3,2,1,0:T(8,128)(2,1)}, bf16[8,2,192,384]{3,2,1,0:T(8,128)(2,1)}, u32[]{:S(2)}, u32[]{:S(2)}) collective-permute-start(bf16[8,2,192,384]{3,2,1,0:T(8,128)(2,1)} %send_attn.1), channel_id=1, source_target_pairs={{0,1},{1,0},{2,3},{3,2},{4,5},{5,4},{6,7},{7,6},{8,9},{9,8},{10,11... | collective-permute-start | bytes 7077896 | tf_op jit(solution)/shard_map/ppermute | solution.py:418
  124.6 26.5 %collective-permute-start.62 = (bf16[8,2,192,384]{3,2,1,0:T(8,128)(2,1)}, bf16[8,2,192,384]{3,2,1,0:T(8,128)(2,1)S(1)}, u32[]{:S(2)}, u32[]{:S(2)}) collective-permute-start(bf16[8,2,192,384]{3,2,1,0:T(8,128)(2,1)} %send_outer.1), channel_id=1, source_target_pairs={{0,1},{1,0},{2,3},{3,2},{4,5},{5,4},{6,7},{7,6},{8,9},{9,8},{10,11... | collective-permute-start | bytes 7077896 | tf_op jit(solution)/shard_map/ppermute | solution.py:418
  134.9 27.5 %collective-permute-start.32 = (bf16[8,64,384]{2,1,0:T(8,128)(2,1)}, bf16[8,64,384]{2,1,0:T(8,128)(2,1)}, u32[]{:S(2)}, u32[]{:S(2)}) collective-permute-start(bf16[8,64,384]{2,1,0:T(8,128)(2,1)} %get-tuple-element.103), channel_id=1, source_target_pairs={{0,2},{1,3},{2,0},{3,1},{4,6},{5,7},{6,4},{7,5},{8,10},{9,11},{10,... | collective-permute-start | bytes 1179656 | tf_op jit(solution)/shard_map/ppermute | solution.py:418
  137.4 26.8 %collective-permute-start.42 = (bf16[8,64,384]{2,1,0:T(8,128)(2,1)}, bf16[8,64,384]{2,1,0:T(8,128)(2,1)}, u32[]{:S(2)}, u32[]{:S(2)}) collective-permute-start(bf16[8,64,384]{2,1,0:T(8,128)(2,1)} %get-tuple-element.105), channel_id=1, source_target_pairs={{0,4},{1,5},{2,6},{3,7},{4,0},{5,1},{6,2},{7,3},{8,12},{9,13},{10,... | collective-permute-start | bytes 1179656 | tf_op jit(solution)/shard_map/ppermute | solution.py:418
  138.9 28.0 %collective-permute-start.52 = (bf16[8,64,384]{2,1,0:T(8,128)(2,1)}, bf16[8,64,384]{2,1,0:T(8,128)(2,1)S(1)}, u32[]{:S(2)}, u32[]{:S(2)}) collective-permute-start(bf16[8,64,384]{2,1,0:T(8,128)(2,1)} %get-tuple-element.107), channel_id=1, source_target_pairs={{0,8},{1,9},{2,10},{3,11},{4,12},{5,13},{6,14},{7,15},{8,0},{9,1},... | collective-permute-start | bytes 1179656 | tf_op jit(solution)/shard_map/ppermute | solution.py:418
  150.6 17.1 %collective-permute-start.1 = (bf16[8,64,384]{2,1,0:T(8,128)(2,1)}, bf16[8,64,384]{2,1,0:T(8,128)(2,1)S(1)}, u32[]{:S(2)}, u32[]{:S(2)}) collective-permute-start(bf16[8,64,384]{2,1,0:T(8,128)(2,1)} %get-tuple-element.82), channel_id=1, source_target_pairs={{0,2},{1,3},{2,0},{3,1},{4,6},{5,7},{6,4},{7,5},{8,10},{9,11},{10,... | collective-permute-start | bytes 1179656 | tf_op jit(solution)/shard_map/ppermute | solution.py:418
  151.1 18.3 %collective-permute-start.11 = (bf16[8,64,384]{2,1,0:T(8,128)(2,1)}, bf16[8,64,384]{2,1,0:T(8,128)(2,1)S(1)}, u32[]{:S(2)}, u32[]{:S(2)}) collective-permute-start(bf16[8,64,384]{2,1,0:T(8,128)(2,1)} %get-tuple-element.84), channel_id=1, source_target_pairs={{0,4},{1,5},{2,6},{3,7},{4,0},{5,1},{6,2},{7,3},{8,12},{9,13},{10,... | collective-permute-start | bytes 1179656 | tf_op jit(solution)/shard_map/ppermute | solution.py:418
  167.7 13.8 %collective-permute-start.83 = (bf16[8,64,384]{2,1,0:T(8,128)(2,1)S(1)}, bf16[8,64,384]{2,1,0:T(8,128)(2,1)S(1)}, u32[]{:S(2)}, u32[]{:S(2)}) collective-permute-start(bf16[8,64,384]{2,1,0:T(8,128)(2,1)S(1)} %copy-done.34), channel_id=1, source_target_pairs={{0,8},{1,9},{2,10},{3,11},{4,12},{5,13},{6,14},{7,15},{8,0},{9,1},... | collective-permute-start | bytes 1179656 | tf_op jit(solution)/shard_map/ppermute | solution.py:418
  169.4 13.8 %collective-permute-start.33 = (bf16[4,64,384]{2,1,0:T(8,128)(2,1)S(1)}, bf16[4,64,384]{2,1,0:T(8,128)(2,1)S(1)}, u32[]{:S(2)}, u32[]{:S(2)}) collective-permute-start(bf16[4,64,384]{2,1,0:T(8,128)(2,1)S(1)} %get-tuple-element.126), channel_id=1, source_target_pairs={{0,4},{1,5},{2,6},{3,7},{4,0},{5,1},{6,2},{7,3},{8,12},{9,13},{10,... | collective-permute-start | bytes 589832 | tf_op jit(solution)/shard_map/ppermute | solution.py:418
  262.1 22.5 %collective-permute-start.40 = (bf16[8,64,384]{2,1,0:T(8,128)(2,1)S(1)}, bf16[8,64,384]{2,1,0:T(8,128)(2,1)S(1)}, u32[]{:S(2)}, u32[]{:S(2)}) collective-permute-start(bf16[8,64,384]{2,1,0:T(8,128)(2,1)S(1)} %pad_maximum_fusion.3.refs_0_), channel_id=1, source_target_pairs={{0,1},{1,0},{2,3},{3,2},{4,5},{5,4},{6,7},{7,6},{8,9},{9,8},{10,11... | collective-permute-start | bytes 1179656 | tf_op jit(solution)/shard_map/ppermute | solution.py:418
  262.1 23.1 %collective-permute-start.39 = (bf16[8,64,384]{2,1,0:T(8,128)(2,1)S(1)}, bf16[8,64,384]{2,1,0:T(8,128)(2,1)}, u32[]{:S(2)}, u32[]{:S(2)}) collective-permute-start(bf16[8,64,384]{2,1,0:T(8,128)(2,1)S(1)} %pad_maximum_fusion.3.refs_0_), channel_id=1, source_target_pairs={{0,2},{1,3},{2,0},{3,1},{4,6},{5,7},{6,4},{7,5},{8,10},{9,11},{10,... | collective-permute-start | bytes 1179656 | tf_op jit(solution)/shard_map/ppermute | solution.py:418
  265.9 16.6 %collective-permute-start.79 = (bf16[4,64,384]{2,1,0:T(8,128)(2,1)S(1)}, bf16[4,64,384]{2,1,0:T(8,128)(2,1)S(1)}, u32[]{:S(2)}, u32[]{:S(2)}) collective-permute-start(bf16[4,64,384]{2,1,0:T(8,128)(2,1)S(1)} %pad_maximum_fusion.16), channel_id=1, source_target_pairs={{0,2},{1,3},{2,0},{3,1},{4,6},{5,7},{6,4},{7,5},{8,10},{9,11},{10,... | collective-permute-start | bytes 589832 | tf_op jit(solution)/shard_map/ppermute | solution.py:418
  270.1 14.4 %collective-permute-start.89 = (bf16[4,64,384]{2,1,0:T(8,128)(2,1)S(1)}, bf16[4,64,384]{2,1,0:T(8,128)(2,1)S(1)}, u32[]{:S(2)}, u32[]{:S(2)}) collective-permute-start(bf16[4,64,384]{2,1,0:T(8,128)(2,1)S(1)} %pad_maximum_fusion.17), channel_id=1, source_target_pairs={{0,2},{1,3},{2,0},{3,1},{4,6},{5,7},{6,4},{7,5},{8,10},{9,11},{10,... | collective-permute-start | bytes 589832 | tf_op jit(solution)/shard_map/ppermute | solution.py:418
  285.7 13.6 %collective-permute-start.8 = (bf16[8,64,384]{2,1,0:T(8,128)(2,1)S(1)}, bf16[8,64,384]{2,1,0:T(8,128)(2,1)S(1)}, u32[]{:S(2)}, u32[]{:S(2)}) collective-permute-start(bf16[8,64,384]{2,1,0:T(8,128)(2,1)S(1)} %pad_maximum_fusion.refs_0_), channel_id=1, source_target_pairs={{0,2},{1,3},{2,0},{3,1},{4,6},{5,7},{6,4},{7,5},{8,10},{9,11},{10,... | collective-permute-start | bytes 1179656 | tf_op jit(solution)/shard_map/ppermute | solution.py:418
  299.3 18.3 %collective-permute-start.81 = (bf16[8,64,384]{2,1,0:T(8,128)(2,1)S(1)}, bf16[8,64,384]{2,1,0:T(8,128)(2,1)}, u32[]{:S(2)}, u32[]{:S(2)}) collective-permute-start(bf16[8,64,384]{2,1,0:T(8,128)(2,1)S(1)} %pad_maximum_fusion.7.refs_4_), channel_id=1, source_target_pairs={{0,1},{1,0},{2,3},{3,2},{4,5},{5,4},{6,7},{7,6},{8,9},{9,8},{10,11... | collective-permute-start | bytes 1179656 | tf_op jit(solution)/shard_map/ppermute | solution.py:418
  299.4 18.7 %collective-permute-start.80 = (bf16[8,64,384]{2,1,0:T(8,128)(2,1)S(1)}, bf16[8,64,384]{2,1,0:T(8,128)(2,1)}, u32[]{:S(2)}, u32[]{:S(2)}) collective-permute-start(bf16[8,64,384]{2,1,0:T(8,128)(2,1)S(1)} %pad_maximum_fusion.7.refs_4_), channel_id=1, source_target_pairs={{0,4},{1,5},{2,6},{3,7},{4,0},{5,1},{6,2},{7,3},{8,12},{9,13},{10,... | collective-permute-start | bytes 1179656 | tf_op jit(solution)/shard_map/ppermute | solution.py:418
  304.6 13.6 %collective-permute-start.91 = (bf16[8,64,384]{2,1,0:T(8,128)(2,1)S(1)}, bf16[8,64,384]{2,1,0:T(8,128)(2,1)}, u32[]{:S(2)}, u32[]{:S(2)}) collective-permute-start(bf16[8,64,384]{2,1,0:T(8,128)(2,1)S(1)} %pad_maximum_fusion.8.refs_8_), channel_id=1, source_target_pairs={{0,1},{1,0},{2,3},{3,2},{4,5},{5,4},{6,7},{7,6},{8,9},{9,8},{10,11... | collective-permute-start | bytes 1179656 | tf_op jit(solution)/shard_map/ppermute | solution.py:418
  304.6 14.0 %collective-permute-start.90 = (bf16[8,64,384]{2,1,0:T(8,128)(2,1)S(1)}, bf16[8,64,384]{2,1,0:T(8,128)(2,1)}, u32[]{:S(2)}, u32[]{:S(2)}) collective-permute-start(bf16[8,64,384]{2,1,0:T(8,128)(2,1)S(1)} %pad_maximum_fusion.8.refs_8_), channel_id=1, source_target_pairs={{0,8},{1,9},{2,10},{3,11},{4,12},{5,13},{6,14},{7,15},{8,0},{9,1},... | collective-permute-start | bytes 1179656 | tf_op jit(solution)/shard_map/ppermute | solution.py:418
  324.4 70.1 %collective-permute-start.19 = (bf16[8,64,384]{2,1,0:T(8,128)(2,1)S(1)}, bf16[8,64,384]{2,1,0:T(8,128)(2,1)}, u32[]{:S(2)}, u32[]{:S(2)}) collective-permute-start(bf16[8,64,384]{2,1,0:T(8,128)(2,1)S(1)} %pad_maximum_fusion.1.refs_4_), channel_id=1, source_target_pairs={{0,1},{1,0},{2,3},{3,2},{4,5},{5,4},{6,7},{7,6},{8,9},{9,8},{10,11... | collective-permute-start | bytes 1179656 | tf_op jit(solution)/shard_map/ppermute | solution.py:418
  325.9 68.5 %collective-permute-start.29 = (bf16[8,64,384]{2,1,0:T(8,128)(2,1)S(1)}, bf16[8,64,384]{2,1,0:T(8,128)(2,1)}, u32[]{:S(2)}, u32[]{:S(2)}) collective-permute-start(bf16[8,64,384]{2,1,0:T(8,128)(2,1)S(1)} %pad_maximum_fusion.2.refs_8_), channel_id=1, source_target_pairs={{0,1},{1,0},{2,3},{3,2},{4,5},{5,4},{6,7},{7,6},{8,9},{9,8},{10,11... | collective-permute-start | bytes 1179656 | tf_op jit(solution)/shard_map/ppermute | solution.py:418
  326.0 68.5 %collective-permute-start.10 = (bf16[8,64,384]{2,1,0:T(8,128)(2,1)}, bf16[8,64,384]{2,1,0:T(8,128)(2,1)}, u32[]{:S(2)}, u32[]{:S(2)}) collective-permute-start(bf16[8,64,384]{2,1,0:T(8,128)(2,1)} %copy-done.20), channel_id=1, source_target_pairs={{0,1},{1,0},{2,3},{3,2},{4,5},{5,4},{6,7},{7,6},{8,9},{9,8},{10,11... | collective-permute-start | bytes 1179656 | tf_op jit(solution)/shard_map/ppermute | solution.py:418
  326.4 68.0 %collective-permute-start.20 = (bf16[8,64,384]{2,1,0:T(8,128)(2,1)}, bf16[8,64,384]{2,1,0:T(8,128)(2,1)}, u32[]{:S(2)}, u32[]{:S(2)}) collective-permute-start(bf16[8,64,384]{2,1,0:T(8,128)(2,1)} %copy-done.21), channel_id=1, source_target_pairs={{0,1},{1,0},{2,3},{3,2},{4,5},{5,4},{6,7},{7,6},{8,9},{9,8},{10,11... | collective-permute-start | bytes 1179656 | tf_op jit(solution)/shard_map/ppermute | solution.py:418
  326.5 68.0 %collective-permute-start.30 = (bf16[8,64,384]{2,1,0:T(8,128)(2,1)}, bf16[8,64,384]{2,1,0:T(8,128)(2,1)}, u32[]{:S(2)}, u32[]{:S(2)}) collective-permute-start(bf16[8,64,384]{2,1,0:T(8,128)(2,1)} %copy-done.22), channel_id=1, source_target_pairs={{0,1},{1,0},{2,3},{3,2},{4,5},{5,4},{6,7},{7,6},{8,9},{9,8},{10,11... | collective-permute-start | bytes 1179656 | tf_op jit(solution)/shard_map/ppermute | solution.py:418
  (105 other events, 1388.5 us)

commit v3 on v1

v3 whole, which is shorter than its diff:
```python
import functools
import jax
import jax.numpy as jnp
from jax import lax
from jax.experimental import pallas as pl
from jax.experimental.pallas import tpu as pltpu
from jax.sharding import PartitionSpec as P

H = 12
EPS = 1e-12
f32 = jnp.float32
bf16 = jnp.bfloat16
sd = jax.ShapeDtypeStruct
HBM = pl.BlockSpec(memory_space=pl.ANY)
VMEM = pl.BlockSpec(memory_space=pltpu.VMEM)
SMEM = pl.BlockSpec(memory_space=pltpu.SMEM)
LIMIT = 60 * 1024 * 1024
CHUNK = 384
HALF = CHUNK // 2


def params():
    return pltpu.CompilerParams(vmem_limit_bytes=LIMIT)


def cost(flops, nbytes=1 << 20):
    return pl.CostEstimate(flops=int(flops), transcendentals=0, bytes_accessed=int(nbytes))


def nn(a, b):
    return lax.dot_general(a, b, (((1,), (0,)), ((), ())), preferred_element_type=f32)


def nt(a, b):
    return lax.dot_general(a, b, (((1,), (1,)), ((), ())), preferred_element_type=f32)


def tn(a, b):
    return lax.dot_general(a, b, (((0,), (0,)), ((), ())), preferred_element_type=f32)


def row_mean(v):
    return jnp.mean(v, -1, keepdims=True)


def ds(start, size, align=None):
    return pl.ds(pl.multiple_of(start, align or size), size)


FWD_IN = ("x", "wq", "wk", "wv", "wo", "wi", "w2", "dout")
FWD_OUT = ("q", "k", "v", "mixed", "xhat", "rstd", "fin", "out", "dffn")


def row(ref):
    return ref[...].reshape(1, ref.shape[0])


def both(low, v):
    zero = jnp.zeros_like(v)
    return jnp.concatenate([jnp.where(low, v, zero), jnp.where(low, zero, v)], 0)


def pairs_of(width, size):
    return [slice(2 * size * p, 2 * size * (p + 1)) for p in range(width // (2 * size))]


def attention(lens, q, k, v, mixed, lse):
    rows, width = q.shape
    seqs = lens.shape[0]
    length = rows // seqs
    size = width // H
    low = lax.broadcasted_iota(jnp.int32, (length, 2 * size), 1) < size
    pos = lax.broadcasted_iota(jnp.int32, (2, length, 1), 1)

    def chain(s, _):
        r = ds(s * length, length, 32)
        live = pos < lens[s]
        cols = pairs_of(width, size)
        scores = [nt(both(low, k[r, c]), q[r, c]) for c in cols]
        for p, c in enumerate(cols):
            st = jnp.where(live, scores[p].reshape(2, length, length), -1e9)
            top = jnp.max(st, 1, keepdims=True)
            e = jnp.exp(st - top)
            total = jnp.sum(e, 1, keepdims=True)
            lse[s, pl.ds(2 * p, 2), :] = (top + jnp.log(total)).reshape(2, length)
            prob = (e * (1.0 / total)).astype(bf16).reshape(2 * length, length)
            mixed[r, c] = tn(prob, both(low, v[r, c])).astype(bf16)
        return 0

    lax.fori_loop(0, seqs, chain, 0)


def put_send(out, grad, base, chunk0, me, rows_are_chunks):
    size = grad.shape[0 if rows_are_chunks else 1]
    for i in range(size // CHUNK):
        for t in range(2):
            if rows_are_chunks:
                value = grad[i * CHUNK + t * HALF : i * CHUNK + (t + 1) * HALF, :]
            else:
                value = grad[t * HALF : (t + 1) * HALF, i * CHUNK : (i + 1) * CHUNK]
            out[((chunk0 + i) ^ me[1]) * 2 + (t ^ me[2]) - base] = value.astype(bf16)


def fwd_kernel(*refs):
    lens, me = refs[:2]
    bq, bv, bo, g1, s1, bi, b2, g2, s2 = refs[2:11]
    src = dict(zip(FWD_IN, refs[11:19]))
    lse, small = refs[19:21]
    dst = dict(zip(FWD_OUT, refs[21:30]))
    hid_h, slope_h, send_h = refs[30:33]
    rest = refs[33:]
    vin = dict(zip(FWD_IN, rest[:8]))
    vout = dict(zip(FWD_OUT, rest[8:17]))
    hid, slope, send, acc, sem_in, sem_out, sem_ff, sem_send = rest[17:]
    rows, width = vin["x"].shape
    ff = vin["wi"].shape[1]
    seqs = lens.shape[0]
    length = rows // seqs

    def load(name):
        return pltpu.make_async_copy(src[name], vin[name], sem_in.at[FWD_IN.index(name)])

    def store(name):
        return pltpu.make_async_copy(vout[name], dst[name], sem_out.at[FWD_OUT.index(name)])

    x, q, k, v, mixed = vin["x"], vout["q"], vout["k"], vout["v"], vout["mixed"]
    for name in ("x", "wq", "wk"):
        load(name).start()
    load("x").wait()
    load("wq").wait()
    load("wv").start()
    load("wo").start()
    q[...] = ((nn(x[...], vin["wq"][...]) + row(bq)).astype(bf16).astype(f32) * 0.125).astype(bf16)
    store("q").start()
    load("wk").wait()
    load("wi").start()
    k[...] = nn(x[...], vin["wk"][...]).astype(bf16)
    store("k").start()
    load("wv").wait()
    load("w2").start()
    load("dout").start()
    v[...] = (nn(x[...], vin["wv"][...]) + row(bv)).astype(bf16)
    store("v").start()
    attention(lens, q, k, v, mixed, lse)
    store("mixed").start()
    load("wo").wait()
    xhat, rstd, fin = vout["xhat"], vout["rstd"], vout["fin"]
    acc[...] = nn(mixed[...], vin["wo"][...])
    R = length
    gain1, shift1, bias_o = row(g1), row(s1), row(bo)

    def norm_one(n, _):
        r = ds(n * R, R, 32)
        h = acc[r, :] + bias_o + x[r, :].astype(f32)
        centre = h - row_mean(h)
        scale = lax.rsqrt(row_mean(centre * centre) + EPS)
        unit = centre * scale
        xhat[r, :] = unit
        rstd[r, :] = scale
        fin[r, :] = (unit * gain1 + shift1).astype(bf16)
        return 0

    lax.fori_loop(0, rows // R, norm_one, 0)
    store("rstd").start()
    store("fin").start()
    store("xhat").start()
    wi, w2 = vin["wi"], vin["w2"]
    load("wi").wait()
    load("w2").wait()
    RB = 320
    part_ff = ff // width

    def ff_copies(n):
        c = ds(n * width, width)
        return (
            pltpu.make_async_copy(hid.at[:, c], hid_h.at[:, c], sem_ff.at[0, n]),
            pltpu.make_async_copy(slope.at[:, c], slope_h.at[:, c], sem_ff.at[1, n]),
        )

    def feed(n, _):
        c = ds(n * width, width)
        bias_i = bi[ds(n * width, width)].reshape(1, width)
        for i in range(rows // RB):
            r = slice(i * RB, (i + 1) * RB)
            u = nn(fin[r, :], wi[:, c]) + bias_i
            cdf = 0.5 * lax.erf(u * 0.7071067811865476) + 0.5
            hid[r, c] = (u * cdf).astype(bf16)
            slope[r, c] = (cdf + u * jnp.exp(-0.5 * (u * u)) * 0.3989422804014327).astype(bf16)
            part = nn(hid[r, c], w2[c, :])
            acc[r, :] = jnp.where(n == 0, part, acc[r, :] + part)
        for one in ff_copies(n):
            one.start()
        return 0

    lax.fori_loop(0, part_ff, feed, 0)
    load("dout").wait()
    dout, out, dffn = vin["dout"], vout["out"], vout["dffn"]
    small[...] = jnp.zeros_like(small)
    gain2, shift2, bias_2 = row(g2), row(s2), row(b2)
    pos = lax.broadcasted_iota(jnp.int32, (R, 1), 0)

    def norm_two(n, _):
        r = ds(n * R, R, 32)
        keep = jnp.where(pos < lens[n], 1.0, 0.0).astype(f32)
        h = xhat[r, :] * gain1 + shift1 + (acc[r, :] + bias_2).astype(bf16).astype(f32)
        centre = h - row_mean(h)
        scale = lax.rsqrt(row_mean(centre * centre) + EPS)
        unit = centre * scale
        out[r, :] = ((unit * gain2 + shift2) * keep).astype(bf16)
        g = dout[r, :].astype(f32) * keep
        e = g * gain2
        low = (scale * (e - row_mean(e) - unit * row_mean(e * unit))).astype(bf16)
        dffn[r, :] = low
        small[0:1, :] += jnp.sum(g * unit, 0, keepdims=True)
        small[1:2, :] += jnp.sum(g, 0, keepdims=True)
        small[2:3, :] += jnp.sum(low.astype(f32), 0, keepdims=True)
        return 0

    lax.fori_loop(0, seqs, norm_two, 0)
    store("dffn").start()
    store("out").start()
    far = ds((1 - me[0]) * CHUNK, CHUNK)

    def send_copy(n):
        part = pl.ds(4 * (n ^ (me[1] >> 1)), 4)
        return pltpu.make_async_copy(send.at[part], send_h.at[part], sem_send.at[n])

    def grads(n, _):
        put_send(send, tn(hid[:, ds(n * width, width)], dffn[:, far]), 0, 2 * n, me, True)
        send_copy(n).start()
        return 0

    lax.fori_loop(0, part_ff, grads, 0)
    for name in FWD_OUT:
        store(name).wait()
    for n in range(part_ff):
        for one in ff_copies(n):
            one.wait()
        send_copy(n).wait()


def forward(lens, me, vectors, arrays):
    rows, width = arrays[0].shape
    ff = arrays[5].shape[1]
    seqs = lens.shape[0]
    like = lambda shape, dtype=bf16: sd(shape, dtype)
    thin = like((rows, width))
    outs = [thin, thin, thin, thin, like((rows, width), f32), like((rows, 1), f32), thin, thin, thin]
    wide = [like((rows, ff)), like((rows, ff)), like((16, HALF, CHUNK))]
    dma = pltpu.SemaphoreType.DMA
    return pl.pallas_call(
        fwd_kernel,
        in_specs=[SMEM, SMEM] + [VMEM] * 9 + [HBM] * 8,
        out_specs=[VMEM, VMEM] + [HBM] * 12,
        out_shape=[like((seqs, H, rows // seqs), f32), like((8, width), f32)] + outs + wide,
        scratch_shapes=[pltpu.VMEM(a.shape, a.dtype) for a in arrays]
        + [pltpu.VMEM(o.shape, o.dtype) for o in outs + wide]
        + [pltpu.VMEM((rows, width), f32), dma((8,)), dma((9,)), dma((2, ff // width)), dma((ff // width,))],
        compiler_params=params(),
        cost_estimate=cost(28e9),
        name="forward",
    )(lens, me, *vectors, *arrays)


def pre_kernel(me, dffn, w2, slope, fin, small2, dpre_o, send_o, small):
    p = pl.program_id(0)
    n = p ^ (me[1] >> 1)

    @pl.when(p == 0)
    def _():
        small[0:8, :] = small2[...]
        small[8:16, :] = jnp.zeros((8, small.shape[1]), f32)

    d = (nt(dffn[...], w2[...]) * slope[...].astype(f32)).astype(bf16)
    dpre_o[...] = d
    small[pl.ds(8 + n, 1), :] = jnp.sum(d.astype(f32), 0, keepdims=True)
    put_send(send_o, tn(fin[...], dpre_o[...]), 4 * p, 2 * n, me, False)


def pre_call(me, dffn, w2, slope, fin, small2):
    rows, width = dffn.shape
    ff = w2.shape[0]
    at = lambda p, me: p ^ (me[1] >> 1)
    return pl.pallas_call(
        pre_kernel,
        grid_spec=pltpu.PrefetchScalarGridSpec(
            num_scalar_prefetch=1,
            grid=(ff // width,),
            in_specs=[
                pl.BlockSpec((rows, width), lambda p, me: (0, 0)),
                pl.BlockSpec((width, width), lambda p, me: (at(p, me), 0)),
                pl.BlockSpec((rows, width), lambda p, me: (0, at(p, me))),
                pl.BlockSpec((rows, CHUNK), lambda p, me: (0, 1 - me[0])),
                pl.BlockSpec((8, width), lambda p, me: (0, 0)),
            ],
            out_specs=[
                pl.BlockSpec((rows, width), lambda p, me: (0, at(p, me))),
                pl.BlockSpec((4, HALF, CHUNK), lambda p, me: (p, 0, 0)),
                pl.BlockSpec((16, width), lambda p, me: (0, 0)),
            ],
        ),
        out_shape=[sd((rows, ff), bf16), sd((16, HALF, CHUNK), bf16), sd((16, width), f32)],
        compiler_params=params(),
        cost_estimate=cost(8e9),
        name="pre_bwd",
    )(me, dffn, w2, slope, fin, small2)


BWD_IN = ("dffn", "xhat", "rstd", "wo", "q", "k", "v", "lse", "x", "mixed")


def attention_bwd(lens, q, k, v, dm, lse, d, small):
    rows, width = q.shape
    seqs = lens.shape[0]
    length = rows // seqs
    size = width // H
    low = lax.broadcasted_iota(jnp.int32, (length, 2 * size), 1) < size
    pos = lax.broadcasted_iota(jnp.int32, (2, length, 1), 1)

    def chain(s, _):
        r = ds(s * length, length, 32)
        live = pos < lens[s]
        cols = pairs_of(width, size)
        first = []
        for c in cols:
            k2 = both(low, k[r, c])
            first.append((k2, nt(k2, q[r, c]), nt(both(low, v[r, c]), dm[r, c])))
        for p, c in enumerate(cols):
            k2, st, dprob = first[p]
            st = jnp.where(live, st.reshape(2, length, length), -1e9)
            dprob = dprob.reshape(2, length, length)
            prob = jnp.exp(st - lse[s, pl.ds(2 * p, 2), :].reshape(2, 1, length))
            delta = jnp.sum(prob * dprob, 1, keepdims=True)
            dst = (prob * (dprob - delta)).astype(bf16).reshape(2 * length, length)
            dv = nn(prob.astype(bf16).reshape(2 * length, length), dm[r, c])
            dk = nn(dst, q[r, c])
            dq = (tn(dst, k2) * 0.125).astype(bf16)
            dv = jnp.where(low, dv[:length], dv[length:]).astype(bf16)
            d[r, c] = dq
            d[r, slice(width + c.start, width + c.stop)] = jnp.where(low, dk[:length], dk[length:]).astype(bf16)
            d[r, slice(2 * width + c.start, 2 * width + c.stop)] = dv
            small[6:7, c] += jnp.sum(dq.astype(f32), 0, keepdims=True)
            small[7:8, c] += jnp.sum(dv.astype(f32), 0, keepdims=True)
        return 0

    lax.fori_loop(0, seqs, chain, 0)


def bwd_kernel(*refs):
    lens, me, g1, small1, dpre_h, wi_h = refs[:6]
    src = dict(zip(BWD_IN, refs[6:16]))
    small, dh1_h, d_h, send_h = refs[16:20]
    dpre, wi = refs[20:22]
    vin = dict(zip(BWD_IN, refs[22:32]))
    dh1, d, send, acc, dm, sem_ff, sem_in, sem_out, sem_send = refs[32:]
    rows, width = acc.shape
    part_ff = dpre.shape[1] // width
    seqs = lens.shape[0]
    R = rows // seqs

    def load(name):
        return pltpu.make_async_copy(src[name], vin[name], sem_in.at[BWD_IN.index(name)])

    def ff_copies(n):
        c = slice(n * width, (n + 1) * width)
        return (
            pltpu.make_async_copy(dpre_h.at[:, c], dpre.at[:, c], sem_ff.at[0, n]),
            pltpu.make_async_copy(wi_h.at[:, c], wi.at[:, c], sem_ff.at[1, n]),
        )

    for n in range(part_ff):
        for one in ff_copies(n):
            one.start()
    for name in BWD_IN:
        load(name).start()
    for n in range(part_ff):
        c = slice(n * width, (n + 1) * width)
        for one in ff_copies(n):
            one.wait()
        part = nt(dpre[:, c], wi[:, c])
        acc[...] = part if n == 0 else acc[...] + part
    small[...] = small1[...]
    gain1 = row(g1)
    dffn, xhat, rstd = vin["dffn"], vin["xhat"], vin["rstd"]
    for name in ("dffn", "xhat", "rstd"):
        load(name).wait()
    dob = slice(3 * width, 4 * width)

    def norm_one(i, _):
        r = ds(i * R, R, 32)
        g = dffn[r, :].astype(f32) + acc[r, :].astype(bf16).astype(f32)
        unit = xhat[r, :]
        e = g * gain1
        v = rstd[r, :] * (e - row_mean(e) - unit * row_mean(e * unit))
        dh1[r, :] = v
        low = v.astype(bf16)
        d[r, dob] = low
        small[3:4, :] += jnp.sum(g * unit, 0, keepdims=True)
        small[4:5, :] += jnp.sum(g, 0, keepdims=True)
        small[5:6, :] += jnp.sum(low.astype(f32), 0, keepdims=True)
        return 0

    lax.fori_loop(0, seqs, norm_one, 0)
    dh1_copy = pltpu.make_async_copy(dh1, dh1_h, sem_out.at[0])
    dh1_copy.start()
    load("wo").wait()
    dm[...] = nt(d[:, dob], vin["wo"][...]).astype(bf16)
    for name in ("q", "k", "v", "lse"):
        load(name).wait()
    attention_bwd(lens, vin["q"], vin["k"], vin["v"], dm, vin["lse"], d, small)
    d_copy = pltpu.make_async_copy(d, d_h, sem_out.at[1])
    d_copy.start()
    load("x").wait()
    load("mixed").wait()
    far = ds((1 - me[0]) * CHUNK, CHUNK)

    def send_copy(n):
        part = pl.ds(4 * (n ^ (me[1] >> 1)), 4)
        return pltpu.make_async_copy(send.at[part], send_h.at[part], sem_send.at[n])

    for n in range(4):
        left = vin["mixed" if n == 3 else "x"]
        put_send(send, tn(left[:, far], d[:, n * width : (n + 1) * width]), 0, 2 * n, me, False)
        send_copy(n).start()
    dh1_copy.wait()
    d_copy.wait()
    for n in range(4):
        send_copy(n).wait()


def bwd_call(lens, me, g1, small1, dpre, wi, arrays):
    rows, width = arrays[0].shape
    ff = wi.shape[1]
    dma = pltpu.SemaphoreType.DMA
    vm = lambda a: pltpu.VMEM(a.shape, a.dtype)
    outs = [sd((rows, width), f32), sd((rows, 4 * width), bf16), sd((16, HALF, CHUNK), bf16)]
    return pl.pallas_call(
        bwd_kernel,
        in_specs=[SMEM, SMEM, VMEM, VMEM] + [HBM] * 12,
        out_specs=[VMEM] + [HBM] * 3,
        out_shape=[sd((16, width), f32)] + outs,
        scratch_shapes=[vm(dpre), vm(wi)] + [vm(a) for a in arrays] + [vm(o) for o in outs]
        + [pltpu.VMEM((rows, width), f32), pltpu.VMEM((rows, width), bf16)]
        + [dma((2, ff // width)), dma((10,)), dma((2,)), dma((4,))],
        compiler_params=params(),
        cost_estimate=cost(22e9),
        name="backward",
    )(lens, me, g1, small1, dpre, wi, *arrays)


def dx_kernel(dh1_h, d_h, wq_h, wk_h, wv_h, o_h, dh1, d, wq, wk, wv, o, sem, sem_out):
    width = dh1.shape[1]
    loads = []
    for n, (w_h, w) in enumerate(((wq_h, wq), (wk_h, wk), (wv_h, wv))):
        c = slice(n * width, (n + 1) * width)
        loads.append(pltpu.make_async_copy(d_h.at[:, c], d.at[:, c], sem.at[2 * n]))
        loads.append(pltpu.make_async_copy(w_h, w, sem.at[2 * n + 1]))
    loads.insert(2, pltpu.make_async_copy(dh1_h, dh1, sem.at[6]))
    for one in loads:
        one.start()
    loads[0].wait()
    loads[1].wait()
    part = nt(d[:, :width], wq[...])
    loads[2].wait()
    o[...] = dh1[...] + part
    loads[3].wait()
    loads[4].wait()
    o[...] = o[...] + nt(d[:, width : 2 * width], wk[...])
    loads[5].wait()
    loads[6].wait()
    half = dh1.shape[0] // 2
    stores = []
    for i in range(2):
        r = slice(i * half, (i + 1) * half)
        o[r, :] = o[r, :] + nt(d[r, 2 * width : 3 * width], wv[...])
        stores.append(pltpu.make_async_copy(o.at[r, :], o_h.at[r, :], sem_out.at[i]))
        stores[i].start()
    for one in stores:
        one.wait()


def dx_call(dh1, d, wq, wk, wv):
    rows, width = dh1.shape
    dma = pltpu.SemaphoreType.DMA
    return pl.pallas_call(
        dx_kernel,
        in_specs=[HBM] * 5,
        out_specs=HBM,
        out_shape=sd((rows, width), f32),
        scratch_shapes=[
            pltpu.VMEM((rows, width), f32), pltpu.VMEM((rows, 3 * width), bf16), pltpu.VMEM(wq.shape, bf16),
            pltpu.VMEM(wq.shape, bf16), pltpu.VMEM(wq.shape, bf16), pltpu.VMEM((rows, width), f32), dma((7,)), dma((2,)),
        ],
        compiler_params=params(),
        cost_estimate=cost(5e9),
        name="dx",
    )(dh1, d, wq, wk, wv)


def bit(value, name):
    return (value >> "xya".index(name)) & 1


def pair_grad(kind, pair, refs):
    if kind == "attn":
        x, mixed, d = refs
        return tn(jnp.where(pair == 3, mixed[...], x[...]), d[...])
    return tn(refs[0][...], refs[1][...])


def keep_kernel(kind, orders, me, *refs):
    p = pl.program_id(0)
    n_in = 3 if kind == "attn" else 2
    got = refs[n_in]
    outs = refs[n_in + 1 : -1]
    g = refs[-1]
    g[...] = pair_grad(kind, p ^ (me[1] >> 1), refs[:n_in])
    size = HALF // len(orders)
    for i in range(2):
        step = 2 * p + i
        far = ds((i ^ (me[1] & 1)) * CHUNK, CHUNK)
        for t in range(2):
            part = (t ^ me[2]) * HALF
            if kind == "outer":
                grad = g[ds((i ^ (me[1] & 1)) * CHUNK + part, HALF), :]
            else:
                grad = g[ds(part, HALF), far]
            total = (grad + got[2 * i + t].astype(f32)).astype(bf16)
            for n, order in enumerate(orders):
                where = bit(step, order[1]) * 4 + bit(step, order[2]) * 2 + t
                first = bit(step, order[0])
                value = total[n * size : (n + 1) * size]
                if order[0] == "x":
                    outs[2 * n + i][where] = value
                    continue

                @pl.when(first == 0)
                def _():
                    outs[2 * n][where] = value

                @pl.when(first == 1)
                def _():
                    outs[2 * n + 1][where] = value


def grad_specs(kind, rows, flip, pair_of):
    pair = lambda p, me: (0, pair_of(p, me))
    half = lambda p, me: (0, me[0] ^ flip)
    wide = (rows, 2 * CHUNK)
    thin = (rows, CHUNK)
    if kind == "outer":
        return [pl.BlockSpec(wide, pair), pl.BlockSpec(thin, half)]
    if kind == "inner":
        return [pl.BlockSpec(thin, half), pl.BlockSpec(wide, pair)]
    return [pl.BlockSpec(thin, half), pl.BlockSpec(thin, half), pl.BlockSpec(wide, pair)]


def grad_keep(kind, me, args, got, orders):
    rows = args[0].shape[0]
    shape = (8, HALF // len(orders), CHUNK)
    g_shape = (2 * CHUNK, CHUNK) if kind == "outer" else (CHUNK, 2 * CHUNK)
    return pl.pallas_call(
        functools.partial(keep_kernel, kind, orders),
        grid_spec=pltpu.PrefetchScalarGridSpec(
            num_scalar_prefetch=1,
            grid=(4,),
            in_specs=grad_specs(kind, rows, 0, lambda p, me: p ^ (me[1] >> 1))
            + [pl.BlockSpec((4, HALF, CHUNK), lambda p, me: (p, 0, 0))],
            out_specs=[pl.BlockSpec(shape, lambda p, me: (0, 0, 0))] * (2 * len(orders)),
            scratch_shapes=[pltpu.VMEM(g_shape, f32)],
        ),
        out_shape=[sd(shape, bf16)] * (2 * len(orders)),
        compiler_params=params(),
        cost_estimate=cost(3e9),
        name="keep_" + kind,
    )(me, *args, got)


def unpack_kernel(kind, colors, me, *refs):
    ins = refs[: 4 * colors]
    n_out = 4 if kind == "attn" else 1
    outs = refs[4 * colors : 4 * colors + n_out]
    buf, sem = refs[4 * colors + n_out :]
    size = HALF // colors

    def copy(step, slot):
        chunk = step ^ me[1]
        if kind == "outer":
            return [(None, pltpu.make_async_copy(buf.at[slot], outs[0].at[ds(chunk * CHUNK, CHUNK), :], sem.at[slot]))]
        if kind == "inner":
            return [(None, pltpu.make_async_copy(buf.at[slot], outs[0].at[:, ds(chunk * CHUNK, CHUNK)], sem.at[slot]))]
        return [
            (chunk // 2 == m, pltpu.make_async_copy(buf.at[slot], outs[m].at[:, ds((chunk % 2) * CHUNK, CHUNK)], sem.at[slot]))
            for m in range(4)
        ]

    def each(step, slot, act):
        for cond, one in copy(step, slot):
            if cond is None:
                act(one)
            else:
                pl.when(cond)(functools.partial(act, one))

    for step in range(8):
        slot = step % 2
        if step >= 2:
            each(step - 2, slot, lambda one: one.wait())
        for half in range(2):
            place = (half ^ me[0]) * CHUNK
            for n in range(colors):
                own, got = ins[4 * n + 2 * half : 4 * n + 2 * half + 2]
                order = ORDER_OF[n]
                src = got if bit(step, order[0]) else own
                for t in range(2):
                    where = bit(step, order[1]) * 4 + bit(step, order[2]) * 2 + t
                    row = (t ^ me[2]) * HALF + n * size
                    value = src[where].astype(f32)
                    if kind == "outer":
                        buf[slot, ds(row, size, 32), ds(place, CHUNK)] = value
                    else:
                        buf[slot, ds(place + row, size, 32), :] = value
        each(step, slot, lambda one: one.start())
    for step in (6, 7):
        each(step, step % 2, lambda one: one.wait())


ORDER_OF = ("xyab", "yxab", "axyb")


def unpack(kind, me, pieces):
    colors = len(pieces) // 4
    width = 2 * CHUNK
    if kind == "outer":
        out_shape = [sd((8 * CHUNK, width), f32)]
    elif kind == "inner":
        out_shape = [sd((width, 8 * CHUNK), f32)]
    else:
        out_shape = [sd((width, width), f32)] * 4
    buf = (2, CHUNK, width) if kind == "outer" else (2, width, CHUNK)
    return pl.pallas_call(
        functools.partial(unpack_kernel, kind, colors),
        in_specs=[SMEM] + [VMEM] * (4 * colors),
        out_specs=[HBM] * len(out_shape),
        out_shape=out_shape,
        scratch_shapes=[pltpu.VMEM(buf, f32), pltpu.SemaphoreType.DMA((2,))],
        compiler_params=params(),
        cost_estimate=cost(4e9),
        name="unpack_" + kind,
    )(me, *pieces)


SMALL_ROWS = (6, 7, 5, 3, 4, 8, 2, 0, 1)


def small_kernel(parts, *outs):
    width = parts.shape[1]
    total = jnp.sum(parts[...].reshape(parts.shape[0] // 16, 16, width), 0)
    for at, out in zip(SMALL_ROWS, outs):
        for n in range(out.shape[0] // width):
            out[pl.ds(n * width, width)] = total[at + n : at + n + 1, :].reshape(width)


def small_call(parts, ff):
    width = parts.shape[1]
    sizes = [ff if at == 8 else width for at in SMALL_ROWS]
    return pl.pallas_call(
        small_kernel,
        in_specs=[VMEM],
        out_specs=[VMEM] * 9,
        out_shape=[sd((n,), f32) for n in sizes],
        compiler_params=params(),
        cost_estimate=cost(2e9),
        name="vectors",
    )(parts)


AXES = ("dp", "seq")
DP_BIT = {"x": 0, "y": 1, "a": 2, "b": 3}


def swap(value, name):
    dp = lax.axis_size("dp")
    seq = lax.axis_size("seq")
    flip = 1 if name == "c" else seq << (name if isinstance(name, int) else DP_BIT[name])
    return lax.ppermute(value, AXES, [(i, i ^ flip) for i in range(dp * seq)])


def after(value, *earlier):
    return lax.optimization_barrier((value,) + earlier)[0]


def add_halves(keep, got):
    half = keep.shape[0] // 2
    return keep[:half] + got[:half], keep[half:] + got[half:]


def gather(own, order):
    for n, name in enumerate(reversed(order)):
        got = swap(own, name)
        if n + 1 < len(order):
            own = jnp.concatenate([own, got])
    return own, got


def finish(own):
    for extra in range(4, lax.axis_size("dp").bit_length() - 1):
        own = own + swap(own, extra)
    return own


RS_ORDERS = {"outer": ("xyab",), "inner": ("axyb",), "attn": ORDER_OF}


class Line:
    def __init__(self):
        self.last = ()

    def __call__(self, value):
        return lax.optimization_barrier((value,) + self.last)[0]

    def done(self, *values):
        self.last = values


def rows_of(value, start, stop):
    return value[:, start:stop]


class One:
    def __init__(self, line, blocks, order):
        self.line, self.order, self.level = line, order, 0
        self.keep = blocks[0]
        self.got = swap(blocks[1], order[0])

    def step(self):
        got = self.line(self.got)
        self.level += 1
        if self.level == 4:
            self.keep = self.keep + got
            self.line.done(self.keep)
            return finish(self.keep[0])
        self.keep, send = add_halves(self.keep, got)
        self.line.done(self.keep, send)
        self.got = swap(send, self.order[self.level])


class Three:
    def __init__(self, line, blocks):
        self.line = line
        self.keep = dict(zip("ABC", blocks[0::2]))
        self.got = {n: swap(blocks[2 * i + 1], ORDER_OF[i][0]) for i, n in enumerate("ABC")}

    def first(self, n):
        got = self.line(self.got[n])
        self.keep[n], send = add_halves(self.keep[n], got)
        self.line.done(self.keep[n], send)
        self.got[n] = swap(send, ORDER_OF["ABC".index(n)][1])

    def join(self):
        gots = [self.line(self.got[n]) for n in "AB"]
        pairs = [add_halves(self.keep[n], got) for n, got in zip("AB", gots)]
        self.keep["AB"], send = [jnp.concatenate(v, 1) for v in zip(*pairs)]
        self.line.done(self.keep["AB"], send)
        self.got["AB"] = swap(send, "a")

    def second(self):
        got = self.line(self.got["C"])
        self.keep["C"], send = add_halves(self.keep["C"], got)
        self.line.done(self.keep["C"], send)
        self.got["C"] = swap(send, ORDER_OF[2][2])

    def last(self):
        gots = [self.line(self.got[n]) for n in ("AB", "C")]
        pairs = [add_halves(self.keep[n], got) for n, got in zip(("AB", "C"), gots)]
        self.keep, send = [jnp.concatenate(v, 1) for v in zip(*pairs)]
        self.line.done(self.keep, send)
        self.got = swap(send, "b")

    def end(self):
        own = self.keep + self.line(self.got)
        self.line.done(own)
        return finish(own[0])


class Gather:
    def __init__(self, line, own):
        self.line = line
        self.own = own[None]
        self.got = swap(self.own, "b")
        self.pieces = {}

    def first(self):
        both_parts = jnp.concatenate([self.own, self.line(self.got)])
        size = both_parts.shape[1] // 3
        self.own = {"AB": both_parts[:, : 2 * size], "C": both_parts[:, 2 * size :]}
        self.line.done(*self.own.values())
        self.got = {"AB": swap(self.own["AB"], "a"), "C": swap(self.own["C"], ORDER_OF[2][2])}

    def second(self):
        four = jnp.concatenate([self.own["AB"], self.line(self.got["AB"])])
        size = four.shape[1] // 2
        self.own["A"], self.own["B"] = four[:, :size], four[:, size:]
        self.line.done(self.own["A"], self.own["B"])
        for n in "AB":
            self.got[n] = swap(self.own[n], ORDER_OF["ABC".index(n)][1])

    def third(self):
        self.own["C"] = jnp.concatenate([self.own["C"], self.line(self.got["C"])])
        self.line.done(self.own["C"])
        self.got["C"] = swap(self.own["C"], ORDER_OF[2][1])

    def fourth(self, n):
        own = jnp.concatenate([self.own[n], self.line(self.got[n])])
        self.line.done(own)
        self.got[n] = swap(own, ORDER_OF["ABC".index(n)][0])
        self.pieces[n] = [own, None, swap(own, "c"), None]

    def last(self, n):
        got = self.got[n]
        self.pieces[n][1] = got
        self.pieces[n][3] = swap(got, "c")

    def all(self):
        return [v for n in "ABC" for v in self.pieces[n]]


def body(chains_in, lengths, d_out, w_query, b_query, w_key, w_value, b_value, w_output, b_output, gain_one, shift_one,
         w_inner, b_inner, w_outer, b_outer, gain_two, shift_two):
    seqs, length, width = chains_in.shape
    rows = seqs * length
    place = lax.axis_index("dp") * 2 + lax.axis_index("seq")
    me = (place >> jnp.array([0, 1, 4], jnp.int32)) & jnp.array([1, 7, 1], jnp.int32)
    x = chains_in.reshape(rows, width)
    line = Line()
    lse, small2, q, k, v, mixed, xhat, rstd, fin, out, dffn, hid, slope, send = forward(
        lengths, me, (b_query, b_value, b_output, gain_one, shift_one, b_inner, b_outer, gain_two, shift_two),
        (x, w_query, w_key, w_value, w_output, w_inner, w_outer, d_out.reshape(rows, width)),
    )
    got1 = swap(send, "c")
    dpre, send, small1 = pre_call(me, dffn, w_outer, slope, fin, small2)
    got2 = swap(send, "c")
    line.done(dpre)
    blocks = grad_keep("outer", me, (hid, dffn), line(got1), RS_ORDERS["outer"])
    line.done(*blocks)
    r1 = One(line, blocks, "xyab")
    blocks = grad_keep("inner", me, (fin, dpre), line(got2), RS_ORDERS["inner"])
    line.done(*blocks)
    r2 = One(line, blocks, "axyb")
    small, dh1, d, send = bwd_call(
        lengths, me, gain_one, small1, line(dpre), w_inner, (dffn, xhat, rstd, w_output, q, k, v, lse, x, mixed)
    )
    line.done(dh1, d, send)
    r1.step()
    r2.step()
    got3 = swap(line(send), "c")
    d_x = dx_call(line(dh1), d, w_query, w_key, w_value)
    line.done(d_x)
    blocks = grad_keep("attn", me, (x, mixed, d), line(got3), RS_ORDERS["attn"])
    line.done(*blocks)
    r3 = Three(line, blocks)
    r1.step()
    r2.step()
    for n in "ABC":
        r3.first(n)
    r1.step()
    r2.step()
    r3.join()
    r3.second()
    g1 = Gather(line, r1.step())
    g2 = Gather(line, r2.step())
    r3.last()
    g1.first()
    g2.first()
    g3 = Gather(line, r3.end())
    for g in (g1, g2):
        g.second()
        g.third()
    g3.first()
    for n in "ABC":
        g1.fourth(n)
    for n in "ABC":
        g2.fourth(n)
    g3.second()
    g3.third()
    for n in "ABC":
        g1.last(n)
    for n in "ABC":
        g3.fourth(n)
    for n in "ABC":
        g2.last(n)
    for n in "ABC":
        g3.last(n)
    (d_w_outer,) = unpack("outer", me, g1.all())
    (d_w_inner,) = unpack("inner", me, g2.all())
    d_w_query, d_w_key, d_w_value, d_w_output = unpack("attn", me, g3.all())
    vec = small_call(lax.all_gather(small, AXES, axis=0, tiled=True), w_inner.shape[1])
    return (
        out.reshape(seqs, length, width), d_x.reshape(seqs, length, width),
        d_w_query, vec[0], d_w_key, d_w_value, vec[1], d_w_output, vec[2], vec[3], vec[4],
        d_w_inner, vec[5], d_w_outer, vec[6], vec[7], vec[8],
    )


def solution(mesh):
    rows = P(AXES, None, None)
    return jax.shard_map(
        body, mesh=mesh, in_specs=(rows, P(AXES), rows) + (P(),) * 15, out_specs=(rows, rows) + (P(),) * 15, check_vma=False
    )
```

time: 1150 us -> 284 us (0.25)
  the two profiles are of different devices: /device:TPU:0 before, /device:TPU:25 now
where the time goes in v3:
time: 284 us; the launch traced here: 283 us
  Pallas kernels  113 us (40%)
  waiting for transfers between devices  92.5 us (33%)
  starting transfers between devices  53.5 us (19%)
  between operations  14.8 us (5%)
  local copies, waits for them, and re-layouts  4.83 us (2%)
  other arithmetic  4.23 us (1%)
    ppermute x65, waiting for transfers between devices, swap(): return lax.ppermute(value, AXES, [(i, i ^ flip) for i in range(dp * seq)])  92.5 us
    ppermute x65, starting transfers between devices, swap(): return lax.ppermute(value, AXES, [(i, i ^ flip) for i in range(dp * seq)])  53.5 us
    pallas_call x1, Pallas kernels, forward(): pl.pallas_call(fwd_kernel, in_specs=[SMEM, SMEM] + [VMEM] * 9 + [HBM] * 8...  28.4 us
    pallas_call x3, Pallas kernels, grad_keep(): pl.pallas_call(functools.partial(keep_kernel, kind, orders), grid_spec=pl...  23.4 us
    pallas_call x1, Pallas kernels, bwd_call(): pl.pallas_call(bwd_kernel, in_specs=[SMEM, SMEM, VMEM, VMEM] + [HBM] * 12...  22 us
    pallas_call x3, Pallas kernels, unpack(): pl.pallas_call(functools.partial(unpack_kernel, kind, colors), in_specs=[...  21.3 us
    pallas_call x1, Pallas kernels, pre_call(): pl.pallas_call(pre_kernel, grid_spec=pltpu.PrefetchScalarGridSpec(num_sca...  9.83 us
    pallas_call x1, Pallas kernels, dx_call(): pl.pallas_call(dx_kernel, in_specs=[HBM] * 5, out_specs=HBM, out_shape=sd...  6.29 us
  transfers between devices with their start and end apart: 66, of which 21 were waited for; matrix products, arithmetic and copies ran while one was open for 1% of the time, Pallas kernels for 27%

profile of v3, /device:TPU:25, one launch (start us, length us, event | category | flops | bytes accessed | tf_op | source)
XLA Modules:
  0.0 283.3 jit_solution(11069406279502196988)
XLA Ops:
  8.5 28.4 %forward.1 = (f32[4,12,160]{2,1,0:T(8,128)}, f32[8,768]{1,0:T(8,128)}, bf16[640,768]{1,0:T(8,128)(2,1)}, bf16[640,768]{1,0:T(8,128)(2,1)}, bf16[640,768]{1,0:T(8...) custom-call(s32[4]{0:T(128)} %refs_0_.3, ...), custom_call_target="tpu_custom_call" | custom-call | flops 28000000000 | bytes 1048576 | tf_op jit(solution)/shard_map/forward/pallas_call | solution.py:251
  37.6 9.8 %pre_bwd.1 = (bf16[640,3072]{1,0:T(8,128)(2,1)}, bf16[16,192,384]{2,1,0:T(8,128)(2,1)}, f32[16,768]{1,0:T(8,128)}) custom-call(s32[3]{0:T(128)} %shift-right-arithmetic_and_fusion.refs_1_.me, bf16[640,768]{1,0:T(8,128)(2,1)} %get-tuple-element.103.dffn.refs_1_.refs_6_, bf16[3072,768]{1,0:T(8,128)(2,1)} %w2.1, bf16[640,3072]{1,0:T(8,128)(2,1)} %get-tuple-element.104.slope, ...), custom_call_target="tpu_custom_call" | custom-call | flops 8000000000 | bytes 1048576 | tf_op jit(solution)/shard_map/pre_bwd/pallas_call | solution.py:284
  47.5 7.9 %keep_outer.1 = (bf16[8,192,384]{2,1,0:T(8,128)(2,1)}, bf16[8,192,384]{2,1,0:T(8,128)(2,1)}) custom-call(s32[3]{0:T(128)} %shift-right-arithmetic_and_fusion.refs_1_.me, bf16[640,3072]{1,0:T(8,128)(2,1)} %get-tuple-element.110.refs_0_, bf16[640,768]{1,0:T(8,128)(2,1)} %get-tuple-element.103.dffn.refs_1_.refs_6_, ...), custom_call_target="tpu_custom_call" | custom-call | flops 3000000000 | bytes 1048576 | tf_op jit(solution)/shard_map/keep_outer/pallas_call | solution.py:562
  57.9 7.6 %keep_inner.1 = (bf16[8,192,384]{2,1,0:T(8,128)(2,1)}, bf16[8,192,384]{2,1,0:T(8,128)(2,1)}) custom-call(s32[3]{0:T(128)} %shift-right-arithmetic_and_fusion.refs_1_.me, bf16[640,768]{1,0:T(8,128)(2,1)} %get-tuple-element.105.fin.refs_0_, bf16[640,3072]{1,0:T(8,128)(2,1)} %get-tuple-element.118.refs_1_.refs_4_, bf16[16,192,384]{2,1,0:T(8,128)(2,1)} %copy-done.14), custom_call_target="tpu_custom_call" | custom-call | flops 3000000000 | bytes 1048576 | tf_op jit(solution)/shard_map/keep_inner/pallas_call | solution.py:562
  65.8 22.0 %backward.1 = (f32[16,768]{1,0:T(8,128)}, f32[640,768]{1,0:T(8,128)}, bf16[640,3072]{1,0:T(8,128)(2,1)}, bf16[16,192,384]{2,1,0:T(8,128)(2,1)}) custom-call(s32[4]{0:T(128)} %refs_0_.3, s32[3]{0:T(128)} %shift-right-arithmetic_and_fusion.refs_1_.me, f32[768]{0:T(1024)} %refs_2_.3, f32[16,768]{1,0:T(8,128)} %get-tuple-element.107.refs_3_, ...), custom_call_target="tpu_custom_call" | custom-call | flops 22000001024 | bytes 1048576 | tf_op jit(solution)/shard_map/backward/pallas_call | solution.py:437
  88.0 4.6 %collective-permute-done.2 = bf16[8,192,384]{2,1,0:T(8,128)(2,1)} collective-permute-done((bf16[8,192,384]{2,1,0:T(8,128)(2,1)}, bf16[8,192,384]{2,1,0:T(8,128)(2,1)}, u32[]{:S(2)}, u32[]{:S(2)}) %collective-permute-start.2) | collective-permute-done | bytes 1179680 | tf_op jit(solution)/shard_map/ppermute | solution.py:685
  97.3 6.3 %dx.1 = f32[640,768]{1,0:T(8,128)} custom-call(f32[640,768]{1,0:T(8,128)} %get-tuple-element.131.dh1_h, bf16[640,3072]{1,0:T(8,128)(2,1)} %get-tuple-element.127.d_h.refs_2_, bf16[768,768]{1,0:T(8,128)(2,1)} %wq_h.1, bf16[768,768]{1,0:T(8,128)(2,1)} %wk_h.1, bf16[768,768]{1,0:T(8,128)(2,1)} %wv_h.1), custom_call_target="tpu_custom_call" | custom-call | flops 5000000000 | bytes 1048576 | tf_op jit(solution)/shard_map/dx/pallas_call | solution.py:485
  103.6 7.9 %keep_attn.1 = (bf16[8,64,384]{2,1,0:T(8,128)(2,1)}, bf16[8,64,384]{2,1,0:T(8,128)(2,1)}, bf16[8,64,384]{2,1,0:T(8,128)(2,1)}, bf16[8,64,384]{2,1,0:T(8,128)(2,1...) custom-call(s32[3]{0:T(128)} %shift-right-arithmetic_and_fusion.refs_1_.me, bf16[640,768]{1,0:T(8,128)(2,1)} %bitcast.7, ...), custom_call_target="tpu_custom_call" | custom-call | flops 3000000000 | bytes 1048576 | tf_op jit(solution)/shard_map/keep_attn/pallas_call | solution.py:562
  116.0 5.8 %collective-permute-done.5 = bf16[8,64,384]{2,1,0:T(8,128)(2,1)S(1)} collective-permute-done((bf16[8,64,384]{2,1,0:T(8,128)(2,1)}, bf16[8,64,384]{2,1,0:T(8,128)(2,1)S(1)}, u32[]{:S(2)}, u32[]{:S(2)}) %collective-permute-start.5) | collective-permute-done | bytes 393248 | tf_op jit(solution)/shard_map/ppermute | solution.py:685
  124.4 4.5 %collective-permute-done.10 = bf16[2,192,384]{2,1,0:T(8,128)(2,1)S(1)} collective-permute-done((bf16[2,192,384]{2,1,0:T(8,128)(2,1)S(1)}, bf16[2,192,384]{2,1,0:T(8,128)(2,1)S(1)}, u32[]{:S(2)}, u32[]{:S(2)}) %collective-permute-start.10) | collective-permute-done | bytes 294944 | tf_op jit(solution)/shard_map/ppermute | solution.py:685
  134.0 9.1 %collective-permute-done.16 = bf16[1,192,384]{2,1,0:T(8,128)(2,1)S(1)} collective-permute-done((bf16[1,192,384]{2,1,0:T(8,128)(2,1)S(1)}, bf16[1,192,384]{2,1,0:T(8,128)(2,1)S(1)}, u32[]{:S(2)}, u32[]{:S(2)}) %collective-permute-start.16) | collective-permute-done | bytes 147488 | tf_op jit(solution)/shard_map/ppermute | solution.py:685
  143.2 12.3 %collective-permute-done.15 = bf16[1,192,384]{2,1,0:T(8,128)(2,1)S(1)} collective-permute-done((bf16[1,192,384]{2,1,0:T(8,128)(2,1)S(1)}, bf16[1,192,384]{2,1,0:T(8,128)(2,1)S(1)}, u32[]{:S(2)}, u32[]{:S(2)}) %collective-permute-start.15) | collective-permute-done | bytes 147488 | tf_op jit(solution)/shard_map/ppermute | solution.py:685
  165.0 7.4 %collective-permute-done.26 = bf16[2,128,384]{2,1,0:T(8,128)(2,1)S(1)} collective-permute-done((bf16[2,128,384]{2,1,0:T(8,128)(2,1)S(1)}, bf16[2,128,384]{2,1,0:T(8,128)(2,1)S(1)}, u32[]{:S(2)}, u32[]{:S(2)}) %collective-permute-start.26) | collective-permute-done | bytes 196640 | tf_op jit(solution)/shard_map/ppermute | solution.py:685
  173.7 5.7 %collective-permute-done.24 = bf16[2,128,384]{2,1,0:T(8,128)(2,1)S(1)} collective-permute-done((bf16[2,128,384]{2,1,0:T(8,128)(2,1)S(1)}, bf16[2,128,384]{2,1,0:T(8,128)(2,1)S(1)}, u32[]{:S(2)}, u32[]{:S(2)}) %collective-permute-start.24) | collective-permute-done | bytes 196640 | tf_op jit(solution)/shard_map/ppermute | solution.py:685
  183.0 14.1 %collective-permute-done.31 = bf16[4,64,384]{2,1,0:T(8,128)(2,1)S(1)} collective-permute-done((bf16[4,64,384]{2,1,0:T(8,128)(2,1)S(1)}, bf16[4,64,384]{2,1,0:T(8,128)(2,1)S(1)}, u32[]{:S(2)}, u32[]{:S(2)}) %collective-permute-start.31) | collective-permute-done | bytes 196640 | tf_op jit(solution)/shard_map/ppermute | solution.py:685
  207.5 4.6 %collective-permute-start.51 = (bf16[8,64,384]{2,1,0:T(8,128)(2,1)S(1)}, bf16[8,64,384]{2,1,0:T(8,128)(2,1)S(1)}, u32[]{:S(2)}, u32[]{:S(2)}) collective-permute-start(bf16[8,64,384]{2,1,0:T(8,128)(2,1)S(1)} %pad_maximum_fusion.4.refs_4_), channel_id=1, source_target_pairs={{0,1},{1,0},{2,3},{3,2},{4,5},{5,4},{6,7},{7,6},{8,9},{9,8},{10,11... | collective-permute-start | bytes 1179656 | tf_op jit(solution)/shard_map/ppermute | solution.py:685
  216.5 4.2 %collective-permute-done.50.refs_5_ = bf16[8,64,384]{2,1,0:T(8,128)(2,1)} collective-permute-done((bf16[8,64,384]{2,1,0:T(8,128)(2,1)S(1)}, bf16[8,64,384]{2,1,0:T(8,128)(2,1)}, u32[]{:S(2)}, u32[]{:S(2)}) %collective-permute-start.50) | collective-permute-done | bytes 393248 | tf_op jit(solution)/shard_map/ppermute | solution.py:685
  220.7 3.0 %collective-permute-start.60 = (bf16[8,64,384]{2,1,0:T(8,128)(2,1)S(1)}, bf16[8,64,384]{2,1,0:T(8,128)(2,1)S(1)}, u32[]{:S(2)}, u32[]{:S(2)}) collective-permute-start(bf16[8,64,384]{2,1,0:T(8,128)(2,1)S(1)} %pad_maximum_fusion.1.refs_4_), channel_id=1, source_target_pairs={{0,1},{1,0},{2,3},{3,2},{4,5},{5,4},{6,7},{7,6},{8,9},{9,8},{10,11... | collective-permute-start | bytes 1179656 | tf_op jit(solution)/shard_map/ppermute | solution.py:685
  229.2 5.3 %collective-permute-done.59.refs_5_ = bf16[8,64,384]{2,1,0:T(8,128)(2,1)} collective-permute-done((bf16[8,64,384]{2,1,0:T(8,128)(2,1)S(1)}, bf16[8,64,384]{2,1,0:T(8,128)(2,1)}, u32[]{:S(2)}, u32[]{:S(2)}) %collective-permute-start.59) | collective-permute-done | bytes 393248 | tf_op jit(solution)/shard_map/ppermute | solution.py:685
  236.1 3.1 %collective-permute-done.56.refs_1_ = bf16[8,64,384]{2,1,0:T(8,128)(2,1)} collective-permute-done((bf16[8,64,384]{2,1,0:T(8,128)(2,1)S(1)}, bf16[8,64,384]{2,1,0:T(8,128)(2,1)}, u32[]{:S(2)}, u32[]{:S(2)}) %collective-permute-start.56) | collective-permute-done | bytes 393248 | tf_op jit(solution)/shard_map/ppermute | solution.py:685
  240.9 3.4 %collective-permute-done.40.refs_5_ = bf16[8,64,384]{2,1,0:T(8,128)(2,1)S(1)} collective-permute-done((bf16[8,64,384]{2,1,0:T(8,128)(2,1)S(1)}, bf16[8,64,384]{2,1,0:T(8,128)(2,1)S(1)}, u32[]{:S(2)}, u32[]{:S(2)}) %collective-permute-start.40) | collective-permute-done | bytes 393248 | tf_op jit(solution)/shard_map/ppermute | solution.py:685
  253.2 7.1 %unpack_outer.1 = f32[3072,768]{1,0:T(8,128)} custom-call(s32[3]{0:T(128)} %shift-right-arithmetic_and_fusion.refs_1_.me, bf16[8,64,384]{2,1,0:T(8,128)(2,1)} %copy-done.2, bf16[8,64,384]{2,1,0:T(8,128)(2,1)} %collective-permute-done.56.refs_1_, bf16[8,64,384]{2,1,0:T(8,128)(2,1)} %copy-done.24, bf16[8,64,384]{2,1,0:T(8,128)(2,1)} %collective-permute-done.58.refs_3_, ...), custom_call_target="tpu_custom_call" | custom-call | flops 4000000000 | bytes 1048576 | tf_op jit(solution)/shard_map/unpack_outer/pallas_call | solution.py:640
  260.3 7.1 %unpack_inner.1 = f32[768,3072]{1,0:T(8,128)} custom-call(s32[3]{0:T(128)} %shift-right-arithmetic_and_fusion.refs_1_.me, bf16[8,64,384]{2,1,0:T(8,128)(2,1)} %copy-done.4, bf16[8,64,384]{2,1,0:T(8,128)(2,1)} %collective-permute-done.47.refs_1_, bf16[8,64,384]{2,1,0:T(8,128)(2,1)} %copy-done.18, bf16[8,64,384]{2,1,0:T(8,128)(2,1)} %collective-permute-done.49.refs_3_, ...), custom_call_target="tpu_custom_call" | custom-call | flops 4000000000 | bytes 1048576 | tf_op jit(solution)/shard_map/unpack_inner/pallas_call | solution.py:640
  269.3 7.1 %unpack_attn.1 = (f32[768,768]{1,0:T(8,128)}, f32[768,768]{1,0:T(8,128)}, f32[768,768]{1,0:T(8,128)}, f32[768,768]{1,0:T(8,128)}) custom-call(s32[3]{0:T(128)} %shift-right-arithmetic_and_fusion.refs_1_.me, bf16[8,64,384]{2,1,0:T(8,128)(2,1)} %copy-done.8, bf16[8,64,384]{2,1,0:T(8,128)(2,1)} %copy-done.25, bf16[8,64,384]{2,1,0:T(8,128)(2,1)} %copy-done.29, ...), custom_call_target="tpu_custom_call" | custom-call | flops 4000000000 | bytes 1048576 | tf_op jit(solution)/shard_map/unpack_attn/pallas_call | solution.py:640
  (226 shorter events, 69.9 us)
Async XLA Ops:
  7.2 242.6 %all-gather.2.cloned.1.call-start = ((), (), s32[]{:S(2)}) async-start(), calls=%async_computation | async-start | bytes 1622016 | tf_op jit(solution)/shard_map/all_gather | solution.py:896
  55.3 32.5 %collective-permute-start.3 = (bf16[8,192,384]{2,1,0:T(8,128)(2,1)}, bf16[8,192,384]{2,1,0:T(8,128)(2,1)S(1)}, u32[]{:S(2)}, u32[]{:S(2)}) collective-permute-start(bf16[8,192,384]{2,1,0:T(8,128)(2,1)} %get-tuple-element.114), channel_id=1, source_target_pairs={{0,2},{1,3},{2,0},{3,1},{4,6},{5,7},{6,4},{7,5},{8,10},{9,11},{10,... | collective-permute-start | bytes 3538952 | tf_op jit(solution)/shard_map/ppermute | solution.py:685
  65.6 27.0 %collective-permute-start.2 = (bf16[8,192,384]{2,1,0:T(8,128)(2,1)}, bf16[8,192,384]{2,1,0:T(8,128)(2,1)}, u32[]{:S(2)}, u32[]{:S(2)}) collective-permute-start(bf16[8,192,384]{2,1,0:T(8,128)(2,1)} %get-tuple-element.117), channel_id=1, source_target_pairs={{0,8},{1,9},{2,10},{3,11},{4,12},{5,13},{6,14},{7,15},{8,0},{9,1},... | collective-permute-start | bytes 3538952 | tf_op jit(solution)/shard_map/ppermute | solution.py:685
  95.8 17.4 %collective-permute-start.7 = (bf16[4,192,384]{2,1,0:T(8,128)(2,1)S(1)}, bf16[4,192,384]{2,1,0:T(8,128)(2,1)S(1)}, u32[]{:S(2)}, u32[]{:S(2)}) collective-permute-start(bf16[4,192,384]{2,1,0:T(8,128)(2,1)S(1)} %get-tuple-element.189), channel_id=1, source_target_pairs={{0,4},{1,5},{2,6},{3,7},{4,0},{5,1},{6,2},{7,3},{8,12},{9,13},{10,... | collective-permute-start | bytes 1769480 | tf_op jit(solution)/shard_map/ppermute | solution.py:685
  97.1 17.6 %collective-permute-start.6 = (bf16[4,192,384]{2,1,0:T(8,128)(2,1)S(1)}, bf16[4,192,384]{2,1,0:T(8,128)(2,1)S(1)}, u32[]{:S(2)}, u32[]{:S(2)}) collective-permute-start(bf16[4,192,384]{2,1,0:T(8,128)(2,1)S(1)} %get-tuple-element.187), channel_id=1, source_target_pairs={{0,2},{1,3},{2,0},{3,1},{4,6},{5,7},{6,4},{7,5},{8,10},{9,11},{10,... | collective-permute-start | bytes 1769480 | tf_op jit(solution)/shard_map/ppermute | solution.py:685
  113.3 15.6 %collective-permute-start.10 = (bf16[2,192,384]{2,1,0:T(8,128)(2,1)S(1)}, bf16[2,192,384]{2,1,0:T(8,128)(2,1)S(1)}, u32[]{:S(2)}, u32[]{:S(2)}) collective-permute-start(bf16[2,192,384]{2,1,0:T(8,128)(2,1)S(1)} %get-tuple-element.193), channel_id=1, source_target_pairs={{0,8},{1,9},{2,10},{3,11},{4,12},{5,13},{6,14},{7,15},{8,0},{9,1},... | collective-permute-start | bytes 884744 | tf_op jit(solution)/shard_map/ppermute | solution.py:685
  129.1 26.4 %collective-permute-start.15 = (bf16[1,192,384]{2,1,0:T(8,128)(2,1)S(1)}, bf16[1,192,384]{2,1,0:T(8,128)(2,1)S(1)}, u32[]{:S(2)}, u32[]{:S(2)}) collective-permute-start(bf16[1,192,384]{2,1,0:T(8,128)(2,1)S(1)} %get-tuple-element.201), channel_id=1, source_target_pairs={{0,16},{1,17},{2,18},{3,19},{4,20},{5,21},{6,22},{7,23},{8,24},{9,... | collective-permute-start | bytes 442376 | tf_op jit(solution)/shard_map/ppermute | solution.py:685
  133.4 22.3 %collective-permute-start.18 = (bf16[2,64,384]{2,1,0:T(8,128)(2,1)S(1)}, bf16[2,64,384]{2,1,0:T(8,128)(2,1)S(1)}, u32[]{:S(2)}, u32[]{:S(2)}) collective-permute-start(bf16[2,64,384]{2,1,0:T(8,128)(2,1)S(1)} %get-tuple-element.217), channel_id=1, source_target_pairs={{0,4},{1,5},{2,6},{3,7},{4,0},{5,1},{6,2},{7,3},{8,12},{9,13},{10,... | collective-permute-start | bytes 294920 | tf_op jit(solution)/shard_map/ppermute | solution.py:685
  133.7 22.0 %collective-permute-start.14 = (bf16[2,128,384]{2,1,0:T(8,128)(2,1)S(1)}, bf16[2,128,384]{2,1,0:T(8,128)(2,1)S(1)}, u32[]{:S(2)}, u32[]{:S(2)}) collective-permute-start(bf16[2,128,384]{2,1,0:T(8,128)(2,1)S(1)} %pad_maximum_fusion.13), channel_id=1, source_target_pairs={{0,8},{1,9},{2,10},{3,11},{4,12},{5,13},{6,14},{7,15},{8,0},{9,1},... | collective-permute-start | bytes 589832 | tf_op jit(solution)/shard_map/ppermute | solution.py:685
  143.1 15.6 %collective-permute-start.21 = (bf16[1,192,384]{2,1,0:T(8,128)(2,1)S(1)}, bf16[1,192,384]{2,1,0:T(8,128)(2,1)S(1)}, u32[]{:S(2)}, u32[]{:S(2)}) collective-permute-start(bf16[1,192,384]{2,1,0:T(8,128)(2,1)S(1)} %add.121), channel_id=1, source_target_pairs={{0,16},{1,17},{2,18},{3,19},{4,20},{5,21},{6,22},{7,23},{8,24},{9,... | collective-permute-start | bytes 442376 | tf_op jit(solution)/shard_map/ppermute | solution.py:685
  161.5 18.0 %collective-permute-start.23 = (bf16[2,64,384]{2,1,0:T(8,128)(2,1)S(1)}, bf16[2,64,384]{2,1,0:T(8,128)(2,1)S(1)}, u32[]{:S(2)}, u32[]{:S(2)}) collective-permute-start(bf16[2,64,384]{2,1,0:T(8,128)(2,1)S(1)} %pad_maximum_fusion.20), channel_id=1, source_target_pairs={{0,4},{1,5},{2,6},{3,7},{4,0},{5,1},{6,2},{7,3},{8,12},{9,13},{10,... | collective-permute-start | bytes 294920 | tf_op jit(solution)/shard_map/ppermute | solution.py:685
  162.9 16.5 %collective-permute-start.24 = (bf16[2,128,384]{2,1,0:T(8,128)(2,1)S(1)}, bf16[2,128,384]{2,1,0:T(8,128)(2,1)S(1)}, u32[]{:S(2)}, u32[]{:S(2)}) collective-permute-start(bf16[2,128,384]{2,1,0:T(8,128)(2,1)S(1)} %fusion.1), channel_id=1, source_target_pairs={{0,8},{1,9},{2,10},{3,11},{4,12},{5,13},{6,14},{7,15},{8,0},{9,1},... | collective-permute-start | bytes 589832 | tf_op jit(solution)/shard_map/ppermute | solution.py:685
  164.7 16.2 %collective-permute-start.22 = (bf16[1,192,384]{2,1,0:T(8,128)(2,1)S(1)}, bf16[1,192,384]{2,1,0:T(8,128)(2,1)S(1)}, u32[]{:S(2)}, u32[]{:S(2)}) collective-permute-start(bf16[1,192,384]{2,1,0:T(8,128)(2,1)S(1)} %fusion.10), channel_id=1, source_target_pairs={{0,16},{1,17},{2,18},{3,19},{4,20},{5,21},{6,22},{7,23},{8,24},{9,... | collective-permute-start | bytes 442376 | tf_op jit(solution)/shard_map/ppermute | solution.py:685
  179.4 17.7 %collective-permute-start.29 = (bf16[4,64,384]{2,1,0:T(8,128)(2,1)S(1)}, bf16[4,64,384]{2,1,0:T(8,128)(2,1)S(1)}, u32[]{:S(2)}, u32[]{:S(2)}) collective-permute-start(bf16[4,64,384]{2,1,0:T(8,128)(2,1)S(1)} %get-tuple-element.207), channel_id=1, source_target_pairs={{0,2},{1,3},{2,0},{3,1},{4,6},{5,7},{6,4},{7,5},{8,10},{9,11},{10,... | collective-permute-start | bytes 589832 | tf_op jit(solution)/shard_map/ppermute | solution.py:685
  179.6 17.5 %collective-permute-start.30 = (bf16[4,64,384]{2,1,0:T(8,128)(2,1)S(1)}, bf16[4,64,384]{2,1,0:T(8,128)(2,1)S(1)}, u32[]{:S(2)}, u32[]{:S(2)}) collective-permute-start(bf16[4,64,384]{2,1,0:T(8,128)(2,1)S(1)} %get-tuple-element.208), channel_id=1, source_target_pairs={{0,4},{1,5},{2,6},{3,7},{4,0},{5,1},{6,2},{7,3},{8,12},{9,13},{10,... | collective-permute-start | bytes 589832 | tf_op jit(solution)/shard_map/ppermute | solution.py:685
  181.0 16.3 %collective-permute-start.28 = (bf16[4,64,384]{2,1,0:T(8,128)(2,1)S(1)}, bf16[4,64,384]{2,1,0:T(8,128)(2,1)S(1)}, u32[]{:S(2)}, u32[]{:S(2)}) collective-permute-start(bf16[4,64,384]{2,1,0:T(8,128)(2,1)S(1)} %pad_maximum_fusion.15), channel_id=1, source_target_pairs={{0,2},{1,3},{2,0},{3,1},{4,6},{5,7},{6,4},{7,5},{8,10},{9,11},{10,... | collective-permute-start | bytes 589832 | tf_op jit(solution)/shard_map/ppermute | solution.py:685
  182.5 14.5 %collective-permute-start.31 = (bf16[4,64,384]{2,1,0:T(8,128)(2,1)S(1)}, bf16[4,64,384]{2,1,0:T(8,128)(2,1)S(1)}, u32[]{:S(2)}, u32[]{:S(2)}) collective-permute-start(bf16[4,64,384]{2,1,0:T(8,128)(2,1)S(1)} %pad_maximum_fusion.14), channel_id=1, source_target_pairs={{0,2},{1,3},{2,0},{3,1},{4,6},{5,7},{6,4},{7,5},{8,10},{9,11},{10,... | collective-permute-start | bytes 589832 | tf_op jit(solution)/shard_map/ppermute | solution.py:685
  182.7 19.9 %collective-permute-start.35 = (bf16[2,64,384]{2,1,0:T(8,128)(2,1)S(1)}, bf16[2,64,384]{2,1,0:T(8,128)(2,1)S(1)}, u32[]{:S(2)}, u32[]{:S(2)}) collective-permute-start(bf16[2,64,384]{2,1,0:T(8,128)(2,1)S(1)} %pad_maximum_fusion.19), channel_id=1, source_target_pairs={{0,4},{1,5},{2,6},{3,7},{4,0},{5,1},{6,2},{7,3},{8,12},{9,13},{10,... | collective-permute-start | bytes 294920 | tf_op jit(solution)/shard_map/ppermute | solution.py:685
  197.3 18.6 %collective-permute-start.54 = (bf16[8,64,384]{2,1,0:T(8,128)(2,1)S(1)}, bf16[8,64,384]{2,1,0:T(8,128)(2,1)S(1)}, u32[]{:S(2)}, u32[]{:S(2)}) collective-permute-start(bf16[8,64,384]{2,1,0:T(8,128)(2,1)S(1)} %pad_maximum_fusion.5.refs_8_), channel_id=1, source_target_pairs={{0,1},{1,0},{2,3},{3,2},{4,5},{5,4},{6,7},{7,6},{8,9},{9,8},{10,11... | collective-permute-start | bytes 1179656 | tf_op jit(solution)/shard_map/ppermute | solution.py:685
  198.4 17.6 %collective-permute-start.53 = (bf16[8,64,384]{2,1,0:T(8,128)(2,1)S(1)}, bf16[8,64,384]{2,1,0:T(8,128)(2,1)S(1)}, u32[]{:S(2)}, u32[]{:S(2)}) collective-permute-start(bf16[8,64,384]{2,1,0:T(8,128)(2,1)S(1)} %pad_maximum_fusion.5.refs_8_), channel_id=1, source_target_pairs={{0,8},{1,9},{2,10},{3,11},{4,12},{5,13},{6,14},{7,15},{8,0},{9,1},... | collective-permute-start | bytes 1179656 | tf_op jit(solution)/shard_map/ppermute | solution.py:685
  252.0 15.4 %collective-permute-start.41 = (bf16[8,64,384]{2,1,0:T(8,128)(2,1)S(1)}, bf16[8,64,384]{2,1,0:T(8,128)(2,1)S(1)}, u32[]{:S(2)}, u32[]{:S(2)}) collective-permute-start(bf16[8,64,384]{2,1,0:T(8,128)(2,1)S(1)} %pad_maximum_fusion.7.refs_4_), channel_id=1, source_target_pairs={{0,1},{1,0},{2,3},{3,2},{4,5},{5,4},{6,7},{7,6},{8,9},{9,8},{10,11... | collective-permute-start | bytes 1179656 | tf_op jit(solution)/shard_map/ppermute | solution.py:685
  252.1 15.3 %collective-permute-start.37 = (bf16[8,64,384]{2,1,0:T(8,128)(2,1)S(1)}, bf16[8,64,384]{2,1,0:T(8,128)(2,1)S(1)}, u32[]{:S(2)}, u32[]{:S(2)}) collective-permute-start(bf16[8,64,384]{2,1,0:T(8,128)(2,1)S(1)} %pad_maximum_fusion.6.refs_0_), channel_id=1, source_target_pairs={{0,1},{1,0},{2,3},{3,2},{4,5},{5,4},{6,7},{7,6},{8,9},{9,8},{10,11... | collective-permute-start | bytes 1179656 | tf_op jit(solution)/shard_map/ppermute | solution.py:685
  252.6 14.9 %collective-permute-start.46 = (bf16[8,64,384]{2,1,0:T(8,128)(2,1)S(1)}, bf16[8,64,384]{2,1,0:T(8,128)(2,1)S(1)}, u32[]{:S(2)}, u32[]{:S(2)}) collective-permute-start(bf16[8,64,384]{2,1,0:T(8,128)(2,1)S(1)} %collective-permute-done.44.refs_9_), channel_id=1, source_target_pairs={{0,1},{1,0},{2,3},{3,2},{4,5},{5,4},{6,7},{7,6},{8,9},{9,8},{10,11... | collective-permute-start | bytes 1179656 | tf_op jit(solution)/shard_map/ppermute | solution.py:685
  252.7 14.8 %collective-permute-start.42 = (bf16[8,64,384]{2,1,0:T(8,128)(2,1)S(1)}, bf16[8,64,384]{2,1,0:T(8,128)(2,1)S(1)}, u32[]{:S(2)}, u32[]{:S(2)}) collective-permute-start(bf16[8,64,384]{2,1,0:T(8,128)(2,1)S(1)} %collective-permute-done.40.refs_5_), channel_id=1, source_target_pairs={{0,1},{1,0},{2,3},{3,2},{4,5},{5,4},{6,7},{7,6},{8,9},{9,8},{10,11... | collective-permute-start | bytes 1179656 | tf_op jit(solution)/shard_map/ppermute | solution.py:685
  (75 other events, 962.7 us)
Sparse Core Ops, SparseCore 0:
  133.8 68.1 all-gather.1

commit v4 on v3

--- a/solution.py
+++ b/solution.py
@@ -1,4 +1,5 @@
 import functools
+import math
 import jax
 import jax.numpy as jnp
 from jax import lax
@@ -90,7 +91,11 @@
     lax.fori_loop(0, seqs, chain, 0)
 
 
-def put_send(out, grad, base, chunk0, me, rows_are_chunks):
+SPLIT = 1
+PIECE = HALF // SPLIT
+
+
+def put_send(outs, grad, base, chunk0, me, rows_are_chunks):
     size = grad.shape[0 if rows_are_chunks else 1]
     for i in range(size // CHUNK):
         for t in range(2):
@@ -98,7 +103,9 @@
                 value = grad[i * CHUNK + t * HALF : i * CHUNK + (t + 1) * HALF, :]
             else:
                 value = grad[t * HALF : (t + 1) * HALF, i * CHUNK : (i + 1) * CHUNK]
-            out[((chunk0 + i) ^ me[1]) * 2 + (t ^ me[2]) - base] = value.astype(bf16)
+            value = value.astype(bf16)
+            for n, out in enumerate(outs):
+                out[((chunk0 + i) ^ me[1]) * 2 + (t ^ me[2]) - base] = value[n * PIECE : (n + 1) * PIECE]
 
 
 def fwd_kernel(*refs):
@@ -107,11 +114,14 @@
     src = dict(zip(FWD_IN, refs[11:19]))
     lse, small = refs[19:21]
     dst = dict(zip(FWD_OUT, refs[21:30]))
-    hid_h, slope_h, send_h = refs[30:33]
-    rest = refs[33:]
+    hid_h, slope_h = refs[30:32]
+    send_h = refs[32 : 32 + SPLIT]
+    rest = refs[32 + SPLIT :]
     vin = dict(zip(FWD_IN, rest[:8]))
     vout = dict(zip(FWD_OUT, rest[8:17]))
-    hid, slope, send, acc, sem_in, sem_out, sem_ff, sem_send = rest[17:]
+    hid, slope = rest[17:19]
+    send = rest[19 : 19 + SPLIT]
+    acc, sem_in, sem_out, sem_ff, sem_send = rest[19 + SPLIT :]
     rows, width = vin["x"].shape
     ff = vin["wi"].shape[1]
     seqs = lens.shape[0]
@@ -221,22 +231,24 @@
     store("out").start()
     far = ds((1 - me[0]) * CHUNK, CHUNK)
 
-    def send_copy(n):
+    def send_copies(n):
         part = pl.ds(4 * (n ^ (me[1] >> 1)), 4)
-        return pltpu.make_async_copy(send.at[part], send_h.at[part], sem_send.at[n])
+        return [
+            pltpu.make_async_copy(a.at[part], b.at[part], sem_send.at[i, n]) for i, (a, b) in enumerate(zip(send, send_h))
+        ]
 
     def grads(n, _):
         put_send(send, tn(hid[:, ds(n * width, width)], dffn[:, far]), 0, 2 * n, me, True)
-        send_copy(n).start()
+        for one in send_copies(n):
+            one.start()
         return 0
 
     lax.fori_loop(0, part_ff, grads, 0)
     for name in FWD_OUT:
         store(name).wait()
     for n in range(part_ff):
-        for one in ff_copies(n):
+        for one in ff_copies(n) + tuple(send_copies(n)):
             one.wait()
-        send_copy(n).wait()
 
 
 def forward(lens, me, vectors, arrays):
@@ -246,23 +258,23 @@
     like = lambda shape, dtype=bf16: sd(shape, dtype)
     thin = like((rows, width))
     outs = [thin, thin, thin, thin, like((rows, width), f32), like((rows, 1), f32), thin, thin, thin]
-    wide = [like((rows, ff)), like((rows, ff)), like((16, HALF, CHUNK))]
+    wide = [like((rows, ff)), like((rows, ff))] + [like((16, PIECE, CHUNK))] * SPLIT
     dma = pltpu.SemaphoreType.DMA
     return pl.pallas_call(
         fwd_kernel,
         in_specs=[SMEM, SMEM] + [VMEM] * 9 + [HBM] * 8,
-        out_specs=[VMEM, VMEM] + [HBM] * 12,
+        out_specs=[VMEM, VMEM] + [HBM] * (11 + SPLIT),
         out_shape=[like((seqs, H, rows // seqs), f32), like((8, width), f32)] + outs + wide,
         scratch_shapes=[pltpu.VMEM(a.shape, a.dtype) for a in arrays]
         + [pltpu.VMEM(o.shape, o.dtype) for o in outs + wide]
-        + [pltpu.VMEM((rows, width), f32), dma((8,)), dma((9,)), dma((2, ff // width)), dma((ff // width,))],
+        + [pltpu.VMEM((rows, width), f32), dma((8,)), dma((9,)), dma((2, ff // width)), dma((SPLIT, ff // width))],
         compiler_params=params(),
         cost_estimate=cost(28e9),
         name="forward",
     )(lens, me, *vectors, *arrays)
 
 
-def pre_kernel(me, dffn, w2, slope, fin, small2, dpre_o, send_o, small):
+def pre_kernel(me, dffn, w2, slope, fin, small2, dpre_o, small, *send_o):
     p = pl.program_id(0)
     n = p ^ (me[1] >> 1)
 
@@ -295,18 +307,15 @@
             ],
             out_specs=[
                 pl.BlockSpec((rows, width), lambda p, me: (0, at(p, me))),
-                pl.BlockSpec((4, HALF, CHUNK), lambda p, me: (p, 0, 0)),
                 pl.BlockSpec((16, width), lambda p, me: (0, 0)),
-            ],
+            ]
+            + [pl.BlockSpec((4, PIECE, CHUNK), lambda p, me: (p, 0, 0))] * SPLIT,
         ),
-        out_shape=[sd((rows, ff), bf16), sd((16, HALF, CHUNK), bf16), sd((16, width), f32)],
+        out_shape=[sd((rows, ff), bf16), sd((16, width), f32)] + [sd((16, PIECE, CHUNK), bf16)] * SPLIT,
         compiler_params=params(),
         cost_estimate=cost(8e9),
         name="pre_bwd",
     )(me, dffn, w2, slope, fin, small2)
-
-
-BWD_IN = ("dffn", "xhat", "rstd", "wo", "q", "k", "v", "lse", "x", "mixed")
 
 
 def attention_bwd(lens, q, k, v, dm, lse, d, small):
@@ -346,20 +355,22 @@
     lax.fori_loop(0, seqs, chain, 0)
 
 
-def bwd_kernel(*refs):
-    lens, me, g1, small1, dpre_h, wi_h = refs[:6]
-    src = dict(zip(BWD_IN, refs[6:16]))
-    small, dh1_h, d_h, send_h = refs[16:20]
-    dpre, wi = refs[20:22]
-    vin = dict(zip(BWD_IN, refs[22:32]))
-    dh1, d, send, acc, dm, sem_ff, sem_in, sem_out, sem_send = refs[32:]
+MID_IN = ("dffn", "xhat", "rstd", "wo")
+
+
+def mid_kernel(*refs):
+    g1, small1, dpre_h, wi_h = refs[:4]
+    src = dict(zip(MID_IN, refs[4:8]))
+    small, dh1_h, dob_h, dm_h = refs[8:12]
+    dpre, wi = refs[12:14]
+    vin = dict(zip(MID_IN, refs[14:18]))
+    dh1, dob, dm, acc, sem_ff, sem_in, sem_out = refs[18:]
     rows, width = acc.shape
     part_ff = dpre.shape[1] // width
-    seqs = lens.shape[0]
-    R = rows // seqs
+    R = 160
 
     def load(name):
-        return pltpu.make_async_copy(src[name], vin[name], sem_in.at[BWD_IN.index(name)])
+        return pltpu.make_async_copy(src[name], vin[name], sem_in.at[MID_IN.index(name)])
 
     def ff_copies(n):
         c = slice(n * width, (n + 1) * width)
@@ -371,7 +382,7 @@
     for n in range(part_ff):
         for one in ff_copies(n):
             one.start()
-    for name in BWD_IN:
+    for name in MID_IN:
         load(name).start()
     for n in range(part_ff):
         c = slice(n * width, (n + 1) * width)
@@ -384,7 +395,6 @@
     dffn, xhat, rstd = vin["dffn"], vin["xhat"], vin["rstd"]
     for name in ("dffn", "xhat", "rstd"):
         load(name).wait()
-    dob = slice(3 * width, 4 * width)
 
     def norm_one(i, _):
         r = ds(i * R, R, 32)
@@ -394,58 +404,108 @@
         v = rstd[r, :] * (e - row_mean(e) - unit * row_mean(e * unit))
         dh1[r, :] = v
         low = v.astype(bf16)
-        d[r, dob] = low
+        dob[r, :] = low
         small[3:4, :] += jnp.sum(g * unit, 0, keepdims=True)
         small[4:5, :] += jnp.sum(g, 0, keepdims=True)
         small[5:6, :] += jnp.sum(low.astype(f32), 0, keepdims=True)
         return 0
 
-    lax.fori_loop(0, seqs, norm_one, 0)
-    dh1_copy = pltpu.make_async_copy(dh1, dh1_h, sem_out.at[0])
-    dh1_copy.start()
+    lax.fori_loop(0, rows // R, norm_one, 0)
+    stores = [pltpu.make_async_copy(a, b, sem_out.at[n]) for n, (a, b) in enumerate(((dh1, dh1_h), (dob, dob_h), (dm, dm_h)))]
+    stores[0].start()
+    stores[1].start()
     load("wo").wait()
-    dm[...] = nt(d[:, dob], vin["wo"][...]).astype(bf16)
-    for name in ("q", "k", "v", "lse"):
+    dm[...] = nt(dob[...], vin["wo"][...]).astype(bf16)
+    stores[2].start()
+    for one in stores:
+        one.wait()
+
+
+def mid_call(g1, small1, dpre, wi, arrays):
+    rows, width = arrays[0].shape
+    ff = wi.shape[1]
+    dma = pltpu.SemaphoreType.DMA
+    vm = lambda a: pltpu.VMEM(a.shape, a.dtype)
+    outs = [sd((rows, width), f32), sd((rows, width), bf16), sd((rows, width), bf16)]
+    return pl.pallas_call(
+        mid_kernel,
+        in_specs=[VMEM, VMEM] + [HBM] * 6,
+        out_specs=[VMEM] + [HBM] * 3,
+        out_shape=[sd((16, width), f32)] + outs,
+        scratch_shapes=[vm(dpre), vm(wi)] + [vm(a) for a in arrays] + [vm(o) for o in outs]
+        + [pltpu.VMEM((rows, width), f32), dma((2, ff // width)), dma((4,)), dma((3,))],
+        compiler_params=params(),
+        cost_estimate=cost(10e9),
+        name="mid_bwd",
+    )(g1, small1, dpre, wi, *arrays)
+
+
+ATT_IN = ("q", "k", "v", "dm", "lse", "x", "mixed", "dob")
+
+
+def att_kernel(*refs):
+    lens, me, small1 = refs[:3]
+    src = dict(zip(ATT_IN, refs[3:11]))
+    small, d_h = refs[11:13]
+    send_h = refs[13 : 13 + SPLIT]
+    rest = refs[13 + SPLIT :]
+    vin = dict(zip(ATT_IN, rest[:8]))
+    d = rest[8]
+    send = rest[9 : 9 + SPLIT]
+    sem_in, sem_out, sem_send = rest[9 + SPLIT :]
+    width = d.shape[1] // 4
+
+    def load(name):
+        if name == "dob":
+            return pltpu.make_async_copy(src[name], d.at[:, 3 * width : 4 * width], sem_in.at[7])
+        return pltpu.make_async_copy(src[name], vin[name], sem_in.at[ATT_IN.index(name)])
+
+    for name in ATT_IN:
+        load(name).start()
+    small[...] = small1[...]
+    for name in ("q", "k", "v", "dm", "lse"):
         load(name).wait()
-    attention_bwd(lens, vin["q"], vin["k"], vin["v"], dm, vin["lse"], d, small)
-    d_copy = pltpu.make_async_copy(d, d_h, sem_out.at[1])
+    attention_bwd(lens, vin["q"], vin["k"], vin["v"], vin["dm"], vin["lse"], d, small)
+    load("dob").wait()
+    d_copy = pltpu.make_async_copy(d, d_h, sem_out.at[0])
     d_copy.start()
     load("x").wait()
     load("mixed").wait()
     far = ds((1 - me[0]) * CHUNK, CHUNK)
 
-    def send_copy(n):
+    def send_copies(n):
         part = pl.ds(4 * (n ^ (me[1] >> 1)), 4)
-        return pltpu.make_async_copy(send.at[part], send_h.at[part], sem_send.at[n])
+        return [
+            pltpu.make_async_copy(a.at[part], b.at[part], sem_send.at[i, n]) for i, (a, b) in enumerate(zip(send, send_h))
+        ]
 
     for n in range(4):
         left = vin["mixed" if n == 3 else "x"]
         put_send(send, tn(left[:, far], d[:, n * width : (n + 1) * width]), 0, 2 * n, me, False)
-        send_copy(n).start()
-    dh1_copy.wait()
+        for one in send_copies(n):
+            one.start()
     d_copy.wait()
     for n in range(4):
-        send_copy(n).wait()
-
-
-def bwd_call(lens, me, g1, small1, dpre, wi, arrays):
+        for one in send_copies(n):
+            one.wait()
+
+
+def att_call(lens, me, small1, arrays):
     rows, width = arrays[0].shape
-    ff = wi.shape[1]
     dma = pltpu.SemaphoreType.DMA
     vm = lambda a: pltpu.VMEM(a.shape, a.dtype)
-    outs = [sd((rows, width), f32), sd((rows, 4 * width), bf16), sd((16, HALF, CHUNK), bf16)]
+    outs = [sd((rows, 4 * width), bf16)] + [sd((16, PIECE, CHUNK), bf16)] * SPLIT
     return pl.pallas_call(
-        bwd_kernel,
-        in_specs=[SMEM, SMEM, VMEM, VMEM] + [HBM] * 12,
-        out_specs=[VMEM] + [HBM] * 3,
+        att_kernel,
+        in_specs=[SMEM, SMEM, VMEM] + [HBM] * 8,
+        out_specs=[VMEM] + [HBM] * (1 + SPLIT),
         out_shape=[sd((16, width), f32)] + outs,
-        scratch_shapes=[vm(dpre), vm(wi)] + [vm(a) for a in arrays] + [vm(o) for o in outs]
-        + [pltpu.VMEM((rows, width), f32), pltpu.VMEM((rows, width), bf16)]
-        + [dma((2, ff // width)), dma((10,)), dma((2,)), dma((4,))],
+        scratch_shapes=[vm(a) for a in arrays[:7]] + [pltpu.VMEM((8, 128), bf16)] + [vm(o) for o in outs]
+        + [dma((8,)), dma((1,)), dma((SPLIT, 4))],
         compiler_params=params(),
-        cost_estimate=cost(22e9),
-        name="backward",
-    )(lens, me, g1, small1, dpre, wi, *arrays)
+        cost_estimate=cost(12e9),
+        name="att_bwd",
+    )(lens, me, small1, *arrays)
 
 
 def dx_kernel(dh1_h, d_h, wq_h, wk_h, wv_h, o_h, dh1, d, wq, wk, wv, o, sem, sem_out):
@@ -511,8 +571,8 @@
 def keep_kernel(kind, orders, me, *refs):
     p = pl.program_id(0)
     n_in = 3 if kind == "attn" else 2
-    got = refs[n_in]
-    outs = refs[n_in + 1 : -1]
+    gots = refs[n_in : n_in + SPLIT]
+    outs = refs[n_in + SPLIT : -1]
     g = refs[-1]
     g[...] = pair_grad(kind, p ^ (me[1] >> 1), refs[:n_in])
     size = HALF // len(orders)
@@ -525,7 +585,8 @@
                 grad = g[ds((i ^ (me[1] & 1)) * CHUNK + part, HALF), :]
             else:
                 grad = g[ds(part, HALF), far]
-            total = (grad + got[2 * i + t].astype(f32)).astype(bf16)
+            got = jnp.concatenate([v[2 * i + t] for v in gots])
+            total = (grad + got.astype(f32)).astype(bf16)
             for n, order in enumerate(orders):
                 where = bit(step, order[1]) * 4 + bit(step, order[2]) * 2 + t
                 first = bit(step, order[0])
@@ -565,7 +626,7 @@
             num_scalar_prefetch=1,
             grid=(4,),
             in_specs=grad_specs(kind, rows, 0, lambda p, me: p ^ (me[1] >> 1))
-            + [pl.BlockSpec((4, HALF, CHUNK), lambda p, me: (p, 0, 0))],
+            + [pl.BlockSpec((4, PIECE, CHUNK), lambda p, me: (p, 0, 0))] * SPLIT,
             out_specs=[pl.BlockSpec(shape, lambda p, me: (0, 0, 0))] * (2 * len(orders)),
             scratch_shapes=[pltpu.VMEM(g_shape, f32)],
         ),
@@ -573,18 +634,32 @@
         compiler_params=params(),
         cost_estimate=cost(3e9),
         name="keep_" + kind,
-    )(me, *args, got)
-
-
-def unpack_kernel(kind, colors, me, *refs):
-    ins = refs[: 4 * colors]
+    )(me, *args, *got)
+
+
+ORDER_OF = ("xyab", "yxab", "axyb")
+
+
+def unpack_kernel(kind, orders, me, *refs):
+    colors = len(orders)
+    n_in = 4 * colors
+    src = refs[:n_in]
     n_out = 4 if kind == "attn" else 1
-    outs = refs[4 * colors : 4 * colors + n_out]
-    buf, sem = refs[4 * colors + n_out :]
+    outs = refs[n_in : n_in + n_out]
+    ins = refs[n_in + n_out : 2 * n_in + n_out]
+    buf, sem_in, sem = refs[2 * n_in + n_out :]
     size = HALF // colors
-
-    def copy(step, slot):
+    slots = buf.shape[0]
+
+    order_in = [n for first in range(2) for n in range(n_in) if n % 2 == first]
+    loads = [pltpu.make_async_copy(src[n], ins[n], sem_in.at[n]) for n in range(n_in)]
+    for n in order_in:
+        loads[n].start()
+    waited = set()
+
+    def copies(step):
         chunk = step ^ me[1]
+        slot = step % slots
         if kind == "outer":
             return [(None, pltpu.make_async_copy(buf.at[slot], outs[0].at[ds(chunk * CHUNK, CHUNK), :], sem.at[slot]))]
         if kind == "inner":
@@ -594,41 +669,40 @@
             for m in range(4)
         ]
 
-    def each(step, slot, act):
-        for cond, one in copy(step, slot):
+    def each(step, act):
+        for cond, one in copies(step):
             if cond is None:
                 act(one)
             else:
                 pl.when(cond)(functools.partial(act, one))
 
     for step in range(8):
-        slot = step % 2
-        if step >= 2:
-            each(step - 2, slot, lambda one: one.wait())
+        slot = step % slots
+        if step >= slots:
+            each(step - slots, lambda one: one.wait())
         for half in range(2):
             place = (half ^ me[0]) * CHUNK
             for n in range(colors):
-                own, got = ins[4 * n + 2 * half : 4 * n + 2 * half + 2]
-                order = ORDER_OF[n]
-                src = got if bit(step, order[0]) else own
+                order = orders[n]
+                at = 4 * n + 2 * half + bit(step, order[0])
+                if at not in waited:
+                    waited.add(at)
+                    loads[at].wait()
                 for t in range(2):
                     where = bit(step, order[1]) * 4 + bit(step, order[2]) * 2 + t
-                    row = (t ^ me[2]) * HALF + n * size
-                    value = src[where].astype(f32)
+                    start = (t ^ me[2]) * HALF + n * size
+                    value = ins[at][where].astype(f32)
                     if kind == "outer":
-                        buf[slot, ds(row, size, 32), ds(place, CHUNK)] = value
+                        buf[slot, ds(start, size, 32), ds(place, CHUNK)] = value
                     else:
-                        buf[slot, ds(place + row, size, 32), :] = value
-        each(step, slot, lambda one: one.start())
-    for step in (6, 7):
-        each(step, step % 2, lambda one: one.wait())
-
-
-ORDER_OF = ("xyab", "yxab", "axyb")
-
-
-def unpack(kind, me, pieces):
-    colors = len(pieces) // 4
+                        buf[slot, ds(place + start, size, 32), :] = value
+        each(step, lambda one: one.start())
+    for step in range(8 - slots, 8):
+        each(step, lambda one: one.wait())
+
+
+def unpack(kind, me, pieces, orders):
+    colors = len(orders)
     width = 2 * CHUNK
     if kind == "outer":
         out_shape = [sd((8 * CHUNK, width), f32)]
@@ -636,13 +710,15 @@
         out_shape = [sd((width, 8 * CHUNK), f32)]
     else:
         out_shape = [sd((width, width), f32)] * 4
-    buf = (2, CHUNK, width) if kind == "outer" else (2, width, CHUNK)
+    buf = (4, CHUNK, width) if kind == "outer" else (4, width, CHUNK)
+    dma = pltpu.SemaphoreType.DMA
     return pl.pallas_call(
-        functools.partial(unpack_kernel, kind, colors),
-        in_specs=[SMEM] + [VMEM] * (4 * colors),
+        functools.partial(unpack_kernel, kind, orders),
+        in_specs=[SMEM] + [HBM] * (4 * colors),
         out_specs=[HBM] * len(out_shape),
         out_shape=out_shape,
-        scratch_shapes=[pltpu.VMEM(buf, f32), pltpu.SemaphoreType.DMA((2,))],
+        scratch_shapes=[pltpu.VMEM(v.shape, v.dtype) for v in pieces]
+        + [pltpu.VMEM(buf, f32), dma((4 * colors,)), dma((4,))],
         compiler_params=params(),
         cost_estimate=cost(4e9),
         name="unpack_" + kind,
@@ -652,16 +728,16 @@
 SMALL_ROWS = (6, 7, 5, 3, 4, 8, 2, 0, 1)
 
 
-def small_kernel(parts, *outs):
-    width = parts.shape[1]
-    total = jnp.sum(parts[...].reshape(parts.shape[0] // 16, 16, width), 0)
+def small_kernel(total, *outs):
+    half = total.shape[1]
     for at, out in zip(SMALL_ROWS, outs):
-        for n in range(out.shape[0] // width):
-            out[pl.ds(n * width, width)] = total[at + n : at + n + 1, :].reshape(width)
-
-
-def small_call(parts, ff):
-    width = parts.shape[1]
+        for n in range(out.shape[0] // half):
+            line = at + n // 2 + (n % 2) * (total.shape[0] // 2)
+            out[pl.ds(n * half, half)] = total[line : line + 1, :].reshape(half)
+
+
+def small_call(total, ff):
+    width = 2 * total.shape[1]
     sizes = [ff if at == 8 else width for at in SMALL_ROWS]
     return pl.pallas_call(
         small_kernel,
@@ -669,9 +745,9 @@
         out_specs=[VMEM] * 9,
         out_shape=[sd((n,), f32) for n in sizes],
         compiler_params=params(),
-        cost_estimate=cost(2e9),
+        cost_estimate=cost(1e9),
         name="vectors",
-    )(parts)
+    )(total)
 
 
 AXES = ("dp", "seq")
@@ -685,143 +761,114 @@
     return lax.ppermute(value, AXES, [(i, i ^ flip) for i in range(dp * seq)])
 
 
-def after(value, *earlier):
-    return lax.optimization_barrier((value,) + earlier)[0]
-
-
-def add_halves(keep, got):
-    half = keep.shape[0] // 2
-    return keep[:half] + got[:half], keep[half:] + got[half:]
-
-
-def gather(own, order):
-    for n, name in enumerate(reversed(order)):
-        got = swap(own, name)
-        if n + 1 < len(order):
-            own = jnp.concatenate([own, got])
-    return own, got
-
-
-def finish(own):
+ORDERS = ("xya", "yax", "axy")
+
+
+def both_halves(keep, got):
+    return keep[0] + got[0], keep[1] + got[1]
+
+
+def reduction(blocks):
+    keeps = [v.reshape((2, 2, 2) + v.shape[1:]) for v in blocks[0::2]]
+    sends = [v.reshape((2, 2, 2) + v.shape[1:]) for v in blocks[1::2]]
+    for level in range(3):
+        gots = yield [(o[level], v) for o, v in zip(ORDERS, sends)]
+        if level < 2:
+            keeps, sends = zip(*[both_halves(k, g) for k, g in zip(keeps, gots)])
+    own = jnp.concatenate([k + g for k, g in zip(keeps, gots)], -2)
+    (got,) = yield [("b", own)]
+    own = own + jnp.concatenate([got[1:], got[:1]])
     for extra in range(4, lax.axis_size("dp").bit_length() - 1):
         own = own + swap(own, extra)
-    return own
-
-
-RS_ORDERS = {"outer": ("xyab",), "inner": ("axyb",), "attn": ORDER_OF}
-
-
-class Line:
+    size = own.shape[1] // 3
+    owns = [own[:, n * size : (n + 1) * size] for n in range(3)]
+    for level in (2, 1):
+        gots = yield [(o[level], v) for o, v in zip(ORDERS, owns)]
+        owns = [jnp.concatenate(v) for v in zip(owns, gots)]
+    gots = yield [(o[0], v) for o, v in zip(ORDERS, owns)] + [("c", v) for v in owns]
+    near, far = gots[:3], gots[3:]
+    others = yield [("c", v) for v in near]
+    return [v for four in zip(owns, near, far, others) for v in four]
+
+
+def vector_sum(small):
+    half = small.shape[1] // 2
+    value = jnp.concatenate([small[:, :half], small[:, half:]])
+    links = ["c"] + list("axyb") + list(range(4, lax.axis_size("dp").bit_length() - 1))
+    for link in links:
+        sent = value.astype(bf16)
+        if isinstance(link, int):
+            got = swap(sent, link)
+        else:
+            (got,) = yield [(link, sent)]
+        value = sent.astype(f32) + got.astype(f32)
+    return value
+
+
+def unroll(v):
+    return v.reshape((-1, v.shape[-1]))
+
+
+class Rounds:
     def __init__(self):
-        self.last = ()
-
-    def __call__(self, value):
-        return lax.optimization_barrier((value,) + self.last)[0]
-
-    def done(self, *values):
-        self.last = values
-
-
-def rows_of(value, start, stop):
-    return value[:, start:stop]
-
-
-class One:
-    def __init__(self, line, blocks, order):
-        self.line, self.order, self.level = line, order, 0
-        self.keep = blocks[0]
-        self.got = swap(blocks[1], order[0])
-
-    def step(self):
-        got = self.line(self.got)
-        self.level += 1
-        if self.level == 4:
-            self.keep = self.keep + got
-            self.line.done(self.keep)
-            return finish(self.keep[0])
-        self.keep, send = add_halves(self.keep, got)
-        self.line.done(self.keep, send)
-        self.got = swap(send, self.order[self.level])
-
-
-class Three:
-    def __init__(self, line, blocks):
-        self.line = line
-        self.keep = dict(zip("ABC", blocks[0::2]))
-        self.got = {n: swap(blocks[2 * i + 1], ORDER_OF[i][0]) for i, n in enumerate("ABC")}
-
-    def first(self, n):
-        got = self.line(self.got[n])
-        self.keep[n], send = add_halves(self.keep[n], got)
-        self.line.done(self.keep[n], send)
-        self.got[n] = swap(send, ORDER_OF["ABC".index(n)][1])
-
-    def join(self):
-        gots = [self.line(self.got[n]) for n in "AB"]
-        pairs = [add_halves(self.keep[n], got) for n, got in zip("AB", gots)]
-        self.keep["AB"], send = [jnp.concatenate(v, 1) for v in zip(*pairs)]
-        self.line.done(self.keep["AB"], send)
-        self.got["AB"] = swap(send, "a")
-
-    def second(self):
-        got = self.line(self.got["C"])
-        self.keep["C"], send = add_halves(self.keep["C"], got)
-        self.line.done(self.keep["C"], send)
-        self.got["C"] = swap(send, ORDER_OF[2][2])
-
-    def last(self):
-        gots = [self.line(self.got[n]) for n in ("AB", "C")]
-        pairs = [add_halves(self.keep[n], got) for n, got in zip(("AB", "C"), gots)]
-        self.keep, send = [jnp.concatenate(v, 1) for v in zip(*pairs)]
-        self.line.done(self.keep, send)
-        self.got = swap(send, "b")
-
-    def end(self):
-        own = self.keep + self.line(self.got)
-        self.line.done(own)
-        return finish(own[0])
-
-
-class Gather:
-    def __init__(self, line, own):
-        self.line = line
-        self.own = own[None]
-        self.got = swap(self.own, "b")
-        self.pieces = {}
-
-    def first(self):
-        both_parts = jnp.concatenate([self.own, self.line(self.got)])
-        size = both_parts.shape[1] // 3
-        self.own = {"AB": both_parts[:, : 2 * size], "C": both_parts[:, 2 * size :]}
-        self.line.done(*self.own.values())
-        self.got = {"AB": swap(self.own["AB"], "a"), "C": swap(self.own["C"], ORDER_OF[2][2])}
-
-    def second(self):
-        four = jnp.concatenate([self.own["AB"], self.line(self.got["AB"])])
-        size = four.shape[1] // 2
-        self.own["A"], self.own["B"] = four[:, :size], four[:, size:]
-        self.line.done(self.own["A"], self.own["B"])
-        for n in "AB":
-            self.got[n] = swap(self.own[n], ORDER_OF["ABC".index(n)][1])
-
-    def third(self):
-        self.own["C"] = jnp.concatenate([self.own["C"], self.line(self.got["C"])])
-        self.line.done(self.own["C"])
-        self.got["C"] = swap(self.own["C"], ORDER_OF[2][1])
-
-    def fourth(self, n):
-        own = jnp.concatenate([self.own[n], self.line(self.got[n])])
-        self.line.done(own)
-        self.got[n] = swap(own, ORDER_OF["ABC".index(n)][0])
-        self.pieces[n] = [own, None, swap(own, "c"), None]
-
-    def last(self, n):
-        got = self.got[n]
-        self.pieces[n][1] = got
-        self.pieces[n][3] = swap(got, "c")
-
-    def all(self):
-        return [v for n in "ABC" for v in self.pieces[n]]
+        self.flows = {}
+        self.results = {}
+        self.wanted = {}
+        self.mark = ()
+
+    def add(self, name, flow):
+        self.flows[name] = flow
+        self.wanted[name] = next(flow)
+
+    def hold(self, value):
+        return lax.optimization_barrier((value,) + self.mark)[0]
+
+    def begin(self, extra=()):
+        self.order = [(name, n) for name in self.wanted for n in range(len(self.wanted[name]))]
+        links = {}
+        alone = {}
+        for name, n in self.order:
+            link, value = self.wanted[name][n]
+            if link == "c":
+                alone[name, n] = value
+            else:
+                links.setdefault(link, []).append((name, n))
+        merged = {}
+        for link, keys in links.items():
+            values = [self.wanted[k][n][1] for k, n in keys]
+            merged[link] = values[0] if len(values) == 1 else jnp.concatenate([unroll(v) for v in values])
+        merged, alone, extra = lax.optimization_barrier((merged, alone, tuple(extra)))
+        self.mark = tuple(merged.values())
+        self.got = {}
+        for link in "baxy":
+            if link not in links:
+                continue
+            keys = links[link]
+            got = swap(merged[link], link)
+            if len(keys) == 1:
+                self.got[keys[0]] = got
+                continue
+            row = 0
+            for k, n in keys:
+                shape = self.wanted[k][n][1].shape
+                count = math.prod(shape[:-1])
+                self.got[k, n] = got[row : row + count].reshape(shape)
+                row += count
+        for key, value in alone.items():
+            self.got[key] = swap(value, "c")
+        return [swap(v, "c") for v in extra]
+
+    def end(self, *beside):
+        got, _ = lax.optimization_barrier((self.got, tuple(beside)))
+        for name in list(self.flows):
+            if name not in self.wanted or (name, 0) not in got:
+                continue
+            values = [got[name, n] for n in range(len(self.wanted[name]))]
+            try:
+                self.wanted[name] = self.flows[name].send(values)
+            except StopIteration as stop:
+                self.results[name] = stop.value
+                del self.flows[name], self.wanted[name]
 
 
 def body(chains_in, lengths, d_out, w_query, b_query, w_key, w_value, b_value, w_output, b_output, gain_one, shift_one,
@@ -831,69 +878,50 @@
     place = lax.axis_index("dp") * 2 + lax.axis_index("seq")
     me = (place >> jnp.array([0, 1, 4], jnp.int32)) & jnp.array([1, 7, 1], jnp.int32)
     x = chains_in.reshape(rows, width)
-    line = Line()
     lse, small2, q, k, v, mixed, xhat, rstd, fin, out, dffn, hid, slope, send = forward(
         lengths, me, (b_query, b_value, b_output, gain_one, shift_one, b_inner, b_outer, gain_two, shift_two),
         (x, w_query, w_key, w_value, w_output, w_inner, w_outer, d_out.reshape(rows, width)),
     )
-    got1 = swap(send, "c")
-    dpre, send, small1 = pre_call(me, dffn, w_outer, slope, fin, small2)
-    got2 = swap(send, "c")
-    line.done(dpre)
-    blocks = grad_keep("outer", me, (hid, dffn), line(got1), RS_ORDERS["outer"])
-    line.done(*blocks)
-    r1 = One(line, blocks, "xyab")
-    blocks = grad_keep("inner", me, (fin, dpre), line(got2), RS_ORDERS["inner"])
-    line.done(*blocks)
-    r2 = One(line, blocks, "axyb")
-    small, dh1, d, send = bwd_call(
-        lengths, me, gain_one, small1, line(dpre), w_inner, (dffn, xhat, rstd, w_output, q, k, v, lse, x, mixed)
-    )
-    line.done(dh1, d, send)
-    r1.step()
-    r2.step()
-    got3 = swap(line(send), "c")
-    d_x = dx_call(line(dh1), d, w_query, w_key, w_value)
-    line.done(d_x)
-    blocks = grad_keep("attn", me, (x, mixed, d), line(got3), RS_ORDERS["attn"])
-    line.done(*blocks)
-    r3 = Three(line, blocks)
-    r1.step()
-    r2.step()
-    for n in "ABC":
-        r3.first(n)
-    r1.step()
-    r2.step()
-    r3.join()
-    r3.second()
-    g1 = Gather(line, r1.step())
-    g2 = Gather(line, r2.step())
-    r3.last()
-    g1.first()
-    g2.first()
-    g3 = Gather(line, r3.end())
-    for g in (g1, g2):
-        g.second()
-        g.third()
-    g3.first()
-    for n in "ABC":
-        g1.fourth(n)
-    for n in "ABC":
-        g2.fourth(n)
-    g3.second()
-    g3.third()
-    for n in "ABC":
-        g1.last(n)
-    for n in "ABC":
-        g3.fourth(n)
-    for n in "ABC":
-        g2.last(n)
-    for n in "ABC":
-        g3.last(n)
-    (d_w_outer,) = unpack("outer", me, g1.all())
-    (d_w_inner,) = unpack("inner", me, g2.all())
-    d_w_query, d_w_key, d_w_value, d_w_output = unpack("attn", me, g3.all())
-    vec = small_call(lax.all_gather(small, AXES, axis=0, tiled=True), w_inner.shape[1])
+    rounds = Rounds()
+    (got,) = rounds.begin([send])
+    dpre, small1, send = pre_call(me, dffn, w_outer, slope, fin, small2)
+    got, send = lax.optimization_barrier((got, send))
+    (got_i,) = rounds.begin([send])
+    blocks = grad_keep("outer", me, (hid, dffn), (got,), ORDERS)
+    rounds.add("outer", reduction(blocks))
+    rounds.begin()
+    blocks = grad_keep("inner", me, (fin, dpre), (rounds.hold(got_i),), ORDERS)
+    rounds.end(*blocks)
+    rounds.add("inner", reduction(blocks))
+    rounds.begin()
+    small, dh1, dob, dm = mid_call(gain_one, small1, rounds.hold(dpre), w_inner, (dffn, xhat, rstd, w_output))
+    rounds.end(dh1, dob, dm)
+    rounds.begin()
+    small, d, send = att_call(lengths, me, small, (q, k, v, rounds.hold(dm), lse, x, mixed, dob))
+    rounds.end(d, send)
+    rounds.add("vectors", vector_sum(small))
+    (got,) = rounds.begin([send])
+    blocks = grad_keep("attn", me, (x, mixed, d), (got,), ORDERS)
+    rounds.end(*blocks)
+    rounds.add("attn", reduction(blocks))
+    rounds.begin()
+    d_x = dx_call(rounds.hold(dh1), d, w_query, w_key, w_value)
+    rounds.end(d_x)
+    for _ in range(3):
+        rounds.begin()
+        rounds.end()
+    rounds.begin()
+    vec = small_call(rounds.hold(rounds.results["vectors"]), w_inner.shape[1])
+    rounds.end(vec[0])
+    rounds.begin()
+    (d_w_outer,) = unpack("outer", me, rounds.hold(rounds.results["outer"]), ORDERS)
+    rounds.end(d_w_outer)
+    rounds.begin()
+    (d_w_inner,) = unpack("inner", me, rounds.hold(rounds.results["inner"]), ORDERS)
+    rounds.end(d_w_inner)
+    rounds.begin()
+    rounds.end()
+    d_w_query, d_w_key, d_w_value, d_w_output = unpack("attn", me, rounds.results["attn"], ORDERS)
     return (
         out.reshape(seqs, length, width), d_x.reshape(seqs, length, width),
         d_w_query, vec[0], d_w_key, d_w_value, vec[1], d_w_output, vec[2], vec[3], vec[4],

time: 284 us -> 251 us (0.88)
  the two profiles are of different devices: /device:TPU:25 before, /device:TPU:0 now
where the time goes in v4:
time: 251 us; the launch traced here: 250 us
  Pallas kernels  112 us (45%)
  waiting for transfers between devices  62.4 us (25%)
  starting transfers between devices  42.9 us (17%)
  local copies, waits for them, and re-layouts  19.2 us (8%)
  other arithmetic  10.4 us (4%)
    ppermute x58, waiting for transfers between devices, swap(): return lax.ppermute(value, AXES, [(i, i ^ flip) for i in range(dp * seq)])  62.4 us
    ppermute x58, starting transfers between devices, swap(): return lax.ppermute(value, AXES, [(i, i ^ flip) for i in range(dp * seq)])  42.9 us
    pallas_call x1, Pallas kernels, forward(): pl.pallas_call(fwd_kernel, in_specs=[SMEM, SMEM] + [VMEM] * 9 + [HBM] * 8...  28.3 us
    pallas_call x3, Pallas kernels, grad_keep(): pl.pallas_call(functools.partial(keep_kernel, kind, orders), grid_spec=pl...  23.6 us
    pallas_call x3, Pallas kernels, unpack(): pl.pallas_call(functools.partial(unpack_kernel, kind, orders), in_specs=[...  18.1 us
    pallas_call x1, Pallas kernels, att_call(): pl.pallas_call(att_kernel, in_specs=[SMEM, SMEM, VMEM] + [HBM] * 8, out_s...  13 us
    pallas_call x1, Pallas kernels, mid_call(): pl.pallas_call(mid_kernel, in_specs=[VMEM, VMEM] + [HBM] * 6, out_specs=[...  11.9 us
    pallas_call x1, Pallas kernels, pre_call(): pl.pallas_call(pre_kernel, grid_spec=pltpu.PrefetchScalarGridSpec(num_sca...  9.83 us
  transfers between devices with their start and end apart: 58, of which 23 were waited for; matrix products, arithmetic and copies ran while one was open for 4% of the time, Pallas kernels for 31%

profile of v4, /device:TPU:0, one launch (start us, length us, event | category | flops | bytes accessed | tf_op | source)
XLA Modules:
  0.0 249.8 jit_solution(15962150474986983099)
XLA Ops:
  1.9 28.3 %forward.1 = (f32[4,12,160]{2,1,0:T(8,128)}, f32[8,768]{1,0:T(8,128)}, bf16[640,768]{1,0:T(8,128)(2,1)}, bf16[640,768]{1,0:T(8,128)(2,1)}, bf16[640,768]{1,0:T(8...) custom-call(s32[4]{0:T(128)} %refs_0_.5, ...), custom_call_target="tpu_custom_call" | custom-call | flops 28000000000 | bytes 1048576 | tf_op jit(solution)/shard_map/forward/pallas_call | solution.py:263
  30.7 9.8 %pre_bwd.1 = (bf16[640,3072]{1,0:T(8,128)(2,1)}, f32[16,768]{1,0:T(8,128)}, bf16[16,192,384]{2,1,0:T(8,128)(2,1)}) custom-call(s32[3]{0:T(128)} %shift-right-arithmetic_and_fusion.refs_1_.me, bf16[640,768]{1,0:T(8,128)(2,1)} %get-tuple-element.240.dffn.refs_1_.refs_4_, bf16[3072,768]{1,0:T(8,128)(2,1)} %w2.1, bf16[640,3072]{1,0:T(8,128)(2,1)} %get-tuple-element.241.slope, ...), custom_call_target="tpu_custom_call" | custom-call | flops 8000000000 | bytes 1048576 | tf_op jit(solution)/shard_map/pre_bwd/pallas_call | solution.py:296
  41.9 8.0 %keep_outer.1 = (bf16[8,64,384]{2,1,0:T(8,128)(2,1)}, bf16[8,64,384]{2,1,0:T(8,128)(2,1)}, bf16[8,64,384]{2,1,0:T(8,128)(2,1)}, bf16[8,64,384]{2,1,0:T(8,128)(2,...) custom-call(s32[3]{0:T(128)} %shift-right-arithmetic_and_fusion.refs_1_.me, ...), custom_call_target="tpu_custom_call" | custom-call | flops 3000000000 | bytes 1048576 | tf_op jit(solution)/shard_map/keep_outer/pallas_call | solution.py:623
  49.9 2.5 %collective-permute-start.1 = (bf16[2,2,2,64,384]{4,3,2,1,0:T(8,128)(2,1)}, bf16[2,2,2,64,384]{4,3,2,1,0:T(8,128)(2,1)S(1)}, u32[]{:S(2)}, u32[]{:S(2)}) collective-permute-start(bf16[2,2,2,64,384]{4,3,2,1,0:T(8,128)(2,1)} %bitcast.281), channel_id=1, source_target_pairs={{0,2},{1,3},{2,0},{3,1},{4,6},{5,7},{6,4},{7,5},{8,10},{9,11},{10,... | collective-permute-start | bytes 1179656 | tf_op jit(solution)/shard_map/ppermute | solution.py:761
  57.9 7.7 %keep_inner.1 = (bf16[8,64,384]{2,1,0:T(8,128)(2,1)}, bf16[8,64,384]{2,1,0:T(8,128)(2,1)}, bf16[8,64,384]{2,1,0:T(8,128)(2,1)}, bf16[8,64,384]{2,1,0:T(8,128)(2,...) custom-call(s32[3]{0:T(128)} %shift-right-arithmetic_and_fusion.refs_1_.me, ...), custom_call_target="tpu_custom_call" | custom-call | flops 3000000000 | bytes 1048576 | tf_op jit(solution)/shard_map/keep_inner/pallas_call | solution.py:623
  70.8 11.9 %mid_bwd.1 = (f32[16,768]{1,0:T(8,128)}, f32[640,768]{1,0:T(8,128)}, bf16[640,768]{1,0:T(8,128)(2,1)}, bf16[640,768]{1,0:T(8,128)(2,1)}) custom-call(f32[768]{0:T(1024)} %refs_0_.4, f32[16,768]{1,0:T(8,128)} %get-tuple-element.244.refs_1_, bf16[640,3072]{1,0:T(8,128)(2,1)} %get-tuple-element.273.refs_1_.refs_2_, bf16[768,3072]{1,0:T(8,128)(2,1)} %refs_3_.3, ...), custom_call_target="tpu_custom_call" | custom-call | flops 10000000000 | bytes 1048576 | tf_op jit(solution)/shard_map/mid_bwd/pallas_call | solution.py:430
  93.2 13.0 %att_bwd.1 = (f32[16,768]{1,0:T(8,128)}, bf16[640,3072]{1,0:T(8,128)(2,1)}, bf16[16,192,384]{2,1,0:T(8,128)(2,1)}) custom-call(s32[4]{0:T(128)} %refs_0_.5, s32[3]{0:T(128)} %shift-right-arithmetic_and_fusion.refs_1_.me, f32[16,768]{1,0:T(8,128)} %get-tuple-element.288.refs_2_, bf16[640,768]{1,0:T(8,128)(2,1)} %get-tuple-element.289.refs_3_, ...), custom_call_target="tpu_custom_call" | custom-call | flops 12000000000 | bytes 1048576 | tf_op jit(solution)/shard_map/att_bwd/pallas_call | solution.py:498
  108.9 2.6 %collective-permute-start.14 = (bf16[2,192,384]{2,1,0:T(8,128)(2,1)S(1)}, bf16[2,192,384]{2,1,0:T(8,128)(2,1)S(1)}, u32[]{:S(2)}, u32[]{:S(2)}) collective-permute-start(bf16[2,192,384]{2,1,0:T(8,128)(2,1)S(1)} %pad_maximum_fusion.25), channel_id=1, source_target_pairs={{0,16},{1,17},{2,18},{3,19},{4,20},{5,21},{6,22},{7,23},{8,24},{9,... | collective-permute-start | bytes 884744 | tf_op jit(solution)/shard_map/ppermute | solution.py:761
  115.4 7.9 %keep_attn.1 = (bf16[8,64,384]{2,1,0:T(8,128)(2,1)}, bf16[8,64,384]{2,1,0:T(8,128)(2,1)}, bf16[8,64,384]{2,1,0:T(8,128)(2,1)}, bf16[8,64,384]{2,1,0:T(8,128)(2,1...) custom-call(s32[3]{0:T(128)} %shift-right-arithmetic_and_fusion.refs_1_.me, bf16[640,768]{1,0:T(8,128)(2,1)} %bitcast.278, ...), custom_call_target="tpu_custom_call" | custom-call | flops 3000000000 | bytes 1048576 | tf_op jit(solution)/shard_map/keep_attn/pallas_call | solution.py:623
  123.3 2.1 collective-permute-done.14
  130.1 2.2 collective-permute-start.19
  132.3 6.3 %dx.1 = f32[640,768]{1,0:T(8,128)} custom-call(f32[640,768]{1,0:T(8,128)} %get-tuple-element.325.dh1_h, bf16[640,3072]{1,0:T(8,128)(2,1)} %get-tuple-element.295.refs_2_.d_h, bf16[768,768]{1,0:T(8,128)(2,1)} %wq_h.1, bf16[768,768]{1,0:T(8,128)(2,1)} %wk_h.1, bf16[768,768]{1,0:T(8,128)(2,1)} %wv_h.1), custom_call_target="tpu_custom_call" | custom-call | flops 5000000000 | bytes 1048576 | tf_op jit(solution)/shard_map/dx/pallas_call | solution.py:545
  141.1 8.2 %collective-permute-done.19 = bf16[672,384]{1,0:T(8,128)(2,1)S(1)} collective-permute-done((bf16[672,384]{1,0:T(8,128)(2,1)S(1)}, bf16[672,384]{1,0:T(8,128)(2,1)S(1)}, u32[]{:S(2)}, u32[]{:S(2)}) %collective-permute-start.19) | collective-permute-done | bytes 516128 | tf_op jit(solution)/shard_map/ppermute | solution.py:761
  152.6 9.1 %collective-permute-done.21 = bf16[640,384]{1,0:T(8,128)(2,1)S(1)} collective-permute-done((bf16[640,384]{1,0:T(8,128)(2,1)S(1)}, bf16[640,384]{1,0:T(8,128)(2,1)S(1)}, u32[]{:S(2)}, u32[]{:S(2)}) %collective-permute-start.21) | collective-permute-done | bytes 491552 | tf_op jit(solution)/shard_map/ppermute | solution.py:761
  163.7 1.8 collective-permute-start.24
  168.0 10.1 %collective-permute-done.24 = bf16[896,384]{1,0:T(8,128)(2,1)S(1)} collective-permute-done((bf16[896,384]{1,0:T(8,128)(2,1)S(1)}, bf16[896,384]{1,0:T(8,128)(2,1)S(1)}, u32[]{:S(2)}, u32[]{:S(2)}) %collective-permute-start.24) | collective-permute-done | bytes 688160 | tf_op jit(solution)/shard_map/ppermute | solution.py:761
  178.2 1.9 collective-permute-done.25
  184.6 2.0 collective-permute-start.30
  186.6 15.7 %collective-permute-done.30 = bf16[416,384]{1,0:T(8,128)(2,1)S(1)} collective-permute-done((bf16[416,384]{1,0:T(8,128)(2,1)S(1)}, bf16[416,384]{1,0:T(8,128)(2,1)S(1)}, u32[]{:S(2)}, u32[]{:S(2)}) %collective-permute-start.30) | collective-permute-done | bytes 319520 | tf_op jit(solution)/shard_map/ppermute | solution.py:761
  208.1 3.2 %collective-permute-done.40 = bf16[2,64,384]{2,1,0:T(8,128)(2,1)S(1)} collective-permute-done((bf16[2,64,384]{2,1,0:T(8,128)(2,1)S(1)}, bf16[2,64,384]{2,1,0:T(8,128)(2,1)S(1)}, u32[]{:S(2)}, u32[]{:S(2)}) %collective-permute-start.40) | collective-permute-done | bytes 98336 | tf_op jit(solution)/shard_map/ppermute | solution.py:761
  219.9 6.0 %unpack_outer.1 = f32[3072,768]{1,0:T(8,128)} custom-call(s32[3]{0:T(128)} %shift-right-arithmetic_and_fusion.refs_1_.me, bf16[8,64,384]{2,1,0:T(8,128)(2,1)} %copy-done.1, bf16[8,64,384]{2,1,0:T(8,128)(2,1)} %bitcast.255, bf16[8,64,384]{2,1,0:T(8,128)(2,1)} %copy-done.25, bf16[8,64,384]{2,1,0:T(8,128)(2,1)} %copy-done.37, bf16[8,64,384]{2,1,0:T(8,128)(2,1)} %copy-done.2, ...), custom_call_target="tpu_custom_call" | custom-call | flops 4000000000 | bytes 1048576 | tf_op jit(solution)/shard_map/unpack_outer/pallas_call | solution.py:715
  228.9 1.7 collective-permute-start.51
  230.6 6.0 %unpack_inner.1 = f32[768,3072]{1,0:T(8,128)} custom-call(s32[3]{0:T(128)} %shift-right-arithmetic_and_fusion.refs_1_.me, bf16[8,64,384]{2,1,0:T(8,128)(2,1)} %copy-done.5, bf16[8,64,384]{2,1,0:T(8,128)(2,1)} %copy-done.28, bf16[8,64,384]{2,1,0:T(8,128)(2,1)} %copy-done.31, bf16[8,64,384]{2,1,0:T(8,128)(2,1)} %copy-done.34, bf16[8,64,384]{2,1,0:T(8,128)(2,1)} %copy-done.6, ...), custom_call_target="tpu_custom_call" | custom-call | flops 4000000000 | bytes 1048576 | tf_op jit(solution)/shard_map/unpack_inner/pallas_call | solution.py:715
  243.6 6.0 %unpack_attn.1 = (f32[768,768]{1,0:T(8,128)}, f32[768,768]{1,0:T(8,128)}, f32[768,768]{1,0:T(8,128)}, f32[768,768]{1,0:T(8,128)}) custom-call(s32[3]{0:T(128)} %shift-right-arithmetic_and_fusion.refs_1_.me, bf16[8,64,384]{2,1,0:T(8,128)(2,1)} %copy-done.11, bf16[8,64,384]{2,1,0:T(8,128)(2,1)} %copy-done.43, bf16[8,64,384]{2,1,0:T(8,128)(2,1)} %copy-done.40, ...), custom_call_target="tpu_custom_call" | custom-call | flops 4000000000 | bytes 1048576 | tf_op jit(solution)/shard_map/unpack_attn/pallas_call | solution.py:715
  (349 shorter events, 73.0 us)
Async XLA Ops:
  40.5 17.4 %collective-permute-start.4 = (bf16[16,192,384]{2,1,0:T(8,128)(2,1)}, bf16[16,192,384]{2,1,0:T(8,128)(2,1)}, u32[]{:S(2)}, u32[]{:S(2)}) collective-permute-start(bf16[16,192,384]{2,1,0:T(8,128)(2,1)} %get-tuple-element.257), channel_id=1, source_target_pairs={{0,1},{1,0},{2,3},{3,2},{4,5},{5,4},{6,7},{7,6},{8,9},{9,8},{10,11... | collective-permute-start | bytes 7077896 | tf_op jit(solution)/shard_map/ppermute | solution.py:761
  49.9 16.8 %collective-permute-start.1 = (bf16[2,2,2,64,384]{4,3,2,1,0:T(8,128)(2,1)}, bf16[2,2,2,64,384]{4,3,2,1,0:T(8,128)(2,1)S(1)}, u32[]{:S(2)}, u32[]{:S(2)}) collective-permute-start(bf16[2,2,2,64,384]{4,3,2,1,0:T(8,128)(2,1)} %bitcast.281), channel_id=1, source_target_pairs={{0,2},{1,3},{2,0},{3,1},{4,6},{5,7},{6,4},{7,5},{8,10},{9,11},{10,... | collective-permute-start | bytes 1179656 | tf_op jit(solution)/shard_map/ppermute | solution.py:761
  52.4 14.3 %collective-permute-start.2 = (bf16[2,2,2,64,384]{4,3,2,1,0:T(8,128)(2,1)}, bf16[2,2,2,64,384]{4,3,2,1,0:T(8,128)(2,1)S(1)}, u32[]{:S(2)}, u32[]{:S(2)}) collective-permute-start(bf16[2,2,2,64,384]{4,3,2,1,0:T(8,128)(2,1)} %bitcast.280), channel_id=1, source_target_pairs={{0,4},{1,5},{2,6},{3,7},{4,0},{5,1},{6,2},{7,3},{8,12},{9,13},{10,... | collective-permute-start | bytes 1179656 | tf_op jit(solution)/shard_map/ppermute | solution.py:761
  53.9 12.8 %collective-permute-start.3 = (bf16[2,2,2,64,384]{4,3,2,1,0:T(8,128)(2,1)}, bf16[2,2,2,64,384]{4,3,2,1,0:T(8,128)(2,1)S(1)}, u32[]{:S(2)}, u32[]{:S(2)}) collective-permute-start(bf16[2,2,2,64,384]{4,3,2,1,0:T(8,128)(2,1)} %bitcast.279), channel_id=1, source_target_pairs={{0,8},{1,9},{2,10},{3,11},{4,12},{5,13},{6,14},{7,15},{8,0},{9,1},... | collective-permute-start | bytes 1179656 | tf_op jit(solution)/shard_map/ppermute | solution.py:761
  69.7 15.2 %collective-permute-start.7 = (bf16[768,384]{1,0:T(8,128)(2,1)}, bf16[768,384]{1,0:T(8,128)(2,1)}, u32[]{:S(2)}, u32[]{:S(2)}) collective-permute-start(bf16[768,384]{1,0:T(8,128)(2,1)} %pad_maximum_fusion.3), channel_id=1, source_target_pairs={{0,8},{1,9},{2,10},{3,11},{4,12},{5,13},{6,14},{7,15},{8,0},{9,1},... | collective-permute-start | bytes 1769480 | tf_op jit(solution)/shard_map/ppermute | solution.py:761
  70.2 16.7 %collective-permute-start.5 = (bf16[768,384]{1,0:T(8,128)(2,1)}, bf16[768,384]{1,0:T(8,128)(2,1)S(1)}, u32[]{:S(2)}, u32[]{:S(2)}) collective-permute-start(bf16[768,384]{1,0:T(8,128)(2,1)} %pad_maximum_fusion.4), channel_id=1, source_target_pairs={{0,2},{1,3},{2,0},{3,1},{4,6},{5,7},{6,4},{7,5},{8,10},{9,11},{10,... | collective-permute-start | bytes 1769480 | tf_op jit(solution)/shard_map/ppermute | solution.py:761
  70.7 16.3 %collective-permute-start.6 = (bf16[768,384]{1,0:T(8,128)(2,1)}, bf16[768,384]{1,0:T(8,128)(2,1)S(1)}, u32[]{:S(2)}, u32[]{:S(2)}) collective-permute-start(bf16[768,384]{1,0:T(8,128)(2,1)} %pad_maximum_fusion.5), channel_id=1, source_target_pairs={{0,4},{1,5},{2,6},{3,7},{4,0},{5,1},{6,2},{7,3},{8,12},{9,13},{10,... | collective-permute-start | bytes 1769480 | tf_op jit(solution)/shard_map/ppermute | solution.py:761
  89.0 18.1 %collective-permute-start.8 = (bf16[384,384]{1,0:T(8,128)(2,1)}, bf16[384,384]{1,0:T(8,128)(2,1)S(1)}, u32[]{:S(2)}, u32[]{:S(2)}) collective-permute-start(bf16[384,384]{1,0:T(8,128)(2,1)} %pad_maximum_fusion.24), channel_id=1, source_target_pairs={{0,4},{1,5},{2,6},{3,7},{4,0},{5,1},{6,2},{7,3},{8,12},{9,13},{10,... | collective-permute-start | bytes 884744 | tf_op jit(solution)/shard_map/ppermute | solution.py:761
  90.1 17.1 %collective-permute-start.9 = (bf16[384,384]{1,0:T(8,128)(2,1)}, bf16[384,384]{1,0:T(8,128)(2,1)S(1)}, u32[]{:S(2)}, u32[]{:S(2)}) collective-permute-start(bf16[384,384]{1,0:T(8,128)(2,1)} %pad_maximum_fusion.22), channel_id=1, source_target_pairs={{0,8},{1,9},{2,10},{3,11},{4,12},{5,13},{6,14},{7,15},{8,0},{9,1},... | collective-permute-start | bytes 884744 | tf_op jit(solution)/shard_map/ppermute | solution.py:761
  91.7 15.6 %collective-permute-start.10 = (bf16[384,384]{1,0:T(8,128)(2,1)S(1)}, bf16[384,384]{1,0:T(8,128)(2,1)S(1)}, u32[]{:S(2)}, u32[]{:S(2)}) collective-permute-start(bf16[384,384]{1,0:T(8,128)(2,1)S(1)} %pad_maximum_fusion.23), channel_id=1, source_target_pairs={{0,2},{1,3},{2,0},{3,1},{4,6},{5,7},{6,4},{7,5},{8,10},{9,11},{10,... | collective-permute-start | bytes 884744 | tf_op jit(solution)/shard_map/ppermute | solution.py:761
  108.9 16.5 %collective-permute-start.14 = (bf16[2,192,384]{2,1,0:T(8,128)(2,1)S(1)}, bf16[2,192,384]{2,1,0:T(8,128)(2,1)S(1)}, u32[]{:S(2)}, u32[]{:S(2)}) collective-permute-start(bf16[2,192,384]{2,1,0:T(8,128)(2,1)S(1)} %pad_maximum_fusion.25), channel_id=1, source_target_pairs={{0,16},{1,17},{2,18},{3,19},{4,20},{5,21},{6,22},{7,23},{8,24},{9,... | collective-permute-start | bytes 884744 | tf_op jit(solution)/shard_map/ppermute | solution.py:761
  127.6 21.8 %collective-permute-start.20 = (bf16[2,192,384]{2,1,0:T(8,128)(2,1)}, bf16[2,192,384]{2,1,0:T(8,128)(2,1)S(1)}, u32[]{:S(2)}, u32[]{:S(2)}) collective-permute-start(bf16[2,192,384]{2,1,0:T(8,128)(2,1)} %pad_maximum_fusion.26), channel_id=1, source_target_pairs={{0,16},{1,17},{2,18},{3,19},{4,20},{5,21},{6,22},{7,23},{8,24},{9,... | collective-permute-start | bytes 884744 | tf_op jit(solution)/shard_map/ppermute | solution.py:761
  128.0 12.8 %collective-permute-start.17 = (bf16[640,384]{1,0:T(8,128)(2,1)S(1)}, bf16[640,384]{1,0:T(8,128)(2,1)S(1)}, u32[]{:S(2)}, u32[]{:S(2)}) collective-permute-start(bf16[640,384]{1,0:T(8,128)(2,1)S(1)} %pad_maximum_fusion.8), channel_id=1, source_target_pairs={{0,2},{1,3},{2,0},{3,1},{4,6},{5,7},{6,4},{7,5},{8,10},{9,11},{10,... | collective-permute-start | bytes 1474568 | tf_op jit(solution)/shard_map/ppermute | solution.py:761
  130.1 19.3 %collective-permute-start.19 = (bf16[672,384]{1,0:T(8,128)(2,1)S(1)}, bf16[672,384]{1,0:T(8,128)(2,1)S(1)}, u32[]{:S(2)}, u32[]{:S(2)}) collective-permute-start(bf16[672,384]{1,0:T(8,128)(2,1)S(1)} %pad_maximum_fusion.6), channel_id=1, source_target_pairs={{0,8},{1,9},{2,10},{3,11},{4,12},{5,13},{6,14},{7,15},{8,0},{9,1},... | collective-permute-start | bytes 1548296 | tf_op jit(solution)/shard_map/ppermute | solution.py:761
  163.7 14.4 %collective-permute-start.24 = (bf16[896,384]{1,0:T(8,128)(2,1)S(1)}, bf16[896,384]{1,0:T(8,128)(2,1)S(1)}, u32[]{:S(2)}, u32[]{:S(2)}) collective-permute-start(bf16[896,384]{1,0:T(8,128)(2,1)S(1)} %pad_maximum_fusion.1), channel_id=1, source_target_pairs={{0,8},{1,9},{2,10},{3,11},{4,12},{5,13},{6,14},{7,15},{8,0},{9,1},... | collective-permute-start | bytes 2064392 | tf_op jit(solution)/shard_map/ppermute | solution.py:761
  165.5 14.7 %collective-permute-start.26 = (bf16[928,384]{1,0:T(8,128)(2,1)S(1)}, bf16[928,384]{1,0:T(8,128)(2,1)S(1)}, u32[]{:S(2)}, u32[]{:S(2)}) collective-permute-start(bf16[928,384]{1,0:T(8,128)(2,1)S(1)} %pad_maximum_fusion), channel_id=1, source_target_pairs={{0,4},{1,5},{2,6},{3,7},{4,0},{5,1},{6,2},{7,3},{8,12},{9,13},{10,... | collective-permute-start | bytes 2138120 | tf_op jit(solution)/shard_map/ppermute | solution.py:761
  166.6 13.6 %collective-permute-start.25 = (bf16[896,384]{1,0:T(8,128)(2,1)S(1)}, bf16[896,384]{1,0:T(8,128)(2,1)S(1)}, u32[]{:S(2)}, u32[]{:S(2)}) collective-permute-start(bf16[896,384]{1,0:T(8,128)(2,1)S(1)} %pad_maximum_fusion.2), channel_id=1, source_target_pairs={{0,2},{1,3},{2,0},{3,1},{4,6},{5,7},{6,4},{7,5},{8,10},{9,11},{10,... | collective-permute-start | bytes 2064392 | tf_op jit(solution)/shard_map/ppermute | solution.py:761
  167.5 12.9 %collective-permute-start.27 = (bf16[8,64,384]{2,1,0:T(8,128)(2,1)S(1)}, bf16[8,64,384]{2,1,0:T(8,128)(2,1)S(1)}, u32[]{:S(2)}, u32[]{:S(2)}) collective-permute-start(bf16[8,64,384]{2,1,0:T(8,128)(2,1)S(1)} %pad_maximum_fusion.13.refs_0_), channel_id=1, source_target_pairs={{0,1},{1,0},{2,3},{3,2},{4,5},{5,4},{6,7},{7,6},{8,9},{9,8},{10,11... | collective-permute-start | bytes 1179656 | tf_op jit(solution)/shard_map/ppermute | solution.py:761
  167.5 12.9 %collective-permute-start.28 = (bf16[8,64,384]{2,1,0:T(8,128)(2,1)S(1)}, bf16[8,64,384]{2,1,0:T(8,128)(2,1)S(1)}, u32[]{:S(2)}, u32[]{:S(2)}) collective-permute-start(bf16[8,64,384]{2,1,0:T(8,128)(2,1)S(1)} %pad_maximum_fusion.14.refs_4_), channel_id=1, source_target_pairs={{0,1},{1,0},{2,3},{3,2},{4,5},{5,4},{6,7},{7,6},{8,9},{9,8},{10,11... | collective-permute-start | bytes 1179656 | tf_op jit(solution)/shard_map/ppermute | solution.py:761
  181.8 20.5 %collective-permute-start.31 = (bf16[8,64,384]{2,1,0:T(8,128)(2,1)S(1)}, bf16[8,64,384]{2,1,0:T(8,128)(2,1)S(1)}, u32[]{:S(2)}, u32[]{:S(2)}) collective-permute-start(bf16[8,64,384]{2,1,0:T(8,128)(2,1)S(1)} %pad_maximum_fusion.16.refs_0_), channel_id=1, source_target_pairs={{0,2},{1,3},{2,0},{3,1},{4,6},{5,7},{6,4},{7,5},{8,10},{9,11},{10,... | collective-permute-start | bytes 1179656 | tf_op jit(solution)/shard_map/ppermute | solution.py:761
  182.7 20.2 %collective-permute-start.32 = (bf16[8,64,384]{2,1,0:T(8,128)(2,1)S(1)}, bf16[8,64,384]{2,1,0:T(8,128)(2,1)S(1)}, u32[]{:S(2)}, u32[]{:S(2)}) collective-permute-start(bf16[8,64,384]{2,1,0:T(8,128)(2,1)S(1)} %pad_maximum_fusion.17.refs_4_), channel_id=1, source_target_pairs={{0,4},{1,5},{2,6},{3,7},{4,0},{5,1},{6,2},{7,3},{8,12},{9,13},{10,... | collective-permute-start | bytes 1179656 | tf_op jit(solution)/shard_map/ppermute | solution.py:761
  184.0 19.0 %collective-permute-start.33 = (bf16[8,64,384]{2,1,0:T(8,128)(2,1)S(1)}, bf16[8,64,384]{2,1,0:T(8,128)(2,1)S(1)}, u32[]{:S(2)}, u32[]{:S(2)}) collective-permute-start(bf16[8,64,384]{2,1,0:T(8,128)(2,1)S(1)} %pad_maximum_fusion.15.refs_8_), channel_id=1, source_target_pairs={{0,8},{1,9},{2,10},{3,11},{4,12},{5,13},{6,14},{7,15},{8,0},{9,1},... | collective-permute-start | bytes 1179656 | tf_op jit(solution)/shard_map/ppermute | solution.py:761
  184.6 18.9 %collective-permute-start.34 = (bf16[8,64,384]{2,1,0:T(8,128)(2,1)S(1)}, bf16[8,64,384]{2,1,0:T(8,128)(2,1)S(1)}, u32[]{:S(2)}, u32[]{:S(2)}) collective-permute-start(bf16[8,64,384]{2,1,0:T(8,128)(2,1)S(1)} %pad_maximum_fusion.16.refs_0_), channel_id=1, source_target_pairs={{0,1},{1,0},{2,3},{3,2},{4,5},{5,4},{6,7},{7,6},{8,9},{9,8},{10,11... | collective-permute-start | bytes 1179656 | tf_op jit(solution)/shard_map/ppermute | solution.py:761
  184.6 17.7 %collective-permute-start.30 = (bf16[416,384]{1,0:T(8,128)(2,1)S(1)}, bf16[416,384]{1,0:T(8,128)(2,1)S(1)}, u32[]{:S(2)}, u32[]{:S(2)}) collective-permute-start(bf16[416,384]{1,0:T(8,128)(2,1)S(1)} %pad_maximum_fusion.21), channel_id=1, source_target_pairs={{0,16},{1,17},{2,18},{3,19},{4,20},{5,21},{6,22},{7,23},{8,24},{9,... | collective-permute-start | bytes 958472 | tf_op jit(solution)/shard_map/ppermute | solution.py:761
  (85 other events, 585.5 us)

commit v5 on v4

--- a/solution.py
+++ b/solution.py
@@ -12,16 +12,16 @@
 f32 = jnp.float32
 bf16 = jnp.bfloat16
 sd = jax.ShapeDtypeStruct
-HBM = pl.BlockSpec(memory_space=pl.ANY)
+ANY = pl.BlockSpec(memory_space=pl.ANY)
+HBM = pl.BlockSpec(memory_space=pltpu.HBM)
 VMEM = pl.BlockSpec(memory_space=pltpu.VMEM)
 SMEM = pl.BlockSpec(memory_space=pltpu.SMEM)
-LIMIT = 60 * 1024 * 1024
 CHUNK = 384
 HALF = CHUNK // 2
 
 
-def params():
-    return pltpu.CompilerParams(vmem_limit_bytes=LIMIT)
+def params(mib=60):
+    return pltpu.CompilerParams(vmem_limit_bytes=mib * 1024 * 1024)
 
 
 def cost(flops, nbytes=1 << 20):
@@ -91,11 +91,7 @@
     lax.fori_loop(0, seqs, chain, 0)
 
 
-SPLIT = 1
-PIECE = HALF // SPLIT
-
-
-def put_send(outs, grad, base, chunk0, me, rows_are_chunks):
+def put_blocks(out, grad, chunk0, me, rows_are_chunks):
     size = grad.shape[0 if rows_are_chunks else 1]
     for i in range(size // CHUNK):
         for t in range(2):
@@ -103,9 +99,11 @@
                 value = grad[i * CHUNK + t * HALF : i * CHUNK + (t + 1) * HALF, :]
             else:
                 value = grad[t * HALF : (t + 1) * HALF, i * CHUNK : (i + 1) * CHUNK]
-            value = value.astype(bf16)
-            for n, out in enumerate(outs):
-                out[((chunk0 + i) ^ me[1]) * 2 + (t ^ me[2]) - base] = value[n * PIECE : (n + 1) * PIECE]
+            out[((chunk0 + i) ^ me[1]) * 2 + (t ^ me[2])] = value.astype(bf16)
+
+
+def pair_part(n, me):
+    return pl.ds(4 * (n ^ (me[1] >> 1)), 4)
 
 
 def fwd_kernel(*refs):
@@ -114,14 +112,14 @@
     src = dict(zip(FWD_IN, refs[11:19]))
     lse, small = refs[19:21]
     dst = dict(zip(FWD_OUT, refs[21:30]))
-    hid_h, slope_h = refs[30:32]
-    send_h = refs[32 : 32 + SPLIT]
-    rest = refs[32 + SPLIT :]
+    dpre_h = refs[30]
+    block_h = refs[31:35]
+    rest = refs[35:]
     vin = dict(zip(FWD_IN, rest[:8]))
     vout = dict(zip(FWD_OUT, rest[8:17]))
-    hid, slope = rest[17:19]
-    send = rest[19 : 19 + SPLIT]
-    acc, sem_in, sem_out, sem_ff, sem_send = rest[19 + SPLIT :]
+    dpre = rest[17]
+    block = rest[18:22]
+    hid, slope, acc, sem_in, sem_out, sem_ff, sem_block = rest[22:]
     rows, width = vin["x"].shape
     ff = vin["wi"].shape[1]
     seqs = lens.shape[0]
@@ -180,13 +178,6 @@
     RB = 320
     part_ff = ff // width
 
-    def ff_copies(n):
-        c = ds(n * width, width)
-        return (
-            pltpu.make_async_copy(hid.at[:, c], hid_h.at[:, c], sem_ff.at[0, n]),
-            pltpu.make_async_copy(slope.at[:, c], slope_h.at[:, c], sem_ff.at[1, n]),
-        )
-
     def feed(n, _):
         c = ds(n * width, width)
         bias_i = bi[ds(n * width, width)].reshape(1, width)
@@ -198,8 +189,6 @@
             slope[r, c] = (cdf + u * jnp.exp(-0.5 * (u * u)) * 0.3989422804014327).astype(bf16)
             part = nn(hid[r, c], w2[c, :])
             acc[r, :] = jnp.where(n == 0, part, acc[r, :] + part)
-        for one in ff_copies(n):
-            one.start()
         return 0
 
     lax.fori_loop(0, part_ff, feed, 0)
@@ -230,25 +219,39 @@
     store("dffn").start()
     store("out").start()
     far = ds((1 - me[0]) * CHUNK, CHUNK)
-
-    def send_copies(n):
-        part = pl.ds(4 * (n ^ (me[1] >> 1)), 4)
-        return [
-            pltpu.make_async_copy(a.at[part], b.at[part], sem_send.at[i, n]) for i, (a, b) in enumerate(zip(send, send_h))
-        ]
+    near = ds(me[0] * CHUNK, CHUNK)
+
+    def block_copy(i, n):
+        part = pair_part(n, me)
+        return pltpu.make_async_copy(block[i].at[part], block_h[i].at[part], sem_block.at[i, n])
+
+    def dpre_copy(n):
+        c = ds(n * width, width)
+        return pltpu.make_async_copy(dpre.at[:, c], dpre_h.at[:, c], sem_ff.at[n])
 
     def grads(n, _):
-        put_send(send, tn(hid[:, ds(n * width, width)], dffn[:, far]), 0, 2 * n, me, True)
-        for one in send_copies(n):
-            one.start()
+        c = ds(n * width, width)
+        put_blocks(block[0], tn(hid[:, c], dffn[:, far]), 2 * n, me, True)
+        block_copy(0, n).start()
+        put_blocks(block[1], tn(hid[:, c], dffn[:, near]), 2 * n, me, True)
+        block_copy(1, n).start()
+        d = (nt(dffn[...], w2[c, :]) * slope[:, c].astype(f32)).astype(bf16)
+        dpre[:, c] = d
+        dpre_copy(n).start()
+        small[pl.ds(8 + n, 1), :] = jnp.sum(d.astype(f32), 0, keepdims=True)
+        put_blocks(block[2], tn(fin[:, far], dpre[:, c]), 2 * n, me, False)
+        block_copy(2, n).start()
+        put_blocks(block[3], tn(fin[:, near], dpre[:, c]), 2 * n, me, False)
+        block_copy(3, n).start()
         return 0
 
     lax.fori_loop(0, part_ff, grads, 0)
     for name in FWD_OUT:
         store(name).wait()
     for n in range(part_ff):
-        for one in ff_copies(n) + tuple(send_copies(n)):
-            one.wait()
+        dpre_copy(n).wait()
+        for i in range(4):
+            block_copy(i, n).wait()
 
 
 def forward(lens, me, vectors, arrays):
@@ -258,64 +261,21 @@
     like = lambda shape, dtype=bf16: sd(shape, dtype)
     thin = like((rows, width))
     outs = [thin, thin, thin, thin, like((rows, width), f32), like((rows, 1), f32), thin, thin, thin]
-    wide = [like((rows, ff)), like((rows, ff))] + [like((16, PIECE, CHUNK))] * SPLIT
+    wide = [like((rows, ff))] + [like((16, HALF, CHUNK))] * 4
     dma = pltpu.SemaphoreType.DMA
     return pl.pallas_call(
         fwd_kernel,
         in_specs=[SMEM, SMEM] + [VMEM] * 9 + [HBM] * 8,
-        out_specs=[VMEM, VMEM] + [HBM] * (11 + SPLIT),
-        out_shape=[like((seqs, H, rows // seqs), f32), like((8, width), f32)] + outs + wide,
+        out_specs=[VMEM, VMEM] + [HBM] * 14,
+        out_shape=[like((seqs, H, rows // seqs), f32), like((16, width), f32)] + outs + wide,
         scratch_shapes=[pltpu.VMEM(a.shape, a.dtype) for a in arrays]
         + [pltpu.VMEM(o.shape, o.dtype) for o in outs + wide]
-        + [pltpu.VMEM((rows, width), f32), dma((8,)), dma((9,)), dma((2, ff // width)), dma((SPLIT, ff // width))],
+        + [pltpu.VMEM((rows, ff), bf16), pltpu.VMEM((rows, ff), bf16), pltpu.VMEM((rows, width), f32)]
+        + [dma((8,)), dma((9,)), dma((ff // width,)), dma((4, ff // width))],
         compiler_params=params(),
         cost_estimate=cost(28e9),
         name="forward",
     )(lens, me, *vectors, *arrays)
-
-
-def pre_kernel(me, dffn, w2, slope, fin, small2, dpre_o, small, *send_o):
-    p = pl.program_id(0)
-    n = p ^ (me[1] >> 1)
-
-    @pl.when(p == 0)
-    def _():
-        small[0:8, :] = small2[...]
-        small[8:16, :] = jnp.zeros((8, small.shape[1]), f32)
-
-    d = (nt(dffn[...], w2[...]) * slope[...].astype(f32)).astype(bf16)
-    dpre_o[...] = d
-    small[pl.ds(8 + n, 1), :] = jnp.sum(d.astype(f32), 0, keepdims=True)
-    put_send(send_o, tn(fin[...], dpre_o[...]), 4 * p, 2 * n, me, False)
-
-
-def pre_call(me, dffn, w2, slope, fin, small2):
-    rows, width = dffn.shape
-    ff = w2.shape[0]
-    at = lambda p, me: p ^ (me[1] >> 1)
-    return pl.pallas_call(
-        pre_kernel,
-        grid_spec=pltpu.PrefetchScalarGridSpec(
-            num_scalar_prefetch=1,
-            grid=(ff // width,),
-            in_specs=[
-                pl.BlockSpec((rows, width), lambda p, me: (0, 0)),
-                pl.BlockSpec((width, width), lambda p, me: (at(p, me), 0)),
-                pl.BlockSpec((rows, width), lambda p, me: (0, at(p, me))),
-                pl.BlockSpec((rows, CHUNK), lambda p, me: (0, 1 - me[0])),
-                pl.BlockSpec((8, width), lambda p, me: (0, 0)),
-            ],
-            out_specs=[
-                pl.BlockSpec((rows, width), lambda p, me: (0, at(p, me))),
-                pl.BlockSpec((16, width), lambda p, me: (0, 0)),
-            ]
-            + [pl.BlockSpec((4, PIECE, CHUNK), lambda p, me: (p, 0, 0))] * SPLIT,
-        ),
-        out_shape=[sd((rows, ff), bf16), sd((16, width), f32)] + [sd((16, PIECE, CHUNK), bf16)] * SPLIT,
-        compiler_params=params(),
-        cost_estimate=cost(8e9),
-        name="pre_bwd",
-    )(me, dffn, w2, slope, fin, small2)
 
 
 def attention_bwd(lens, q, k, v, dm, lse, d, small):
@@ -434,7 +394,7 @@
         out_shape=[sd((16, width), f32)] + outs,
         scratch_shapes=[vm(dpre), vm(wi)] + [vm(a) for a in arrays] + [vm(o) for o in outs]
         + [pltpu.VMEM((rows, width), f32), dma((2, ff // width)), dma((4,)), dma((3,))],
-        compiler_params=params(),
+        compiler_params=params(44),
         cost_estimate=cost(10e9),
         name="mid_bwd",
     )(g1, small1, dpre, wi, *arrays)
@@ -447,12 +407,12 @@
     lens, me, small1 = refs[:3]
     src = dict(zip(ATT_IN, refs[3:11]))
     small, d_h = refs[11:13]
-    send_h = refs[13 : 13 + SPLIT]
-    rest = refs[13 + SPLIT :]
+    block_h = refs[13:15]
+    rest = refs[15:]
     vin = dict(zip(ATT_IN, rest[:8]))
     d = rest[8]
-    send = rest[9 : 9 + SPLIT]
-    sem_in, sem_out, sem_send = rest[9 + SPLIT :]
+    block = rest[9:11]
+    sem_in, sem_out, sem_block = rest[11:]
     width = d.shape[1] // 4
 
     def load(name):
@@ -471,38 +431,36 @@
     d_copy.start()
     load("x").wait()
     load("mixed").wait()
-    far = ds((1 - me[0]) * CHUNK, CHUNK)
-
-    def send_copies(n):
-        part = pl.ds(4 * (n ^ (me[1] >> 1)), 4)
-        return [
-            pltpu.make_async_copy(a.at[part], b.at[part], sem_send.at[i, n]) for i, (a, b) in enumerate(zip(send, send_h))
-        ]
+    sides = (ds((1 - me[0]) * CHUNK, CHUNK), ds(me[0] * CHUNK, CHUNK))
+
+    def block_copy(i, n):
+        part = pair_part(n, me)
+        return pltpu.make_async_copy(block[i].at[part], block_h[i].at[part], sem_block.at[i, n])
 
     for n in range(4):
         left = vin["mixed" if n == 3 else "x"]
-        put_send(send, tn(left[:, far], d[:, n * width : (n + 1) * width]), 0, 2 * n, me, False)
-        for one in send_copies(n):
-            one.start()
+        for i, side in enumerate(sides):
+            put_blocks(block[i], tn(left[:, side], d[:, n * width : (n + 1) * width]), 2 * n, me, False)
+            block_copy(i, n).start()
     d_copy.wait()
     for n in range(4):
-        for one in send_copies(n):
-            one.wait()
+        for i in range(2):
+            block_copy(i, n).wait()
 
 
 def att_call(lens, me, small1, arrays):
     rows, width = arrays[0].shape
     dma = pltpu.SemaphoreType.DMA
     vm = lambda a: pltpu.VMEM(a.shape, a.dtype)
-    outs = [sd((rows, 4 * width), bf16)] + [sd((16, PIECE, CHUNK), bf16)] * SPLIT
+    outs = [sd((rows, 4 * width), bf16)] + [sd((16, HALF, CHUNK), bf16)] * 2
     return pl.pallas_call(
         att_kernel,
         in_specs=[SMEM, SMEM, VMEM] + [HBM] * 8,
-        out_specs=[VMEM] + [HBM] * (1 + SPLIT),
+        out_specs=[VMEM] + [HBM] * 3,
         out_shape=[sd((16, width), f32)] + outs,
         scratch_shapes=[vm(a) for a in arrays[:7]] + [pltpu.VMEM((8, 128), bf16)] + [vm(o) for o in outs]
-        + [dma((8,)), dma((1,)), dma((SPLIT, 4))],
-        compiler_params=params(),
+        + [dma((8,)), dma((1,)), dma((2, 4))],
+        compiler_params=params(44),
         cost_estimate=cost(12e9),
         name="att_bwd",
     )(lens, me, small1, *arrays)
@@ -551,7 +509,7 @@
             pltpu.VMEM((rows, width), f32), pltpu.VMEM((rows, 3 * width), bf16), pltpu.VMEM(wq.shape, bf16),
             pltpu.VMEM(wq.shape, bf16), pltpu.VMEM(wq.shape, bf16), pltpu.VMEM((rows, width), f32), dma((7,)), dma((2,)),
         ],
-        compiler_params=params(),
+        compiler_params=params(30),
         cost_estimate=cost(5e9),
         name="dx",
     )(dh1, d, wq, wk, wv)
@@ -559,85 +517,6 @@
 
 def bit(value, name):
     return (value >> "xya".index(name)) & 1
-
-
-def pair_grad(kind, pair, refs):
-    if kind == "attn":
-        x, mixed, d = refs
-        return tn(jnp.where(pair == 3, mixed[...], x[...]), d[...])
-    return tn(refs[0][...], refs[1][...])
-
-
-def keep_kernel(kind, orders, me, *refs):
-    p = pl.program_id(0)
-    n_in = 3 if kind == "attn" else 2
-    gots = refs[n_in : n_in + SPLIT]
-    outs = refs[n_in + SPLIT : -1]
-    g = refs[-1]
-    g[...] = pair_grad(kind, p ^ (me[1] >> 1), refs[:n_in])
-    size = HALF // len(orders)
-    for i in range(2):
-        step = 2 * p + i
-        far = ds((i ^ (me[1] & 1)) * CHUNK, CHUNK)
-        for t in range(2):
-            part = (t ^ me[2]) * HALF
-            if kind == "outer":
-                grad = g[ds((i ^ (me[1] & 1)) * CHUNK + part, HALF), :]
-            else:
-                grad = g[ds(part, HALF), far]
-            got = jnp.concatenate([v[2 * i + t] for v in gots])
-            total = (grad + got.astype(f32)).astype(bf16)
-            for n, order in enumerate(orders):
-                where = bit(step, order[1]) * 4 + bit(step, order[2]) * 2 + t
-                first = bit(step, order[0])
-                value = total[n * size : (n + 1) * size]
-                if order[0] == "x":
-                    outs[2 * n + i][where] = value
-                    continue
-
-                @pl.when(first == 0)
-                def _():
-                    outs[2 * n][where] = value
-
-                @pl.when(first == 1)
-                def _():
-                    outs[2 * n + 1][where] = value
-
-
-def grad_specs(kind, rows, flip, pair_of):
-    pair = lambda p, me: (0, pair_of(p, me))
-    half = lambda p, me: (0, me[0] ^ flip)
-    wide = (rows, 2 * CHUNK)
-    thin = (rows, CHUNK)
-    if kind == "outer":
-        return [pl.BlockSpec(wide, pair), pl.BlockSpec(thin, half)]
-    if kind == "inner":
-        return [pl.BlockSpec(thin, half), pl.BlockSpec(wide, pair)]
-    return [pl.BlockSpec(thin, half), pl.BlockSpec(thin, half), pl.BlockSpec(wide, pair)]
-
-
-def grad_keep(kind, me, args, got, orders):
-    rows = args[0].shape[0]
-    shape = (8, HALF // len(orders), CHUNK)
-    g_shape = (2 * CHUNK, CHUNK) if kind == "outer" else (CHUNK, 2 * CHUNK)
-    return pl.pallas_call(
-        functools.partial(keep_kernel, kind, orders),
-        grid_spec=pltpu.PrefetchScalarGridSpec(
-            num_scalar_prefetch=1,
-            grid=(4,),
-            in_specs=grad_specs(kind, rows, 0, lambda p, me: p ^ (me[1] >> 1))
-            + [pl.BlockSpec((4, PIECE, CHUNK), lambda p, me: (p, 0, 0))] * SPLIT,
-            out_specs=[pl.BlockSpec(shape, lambda p, me: (0, 0, 0))] * (2 * len(orders)),
-            scratch_shapes=[pltpu.VMEM(g_shape, f32)],
-        ),
-        out_shape=[sd(shape, bf16)] * (2 * len(orders)),
-        compiler_params=params(),
-        cost_estimate=cost(3e9),
-        name="keep_" + kind,
-    )(me, *args, *got)
-
-
-ORDER_OF = ("xyab", "yxab", "axyb")
 
 
 def unpack_kernel(kind, orders, me, *refs):
@@ -689,7 +568,8 @@
                     waited.add(at)
                     loads[at].wait()
                 for t in range(2):
-                    where = bit(step, order[1]) * 4 + bit(step, order[2]) * 2 + t
+                    bits = [t if c == "b" else bit(step, c) for c in order]
+                    where = bits[1] * 4 + bits[2] * 2 + bits[3]
                     start = (t ^ me[2]) * HALF + n * size
                     value = ins[at][where].astype(f32)
                     if kind == "outer":
@@ -714,12 +594,12 @@
     dma = pltpu.SemaphoreType.DMA
     return pl.pallas_call(
         functools.partial(unpack_kernel, kind, orders),
-        in_specs=[SMEM] + [HBM] * (4 * colors),
+        in_specs=[SMEM] + [ANY] * (4 * colors),
         out_specs=[HBM] * len(out_shape),
         out_shape=out_shape,
         scratch_shapes=[pltpu.VMEM(v.shape, v.dtype) for v in pieces]
         + [pltpu.VMEM(buf, f32), dma((4 * colors,)), dma((4,))],
-        compiler_params=params(),
+        compiler_params=params(24),
         cost_estimate=cost(4e9),
         name="unpack_" + kind,
     )(me, *pieces)
@@ -744,7 +624,7 @@
         in_specs=[VMEM],
         out_specs=[VMEM] * 9,
         out_shape=[sd((n,), f32) for n in sizes],
-        compiler_params=params(),
+        compiler_params=params(4),
         cost_estimate=cost(1e9),
         name="vectors",
     )(total)
@@ -761,30 +641,34 @@
     return lax.ppermute(value, AXES, [(i, i ^ flip) for i in range(dp * seq)])
 
 
-ORDERS = ("xya", "yax", "axy")
-
-
-def both_halves(keep, got):
-    return keep[0] + got[0], keep[1] + got[1]
-
-
-def reduction(blocks):
-    keeps = [v.reshape((2, 2, 2) + v.shape[1:]) for v in blocks[0::2]]
-    sends = [v.reshape((2, 2, 2) + v.shape[1:]) for v in blocks[1::2]]
+ORDERS = ("xyab", "yaxb", "axyb")
+
+
+def pick(value, at, n):
+    return lax.index_in_dim(value, n, at, keepdims=False)
+
+
+def reduction(keep, got):
+    size = HALF // 3
+    shape = (2, 2, 2, 2, HALF, CHUNK)
+    keeps = [keep.reshape(shape)[..., n * size : (n + 1) * size, :] for n in range(3)]
+    gots = [got.reshape(shape)[..., n * size : (n + 1) * size, :] for n in range(3)]
+    dims = ["ayxb"] * 3
     for level in range(3):
+        places = [d.index(o[level]) for d, o in zip(dims, ORDERS)]
+        sends = [pick(k, at, 1) + pick(g, at, 1) for k, g, at in zip(keeps, gots, places)]
+        keeps = [pick(k, at, 0) + pick(g, at, 0) for k, g, at in zip(keeps, gots, places)]
+        dims = [d.replace(o[level], "") for d, o in zip(dims, ORDERS)]
         gots = yield [(o[level], v) for o, v in zip(ORDERS, sends)]
-        if level < 2:
-            keeps, sends = zip(*[both_halves(k, g) for k, g in zip(keeps, gots)])
-    own = jnp.concatenate([k + g for k, g in zip(keeps, gots)], -2)
-    (got,) = yield [("b", own)]
-    own = own + jnp.concatenate([got[1:], got[:1]])
+    owns = [k + g for k, g in zip(keeps, gots)]
+    gots = yield [(o[3], v) for o, v in zip(ORDERS, owns)]
+    owns = [v + jnp.concatenate([g[1:], g[:1]]) for v, g in zip(owns, gots)]
     for extra in range(4, lax.axis_size("dp").bit_length() - 1):
-        own = own + swap(own, extra)
-    size = own.shape[1] // 3
-    owns = [own[:, n * size : (n + 1) * size] for n in range(3)]
+        owns = [v + swap(v, extra) for v in owns]
     for level in (2, 1):
         gots = yield [(o[level], v) for o, v in zip(ORDERS, owns)]
-        owns = [jnp.concatenate(v) for v in zip(owns, gots)]
+        owns = [jnp.stack(v) for v in zip(owns, gots)]
+    owns = [v.reshape((8, size, CHUNK)) for v in owns]
     gots = yield [(o[0], v) for o, v in zip(ORDERS, owns)] + [("c", v) for v in owns]
     near, far = gots[:3], gots[3:]
     others = yield [("c", v) for v in near]
@@ -823,8 +707,8 @@
     def hold(self, value):
         return lax.optimization_barrier((value,) + self.mark)[0]
 
-    def begin(self, extra=()):
-        self.order = [(name, n) for name in self.wanted for n in range(len(self.wanted[name]))]
+    def begin(self, extra=(), skip=()):
+        self.order = [(name, n) for name in self.wanted if name not in skip for n in range(len(self.wanted[name]))]
         links = {}
         alone = {}
         for name, n in self.order:
@@ -878,36 +762,28 @@
     place = lax.axis_index("dp") * 2 + lax.axis_index("seq")
     me = (place >> jnp.array([0, 1, 4], jnp.int32)) & jnp.array([1, 7, 1], jnp.int32)
     x = chains_in.reshape(rows, width)
-    lse, small2, q, k, v, mixed, xhat, rstd, fin, out, dffn, hid, slope, send = forward(
+    lse, small, q, k, v, mixed, xhat, rstd, fin, out, dffn, dpre, send_o, keep_o, send_i, keep_i = forward(
         lengths, me, (b_query, b_value, b_output, gain_one, shift_one, b_inner, b_outer, gain_two, shift_two),
         (x, w_query, w_key, w_value, w_output, w_inner, w_outer, d_out.reshape(rows, width)),
     )
     rounds = Rounds()
-    (got,) = rounds.begin([send])
-    dpre, small1, send = pre_call(me, dffn, w_outer, slope, fin, small2)
-    got, send = lax.optimization_barrier((got, send))
-    (got_i,) = rounds.begin([send])
-    blocks = grad_keep("outer", me, (hid, dffn), (got,), ORDERS)
-    rounds.add("outer", reduction(blocks))
+    got_o, got_i = rounds.begin([send_o, send_i])
+    rounds.add("outer", reduction(keep_o, got_o))
     rounds.begin()
-    blocks = grad_keep("inner", me, (fin, dpre), (rounds.hold(got_i),), ORDERS)
-    rounds.end(*blocks)
-    rounds.add("inner", reduction(blocks))
+    small, dh1, dob, dm = mid_call(gain_one, small, rounds.hold(dpre), w_inner, (dffn, xhat, rstd, w_output))
+    got_i, dm = lax.optimization_barrier((got_i, dm))
+    rounds.end(dh1, dob, dm)
+    rounds.add("inner", reduction(keep_i, got_i))
     rounds.begin()
-    small, dh1, dob, dm = mid_call(gain_one, small1, rounds.hold(dpre), w_inner, (dffn, xhat, rstd, w_output))
-    rounds.end(dh1, dob, dm)
-    rounds.begin()
-    small, d, send = att_call(lengths, me, small, (q, k, v, rounds.hold(dm), lse, x, mixed, dob))
+    small, d, send, keep = att_call(lengths, me, small, (q, k, v, rounds.hold(dm), lse, x, mixed, dob))
     rounds.end(d, send)
     rounds.add("vectors", vector_sum(small))
     (got,) = rounds.begin([send])
-    blocks = grad_keep("attn", me, (x, mixed, d), (got,), ORDERS)
-    rounds.end(*blocks)
-    rounds.add("attn", reduction(blocks))
-    rounds.begin()
     d_x = dx_call(rounds.hold(dh1), d, w_query, w_key, w_value)
-    rounds.end(d_x)
-    for _ in range(3):
+    got, d_x = lax.optimization_barrier((got, d_x))
+    rounds.end(got)
+    rounds.add("attn", reduction(keep, got))
+    for _ in range(4):
         rounds.begin()
         rounds.end()
     rounds.begin()

time: 251 us -> 226 us (0.900)
  Pallas kernels: 112 us -> 92.4 us
  local copies, waits for them, and re-layouts: 19.2 us -> 1.49 us
  waiting for transfers between devices: 62.4 us -> 74.2 us
  other arithmetic: 10.4 us -> 7.19 us
    pallas_call x4 -> x0, Pallas kernels: 33.4 us -> none  [the longest x3 23.6 us: grad_keep(): pl.pallas_call(functools.partial(keep_kernel, kind, orders), grid_spec=pl...]
    ppermute x58 -> x55, waiting for transfers between devices: 62.4 us -> 74.2 us  [swap(): return lax.ppermute(value, AXES, [(i, i ^ flip) for i in range(dp * seq)])]
    pallas_call x1, Pallas kernels: 28.3 us -> 39.1 us  [forward(): pl.pallas_call(fwd_kernel, in_specs=[SMEM, SMEM] + [VMEM] * 9 + [HBM] * 8...]
    unnamed x98 -> x44, local copies, waits for them, and re-layouts: 9.33 us -> 0.26 us
    slice x22 -> x9, local copies, waits for them, and re-layouts: 6.18 us -> 0.11 us  [reduction(): owns = [v + jnp.concatenate([g[1:], g[:1]]) for v, g in zip(owns, gots)]]
    concatenate x16 -> x24, other arithmetic: 4.72 us -> 1.11 us  [begin(): jnp.concatenate([unroll(v) for v in values])]
    slice x40 -> x50, local copies, waits for them, and re-layouts: 3.71 us -> 1.12 us  [begin(): self.got[k, n] = got[row:row + count].reshape(shape)]
    pallas_call x1, Pallas kernels: 13 us -> 15.6 us  [att_call(): pl.pallas_call(att_kernel, in_specs=[SMEM, SMEM, VMEM] + [HBM] * 8, out_s...]
  transfers between devices with their start and end apart: 58 -> 55, of which waited for: 23 -> 24; matrix products, arithmetic and copies ran while one was open for 4% -> 2% of each run, Pallas kernels for 31% -> 21%
where the time goes in v5:
time: 226 us; the launch traced here: 223 us
  Pallas kernels  92.4 us (41%)
  waiting for transfers between devices  74.2 us (33%)
  starting transfers between devices  45.2 us (20%)
  other arithmetic  7.19 us (3%)
  between operations  2.62 us (1%)
    ppermute x55, waiting for transfers between devices, swap(): return lax.ppermute(value, AXES, [(i, i ^ flip) for i in range(dp * seq)])  74.2 us
    ppermute x55, starting transfers between devices, swap(): return lax.ppermute(value, AXES, [(i, i ^ flip) for i in range(dp * seq)])  45.2 us
    pallas_call x1, Pallas kernels, forward(): pl.pallas_call(fwd_kernel, in_specs=[SMEM, SMEM] + [VMEM] * 9 + [HBM] * 8...  39.1 us
    pallas_call x3, Pallas kernels, unpack(): pl.pallas_call(functools.partial(unpack_kernel, kind, orders), in_specs=[...  20 us
    pallas_call x1, Pallas kernels, att_call(): pl.pallas_call(att_kernel, in_specs=[SMEM, SMEM, VMEM] + [HBM] * 8, out_s...  15.6 us
    pallas_call x1, Pallas kernels, mid_call(): pl.pallas_call(mid_kernel, in_specs=[VMEM, VMEM] + [HBM] * 6, out_specs=[...  10.8 us
    pallas_call x1, Pallas kernels, dx_call(): pl.pallas_call(dx_kernel, in_specs=[HBM] * 5, out_specs=HBM, out_shape=sd...  6.21 us
  transfers between devices with their start and end apart: 55, of which 24 were waited for; matrix products, arithmetic and copies ran while one was open for 2% of the time, Pallas kernels for 21%

profile of v5, /device:TPU:0, one launch (start us, length us, event | category | flops | bytes accessed | tf_op | source)
XLA Modules:
  0.0 223.0 jit_solution(6184182069978784247)
XLA Ops:
  1.9 39.1 %forward.1 = (f32[4,12,160]{2,1,0:T(8,128)}, f32[16,768]{1,0:T(8,128)}, bf16[640,768]{1,0:T(8,128)(2,1)}, bf16[640,768]{1,0:T(8,128)(2,1)}, bf16[640,768]{1,0:T(...) custom-call(s32[4]{0:T(128)} %refs_0_.5, ...), custom_call_target="tpu_custom_call" | custom-call | flops 28000000000 | bytes 1048576 | tf_op jit(solution)/shard_map/forward/pallas_call | solution.py:266
  41.6 4.3 %collective-permute-done = bf16[16,192,384]{2,1,0:T(8,128)(2,1)S(1)} collective-permute-done((bf16[16,192,384]{2,1,0:T(8,128)(2,1)}, bf16[16,192,384]{2,1,0:T(8,128)(2,1)S(1)}, u32[]{:S(2)}, u32[]{:S(2)}) %collective-permute-start) | collective-permute-done | bytes 2359328 | tf_op jit(solution)/shard_map/ppermute | solution.py:641
  48.2 2.9 %collective-permute-start.1 = (bf16[2,2,2,64,384]{4,3,2,1,0:T(8,128)(2,1)S(1)}, bf16[2,2,2,64,384]{4,3,2,1,0:T(8,128)(2,1)S(1)}, u32[]{:S(2)}, u32[]{:S(2)}) collective-permute-start(bf16[2,2,2,64,384]{4,3,2,1,0:T(8,128)(2,1)S(1)} %fusion.7), channel_id=1, source_target_pairs={{0,2},{1,3},{2,0},{3,1},{4,6},{5,7},{6,4},{7,5},{8,10},{9,11},{10,... | collective-permute-start | bytes 1179656 | tf_op jit(solution)/shard_map/ppermute | solution.py:641
  54.4 10.8 %mid_bwd.1 = (f32[16,768]{1,0:T(8,128)S(1)}, f32[640,768]{1,0:T(8,128)S(1)}, bf16[640,768]{1,0:T(8,128)(2,1)S(1)}, bf16[640,768]{1,0:T(8,128)(2,1)S(1)}) custom-call(f32[768]{0:T(1024)S(1)} %copy-done.6, f32[16,768]{1,0:T(8,128)S(1)} %copy-done.16, bf16[640,3072]{1,0:T(8,128)(2,1)} %get-tuple-element.236.refs_2_, bf16[768,3072]{1,0:T(8,128)(2,1)} %refs_3_.3, ...), custom_call_target="tpu_custom_call" | custom-call | flops 10000000000 | bytes 1048576 | tf_op jit(solution)/shard_map/mid_bwd/pallas_call | solution.py:390
  68.1 15.6 %att_bwd.1 = (f32[16,768]{1,0:T(8,128)S(1)}, bf16[640,3072]{1,0:T(8,128)(2,1)}, bf16[16,192,384]{2,1,0:T(8,128)(2,1)S(1)}, bf16[16,192,384]{2,1,0:T(8,128)(2,1)}) custom-call(s32[4]{0:T(128)S(1)} %copy-done.7, s32[3]{0:T(128)S(1)} %copy-done, f32[16,768]{1,0:T(8,128)S(1)} %get-tuple-element.253.refs_2_, bf16[640,768]{1,0:T(8,128)(2,1)S(1)} %copy-done.11, ...), custom_call_target="tpu_custom_call" | custom-call | flops 12000000000 | bytes 1048576 | tf_op jit(solution)/shard_map/att_bwd/pallas_call | solution.py:456
  88.7 6.2 %dx.1 = f32[640,768]{1,0:T(8,128)} custom-call(f32[640,768]{1,0:T(8,128)S(1)} %get-tuple-element.273.dh1_h, bf16[640,3072]{1,0:T(8,128)(2,1)S(1)} %copy-done.8, bf16[768,768]{1,0:T(8,128)(2,1)S(1)} %copy-done.2, bf16[768,768]{1,0:T(8,128)(2,1)S(1)} %copy-done.3, bf16[768,768]{1,0:T(8,128)(2,1)S(1)} %copy-done.4), custom_call_target="tpu_custom_call" | custom-call | flops 5000000000 | bytes 1048576 | tf_op jit(solution)/shard_map/dx/pallas_call | solution.py:503
  96.7 2.6 %collective-permute-start.16 = (bf16[384,384]{1,0:T(8,128)(2,1)S(1)}, bf16[384,384]{1,0:T(8,128)(2,1)S(1)}, u32[]{:S(2)}, u32[]{:S(2)}) collective-permute-start(bf16[384,384]{1,0:T(8,128)(2,1)S(1)} %pad_maximum_fusion.29), channel_id=1, source_target_pairs={{0,16},{1,17},{2,18},{3,19},{4,20},{5,21},{6,22},{7,23},{8,24},{9,... | collective-permute-start | bytes 884744 | tf_op jit(solution)/shard_map/ppermute | solution.py:641
  101.9 10.6 %collective-permute-done.16 = bf16[384,384]{1,0:T(8,128)(2,1)S(1)} collective-permute-done((bf16[384,384]{1,0:T(8,128)(2,1)S(1)}, bf16[384,384]{1,0:T(8,128)(2,1)S(1)}, u32[]{:S(2)}, u32[]{:S(2)}) %collective-permute-start.16) | collective-permute-done | bytes 294944 | tf_op jit(solution)/shard_map/ppermute | solution.py:641
  112.7 5.9 %collective-permute-done.15 = bf16[672,384]{1,0:T(8,128)(2,1)S(1)} collective-permute-done((bf16[672,384]{1,0:T(8,128)(2,1)S(1)}, bf16[672,384]{1,0:T(8,128)(2,1)S(1)}, u32[]{:S(2)}, u32[]{:S(2)}) %collective-permute-start.15) | collective-permute-done | bytes 516128 | tf_op jit(solution)/shard_map/ppermute | solution.py:641
  122.1 4.5 %collective-permute-done.17 = bf16[384,384]{1,0:T(8,128)(2,1)S(1)} collective-permute-done((bf16[384,384]{1,0:T(8,128)(2,1)S(1)}, bf16[384,384]{1,0:T(8,128)(2,1)S(1)}, u32[]{:S(2)}, u32[]{:S(2)}) %collective-permute-start.17) | collective-permute-done | bytes 294944 | tf_op jit(solution)/shard_map/ppermute | solution.py:641
  126.7 4.7 %collective-permute-done.18 = bf16[384,384]{1,0:T(8,128)(2,1)S(1)} collective-permute-done((bf16[384,384]{1,0:T(8,128)(2,1)S(1)}, bf16[384,384]{1,0:T(8,128)(2,1)S(1)}, u32[]{:S(2)}, u32[]{:S(2)}) %collective-permute-start.18) | collective-permute-done | bytes 294944 | tf_op jit(solution)/shard_map/ppermute | solution.py:641
  131.4 3.1 %collective-permute-done.20 = bf16[384,384]{1,0:T(8,128)(2,1)S(1)} collective-permute-done((bf16[384,384]{1,0:T(8,128)(2,1)S(1)}, bf16[384,384]{1,0:T(8,128)(2,1)S(1)}, u32[]{:S(2)}, u32[]{:S(2)}) %collective-permute-start.20) | collective-permute-done | bytes 294944 | tf_op jit(solution)/shard_map/ppermute | solution.py:641
  137.6 5.4 %collective-permute-done.21 = bf16[512,384]{1,0:T(8,128)(2,1)S(1)} collective-permute-done((bf16[512,384]{1,0:T(8,128)(2,1)S(1)}, bf16[512,384]{1,0:T(8,128)(2,1)S(1)}, u32[]{:S(2)}, u32[]{:S(2)}) %collective-permute-start.21) | collective-permute-done | bytes 393248 | tf_op jit(solution)/shard_map/ppermute | solution.py:641
  143.2 2.1 collective-permute-done.23
  146.0 2.2 %collective-permute-start.25 = (bf16[768,384]{1,0:T(8,128)(2,1)S(1)}, bf16[768,384]{1,0:T(8,128)(2,1)S(1)}, u32[]{:S(2)}, u32[]{:S(2)}) collective-permute-start(bf16[768,384]{1,0:T(8,128)(2,1)S(1)} %pad_maximum_fusion.5), channel_id=1, source_target_pairs={{0,4},{1,5},{2,6},{3,7},{4,0},{5,1},{6,2},{7,3},{8,12},{9,13},{10,... | collective-permute-start | bytes 1769480 | tf_op jit(solution)/shard_map/ppermute | solution.py:641
  148.2 3.1 %collective-permute-start.26 = (bf16[768,384]{1,0:T(8,128)(2,1)S(1)}, bf16[768,384]{1,0:T(8,128)(2,1)S(1)}, u32[]{:S(2)}, u32[]{:S(2)}) collective-permute-start(bf16[768,384]{1,0:T(8,128)(2,1)S(1)} %pad_maximum_fusion.3), channel_id=1, source_target_pairs={{0,8},{1,9},{2,10},{3,11},{4,12},{5,13},{6,14},{7,15},{8,0},{9,1},... | collective-permute-start | bytes 1769480 | tf_op jit(solution)/shard_map/ppermute | solution.py:641
  152.7 6.9 %collective-permute-done.24 = bf16[416,384]{1,0:T(8,128)(2,1)S(1)} collective-permute-done((bf16[416,384]{1,0:T(8,128)(2,1)S(1)}, bf16[416,384]{1,0:T(8,128)(2,1)S(1)}, u32[]{:S(2)}, u32[]{:S(2)}) %collective-permute-start.24) | collective-permute-done | bytes 319520 | tf_op jit(solution)/shard_map/ppermute | solution.py:641
  160.3 6.0 %collective-permute-done.26 = bf16[768,384]{1,0:T(8,128)(2,1)S(1)} collective-permute-done((bf16[768,384]{1,0:T(8,128)(2,1)S(1)}, bf16[768,384]{1,0:T(8,128)(2,1)S(1)}, u32[]{:S(2)}, u32[]{:S(2)}) %collective-permute-start.26) | collective-permute-done | bytes 589856 | tf_op jit(solution)/shard_map/ppermute | solution.py:641
  167.6 1.8 collective-permute-start.32
  172.2 8.5 %collective-permute-done.31 = bf16[640,384]{1,0:T(8,128)(2,1)S(1)} collective-permute-done((bf16[640,384]{1,0:T(8,128)(2,1)S(1)}, bf16[640,384]{1,0:T(8,128)(2,1)S(1)}, u32[]{:S(2)}, u32[]{:S(2)}) %collective-permute-start.31) | collective-permute-done | bytes 491552 | tf_op jit(solution)/shard_map/ppermute | solution.py:641
  187.9 3.3 %collective-permute-done.40 = bf16[2,2,64,384]{3,2,1,0:T(8,128)(2,1)S(1)} collective-permute-done((bf16[2,2,64,384]{3,2,1,0:T(8,128)(2,1)S(1)}, bf16[2,2,64,384]{3,2,1,0:T(8,128)(2,1)S(1)}, u32[]{:S(2)}, u32[]{:S(2)}) %collective-permute-start.40) | collective-permute-done | bytes 196640 | tf_op jit(solution)/shard_map/ppermute | solution.py:641
  192.5 6.7 %unpack_outer.1 = f32[3072,768]{1,0:T(8,128)} custom-call(s32[3]{0:T(128)S(1)} %copy-done, bf16[8,64,384]{2,1,0:T(8,128)(2,1)S(1)} %bitcast.392, bf16[8,64,384]{2,1,0:T(8,128)(2,1)S(1)} %bitcast.410, bf16[8,64,384]{2,1,0:T(8,128)(2,1)S(1)} %collective-permute-done.28.refs_2_, bf16[8,64,384]{2,1,0:T(8,128)(2,1)S(1)} %collective-permute-done.37.refs_3_, ...), custom_call_target="tpu_custom_call" | custom-call | flops 4000000000 | bytes 1048576 | tf_op jit(solution)/shard_map/unpack_outer/pallas_call | solution.py:595
  204.0 6.7 %unpack_inner.1 = f32[768,3072]{1,0:T(8,128)} custom-call(s32[3]{0:T(128)S(1)} %copy-done, bf16[8,64,384]{2,1,0:T(8,128)(2,1)S(1)} %bitcast.401, bf16[8,64,384]{2,1,0:T(8,128)(2,1)S(1)} %bitcast.414, bf16[8,64,384]{2,1,0:T(8,128)(2,1)S(1)} %collective-permute-done.34.refs_2_, bf16[8,64,384]{2,1,0:T(8,128)(2,1)S(1)} %collective-permute-done.43.refs_3_, ...), custom_call_target="tpu_custom_call" | custom-call | flops 4000000000 | bytes 1048576 | tf_op jit(solution)/shard_map/unpack_inner/pallas_call | solution.py:595
  216.1 6.7 %unpack_attn.1 = (f32[768,768]{1,0:T(8,128)}, f32[768,768]{1,0:T(8,128)}, f32[768,768]{1,0:T(8,128)}, f32[768,768]{1,0:T(8,128)}) custom-call(s32[3]{0:T(128)S(1)} %copy-done, bf16[8,64,384]{2,1,0:T(8,128)(2,1)S(1)} %bitcast.419, bf16[8,64,384]{2,1,0:T(8,128)(2,1)S(1)} %collective-permute-done.46.refs_1_, ...), custom_call_target="tpu_custom_call" | custom-call | flops 4000000000 | bytes 1048576 | tf_op jit(solution)/shard_map/unpack_attn/pallas_call | solution.py:595
  (303 shorter events, 50.6 us)
Async XLA Ops:
  41.5 23.7 %collective-permute-start.4 = (bf16[16,192,384]{2,1,0:T(8,128)(2,1)}, bf16[16,192,384]{2,1,0:T(8,128)(2,1)S(1)}, u32[]{:S(2)}, u32[]{:S(2)}) collective-permute-start(bf16[16,192,384]{2,1,0:T(8,128)(2,1)} %get-tuple-element.242), channel_id=1, source_target_pairs={{0,1},{1,0},{2,3},{3,2},{4,5},{5,4},{6,7},{7,6},{8,9},{9,8},{10,11... | collective-permute-start | bytes 7077896 | tf_op jit(solution)/shard_map/ppermute | solution.py:641
  48.2 17.3 %collective-permute-start.1 = (bf16[2,2,2,64,384]{4,3,2,1,0:T(8,128)(2,1)S(1)}, bf16[2,2,2,64,384]{4,3,2,1,0:T(8,128)(2,1)S(1)}, u32[]{:S(2)}, u32[]{:S(2)}) collective-permute-start(bf16[2,2,2,64,384]{4,3,2,1,0:T(8,128)(2,1)S(1)} %fusion.7), channel_id=1, source_target_pairs={{0,2},{1,3},{2,0},{3,1},{4,6},{5,7},{6,4},{7,5},{8,10},{9,11},{10,... | collective-permute-start | bytes 1179656 | tf_op jit(solution)/shard_map/ppermute | solution.py:641
  51.2 14.4 %collective-permute-start.2 = (bf16[2,2,2,64,384]{4,3,2,1,0:T(8,128)(2,1)S(1)}, bf16[2,2,2,64,384]{4,3,2,1,0:T(8,128)(2,1)S(1)}, u32[]{:S(2)}, u32[]{:S(2)}) collective-permute-start(bf16[2,2,2,64,384]{4,3,2,1,0:T(8,128)(2,1)S(1)} %fusion.6), channel_id=1, source_target_pairs={{0,4},{1,5},{2,6},{3,7},{4,0},{5,1},{6,2},{7,3},{8,12},{9,13},{10,... | collective-permute-start | bytes 1179656 | tf_op jit(solution)/shard_map/ppermute | solution.py:641
  52.7 12.9 %collective-permute-start.3 = (bf16[2,2,2,64,384]{4,3,2,1,0:T(8,128)(2,1)S(1)}, bf16[2,2,2,64,384]{4,3,2,1,0:T(8,128)(2,1)S(1)}, u32[]{:S(2)}, u32[]{:S(2)}) collective-permute-start(bf16[2,2,2,64,384]{4,3,2,1,0:T(8,128)(2,1)S(1)} %get-tuple-element.233), channel_id=1, source_target_pairs={{0,8},{1,9},{2,10},{3,11},{4,12},{5,13},{6,14},{7,15},{8,0},{9,1},... | collective-permute-start | bytes 1179656 | tf_op jit(solution)/shard_map/ppermute | solution.py:641
  66.0 17.7 %collective-permute-start.5 = (bf16[768,384]{1,0:T(8,128)(2,1)S(1)}, bf16[768,384]{1,0:T(8,128)(2,1)S(1)}, u32[]{:S(2)}, u32[]{:S(2)}) collective-permute-start(bf16[768,384]{1,0:T(8,128)(2,1)S(1)} %pad_maximum_fusion.1), channel_id=1, source_target_pairs={{0,2},{1,3},{2,0},{3,1},{4,6},{5,7},{6,4},{7,5},{8,10},{9,11},{10,... | collective-permute-start | bytes 1769480 | tf_op jit(solution)/shard_map/ppermute | solution.py:641
  66.6 17.2 %collective-permute-start.6 = (bf16[768,384]{1,0:T(8,128)(2,1)S(1)}, bf16[768,384]{1,0:T(8,128)(2,1)S(1)}, u32[]{:S(2)}, u32[]{:S(2)}) collective-permute-start(bf16[768,384]{1,0:T(8,128)(2,1)S(1)} %pad_maximum_fusion.2), channel_id=1, source_target_pairs={{0,4},{1,5},{2,6},{3,7},{4,0},{5,1},{6,2},{7,3},{8,12},{9,13},{10,... | collective-permute-start | bytes 1769480 | tf_op jit(solution)/shard_map/ppermute | solution.py:641
  67.1 16.8 %collective-permute-start.7 = (bf16[768,384]{1,0:T(8,128)(2,1)S(1)}, bf16[768,384]{1,0:T(8,128)(2,1)S(1)}, u32[]{:S(2)}, u32[]{:S(2)}) collective-permute-start(bf16[768,384]{1,0:T(8,128)(2,1)S(1)} %pad_maximum_fusion), channel_id=1, source_target_pairs={{0,8},{1,9},{2,10},{3,11},{4,12},{5,13},{6,14},{7,15},{8,0},{9,1},... | collective-permute-start | bytes 1769480 | tf_op jit(solution)/shard_map/ppermute | solution.py:641
  96.7 15.8 %collective-permute-start.16 = (bf16[384,384]{1,0:T(8,128)(2,1)S(1)}, bf16[384,384]{1,0:T(8,128)(2,1)S(1)}, u32[]{:S(2)}, u32[]{:S(2)}) collective-permute-start(bf16[384,384]{1,0:T(8,128)(2,1)S(1)} %pad_maximum_fusion.29), channel_id=1, source_target_pairs={{0,16},{1,17},{2,18},{3,19},{4,20},{5,21},{6,22},{7,23},{8,24},{9,... | collective-permute-start | bytes 884744 | tf_op jit(solution)/shard_map/ppermute | solution.py:641
  99.4 19.2 %collective-permute-start.15 = (bf16[672,384]{1,0:T(8,128)(2,1)S(1)}, bf16[672,384]{1,0:T(8,128)(2,1)S(1)}, u32[]{:S(2)}, u32[]{:S(2)}) collective-permute-start(bf16[672,384]{1,0:T(8,128)(2,1)S(1)} %pad_maximum_fusion.6), channel_id=1, source_target_pairs={{0,8},{1,9},{2,10},{3,11},{4,12},{5,13},{6,14},{7,15},{8,0},{9,1},... | collective-permute-start | bytes 1548296 | tf_op jit(solution)/shard_map/ppermute | solution.py:641
  99.8 12.7 %collective-permute-start.13 = (bf16[640,384]{1,0:T(8,128)(2,1)S(1)}, bf16[640,384]{1,0:T(8,128)(2,1)S(1)}, u32[]{:S(2)}, u32[]{:S(2)}) collective-permute-start(bf16[640,384]{1,0:T(8,128)(2,1)S(1)} %pad_maximum_fusion.7), channel_id=1, source_target_pairs={{0,2},{1,3},{2,0},{3,1},{4,6},{5,7},{6,4},{7,5},{8,10},{9,11},{10,... | collective-permute-start | bytes 1474568 | tf_op jit(solution)/shard_map/ppermute | solution.py:641
  100.8 11.8 %collective-permute-start.14 = (bf16[640,384]{1,0:T(8,128)(2,1)S(1)}, bf16[640,384]{1,0:T(8,128)(2,1)S(1)}, u32[]{:S(2)}, u32[]{:S(2)}) collective-permute-start(bf16[640,384]{1,0:T(8,128)(2,1)S(1)} %pad_maximum_fusion.8), channel_id=1, source_target_pairs={{0,4},{1,5},{2,6},{3,7},{4,0},{5,1},{6,2},{7,3},{8,12},{9,13},{10,... | collective-permute-start | bytes 1474568 | tf_op jit(solution)/shard_map/ppermute | solution.py:641
  120.7 13.9 %collective-permute-start.20 = (bf16[384,384]{1,0:T(8,128)(2,1)S(1)}, bf16[384,384]{1,0:T(8,128)(2,1)S(1)}, u32[]{:S(2)}, u32[]{:S(2)}) collective-permute-start(bf16[384,384]{1,0:T(8,128)(2,1)S(1)} %pad_maximum_fusion.31), channel_id=1, source_target_pairs={{0,16},{1,17},{2,18},{3,19},{4,20},{5,21},{6,22},{7,23},{8,24},{9,... | collective-permute-start | bytes 884744 | tf_op jit(solution)/shard_map/ppermute | solution.py:641
  121.2 13.4 %collective-permute-start.19 = (bf16[416,384]{1,0:T(8,128)(2,1)S(1)}, bf16[416,384]{1,0:T(8,128)(2,1)S(1)}, u32[]{:S(2)}, u32[]{:S(2)}) collective-permute-start(bf16[416,384]{1,0:T(8,128)(2,1)S(1)} %pad_maximum_fusion.24), channel_id=1, source_target_pairs={{0,2},{1,3},{2,0},{3,1},{4,6},{5,7},{6,4},{7,5},{8,10},{9,11},{10,... | collective-permute-start | bytes 958472 | tf_op jit(solution)/shard_map/ppermute | solution.py:641
  146.0 13.7 %collective-permute-start.25 = (bf16[768,384]{1,0:T(8,128)(2,1)S(1)}, bf16[768,384]{1,0:T(8,128)(2,1)S(1)}, u32[]{:S(2)}, u32[]{:S(2)}) collective-permute-start(bf16[768,384]{1,0:T(8,128)(2,1)S(1)} %pad_maximum_fusion.5), channel_id=1, source_target_pairs={{0,4},{1,5},{2,6},{3,7},{4,0},{5,1},{6,2},{7,3},{8,12},{9,13},{10,... | collective-permute-start | bytes 1769480 | tf_op jit(solution)/shard_map/ppermute | solution.py:641
  148.2 18.0 %collective-permute-start.26 = (bf16[768,384]{1,0:T(8,128)(2,1)S(1)}, bf16[768,384]{1,0:T(8,128)(2,1)S(1)}, u32[]{:S(2)}, u32[]{:S(2)}) collective-permute-start(bf16[768,384]{1,0:T(8,128)(2,1)S(1)} %pad_maximum_fusion.3), channel_id=1, source_target_pairs={{0,8},{1,9},{2,10},{3,11},{4,12},{5,13},{6,14},{7,15},{8,0},{9,1},... | collective-permute-start | bytes 1769480 | tf_op jit(solution)/shard_map/ppermute | solution.py:641
  151.3 15.0 %collective-permute-start.27 = (bf16[768,384]{1,0:T(8,128)(2,1)S(1)}, bf16[768,384]{1,0:T(8,128)(2,1)S(1)}, u32[]{:S(2)}, u32[]{:S(2)}) collective-permute-start(bf16[768,384]{1,0:T(8,128)(2,1)S(1)} %pad_maximum_fusion.4), channel_id=1, source_target_pairs={{0,2},{1,3},{2,0},{3,1},{4,6},{5,7},{6,4},{7,5},{8,10},{9,11},{10,... | collective-permute-start | bytes 1769480 | tf_op jit(solution)/shard_map/ppermute | solution.py:641
  152.7 13.7 %collective-permute-start.28 = (bf16[8,64,384]{2,1,0:T(8,128)(2,1)S(1)}, bf16[8,64,384]{2,1,0:T(8,128)(2,1)S(1)}, u32[]{:S(2)}, u32[]{:S(2)}) collective-permute-start(bf16[8,64,384]{2,1,0:T(8,128)(2,1)S(1)} %bitcast.391), channel_id=1, source_target_pairs={{0,1},{1,0},{2,3},{3,2},{4,5},{5,4},{6,7},{7,6},{8,9},{9,8},{10,11... | collective-permute-start | bytes 1179656 | tf_op jit(solution)/shard_map/ppermute | solution.py:641
  167.1 13.6 %collective-permute-start.31 = (bf16[640,384]{1,0:T(8,128)(2,1)S(1)}, bf16[640,384]{1,0:T(8,128)(2,1)S(1)}, u32[]{:S(2)}, u32[]{:S(2)}) collective-permute-start(bf16[640,384]{1,0:T(8,128)(2,1)S(1)} %pad_maximum_fusion.9), channel_id=1, source_target_pairs={{0,8},{1,9},{2,10},{3,11},{4,12},{5,13},{6,14},{7,15},{8,0},{9,1},... | collective-permute-start | bytes 1474568 | tf_op jit(solution)/shard_map/ppermute | solution.py:641
  167.6 13.4 %collective-permute-start.32 = (bf16[640,384]{1,0:T(8,128)(2,1)S(1)}, bf16[640,384]{1,0:T(8,128)(2,1)S(1)}, u32[]{:S(2)}, u32[]{:S(2)}) collective-permute-start(bf16[640,384]{1,0:T(8,128)(2,1)S(1)} %pad_maximum_fusion.10), channel_id=1, source_target_pairs={{0,2},{1,3},{2,0},{3,1},{4,6},{5,7},{6,4},{7,5},{8,10},{9,11},{10,... | collective-permute-start | bytes 1474568 | tf_op jit(solution)/shard_map/ppermute | solution.py:641
  169.4 13.0 %collective-permute-start.33 = (bf16[640,384]{1,0:T(8,128)(2,1)S(1)}, bf16[640,384]{1,0:T(8,128)(2,1)S(1)}, u32[]{:S(2)}, u32[]{:S(2)}) collective-permute-start(bf16[640,384]{1,0:T(8,128)(2,1)S(1)} %pad_maximum_fusion.11), channel_id=1, source_target_pairs={{0,4},{1,5},{2,6},{3,7},{4,0},{5,1},{6,2},{7,3},{8,12},{9,13},{10,... | collective-permute-start | bytes 1474568 | tf_op jit(solution)/shard_map/ppermute | solution.py:641
  185.8 13.4 %collective-permute-start.43 = (bf16[8,64,384]{2,1,0:T(8,128)(2,1)S(1)}, bf16[8,64,384]{2,1,0:T(8,128)(2,1)S(1)}, u32[]{:S(2)}, u32[]{:S(2)}) collective-permute-start(bf16[8,64,384]{2,1,0:T(8,128)(2,1)S(1)} %bitcast.413), channel_id=1, source_target_pairs={{0,1},{1,0},{2,3},{3,2},{4,5},{5,4},{6,7},{7,6},{8,9},{9,8},{10,11... | collective-permute-start | bytes 1179656 | tf_op jit(solution)/shard_map/ppermute | solution.py:641
  185.8 13.4 %collective-permute-start.44 = (bf16[8,64,384]{2,1,0:T(8,128)(2,1)S(1)}, bf16[8,64,384]{2,1,0:T(8,128)(2,1)S(1)}, u32[]{:S(2)}, u32[]{:S(2)}) collective-permute-start(bf16[8,64,384]{2,1,0:T(8,128)(2,1)S(1)} %bitcast.415), channel_id=1, source_target_pairs={{0,1},{1,0},{2,3},{3,2},{4,5},{5,4},{6,7},{7,6},{8,9},{9,8},{10,11... | collective-permute-start | bytes 1179656 | tf_op jit(solution)/shard_map/ppermute | solution.py:641
  186.3 12.9 %collective-permute-start.45 = (bf16[8,64,384]{2,1,0:T(8,128)(2,1)S(1)}, bf16[8,64,384]{2,1,0:T(8,128)(2,1)S(1)}, u32[]{:S(2)}, u32[]{:S(2)}) collective-permute-start(bf16[8,64,384]{2,1,0:T(8,128)(2,1)S(1)} %bitcast.411), channel_id=1, source_target_pairs={{0,1},{1,0},{2,3},{3,2},{4,5},{5,4},{6,7},{7,6},{8,9},{9,8},{10,11... | collective-permute-start | bytes 1179656 | tf_op jit(solution)/shard_map/ppermute | solution.py:641
  186.3 12.9 %collective-permute-start.41 = (bf16[2,2,64,384]{3,2,1,0:T(8,128)(2,1)S(1)}, bf16[2,2,64,384]{3,2,1,0:T(8,128)(2,1)S(1)}, u32[]{:S(2)}, u32[]{:S(2)}) collective-permute-start(bf16[2,2,64,384]{3,2,1,0:T(8,128)(2,1)S(1)} %get-tuple-element.361), channel_id=1, source_target_pairs={{0,8},{1,9},{2,10},{3,11},{4,12},{5,13},{6,14},{7,15},{8,0},{9,1},... | collective-permute-start | bytes 589832 | tf_op jit(solution)/shard_map/ppermute | solution.py:641
  (54 other events, 348.9 us)

commit v6 on v5

--- a/solution.py
+++ b/solution.py
@@ -38,6 +38,11 @@
 
 def tn(a, b):
     return lax.dot_general(a, b, (((0,), (0,)), ((), ())), preferred_element_type=f32)
+
+
+def own_place():
+    dp = lax.axis_index("dp")
+    return lax.axis_index("seq"), dp & 7, (dp >> 3) & 1
 
 
 def row_mean(v):
@@ -91,14 +96,22 @@
     lax.fori_loop(0, seqs, chain, 0)
 
 
-def put_blocks(out, grad, chunk0, me, rows_are_chunks):
-    size = grad.shape[0 if rows_are_chunks else 1]
-    for i in range(size // CHUNK):
+def put_blocks(outs, grad, chunk0, me, rows_are_chunks):
+    for i in range(2):
+        for n, out in enumerate(outs):
+            half = (me[0] ^ (1 - n)) * CHUNK
+            for t in range(2):
+                if rows_are_chunks:
+                    value = grad[i * CHUNK + t * HALF : i * CHUNK + (t + 1) * HALF, ds(half, CHUNK)]
+                else:
+                    value = grad[ds(half + t * HALF, HALF), i * CHUNK : (i + 1) * CHUNK]
+                out[((chunk0 + i) ^ me[1]) * 2 + (t ^ me[2])] = value.astype(bf16)
+
+
+def put_side(out, grad, chunk0, me):
+    for i in range(2):
         for t in range(2):
-            if rows_are_chunks:
-                value = grad[i * CHUNK + t * HALF : i * CHUNK + (t + 1) * HALF, :]
-            else:
-                value = grad[t * HALF : (t + 1) * HALF, i * CHUNK : (i + 1) * CHUNK]
+            value = grad[t * HALF : (t + 1) * HALF, i * CHUNK : (i + 1) * CHUNK]
             out[((chunk0 + i) ^ me[1]) * 2 + (t ^ me[2])] = value.astype(bf16)
 
 
@@ -119,7 +132,7 @@
     vout = dict(zip(FWD_OUT, rest[8:17]))
     dpre = rest[17]
     block = rest[18:22]
-    hid, slope, acc, sem_in, sem_out, sem_ff, sem_block = rest[22:]
+    hid, slope, acc, both_grad, sem_in, sem_out, sem_ff, sem_block = rest[22:]
     rows, width = vin["x"].shape
     ff = vin["wi"].shape[1]
     seqs = lens.shape[0]
@@ -218,9 +231,6 @@
     lax.fori_loop(0, seqs, norm_two, 0)
     store("dffn").start()
     store("out").start()
-    far = ds((1 - me[0]) * CHUNK, CHUNK)
-    near = ds(me[0] * CHUNK, CHUNK)
-
     def block_copy(i, n):
         part = pair_part(n, me)
         return pltpu.make_async_copy(block[i].at[part], block_h[i].at[part], sem_block.at[i, n])
@@ -231,17 +241,17 @@
 
     def grads(n, _):
         c = ds(n * width, width)
-        put_blocks(block[0], tn(hid[:, c], dffn[:, far]), 2 * n, me, True)
+        both_grad[...] = tn(hid[:, c], dffn[...])
+        put_blocks(block[0:2], both_grad, 2 * n, me, True)
         block_copy(0, n).start()
-        put_blocks(block[1], tn(hid[:, c], dffn[:, near]), 2 * n, me, True)
         block_copy(1, n).start()
         d = (nt(dffn[...], w2[c, :]) * slope[:, c].astype(f32)).astype(bf16)
         dpre[:, c] = d
         dpre_copy(n).start()
         small[pl.ds(8 + n, 1), :] = jnp.sum(d.astype(f32), 0, keepdims=True)
-        put_blocks(block[2], tn(fin[:, far], dpre[:, c]), 2 * n, me, False)
+        both_grad[...] = tn(fin[...], dpre[:, c])
+        put_blocks(block[2:4], both_grad, 2 * n, me, False)
         block_copy(2, n).start()
-        put_blocks(block[3], tn(fin[:, near], dpre[:, c]), 2 * n, me, False)
         block_copy(3, n).start()
         return 0
 
@@ -271,7 +281,7 @@
         scratch_shapes=[pltpu.VMEM(a.shape, a.dtype) for a in arrays]
         + [pltpu.VMEM(o.shape, o.dtype) for o in outs + wide]
         + [pltpu.VMEM((rows, ff), bf16), pltpu.VMEM((rows, ff), bf16), pltpu.VMEM((rows, width), f32)]
-        + [dma((8,)), dma((9,)), dma((ff // width,)), dma((4, ff // width))],
+        + [pltpu.VMEM((width, width), f32), dma((8,)), dma((9,)), dma((ff // width,)), dma((4, ff // width))],
         compiler_params=params(),
         cost_estimate=cost(28e9),
         name="forward",
@@ -333,7 +343,7 @@
         return pltpu.make_async_copy(src[name], vin[name], sem_in.at[MID_IN.index(name)])
 
     def ff_copies(n):
-        c = slice(n * width, (n + 1) * width)
+        c = ds(n * width, width)
         return (
             pltpu.make_async_copy(dpre_h.at[:, c], dpre.at[:, c], sem_ff.at[0, n]),
             pltpu.make_async_copy(wi_h.at[:, c], wi.at[:, c], sem_ff.at[1, n]),
@@ -344,12 +354,15 @@
             one.start()
     for name in MID_IN:
         load(name).start()
-    for n in range(part_ff):
-        c = slice(n * width, (n + 1) * width)
+    def products(n, _):
+        c = ds(n * width, width)
         for one in ff_copies(n):
             one.wait()
         part = nt(dpre[:, c], wi[:, c])
-        acc[...] = part if n == 0 else acc[...] + part
+        acc[...] = jnp.where(n == 0, part, acc[...] + part)
+        return 0
+
+    lax.fori_loop(0, part_ff, products, 0)
     small[...] = small1[...]
     gain1 = row(g1)
     dffn, xhat, rstd = vin["dffn"], vin["xhat"], vin["rstd"]
@@ -431,16 +444,16 @@
     d_copy.start()
     load("x").wait()
     load("mixed").wait()
-    sides = (ds((1 - me[0]) * CHUNK, CHUNK), ds(me[0] * CHUNK, CHUNK))
-
     def block_copy(i, n):
         part = pair_part(n, me)
         return pltpu.make_async_copy(block[i].at[part], block_h[i].at[part], sem_block.at[i, n])
 
+    sides = (ds((1 - me[0]) * CHUNK, CHUNK), ds(me[0] * CHUNK, CHUNK))
+
     for n in range(4):
         left = vin["mixed" if n == 3 else "x"]
         for i, side in enumerate(sides):
-            put_blocks(block[i], tn(left[:, side], d[:, n * width : (n + 1) * width]), 2 * n, me, False)
+            put_side(block[i], tn(left[:, side], d[:, n * width : (n + 1) * width]), 2 * n, me)
             block_copy(i, n).start()
     d_copy.wait()
     for n in range(4):
@@ -519,7 +532,8 @@
     return (value >> "xya".index(name)) & 1
 
 
-def unpack_kernel(kind, orders, me, *refs):
+def unpack_kernel(kind, orders, *refs):
+    me = own_place()
     colors = len(orders)
     n_in = 4 * colors
     src = refs[:n_in]
@@ -527,7 +541,7 @@
     outs = refs[n_in : n_in + n_out]
     ins = refs[n_in + n_out : 2 * n_in + n_out]
     buf, sem_in, sem = refs[2 * n_in + n_out :]
-    size = HALF // colors
+    sizes = [src[4 * n].shape[1] for n in range(colors)]
     slots = buf.shape[0]
 
     order_in = [n for first in range(2) for n in range(n_in) if n % 2 == first]
@@ -562,7 +576,7 @@
         for half in range(2):
             place = (half ^ me[0]) * CHUNK
             for n in range(colors):
-                order = orders[n]
+                order, size, first = orders[n], sizes[n], sum(sizes[:n])
                 at = 4 * n + 2 * half + bit(step, order[0])
                 if at not in waited:
                     waited.add(at)
@@ -570,18 +584,18 @@
                 for t in range(2):
                     bits = [t if c == "b" else bit(step, c) for c in order]
                     where = bits[1] * 4 + bits[2] * 2 + bits[3]
-                    start = (t ^ me[2]) * HALF + n * size
+                    start = (t ^ me[2]) * HALF + first
                     value = ins[at][where].astype(f32)
                     if kind == "outer":
-                        buf[slot, ds(start, size, 32), ds(place, CHUNK)] = value
+                        buf[slot, ds(start, size, 16), ds(place, CHUNK)] = value
                     else:
-                        buf[slot, ds(place + start, size, 32), :] = value
+                        buf[slot, ds(place + start, size, 16), :] = value
         each(step, lambda one: one.start())
     for step in range(8 - slots, 8):
         each(step, lambda one: one.wait())
 
 
-def unpack(kind, me, pieces, orders):
+def unpack(kind, pieces, orders):
     colors = len(orders)
     width = 2 * CHUNK
     if kind == "outer":
@@ -594,7 +608,7 @@
     dma = pltpu.SemaphoreType.DMA
     return pl.pallas_call(
         functools.partial(unpack_kernel, kind, orders),
-        in_specs=[SMEM] + [ANY] * (4 * colors),
+        in_specs=[ANY] * (4 * colors),
         out_specs=[HBM] * len(out_shape),
         out_shape=out_shape,
         scratch_shapes=[pltpu.VMEM(v.shape, v.dtype) for v in pieces]
@@ -602,7 +616,7 @@
         compiler_params=params(24),
         cost_estimate=cost(4e9),
         name="unpack_" + kind,
-    )(me, *pieces)
+    )(*pieces)
 
 
 SMALL_ROWS = (6, 7, 5, 3, 4, 8, 2, 0, 1)
@@ -648,11 +662,18 @@
     return lax.index_in_dim(value, n, at, keepdims=False)
 
 
-def reduction(keep, got):
-    size = HALF // 3
+def cut(value, sizes):
+    return [value[..., sum(sizes[:n]) : sum(sizes[: n + 1]), :] for n in range(len(sizes))]
+
+
+EVEN = (64, 64, 64)
+LEAN = (80, 64, 48)
+
+
+def reduction(keep, got, down=EVEN, up=EVEN):
     shape = (2, 2, 2, 2, HALF, CHUNK)
-    keeps = [keep.reshape(shape)[..., n * size : (n + 1) * size, :] for n in range(3)]
-    gots = [got.reshape(shape)[..., n * size : (n + 1) * size, :] for n in range(3)]
+    keeps = cut(keep.reshape(shape), down)
+    gots = cut(got.reshape(shape), down)
     dims = ["ayxb"] * 3
     for level in range(3):
         places = [d.index(o[level]) for d, o in zip(dims, ORDERS)]
@@ -660,15 +681,16 @@
         keeps = [pick(k, at, 0) + pick(g, at, 0) for k, g, at in zip(keeps, gots, places)]
         dims = [d.replace(o[level], "") for d, o in zip(dims, ORDERS)]
         gots = yield [(o[level], v) for o, v in zip(ORDERS, sends)]
-    owns = [k + g for k, g in zip(keeps, gots)]
-    gots = yield [(o[3], v) for o, v in zip(ORDERS, owns)]
-    owns = [v + jnp.concatenate([g[1:], g[:1]]) for v, g in zip(owns, gots)]
+    own = jnp.concatenate([k + g for k, g in zip(keeps, gots)], -2)
+    (got,) = yield [("b", own)]
+    own = own + jnp.concatenate([got[1:], got[:1]])
     for extra in range(4, lax.axis_size("dp").bit_length() - 1):
-        owns = [v + swap(v, extra) for v in owns]
+        own = own + swap(own, extra)
+    owns = cut(own, up)
     for level in (2, 1):
         gots = yield [(o[level], v) for o, v in zip(ORDERS, owns)]
         owns = [jnp.stack(v) for v in zip(owns, gots)]
-    owns = [v.reshape((8, size, CHUNK)) for v in owns]
+    owns = [v.reshape((8,) + v.shape[-2:]) for v in owns]
     gots = yield [(o[0], v) for o, v in zip(ORDERS, owns)] + [("c", v) for v in owns]
     near, far = gots[:3], gots[3:]
     others = yield [("c", v) for v in near]
@@ -790,14 +812,14 @@
     vec = small_call(rounds.hold(rounds.results["vectors"]), w_inner.shape[1])
     rounds.end(vec[0])
     rounds.begin()
-    (d_w_outer,) = unpack("outer", me, rounds.hold(rounds.results["outer"]), ORDERS)
+    (d_w_outer,) = unpack("outer", rounds.hold(rounds.results["outer"]), ORDERS)
     rounds.end(d_w_outer)
     rounds.begin()
-    (d_w_inner,) = unpack("inner", me, rounds.hold(rounds.results["inner"]), ORDERS)
+    (d_w_inner,) = unpack("inner", rounds.hold(rounds.results["inner"]), ORDERS)
     rounds.end(d_w_inner)
     rounds.begin()
     rounds.end()
-    d_w_query, d_w_key, d_w_value, d_w_output = unpack("attn", me, rounds.results["attn"], ORDERS)
+    d_w_query, d_w_key, d_w_value, d_w_output = unpack("attn", rounds.results["attn"], ORDERS)
     return (
         out.reshape(seqs, length, width), d_x.reshape(seqs, length, width),
         d_w_query, vec[0], d_w_key, d_w_value, vec[1], d_w_output, vec[2], vec[3], vec[4],

time: 226 us -> 217 us (0.960); the launches traced: 223 us -> 216 us
  Pallas kernels: 92.4 us -> 87.6 us
  starting transfers between devices: 45.2 us -> 41.8 us
    ppermute x55, starting transfers between devices: 45.2 us -> 41.8 us  [swap(): return lax.ppermute(value, AXES, [(i, i ^ flip) for i in range(dp * seq)])]
  transfers between devices with their start and end apart: 55 -> 55, of which waited for: 24 -> 26; matrix products, arithmetic and copies ran while one was open for 2% -> 2% of each run, Pallas kernels for 21% -> 20%
where the time goes in v6:
time: 217 us; the launch traced here: 216 us
  Pallas kernels  87.6 us (40%)
  waiting for transfers between devices  75.2 us (35%)
  starting transfers between devices  41.8 us (19%)
  other arithmetic  7.16 us (3%)
  between operations  2.39 us (1%)
  local copies, waits for them, and re-layouts  2.21 us (1%)
    ppermute x55, waiting for transfers between devices, swap(): return lax.ppermute(value, AXES, [(i, i ^ flip) for i in range(dp * seq)])  75.2 us
    ppermute x55, starting transfers between devices, swap(): return lax.ppermute(value, AXES, [(i, i ^ flip) for i in range(dp * seq)])  41.8 us
    pallas_call x1, Pallas kernels, forward(): pl.pallas_call(fwd_kernel, in_specs=[SMEM, SMEM] + [VMEM] * 9 + [HBM] * 8...  37.6 us
    pallas_call x3, Pallas kernels, unpack(): pl.pallas_call(functools.partial(unpack_kernel, kind, orders), in_specs=[...  18.4 us
    pallas_call x1, Pallas kernels, att_call(): pl.pallas_call(att_kernel, in_specs=[SMEM, SMEM, VMEM] + [HBM] * 8, out_s...  15.8 us
    pallas_call x1, Pallas kernels, mid_call(): pl.pallas_call(mid_kernel, in_specs=[VMEM, VMEM] + [HBM] * 6, out_specs=[...  9.22 us
    pallas_call x1, Pallas kernels, dx_call(): pl.pallas_call(dx_kernel, in_specs=[HBM] * 5, out_specs=HBM, out_shape=sd...  6 us
  transfers between devices with their start and end apart: 55, of which 26 were waited for; matrix products, arithmetic and copies ran while one was open for 2% of the time, Pallas kernels for 20%

profile of v6, /device:TPU:0, one launch (start us, length us, event | category | flops | bytes accessed | tf_op | source)
XLA Modules:
  0.0 216.4 jit_solution(7850107902054157047)
XLA Ops:
  1.9 37.6 %forward.1 = (f32[4,12,160]{2,1,0:T(8,128)}, f32[16,768]{1,0:T(8,128)}, bf16[640,768]{1,0:T(8,128)(2,1)}, bf16[640,768]{1,0:T(8,128)(2,1)}, bf16[640,768]{1,0:T(...) custom-call(s32[4]{0:T(128)} %refs_0_.5, ...), custom_call_target="tpu_custom_call" | custom-call | flops 28000000000 | bytes 1048576 | tf_op jit(solution)/shard_map/forward/pallas_call | solution.py:276
  40.2 4.3 %collective-permute-done = bf16[16,192,384]{2,1,0:T(8,128)(2,1)S(1)} collective-permute-done((bf16[16,192,384]{2,1,0:T(8,128)(2,1)}, bf16[16,192,384]{2,1,0:T(8,128)(2,1)S(1)}, u32[]{:S(2)}, u32[]{:S(2)}) %collective-permute-start) | collective-permute-done | bytes 2359328 | tf_op jit(solution)/shard_map/ppermute | solution.py:655
  46.8 2.8 %collective-permute-start.1 = (bf16[2,2,2,64,384]{4,3,2,1,0:T(8,128)(2,1)S(1)}, bf16[2,2,2,64,384]{4,3,2,1,0:T(8,128)(2,1)S(1)}, u32[]{:S(2)}, u32[]{:S(2)}) collective-permute-start(bf16[2,2,2,64,384]{4,3,2,1,0:T(8,128)(2,1)S(1)} %fusion.7), channel_id=1, source_target_pairs={{0,2},{1,3},{2,0},{3,1},{4,6},{5,7},{6,4},{7,5},{8,10},{9,11},{10,... | collective-permute-start | bytes 1179656 | tf_op jit(solution)/shard_map/ppermute | solution.py:655
  52.9 9.2 %mid_bwd.1 = (f32[16,768]{1,0:T(8,128)S(1)}, f32[640,768]{1,0:T(8,128)S(1)}, bf16[640,768]{1,0:T(8,128)(2,1)S(1)}, bf16[640,768]{1,0:T(8,128)(2,1)S(1)}) custom-call(f32[768]{0:T(1024)S(1)} %copy-done.6, f32[16,768]{1,0:T(8,128)S(1)} %copy-done.16, bf16[640,3072]{1,0:T(8,128)(2,1)} %get-tuple-element.230.refs_2_, bf16[768,3072]{1,0:T(8,128)(2,1)} %refs_3_.3, ...), custom_call_target="tpu_custom_call" | custom-call | flops 10000000000 | bytes 1048576 | tf_op jit(solution)/shard_map/mid_bwd/pallas_call | solution.py:403
  65.0 15.8 %att_bwd.1 = (f32[16,768]{1,0:T(8,128)S(1)}, bf16[640,3072]{1,0:T(8,128)(2,1)}, bf16[16,192,384]{2,1,0:T(8,128)(2,1)S(1)}, bf16[16,192,384]{2,1,0:T(8,128)(2,1)}) custom-call(s32[4]{0:T(128)S(1)} %copy-done.7, s32[3]{0:T(128)S(1)} %copy-done, f32[16,768]{1,0:T(8,128)S(1)} %get-tuple-element.247.refs_2_, bf16[640,768]{1,0:T(8,128)(2,1)S(1)} %copy-done.11, ...), custom_call_target="tpu_custom_call" | custom-call | flops 12000000000 | bytes 1048576 | tf_op jit(solution)/shard_map/att_bwd/pallas_call | solution.py:469
  85.8 6.0 %dx.1 = f32[640,768]{1,0:T(8,128)} custom-call(f32[640,768]{1,0:T(8,128)S(1)} %get-tuple-element.267.dh1_h, bf16[640,3072]{1,0:T(8,128)(2,1)S(1)} %copy-done.8, bf16[768,768]{1,0:T(8,128)(2,1)S(1)} %copy-done.2, bf16[768,768]{1,0:T(8,128)(2,1)S(1)} %copy-done.3, bf16[768,768]{1,0:T(8,128)(2,1)S(1)} %copy-done.4), custom_call_target="tpu_custom_call" | custom-call | flops 5000000000 | bytes 1048576 | tf_op jit(solution)/shard_map/dx/pallas_call | solution.py:516
  96.8 2.6 %collective-permute-start.16 = (bf16[2,192,384]{2,1,0:T(8,128)(2,1)S(1)}, bf16[2,192,384]{2,1,0:T(8,128)(2,1)S(1)}, u32[]{:S(2)}, u32[]{:S(2)}) collective-permute-start(bf16[2,192,384]{2,1,0:T(8,128)(2,1)S(1)} %pad_maximum_fusion.29), channel_id=1, source_target_pairs={{0,16},{1,17},{2,18},{3,19},{4,20},{5,21},{6,22},{7,23},{8,24},{9,... | collective-permute-start | bytes 884744 | tf_op jit(solution)/shard_map/ppermute | solution.py:655
  99.4 7.6 %collective-permute-done.13 = bf16[640,384]{1,0:T(8,128)(2,1)S(1)} collective-permute-done((bf16[640,384]{1,0:T(8,128)(2,1)S(1)}, bf16[640,384]{1,0:T(8,128)(2,1)S(1)}, u32[]{:S(2)}, u32[]{:S(2)}) %collective-permute-start.13) | collective-permute-done | bytes 491552 | tf_op jit(solution)/shard_map/ppermute | solution.py:655
  107.3 6.0 %collective-permute-done.15 = bf16[672,384]{1,0:T(8,128)(2,1)S(1)} collective-permute-done((bf16[672,384]{1,0:T(8,128)(2,1)S(1)}, bf16[672,384]{1,0:T(8,128)(2,1)S(1)}, u32[]{:S(2)}, u32[]{:S(2)}) %collective-permute-start.15) | collective-permute-done | bytes 516128 | tf_op jit(solution)/shard_map/ppermute | solution.py:655
  115.9 2.5 %collective-permute-start.18 = (bf16[384,384]{1,0:T(8,128)(2,1)S(1)}, bf16[384,384]{1,0:T(8,128)(2,1)S(1)}, u32[]{:S(2)}, u32[]{:S(2)}) collective-permute-start(bf16[384,384]{1,0:T(8,128)(2,1)S(1)} %pad_maximum_fusion.30), channel_id=1, source_target_pairs={{0,8},{1,9},{2,10},{3,11},{4,12},{5,13},{6,14},{7,15},{8,0},{9,1},... | collective-permute-start | bytes 884744 | tf_op jit(solution)/shard_map/ppermute | solution.py:655
  119.3 2.4 %collective-permute-done.17 = bf16[384,384]{1,0:T(8,128)(2,1)S(1)} collective-permute-done((bf16[384,384]{1,0:T(8,128)(2,1)S(1)}, bf16[384,384]{1,0:T(8,128)(2,1)S(1)}, u32[]{:S(2)}, u32[]{:S(2)}) %collective-permute-start.17) | collective-permute-done | bytes 294944 | tf_op jit(solution)/shard_map/ppermute | solution.py:655
  121.7 5.8 %collective-permute-done.18 = bf16[384,384]{1,0:T(8,128)(2,1)S(1)} collective-permute-done((bf16[384,384]{1,0:T(8,128)(2,1)S(1)}, bf16[384,384]{1,0:T(8,128)(2,1)S(1)}, u32[]{:S(2)}, u32[]{:S(2)}) %collective-permute-start.18) | collective-permute-done | bytes 294944 | tf_op jit(solution)/shard_map/ppermute | solution.py:655
  127.6 4.4 %collective-permute-done.20 = bf16[2,192,384]{2,1,0:T(8,128)(2,1)S(1)} collective-permute-done((bf16[2,192,384]{2,1,0:T(8,128)(2,1)S(1)}, bf16[2,192,384]{2,1,0:T(8,128)(2,1)S(1)}, u32[]{:S(2)}, u32[]{:S(2)}) %collective-permute-start.20) | collective-permute-done | bytes 294944 | tf_op jit(solution)/shard_map/ppermute | solution.py:655
  135.2 5.2 %collective-permute-done.21 = bf16[512,384]{1,0:T(8,128)(2,1)S(1)} collective-permute-done((bf16[512,384]{1,0:T(8,128)(2,1)S(1)}, bf16[512,384]{1,0:T(8,128)(2,1)S(1)}, u32[]{:S(2)}, u32[]{:S(2)}) %collective-permute-start.21) | collective-permute-done | bytes 393248 | tf_op jit(solution)/shard_map/ppermute | solution.py:655
  140.6 4.1 %collective-permute-done.23 = bf16[544,384]{1,0:T(8,128)(2,1)S(1)} collective-permute-done((bf16[544,384]{1,0:T(8,128)(2,1)S(1)}, bf16[544,384]{1,0:T(8,128)(2,1)S(1)}, u32[]{:S(2)}, u32[]{:S(2)}) %collective-permute-start.23) | collective-permute-done | bytes 417824 | tf_op jit(solution)/shard_map/ppermute | solution.py:655
  147.0 2.9 %collective-permute-start.26 = (bf16[768,384]{1,0:T(8,128)(2,1)S(1)}, bf16[768,384]{1,0:T(8,128)(2,1)S(1)}, u32[]{:S(2)}, u32[]{:S(2)}) collective-permute-start(bf16[768,384]{1,0:T(8,128)(2,1)S(1)} %pad_maximum_fusion.3), channel_id=1, source_target_pairs={{0,8},{1,9},{2,10},{3,11},{4,12},{5,13},{6,14},{7,15},{8,0},{9,1},... | collective-permute-start | bytes 1769480 | tf_op jit(solution)/shard_map/ppermute | solution.py:655
  150.6 7.9 %collective-permute-done.24 = bf16[416,384]{1,0:T(8,128)(2,1)S(1)} collective-permute-done((bf16[416,384]{1,0:T(8,128)(2,1)S(1)}, bf16[416,384]{1,0:T(8,128)(2,1)S(1)}, u32[]{:S(2)}, u32[]{:S(2)}) %collective-permute-start.24) | collective-permute-done | bytes 319520 | tf_op jit(solution)/shard_map/ppermute | solution.py:655
  159.0 5.8 %collective-permute-done.26 = bf16[768,384]{1,0:T(8,128)(2,1)S(1)} collective-permute-done((bf16[768,384]{1,0:T(8,128)(2,1)S(1)}, bf16[768,384]{1,0:T(8,128)(2,1)S(1)}, u32[]{:S(2)}, u32[]{:S(2)}) %collective-permute-start.26) | collective-permute-done | bytes 589856 | tf_op jit(solution)/shard_map/ppermute | solution.py:655
  169.7 7.2 %collective-permute-done.31 = bf16[640,384]{1,0:T(8,128)(2,1)S(1)} collective-permute-done((bf16[640,384]{1,0:T(8,128)(2,1)S(1)}, bf16[640,384]{1,0:T(8,128)(2,1)S(1)}, u32[]{:S(2)}, u32[]{:S(2)}) %collective-permute-start.31) | collective-permute-done | bytes 491552 | tf_op jit(solution)/shard_map/ppermute | solution.py:655
  182.1 4.8 %collective-permute-done.40 = bf16[2,2,64,384]{3,2,1,0:T(8,128)(2,1)S(1)} collective-permute-done((bf16[2,2,64,384]{3,2,1,0:T(8,128)(2,1)S(1)}, bf16[2,2,64,384]{3,2,1,0:T(8,128)(2,1)S(1)}, u32[]{:S(2)}, u32[]{:S(2)}) %collective-permute-start.40) | collective-permute-done | bytes 196640 | tf_op jit(solution)/shard_map/ppermute | solution.py:655
  187.9 6.1 %unpack_outer.1 = f32[3072,768]{1,0:T(8,128)} custom-call(bf16[8,64,384]{2,1,0:T(8,128)(2,1)S(1)} %bitcast.376, bf16[8,64,384]{2,1,0:T(8,128)(2,1)S(1)} %bitcast.394, bf16[8,64,384]{2,1,0:T(8,128)(2,1)S(1)} %collective-permute-done.28.refs_2_, bf16[8,64,384]{2,1,0:T(8,128)(2,1)S(1)} %collective-permute-done.37.refs_3_, bf16[8,64,384]{2,1,0:T(8,128)(2,1)S(1)} %bitcast.379, ...), custom_call_target="tpu_custom_call" | custom-call | flops 4000000000 | bytes 1048576 | tf_op jit(solution)/shard_map/unpack_outer/pallas_call | solution.py:609
  197.7 6.1 %unpack_inner.1 = f32[768,3072]{1,0:T(8,128)} custom-call(bf16[8,64,384]{2,1,0:T(8,128)(2,1)S(1)} %bitcast.385, bf16[8,64,384]{2,1,0:T(8,128)(2,1)S(1)} %bitcast.398, bf16[8,64,384]{2,1,0:T(8,128)(2,1)S(1)} %collective-permute-done.34.refs_2_, bf16[8,64,384]{2,1,0:T(8,128)(2,1)S(1)} %collective-permute-done.43.refs_3_, bf16[8,64,384]{2,1,0:T(8,128)(2,1)S(1)} %bitcast.388, ...), custom_call_target="tpu_custom_call" | custom-call | flops 4000000000 | bytes 1048576 | tf_op jit(solution)/shard_map/unpack_inner/pallas_call | solution.py:609
  203.8 2.5 %collective-permute-done.46.refs_1_ = bf16[8,64,384]{2,1,0:T(8,128)(2,1)S(1)} collective-permute-done((bf16[8,64,384]{2,1,0:T(8,128)(2,1)S(1)}, bf16[8,64,384]{2,1,0:T(8,128)(2,1)S(1)}, u32[]{:S(2)}, u32[]{:S(2)}) %collective-permute-start.46) | collective-permute-done | bytes 393248 | tf_op jit(solution)/shard_map/ppermute | solution.py:655
  210.0 6.2 %unpack_attn.1 = (f32[768,768]{1,0:T(8,128)}, f32[768,768]{1,0:T(8,128)}, f32[768,768]{1,0:T(8,128)}, f32[768,768]{1,0:T(8,128)}) custom-call(bf16[8,64,384]{2,1,0:T(8,128)(2,1)S(1)} %bitcast.403, bf16[8,64,384]{2,1,0:T(8,128)(2,1)S(1)} %collective-permute-done.46.refs_1_, bf16[8,64,384]{2,1,0:T(8,128)(2,1)S(1)} %collective-permute-done.49.refs_2_, ...), custom_call_target="tpu_custom_call" | custom-call | flops 4000000000 | bytes 1048576 | tf_op jit(solution)/shard_map/unpack_attn/pallas_call | solution.py:609
  (290 shorter events, 48.3 us)
Async XLA Ops:
  40.1 22.0 %collective-permute-start.4 = (bf16[16,192,384]{2,1,0:T(8,128)(2,1)}, bf16[16,192,384]{2,1,0:T(8,128)(2,1)S(1)}, u32[]{:S(2)}, u32[]{:S(2)}) collective-permute-start(bf16[16,192,384]{2,1,0:T(8,128)(2,1)} %get-tuple-element.236), channel_id=1, source_target_pairs={{0,1},{1,0},{2,3},{3,2},{4,5},{5,4},{6,7},{7,6},{8,9},{9,8},{10,11... | collective-permute-start | bytes 7077896 | tf_op jit(solution)/shard_map/ppermute | solution.py:655
  46.8 15.7 %collective-permute-start.1 = (bf16[2,2,2,64,384]{4,3,2,1,0:T(8,128)(2,1)S(1)}, bf16[2,2,2,64,384]{4,3,2,1,0:T(8,128)(2,1)S(1)}, u32[]{:S(2)}, u32[]{:S(2)}) collective-permute-start(bf16[2,2,2,64,384]{4,3,2,1,0:T(8,128)(2,1)S(1)} %fusion.7), channel_id=1, source_target_pairs={{0,2},{1,3},{2,0},{3,1},{4,6},{5,7},{6,4},{7,5},{8,10},{9,11},{10,... | collective-permute-start | bytes 1179656 | tf_op jit(solution)/shard_map/ppermute | solution.py:655
  49.6 12.8 %collective-permute-start.2 = (bf16[2,2,2,64,384]{4,3,2,1,0:T(8,128)(2,1)S(1)}, bf16[2,2,2,64,384]{4,3,2,1,0:T(8,128)(2,1)S(1)}, u32[]{:S(2)}, u32[]{:S(2)}) collective-permute-start(bf16[2,2,2,64,384]{4,3,2,1,0:T(8,128)(2,1)S(1)} %fusion.6), channel_id=1, source_target_pairs={{0,4},{1,5},{2,6},{3,7},{4,0},{5,1},{6,2},{7,3},{8,12},{9,13},{10,... | collective-permute-start | bytes 1179656 | tf_op jit(solution)/shard_map/ppermute | solution.py:655
  62.9 17.9 %collective-permute-start.5 = (bf16[768,384]{1,0:T(8,128)(2,1)S(1)}, bf16[768,384]{1,0:T(8,128)(2,1)S(1)}, u32[]{:S(2)}, u32[]{:S(2)}) collective-permute-start(bf16[768,384]{1,0:T(8,128)(2,1)S(1)} %pad_maximum_fusion.1), channel_id=1, source_target_pairs={{0,2},{1,3},{2,0},{3,1},{4,6},{5,7},{6,4},{7,5},{8,10},{9,11},{10,... | collective-permute-start | bytes 1769480 | tf_op jit(solution)/shard_map/ppermute | solution.py:655
  63.5 17.4 %collective-permute-start.6 = (bf16[768,384]{1,0:T(8,128)(2,1)S(1)}, bf16[768,384]{1,0:T(8,128)(2,1)S(1)}, u32[]{:S(2)}, u32[]{:S(2)}) collective-permute-start(bf16[768,384]{1,0:T(8,128)(2,1)S(1)} %pad_maximum_fusion.2), channel_id=1, source_target_pairs={{0,4},{1,5},{2,6},{3,7},{4,0},{5,1},{6,2},{7,3},{8,12},{9,13},{10,... | collective-permute-start | bytes 1769480 | tf_op jit(solution)/shard_map/ppermute | solution.py:655
  64.0 17.0 %collective-permute-start.7 = (bf16[768,384]{1,0:T(8,128)(2,1)S(1)}, bf16[768,384]{1,0:T(8,128)(2,1)S(1)}, u32[]{:S(2)}, u32[]{:S(2)}) collective-permute-start(bf16[768,384]{1,0:T(8,128)(2,1)S(1)} %pad_maximum_fusion), channel_id=1, source_target_pairs={{0,8},{1,9},{2,10},{3,11},{4,12},{5,13},{6,14},{7,15},{8,0},{9,1},... | collective-permute-start | bytes 1769480 | tf_op jit(solution)/shard_map/ppermute | solution.py:655
  81.5 11.6 %collective-permute-start.8 = (bf16[16,192,384]{2,1,0:T(8,128)(2,1)S(1)}, bf16[16,192,384]{2,1,0:T(8,128)(2,1)S(1)}, u32[]{:S(2)}, u32[]{:S(2)}) collective-permute-start(bf16[16,192,384]{2,1,0:T(8,128)(2,1)S(1)} %get-tuple-element.263), channel_id=1, source_target_pairs={{0,1},{1,0},{2,3},{3,2},{4,5},{5,4},{6,7},{7,6},{8,9},{9,8},{10,11... | collective-permute-start | bytes 7077896 | tf_op jit(solution)/shard_map/ppermute | solution.py:655
  93.8 19.4 %collective-permute-start.15 = (bf16[672,384]{1,0:T(8,128)(2,1)S(1)}, bf16[672,384]{1,0:T(8,128)(2,1)S(1)}, u32[]{:S(2)}, u32[]{:S(2)}) collective-permute-start(bf16[672,384]{1,0:T(8,128)(2,1)S(1)} %pad_maximum_fusion.6), channel_id=1, source_target_pairs={{0,8},{1,9},{2,10},{3,11},{4,12},{5,13},{6,14},{7,15},{8,0},{9,1},... | collective-permute-start | bytes 1548296 | tf_op jit(solution)/shard_map/ppermute | solution.py:655
  94.8 12.2 %collective-permute-start.13 = (bf16[640,384]{1,0:T(8,128)(2,1)S(1)}, bf16[640,384]{1,0:T(8,128)(2,1)S(1)}, u32[]{:S(2)}, u32[]{:S(2)}) collective-permute-start(bf16[640,384]{1,0:T(8,128)(2,1)S(1)} %pad_maximum_fusion.7), channel_id=1, source_target_pairs={{0,2},{1,3},{2,0},{3,1},{4,6},{5,7},{6,4},{7,5},{8,10},{9,11},{10,... | collective-permute-start | bytes 1474568 | tf_op jit(solution)/shard_map/ppermute | solution.py:655
  95.3 11.9 %collective-permute-start.14 = (bf16[640,384]{1,0:T(8,128)(2,1)S(1)}, bf16[640,384]{1,0:T(8,128)(2,1)S(1)}, u32[]{:S(2)}, u32[]{:S(2)}) collective-permute-start(bf16[640,384]{1,0:T(8,128)(2,1)S(1)} %pad_maximum_fusion.8), channel_id=1, source_target_pairs={{0,4},{1,5},{2,6},{3,7},{4,0},{5,1},{6,2},{7,3},{8,12},{9,13},{10,... | collective-permute-start | bytes 1474568 | tf_op jit(solution)/shard_map/ppermute | solution.py:655
  96.8 16.5 %collective-permute-start.16 = (bf16[2,192,384]{2,1,0:T(8,128)(2,1)S(1)}, bf16[2,192,384]{2,1,0:T(8,128)(2,1)S(1)}, u32[]{:S(2)}, u32[]{:S(2)}) collective-permute-start(bf16[2,192,384]{2,1,0:T(8,128)(2,1)S(1)} %pad_maximum_fusion.29), channel_id=1, source_target_pairs={{0,16},{1,17},{2,18},{3,19},{4,20},{5,21},{6,22},{7,23},{8,24},{9,... | collective-permute-start | bytes 884744 | tf_op jit(solution)/shard_map/ppermute | solution.py:655
  114.0 13.5 %collective-permute-start.19 = (bf16[416,384]{1,0:T(8,128)(2,1)S(1)}, bf16[416,384]{1,0:T(8,128)(2,1)S(1)}, u32[]{:S(2)}, u32[]{:S(2)}) collective-permute-start(bf16[416,384]{1,0:T(8,128)(2,1)S(1)} %pad_maximum_fusion.24), channel_id=1, source_target_pairs={{0,2},{1,3},{2,0},{3,1},{4,6},{5,7},{6,4},{7,5},{8,10},{9,11},{10,... | collective-permute-start | bytes 958472 | tf_op jit(solution)/shard_map/ppermute | solution.py:655
  115.9 11.6 %collective-permute-start.18 = (bf16[384,384]{1,0:T(8,128)(2,1)S(1)}, bf16[384,384]{1,0:T(8,128)(2,1)S(1)}, u32[]{:S(2)}, u32[]{:S(2)}) collective-permute-start(bf16[384,384]{1,0:T(8,128)(2,1)S(1)} %pad_maximum_fusion.30), channel_id=1, source_target_pairs={{0,8},{1,9},{2,10},{3,11},{4,12},{5,13},{6,14},{7,15},{8,0},{9,1},... | collective-permute-start | bytes 884744 | tf_op jit(solution)/shard_map/ppermute | solution.py:655
  118.4 13.7 %collective-permute-start.20 = (bf16[2,192,384]{2,1,0:T(8,128)(2,1)S(1)}, bf16[2,192,384]{2,1,0:T(8,128)(2,1)S(1)}, u32[]{:S(2)}, u32[]{:S(2)}) collective-permute-start(bf16[2,192,384]{2,1,0:T(8,128)(2,1)S(1)} %pad_maximum_fusion.31), channel_id=1, source_target_pairs={{0,16},{1,17},{2,18},{3,19},{4,20},{5,21},{6,22},{7,23},{8,24},{9,... | collective-permute-start | bytes 884744 | tf_op jit(solution)/shard_map/ppermute | solution.py:655
  145.4 13.0 %collective-permute-start.25 = (bf16[768,384]{1,0:T(8,128)(2,1)S(1)}, bf16[768,384]{1,0:T(8,128)(2,1)S(1)}, u32[]{:S(2)}, u32[]{:S(2)}) collective-permute-start(bf16[768,384]{1,0:T(8,128)(2,1)S(1)} %pad_maximum_fusion.5), channel_id=1, source_target_pairs={{0,4},{1,5},{2,6},{3,7},{4,0},{5,1},{6,2},{7,3},{8,12},{9,13},{10,... | collective-permute-start | bytes 1769480 | tf_op jit(solution)/shard_map/ppermute | solution.py:655
  147.0 11.5 %collective-permute-start.24 = (bf16[416,384]{1,0:T(8,128)(2,1)S(1)}, bf16[416,384]{1,0:T(8,128)(2,1)S(1)}, u32[]{:S(2)}, u32[]{:S(2)}) collective-permute-start(bf16[416,384]{1,0:T(8,128)(2,1)S(1)} %pad_maximum_fusion.25), channel_id=1, source_target_pairs={{0,16},{1,17},{2,18},{3,19},{4,20},{5,21},{6,22},{7,23},{8,24},{9,... | collective-permute-start | bytes 958472 | tf_op jit(solution)/shard_map/ppermute | solution.py:655
  147.0 17.9 %collective-permute-start.26 = (bf16[768,384]{1,0:T(8,128)(2,1)S(1)}, bf16[768,384]{1,0:T(8,128)(2,1)S(1)}, u32[]{:S(2)}, u32[]{:S(2)}) collective-permute-start(bf16[768,384]{1,0:T(8,128)(2,1)S(1)} %pad_maximum_fusion.3), channel_id=1, source_target_pairs={{0,8},{1,9},{2,10},{3,11},{4,12},{5,13},{6,14},{7,15},{8,0},{9,1},... | collective-permute-start | bytes 1769480 | tf_op jit(solution)/shard_map/ppermute | solution.py:655
  149.9 15.1 %collective-permute-start.27 = (bf16[768,384]{1,0:T(8,128)(2,1)S(1)}, bf16[768,384]{1,0:T(8,128)(2,1)S(1)}, u32[]{:S(2)}, u32[]{:S(2)}) collective-permute-start(bf16[768,384]{1,0:T(8,128)(2,1)S(1)} %pad_maximum_fusion.4), channel_id=1, source_target_pairs={{0,2},{1,3},{2,0},{3,1},{4,6},{5,7},{6,4},{7,5},{8,10},{9,11},{10,... | collective-permute-start | bytes 1769480 | tf_op jit(solution)/shard_map/ppermute | solution.py:655
  150.6 14.4 %collective-permute-start.28 = (bf16[8,64,384]{2,1,0:T(8,128)(2,1)S(1)}, bf16[8,64,384]{2,1,0:T(8,128)(2,1)S(1)}, u32[]{:S(2)}, u32[]{:S(2)}) collective-permute-start(bf16[8,64,384]{2,1,0:T(8,128)(2,1)S(1)} %bitcast.375), channel_id=1, source_target_pairs={{0,1},{1,0},{2,3},{3,2},{4,5},{5,4},{6,7},{7,6},{8,9},{9,8},{10,11... | collective-permute-start | bytes 1179656 | tf_op jit(solution)/shard_map/ppermute | solution.py:655
  180.3 13.7 %collective-permute-start.43 = (bf16[8,64,384]{2,1,0:T(8,128)(2,1)S(1)}, bf16[8,64,384]{2,1,0:T(8,128)(2,1)S(1)}, u32[]{:S(2)}, u32[]{:S(2)}) collective-permute-start(bf16[8,64,384]{2,1,0:T(8,128)(2,1)S(1)} %bitcast.397), channel_id=1, source_target_pairs={{0,1},{1,0},{2,3},{3,2},{4,5},{5,4},{6,7},{7,6},{8,9},{9,8},{10,11... | collective-permute-start | bytes 1179656 | tf_op jit(solution)/shard_map/ppermute | solution.py:655
  180.3 13.7 %collective-permute-start.44 = (bf16[8,64,384]{2,1,0:T(8,128)(2,1)S(1)}, bf16[8,64,384]{2,1,0:T(8,128)(2,1)S(1)}, u32[]{:S(2)}, u32[]{:S(2)}) collective-permute-start(bf16[8,64,384]{2,1,0:T(8,128)(2,1)S(1)} %bitcast.399), channel_id=1, source_target_pairs={{0,1},{1,0},{2,3},{3,2},{4,5},{5,4},{6,7},{7,6},{8,9},{9,8},{10,11... | collective-permute-start | bytes 1179656 | tf_op jit(solution)/shard_map/ppermute | solution.py:655
  180.8 13.2 %collective-permute-start.45 = (bf16[8,64,384]{2,1,0:T(8,128)(2,1)S(1)}, bf16[8,64,384]{2,1,0:T(8,128)(2,1)S(1)}, u32[]{:S(2)}, u32[]{:S(2)}) collective-permute-start(bf16[8,64,384]{2,1,0:T(8,128)(2,1)S(1)} %bitcast.395), channel_id=1, source_target_pairs={{0,1},{1,0},{2,3},{3,2},{4,5},{5,4},{6,7},{7,6},{8,9},{9,8},{10,11... | collective-permute-start | bytes 1179656 | tf_op jit(solution)/shard_map/ppermute | solution.py:655
  180.8 13.1 %collective-permute-start.41 = (bf16[2,2,64,384]{3,2,1,0:T(8,128)(2,1)S(1)}, bf16[2,2,64,384]{3,2,1,0:T(8,128)(2,1)S(1)}, u32[]{:S(2)}, u32[]{:S(2)}) collective-permute-start(bf16[2,2,64,384]{3,2,1,0:T(8,128)(2,1)S(1)} %get-tuple-element.349), channel_id=1, source_target_pairs={{0,8},{1,9},{2,10},{3,11},{4,12},{5,13},{6,14},{7,15},{8,0},{9,1},... | collective-permute-start | bytes 589832 | tf_op jit(solution)/shard_map/ppermute | solution.py:655
  194.8 11.5 %collective-permute-start.46 = (bf16[8,64,384]{2,1,0:T(8,128)(2,1)S(1)}, bf16[8,64,384]{2,1,0:T(8,128)(2,1)S(1)}, u32[]{:S(2)}, u32[]{:S(2)}) collective-permute-start(bf16[8,64,384]{2,1,0:T(8,128)(2,1)S(1)} %bitcast.402), channel_id=1, source_target_pairs={{0,2},{1,3},{2,0},{3,1},{4,6},{5,7},{6,4},{7,5},{8,10},{9,11},{10,... | collective-permute-start | bytes 1179656 | tf_op jit(solution)/shard_map/ppermute | solution.py:655
  (58 other events, 351.9 us)

commit v7 on v6

--- a/solution.py
+++ b/solution.py
@@ -473,7 +473,7 @@
         out_shape=[sd((16, width), f32)] + outs,
         scratch_shapes=[vm(a) for a in arrays[:7]] + [pltpu.VMEM((8, 128), bf16)] + [vm(o) for o in outs]
         + [dma((8,)), dma((1,)), dma((2, 4))],
-        compiler_params=params(44),
+        compiler_params=params(50),
         cost_estimate=cost(12e9),
         name="att_bwd",
     )(lens, me, small1, *arrays)
@@ -522,7 +522,7 @@
             pltpu.VMEM((rows, width), f32), pltpu.VMEM((rows, 3 * width), bf16), pltpu.VMEM(wq.shape, bf16),
             pltpu.VMEM(wq.shape, bf16), pltpu.VMEM(wq.shape, bf16), pltpu.VMEM((rows, width), f32), dma((7,)), dma((2,)),
         ],
-        compiler_params=params(30),
+        compiler_params=params(40),
         cost_estimate=cost(5e9),
         name="dx",
     )(dh1, d, wq, wk, wv)
@@ -532,16 +532,19 @@
     return (value >> "xya".index(name)) & 1
 
 
-def unpack_kernel(kind, orders, *refs):
+def unpack_kernel(kind, orders, halves, *refs):
     me = own_place()
     colors = len(orders)
-    n_in = 4 * colors
+    per = 2 * len(halves)
+    n_in = per * colors
     src = refs[:n_in]
+    if halves == (1,):
+        refs = refs[:n_in] + refs[n_in + 4 :]
     n_out = 4 if kind == "attn" else 1
     outs = refs[n_in : n_in + n_out]
     ins = refs[n_in + n_out : 2 * n_in + n_out]
     buf, sem_in, sem = refs[2 * n_in + n_out :]
-    sizes = [src[4 * n].shape[1] for n in range(colors)]
+    sizes = [src[per * n].shape[1] for n in range(colors)]
     slots = buf.shape[0]
 
     order_in = [n for first in range(2) for n in range(n_in) if n % 2 == first]
@@ -557,8 +560,10 @@
             return [(None, pltpu.make_async_copy(buf.at[slot], outs[0].at[ds(chunk * CHUNK, CHUNK), :], sem.at[slot]))]
         if kind == "inner":
             return [(None, pltpu.make_async_copy(buf.at[slot], outs[0].at[:, ds(chunk * CHUNK, CHUNK)], sem.at[slot]))]
+        rows = pl.ds(0, 2 * CHUNK) if len(halves) == 2 else ds((halves[0] ^ me[0]) * CHUNK, CHUNK)
+        cols = ds((chunk % 2) * CHUNK, CHUNK)
         return [
-            (chunk // 2 == m, pltpu.make_async_copy(buf.at[slot], outs[m].at[:, ds((chunk % 2) * CHUNK, CHUNK)], sem.at[slot]))
+            (chunk // 2 == m, pltpu.make_async_copy(buf.at[slot, rows], outs[m].at[rows, cols], sem.at[slot]))
             for m in range(4)
         ]
 
@@ -573,11 +578,11 @@
         slot = step % slots
         if step >= slots:
             each(step - slots, lambda one: one.wait())
-        for half in range(2):
+        for half in halves:
             place = (half ^ me[0]) * CHUNK
             for n in range(colors):
                 order, size, first = orders[n], sizes[n], sum(sizes[:n])
-                at = 4 * n + 2 * half + bit(step, order[0])
+                at = per * n + (2 * half if len(halves) == 2 else 0) + bit(step, order[0])
                 if at not in waited:
                     waited.add(at)
                     loads[at].wait()
@@ -595,7 +600,7 @@
         each(step, lambda one: one.wait())
 
 
-def unpack(kind, pieces, orders):
+def unpack(kind, pieces, orders, halves=(0, 1), into=()):
     colors = len(orders)
     width = 2 * CHUNK
     if kind == "outer":
@@ -607,16 +612,17 @@
     buf = (4, CHUNK, width) if kind == "outer" else (4, width, CHUNK)
     dma = pltpu.SemaphoreType.DMA
     return pl.pallas_call(
-        functools.partial(unpack_kernel, kind, orders),
-        in_specs=[ANY] * (4 * colors),
+        functools.partial(unpack_kernel, kind, orders, halves),
+        in_specs=[ANY] * len(pieces) + [HBM] * len(into),
         out_specs=[HBM] * len(out_shape),
         out_shape=out_shape,
         scratch_shapes=[pltpu.VMEM(v.shape, v.dtype) for v in pieces]
-        + [pltpu.VMEM(buf, f32), dma((4 * colors,)), dma((4,))],
-        compiler_params=params(24),
+        + [pltpu.VMEM(buf, f32), dma((len(pieces),)), dma((4,))],
+        compiler_params=params(22),
         cost_estimate=cost(4e9),
         name="unpack_" + kind,
-    )(*pieces)
+        input_output_aliases={len(pieces) + n: n for n in range(len(into))},
+    )(*pieces, *into)
 
 
 SMALL_ROWS = (6, 7, 5, 3, 4, 8, 2, 0, 1)
@@ -693,7 +699,7 @@
     owns = [v.reshape((8,) + v.shape[-2:]) for v in owns]
     gots = yield [(o[0], v) for o, v in zip(ORDERS, owns)] + [("c", v) for v in owns]
     near, far = gots[:3], gots[3:]
-    others = yield [("c", v) for v in near]
+    others = yield [("c", v) for v in near], (owns, near)
     return [v for four in zip(owns, near, far, others) for v in four]
 
 
@@ -719,6 +725,7 @@
     def __init__(self):
         self.flows = {}
         self.results = {}
+        self.parts = {}
         self.wanted = {}
         self.mark = ()
 
@@ -771,7 +778,10 @@
                 continue
             values = [got[name, n] for n in range(len(self.wanted[name]))]
             try:
-                self.wanted[name] = self.flows[name].send(values)
+                wanted = self.flows[name].send(values)
+                if isinstance(wanted, tuple):
+                    wanted, self.parts[name] = wanted
+                self.wanted[name] = wanted
             except StopIteration as stop:
                 self.results[name] = stop.value
                 del self.flows[name], self.wanted[name]
@@ -818,8 +828,12 @@
     (d_w_inner,) = unpack("inner", rounds.hold(rounds.results["inner"]), ORDERS)
     rounds.end(d_w_inner)
     rounds.begin()
+    owns, nears = rounds.hold(rounds.parts["attn"])
+    grads = unpack("attn", [v for two in zip(owns, nears) for v in two], ORDERS, (0,))
     rounds.end()
-    d_w_query, d_w_key, d_w_value, d_w_output = unpack("attn", rounds.results["attn"], ORDERS)
+    pieces = rounds.results["attn"]
+    far = [v for n in range(3) for v in pieces[4 * n + 2 : 4 * n + 4]]
+    d_w_query, d_w_key, d_w_value, d_w_output = unpack("attn", far, ORDERS, (1,), grads)
     return (
         out.reshape(seqs, length, width), d_x.reshape(seqs, length, width),
         d_w_query, vec[0], d_w_key, d_w_value, vec[1], d_w_output, vec[2], vec[3], vec[4],

time: 217 us -> 213 us (0.982)
    pallas_call x1, Pallas kernels: 15.8 us -> 13.5 us  [att_call(): pl.pallas_call(att_kernel, in_specs=[SMEM, SMEM, VMEM] + [HBM] * 8, out_s...]
    pallas_call x3 -> x4, Pallas kernels: 18.4 us -> 19.2 us  [unpack(): pl.pallas_call(functools.partial(unpack_kernel, kind, orders, halves), in...]
  transfers between devices with their start and end apart: 55 -> 55, of which waited for: 26 -> 24; matrix products, arithmetic and copies ran while one was open for 2% -> 2% of each run, Pallas kernels for 20% -> 21%
where the time goes in v7:
time: 213 us
  Pallas kernels  86.2 us (40%)
  waiting for transfers between devices  73.2 us (34%)
  starting transfers between devices  41 us (19%)
  other arithmetic  7.33 us (3%)
  local copies, waits for them, and re-layouts  2.78 us (1%)
  between operations  2.38 us (1%)
    ppermute x55, waiting for transfers between devices, swap(): return lax.ppermute(value, AXES, [(i, i ^ flip) for i in range(dp * seq)])  73.2 us
    ppermute x55, starting transfers between devices, swap(): return lax.ppermute(value, AXES, [(i, i ^ flip) for i in range(dp * seq)])  41 us
    pallas_call x1, Pallas kernels, forward(): pl.pallas_call(fwd_kernel, in_specs=[SMEM, SMEM] + [VMEM] * 9 + [HBM] * 8...  37.6 us
    pallas_call x4, Pallas kernels, unpack(): pl.pallas_call(functools.partial(unpack_kernel, kind, orders, halves), in...  19.2 us
    pallas_call x1, Pallas kernels, att_call(): pl.pallas_call(att_kernel, in_specs=[SMEM, SMEM, VMEM] + [HBM] * 8, out_s...  13.5 us
    pallas_call x1, Pallas kernels, mid_call(): pl.pallas_call(mid_kernel, in_specs=[VMEM, VMEM] + [HBM] * 6, out_specs=[...  9.22 us
    pallas_call x1, Pallas kernels, dx_call(): pl.pallas_call(dx_kernel, in_specs=[HBM] * 5, out_specs=HBM, out_shape=sd...  6 us
  transfers between devices with their start and end apart: 55, of which 24 were waited for; matrix products, arithmetic and copies ran while one was open for 2% of the time, Pallas kernels for 21%

profile of v7, /device:TPU:0, one launch (start us, length us, event | category | flops | bytes accessed | tf_op | source)
XLA Modules:
  0.0 212.8 jit_solution(11830099004979402707)
XLA Ops:
  1.9 37.6 %forward.1 = (f32[4,12,160]{2,1,0:T(8,128)}, f32[16,768]{1,0:T(8,128)}, bf16[640,768]{1,0:T(8,128)(2,1)}, bf16[640,768]{1,0:T(8,128)(2,1)}, bf16[640,768]{1,0:T(...) custom-call(s32[4]{0:T(128)} %refs_0_.5, ...), custom_call_target="tpu_custom_call" | custom-call | flops 28000000000 | bytes 1048576 | tf_op jit(solution)/shard_map/forward/pallas_call | solution.py:276
  40.2 4.3 %collective-permute-done = bf16[16,192,384]{2,1,0:T(8,128)(2,1)S(1)} collective-permute-done((bf16[16,192,384]{2,1,0:T(8,128)(2,1)}, bf16[16,192,384]{2,1,0:T(8,128)(2,1)S(1)}, u32[]{:S(2)}, u32[]{:S(2)}) %collective-permute-start) | collective-permute-done | bytes 2359328 | tf_op jit(solution)/shard_map/ppermute | solution.py:661
  46.8 2.9 %collective-permute-start.1 = (bf16[2,2,2,64,384]{4,3,2,1,0:T(8,128)(2,1)S(1)}, bf16[2,2,2,64,384]{4,3,2,1,0:T(8,128)(2,1)S(1)}, u32[]{:S(2)}, u32[]{:S(2)}) collective-permute-start(bf16[2,2,2,64,384]{4,3,2,1,0:T(8,128)(2,1)S(1)} %fusion.7), channel_id=1, source_target_pairs={{0,2},{1,3},{2,0},{3,1},{4,6},{5,7},{6,4},{7,5},{8,10},{9,11},{10,... | collective-permute-start | bytes 1179656 | tf_op jit(solution)/shard_map/ppermute | solution.py:661
  52.9 9.2 %mid_bwd.1 = (f32[16,768]{1,0:T(8,128)S(1)}, f32[640,768]{1,0:T(8,128)S(1)}, bf16[640,768]{1,0:T(8,128)(2,1)S(1)}, bf16[640,768]{1,0:T(8,128)(2,1)S(1)}) custom-call(f32[768]{0:T(1024)S(1)} %copy-done.5, f32[16,768]{1,0:T(8,128)S(1)} %copy-done.15, bf16[640,3072]{1,0:T(8,128)(2,1)} %get-tuple-element.240.refs_2_, bf16[768,3072]{1,0:T(8,128)(2,1)} %refs_3_.3, ...), custom_call_target="tpu_custom_call" | custom-call | flops 10000000000 | bytes 1048576 | tf_op jit(solution)/shard_map/mid_bwd/pallas_call | solution.py:403
  65.6 13.5 %att_bwd.1 = (f32[16,768]{1,0:T(8,128)S(1)}, bf16[640,3072]{1,0:T(8,128)(2,1)}, bf16[16,192,384]{2,1,0:T(8,128)(2,1)}, bf16[16,192,384]{2,1,0:T(8,128)(2,1)}) custom-call(s32[4]{0:T(128)S(1)} %copy-done.6, s32[3]{0:T(128)S(1)} %copy-done, f32[16,768]{1,0:T(8,128)S(1)} %get-tuple-element.257.refs_2_, bf16[640,768]{1,0:T(8,128)(2,1)S(1)} %copy-done.11, ...), custom_call_target="tpu_custom_call" | custom-call | flops 12000000000 | bytes 1048576 | tf_op jit(solution)/shard_map/att_bwd/pallas_call | solution.py:469
  84.3 6.0 %dx.1 = f32[640,768]{1,0:T(8,128)} custom-call(f32[640,768]{1,0:T(8,128)S(1)} %get-tuple-element.277.dh1_h, bf16[640,3072]{1,0:T(8,128)(2,1)S(1)} %copy-done.7, bf16[768,768]{1,0:T(8,128)(2,1)S(1)} %copy-done.2, bf16[768,768]{1,0:T(8,128)(2,1)S(1)} %copy-done.3, bf16[768,768]{1,0:T(8,128)(2,1)S(1)} %copy-done.4), custom_call_target="tpu_custom_call" | custom-call | flops 5000000000 | bytes 1048576 | tf_op jit(solution)/shard_map/dx/pallas_call | solution.py:516
  94.9 2.6 %collective-permute-start.16 = (bf16[2,192,384]{2,1,0:T(8,128)(2,1)S(1)}, bf16[2,192,384]{2,1,0:T(8,128)(2,1)S(1)}, u32[]{:S(2)}, u32[]{:S(2)}) collective-permute-start(bf16[2,192,384]{2,1,0:T(8,128)(2,1)S(1)} %pad_maximum_fusion.29), channel_id=1, source_target_pairs={{0,16},{1,17},{2,18},{3,19},{4,20},{5,21},{6,22},{7,23},{8,24},{9,... | collective-permute-start | bytes 884744 | tf_op jit(solution)/shard_map/ppermute | solution.py:661
  97.5 7.6 %collective-permute-done.13 = bf16[640,384]{1,0:T(8,128)(2,1)S(1)} collective-permute-done((bf16[640,384]{1,0:T(8,128)(2,1)S(1)}, bf16[640,384]{1,0:T(8,128)(2,1)S(1)}, u32[]{:S(2)}, u32[]{:S(2)}) %collective-permute-start.13) | collective-permute-done | bytes 491552 | tf_op jit(solution)/shard_map/ppermute | solution.py:661
  105.4 6.3 %collective-permute-done.15 = bf16[672,384]{1,0:T(8,128)(2,1)S(1)} collective-permute-done((bf16[672,384]{1,0:T(8,128)(2,1)S(1)}, bf16[672,384]{1,0:T(8,128)(2,1)S(1)}, u32[]{:S(2)}, u32[]{:S(2)}) %collective-permute-start.15) | collective-permute-done | bytes 516128 | tf_op jit(solution)/shard_map/ppermute | solution.py:661
  114.4 2.5 %collective-permute-start.18 = (bf16[384,384]{1,0:T(8,128)(2,1)S(1)}, bf16[384,384]{1,0:T(8,128)(2,1)S(1)}, u32[]{:S(2)}, u32[]{:S(2)}) collective-permute-start(bf16[384,384]{1,0:T(8,128)(2,1)S(1)} %pad_maximum_fusion.30), channel_id=1, source_target_pairs={{0,8},{1,9},{2,10},{3,11},{4,12},{5,13},{6,14},{7,15},{8,0},{9,1},... | collective-permute-start | bytes 884744 | tf_op jit(solution)/shard_map/ppermute | solution.py:661
  117.6 2.5 %collective-permute-done.17 = bf16[384,384]{1,0:T(8,128)(2,1)S(1)} collective-permute-done((bf16[384,384]{1,0:T(8,128)(2,1)S(1)}, bf16[384,384]{1,0:T(8,128)(2,1)S(1)}, u32[]{:S(2)}, u32[]{:S(2)}) %collective-permute-start.17) | collective-permute-done | bytes 294944 | tf_op jit(solution)/shard_map/ppermute | solution.py:661
  120.2 5.9 %collective-permute-done.18 = bf16[384,384]{1,0:T(8,128)(2,1)S(1)} collective-permute-done((bf16[384,384]{1,0:T(8,128)(2,1)S(1)}, bf16[384,384]{1,0:T(8,128)(2,1)S(1)}, u32[]{:S(2)}, u32[]{:S(2)}) %collective-permute-start.18) | collective-permute-done | bytes 294944 | tf_op jit(solution)/shard_map/ppermute | solution.py:661
  126.2 4.3 %collective-permute-done.20 = bf16[2,192,384]{2,1,0:T(8,128)(2,1)S(1)} collective-permute-done((bf16[2,192,384]{2,1,0:T(8,128)(2,1)S(1)}, bf16[2,192,384]{2,1,0:T(8,128)(2,1)S(1)}, u32[]{:S(2)}, u32[]{:S(2)}) %collective-permute-start.20) | collective-permute-done | bytes 294944 | tf_op jit(solution)/shard_map/ppermute | solution.py:661
  133.6 5.4 %collective-permute-done.21 = bf16[512,384]{1,0:T(8,128)(2,1)S(1)} collective-permute-done((bf16[512,384]{1,0:T(8,128)(2,1)S(1)}, bf16[512,384]{1,0:T(8,128)(2,1)S(1)}, u32[]{:S(2)}, u32[]{:S(2)}) %collective-permute-start.21) | collective-permute-done | bytes 393248 | tf_op jit(solution)/shard_map/ppermute | solution.py:661
  139.7 1.9 collective-permute-done.23
  146.0 11.4 %collective-permute-done.24 = bf16[416,384]{1,0:T(8,128)(2,1)S(1)} collective-permute-done((bf16[416,384]{1,0:T(8,128)(2,1)S(1)}, bf16[416,384]{1,0:T(8,128)(2,1)S(1)}, u32[]{:S(2)}, u32[]{:S(2)}) %collective-permute-start.24) | collective-permute-done | bytes 319520 | tf_op jit(solution)/shard_map/ppermute | solution.py:661
  158.0 5.1 %collective-permute-done.26 = bf16[768,384]{1,0:T(8,128)(2,1)S(1)} collective-permute-done((bf16[768,384]{1,0:T(8,128)(2,1)S(1)}, bf16[768,384]{1,0:T(8,128)(2,1)S(1)}, u32[]{:S(2)}, u32[]{:S(2)}) %collective-permute-start.26) | collective-permute-done | bytes 589856 | tf_op jit(solution)/shard_map/ppermute | solution.py:661
  168.8 5.6 %collective-permute-done.31 = bf16[640,384]{1,0:T(8,128)(2,1)S(1)} collective-permute-done((bf16[640,384]{1,0:T(8,128)(2,1)S(1)}, bf16[640,384]{1,0:T(8,128)(2,1)S(1)}, u32[]{:S(2)}, u32[]{:S(2)}) %collective-permute-start.31) | collective-permute-done | bytes 491552 | tf_op jit(solution)/shard_map/ppermute | solution.py:661
  179.9 4.5 %collective-permute-done.40 = bf16[2,2,64,384]{3,2,1,0:T(8,128)(2,1)S(1)} collective-permute-done((bf16[2,2,64,384]{3,2,1,0:T(8,128)(2,1)S(1)}, bf16[2,2,64,384]{3,2,1,0:T(8,128)(2,1)S(1)}, u32[]{:S(2)}, u32[]{:S(2)}) %collective-permute-start.40) | collective-permute-done | bytes 196640 | tf_op jit(solution)/shard_map/ppermute | solution.py:661
  185.2 6.1 %unpack_outer.1 = f32[3072,768]{1,0:T(8,128)} custom-call(bf16[8,64,384]{2,1,0:T(8,128)(2,1)S(1)} %bitcast.376, bf16[8,64,384]{2,1,0:T(8,128)(2,1)S(1)} %bitcast.394, bf16[8,64,384]{2,1,0:T(8,128)(2,1)S(1)} %collective-permute-done.28.refs_2_, bf16[8,64,384]{2,1,0:T(8,128)(2,1)S(1)} %collective-permute-done.37.refs_3_, bf16[8,64,384]{2,1,0:T(8,128)(2,1)S(1)} %bitcast.379, ...), custom_call_target="tpu_custom_call" | custom-call | flops 4000000000 | bytes 1048576 | tf_op jit(solution)/shard_map/unpack_outer/pallas_call | solution.py:614
  195.4 6.1 %unpack_inner.1 = f32[768,3072]{1,0:T(8,128)} custom-call(bf16[8,64,384]{2,1,0:T(8,128)(2,1)S(1)} %bitcast.385, bf16[8,64,384]{2,1,0:T(8,128)(2,1)S(1)} %bitcast.398, bf16[8,64,384]{2,1,0:T(8,128)(2,1)S(1)} %collective-permute-done.34.refs_2_, bf16[8,64,384]{2,1,0:T(8,128)(2,1)S(1)} %collective-permute-done.43.refs_3_, bf16[8,64,384]{2,1,0:T(8,128)(2,1)S(1)} %bitcast.388, ...), custom_call_target="tpu_custom_call" | custom-call | flops 4000000000 | bytes 1048576 | tf_op jit(solution)/shard_map/unpack_inner/pallas_call | solution.py:614
  201.5 2.2 %collective-permute-done.46.refs_1_ = bf16[8,64,384]{2,1,0:T(8,128)(2,1)S(1)} collective-permute-done((bf16[8,64,384]{2,1,0:T(8,128)(2,1)S(1)}, bf16[8,64,384]{2,1,0:T(8,128)(2,1)S(1)}, u32[]{:S(2)}, u32[]{:S(2)}) %collective-permute-start.46) | collective-permute-done | bytes 393248 | tf_op jit(solution)/shard_map/ppermute | solution.py:661
  205.6 3.5 %unpack_attn.2 = (f32[768,768]{1,0:T(8,128)}, f32[768,768]{1,0:T(8,128)}, f32[768,768]{1,0:T(8,128)}, f32[768,768]{1,0:T(8,128)}) custom-call(bf16[8,64,384]{2,1,0:T(8,128)(2,1)S(1)} %bitcast.406, bf16[8,64,384]{2,1,0:T(8,128)(2,1)S(1)} %collective-permute-done.46.refs_1_, bf16[8,64,384]{2,1,0:T(8,128)(2,1)S(1)} %bitcast.409, ...), custom_call_target="tpu_custom_call" | custom-call | flops 4000000000 | bytes 1048576 | tf_op jit(solution)/shard_map/unpack_attn/pallas_call | solution.py:614
  209.1 3.5 %unpack_attn.3 = (f32[768,768]{1,0:T(8,128)}, f32[768,768]{1,0:T(8,128)}, f32[768,768]{1,0:T(8,128)}, f32[768,768]{1,0:T(8,128)}) custom-call(bf16[8,64,384]{2,1,0:T(8,128)(2,1)S(1)} %collective-permute-done.49.refs_0_, ...), custom_call_target="tpu_custom_call", output_to_operand_aliasing={{0}: (6, {}), {1}: (7, {}), {2}: (8, {}), {3}: (9, {})} | custom-call | flops 4000000000 | bytes 1048576 | tf_op jit(solution)/shard_map/unpack_attn/pallas_call | solution.py:614
  (289 shorter events, 49.9 us)
Async XLA Ops:
  40.1 22.1 %collective-permute-start.4 = (bf16[16,192,384]{2,1,0:T(8,128)(2,1)}, bf16[16,192,384]{2,1,0:T(8,128)(2,1)S(1)}, u32[]{:S(2)}, u32[]{:S(2)}) collective-permute-start(bf16[16,192,384]{2,1,0:T(8,128)(2,1)} %get-tuple-element.246), channel_id=1, source_target_pairs={{0,1},{1,0},{2,3},{3,2},{4,5},{5,4},{6,7},{7,6},{8,9},{9,8},{10,11... | collective-permute-start | bytes 7077896 | tf_op jit(solution)/shard_map/ppermute | solution.py:661
  46.8 16.4 %collective-permute-start.1 = (bf16[2,2,2,64,384]{4,3,2,1,0:T(8,128)(2,1)S(1)}, bf16[2,2,2,64,384]{4,3,2,1,0:T(8,128)(2,1)S(1)}, u32[]{:S(2)}, u32[]{:S(2)}) collective-permute-start(bf16[2,2,2,64,384]{4,3,2,1,0:T(8,128)(2,1)S(1)} %fusion.7), channel_id=1, source_target_pairs={{0,2},{1,3},{2,0},{3,1},{4,6},{5,7},{6,4},{7,5},{8,10},{9,11},{10,... | collective-permute-start | bytes 1179656 | tf_op jit(solution)/shard_map/ppermute | solution.py:661
  49.6 13.6 %collective-permute-start.2 = (bf16[2,2,2,64,384]{4,3,2,1,0:T(8,128)(2,1)S(1)}, bf16[2,2,2,64,384]{4,3,2,1,0:T(8,128)(2,1)S(1)}, u32[]{:S(2)}, u32[]{:S(2)}) collective-permute-start(bf16[2,2,2,64,384]{4,3,2,1,0:T(8,128)(2,1)S(1)} %fusion.6), channel_id=1, source_target_pairs={{0,4},{1,5},{2,6},{3,7},{4,0},{5,1},{6,2},{7,3},{8,12},{9,13},{10,... | collective-permute-start | bytes 1179656 | tf_op jit(solution)/shard_map/ppermute | solution.py:661
  51.2 12.1 %collective-permute-start.3 = (bf16[2,2,2,64,384]{4,3,2,1,0:T(8,128)(2,1)S(1)}, bf16[2,2,2,64,384]{4,3,2,1,0:T(8,128)(2,1)S(1)}, u32[]{:S(2)}, u32[]{:S(2)}) collective-permute-start(bf16[2,2,2,64,384]{4,3,2,1,0:T(8,128)(2,1)S(1)} %get-tuple-element.237), channel_id=1, source_target_pairs={{0,8},{1,9},{2,10},{3,11},{4,12},{5,13},{6,14},{7,15},{8,0},{9,1},... | collective-permute-start | bytes 1179656 | tf_op jit(solution)/shard_map/ppermute | solution.py:661
  63.7 15.5 %collective-permute-start.5 = (bf16[768,384]{1,0:T(8,128)(2,1)S(1)}, bf16[768,384]{1,0:T(8,128)(2,1)S(1)}, u32[]{:S(2)}, u32[]{:S(2)}) collective-permute-start(bf16[768,384]{1,0:T(8,128)(2,1)S(1)} %pad_maximum_fusion.1), channel_id=1, source_target_pairs={{0,2},{1,3},{2,0},{3,1},{4,6},{5,7},{6,4},{7,5},{8,10},{9,11},{10,... | collective-permute-start | bytes 1769480 | tf_op jit(solution)/shard_map/ppermute | solution.py:661
  64.3 15.0 %collective-permute-start.6 = (bf16[768,384]{1,0:T(8,128)(2,1)S(1)}, bf16[768,384]{1,0:T(8,128)(2,1)S(1)}, u32[]{:S(2)}, u32[]{:S(2)}) collective-permute-start(bf16[768,384]{1,0:T(8,128)(2,1)S(1)} %pad_maximum_fusion.2), channel_id=1, source_target_pairs={{0,4},{1,5},{2,6},{3,7},{4,0},{5,1},{6,2},{7,3},{8,12},{9,13},{10,... | collective-permute-start | bytes 1769480 | tf_op jit(solution)/shard_map/ppermute | solution.py:661
  64.8 14.6 %collective-permute-start.7 = (bf16[768,384]{1,0:T(8,128)(2,1)S(1)}, bf16[768,384]{1,0:T(8,128)(2,1)S(1)}, u32[]{:S(2)}, u32[]{:S(2)}) collective-permute-start(bf16[768,384]{1,0:T(8,128)(2,1)S(1)} %pad_maximum_fusion), channel_id=1, source_target_pairs={{0,8},{1,9},{2,10},{3,11},{4,12},{5,13},{6,14},{7,15},{8,0},{9,1},... | collective-permute-start | bytes 1769480 | tf_op jit(solution)/shard_map/ppermute | solution.py:661
  79.9 11.7 %collective-permute-start.8 = (bf16[16,192,384]{2,1,0:T(8,128)(2,1)}, bf16[16,192,384]{2,1,0:T(8,128)(2,1)S(1)}, u32[]{:S(2)}, u32[]{:S(2)}) collective-permute-start(bf16[16,192,384]{2,1,0:T(8,128)(2,1)} %get-tuple-element.273), channel_id=1, source_target_pairs={{0,1},{1,0},{2,3},{3,2},{4,5},{5,4},{6,7},{7,6},{8,9},{9,8},{10,11... | collective-permute-start | bytes 7077896 | tf_op jit(solution)/shard_map/ppermute | solution.py:661
  92.3 19.4 %collective-permute-start.15 = (bf16[672,384]{1,0:T(8,128)(2,1)S(1)}, bf16[672,384]{1,0:T(8,128)(2,1)S(1)}, u32[]{:S(2)}, u32[]{:S(2)}) collective-permute-start(bf16[672,384]{1,0:T(8,128)(2,1)S(1)} %pad_maximum_fusion.6), channel_id=1, source_target_pairs={{0,8},{1,9},{2,10},{3,11},{4,12},{5,13},{6,14},{7,15},{8,0},{9,1},... | collective-permute-start | bytes 1548296 | tf_op jit(solution)/shard_map/ppermute | solution.py:661
  92.9 12.2 %collective-permute-start.13 = (bf16[640,384]{1,0:T(8,128)(2,1)S(1)}, bf16[640,384]{1,0:T(8,128)(2,1)S(1)}, u32[]{:S(2)}, u32[]{:S(2)}) collective-permute-start(bf16[640,384]{1,0:T(8,128)(2,1)S(1)} %pad_maximum_fusion.7), channel_id=1, source_target_pairs={{0,2},{1,3},{2,0},{3,1},{4,6},{5,7},{6,4},{7,5},{8,10},{9,11},{10,... | collective-permute-start | bytes 1474568 | tf_op jit(solution)/shard_map/ppermute | solution.py:661
  93.7 11.6 %collective-permute-start.14 = (bf16[640,384]{1,0:T(8,128)(2,1)S(1)}, bf16[640,384]{1,0:T(8,128)(2,1)S(1)}, u32[]{:S(2)}, u32[]{:S(2)}) collective-permute-start(bf16[640,384]{1,0:T(8,128)(2,1)S(1)} %pad_maximum_fusion.8), channel_id=1, source_target_pairs={{0,4},{1,5},{2,6},{3,7},{4,0},{5,1},{6,2},{7,3},{8,12},{9,13},{10,... | collective-permute-start | bytes 1474568 | tf_op jit(solution)/shard_map/ppermute | solution.py:661
  94.9 16.9 %collective-permute-start.16 = (bf16[2,192,384]{2,1,0:T(8,128)(2,1)S(1)}, bf16[2,192,384]{2,1,0:T(8,128)(2,1)S(1)}, u32[]{:S(2)}, u32[]{:S(2)}) collective-permute-start(bf16[2,192,384]{2,1,0:T(8,128)(2,1)S(1)} %pad_maximum_fusion.29), channel_id=1, source_target_pairs={{0,16},{1,17},{2,18},{3,19},{4,20},{5,21},{6,22},{7,23},{8,24},{9,... | collective-permute-start | bytes 884744 | tf_op jit(solution)/shard_map/ppermute | solution.py:661
  112.5 13.7 %collective-permute-start.19 = (bf16[416,384]{1,0:T(8,128)(2,1)S(1)}, bf16[416,384]{1,0:T(8,128)(2,1)S(1)}, u32[]{:S(2)}, u32[]{:S(2)}) collective-permute-start(bf16[416,384]{1,0:T(8,128)(2,1)S(1)} %pad_maximum_fusion.24), channel_id=1, source_target_pairs={{0,2},{1,3},{2,0},{3,1},{4,6},{5,7},{6,4},{7,5},{8,10},{9,11},{10,... | collective-permute-start | bytes 958472 | tf_op jit(solution)/shard_map/ppermute | solution.py:661
  114.4 11.7 %collective-permute-start.18 = (bf16[384,384]{1,0:T(8,128)(2,1)S(1)}, bf16[384,384]{1,0:T(8,128)(2,1)S(1)}, u32[]{:S(2)}, u32[]{:S(2)}) collective-permute-start(bf16[384,384]{1,0:T(8,128)(2,1)S(1)} %pad_maximum_fusion.30), channel_id=1, source_target_pairs={{0,8},{1,9},{2,10},{3,11},{4,12},{5,13},{6,14},{7,15},{8,0},{9,1},... | collective-permute-start | bytes 884744 | tf_op jit(solution)/shard_map/ppermute | solution.py:661
  116.9 13.7 %collective-permute-start.20 = (bf16[2,192,384]{2,1,0:T(8,128)(2,1)S(1)}, bf16[2,192,384]{2,1,0:T(8,128)(2,1)S(1)}, u32[]{:S(2)}, u32[]{:S(2)}) collective-permute-start(bf16[2,192,384]{2,1,0:T(8,128)(2,1)S(1)} %pad_maximum_fusion.31), channel_id=1, source_target_pairs={{0,16},{1,17},{2,18},{3,19},{4,20},{5,21},{6,22},{7,23},{8,24},{9,... | collective-permute-start | bytes 884744 | tf_op jit(solution)/shard_map/ppermute | solution.py:661
  142.3 15.1 %collective-permute-start.25 = (bf16[768,384]{1,0:T(8,128)(2,1)S(1)}, bf16[768,384]{1,0:T(8,128)(2,1)S(1)}, u32[]{:S(2)}, u32[]{:S(2)}) collective-permute-start(bf16[768,384]{1,0:T(8,128)(2,1)S(1)} %pad_maximum_fusion.5), channel_id=1, source_target_pairs={{0,4},{1,5},{2,6},{3,7},{4,0},{5,1},{6,2},{7,3},{8,12},{9,13},{10,... | collective-permute-start | bytes 1769480 | tf_op jit(solution)/shard_map/ppermute | solution.py:661
  143.6 13.8 %collective-permute-start.24 = (bf16[416,384]{1,0:T(8,128)(2,1)S(1)}, bf16[416,384]{1,0:T(8,128)(2,1)S(1)}, u32[]{:S(2)}, u32[]{:S(2)}) collective-permute-start(bf16[416,384]{1,0:T(8,128)(2,1)S(1)} %pad_maximum_fusion.25), channel_id=1, source_target_pairs={{0,16},{1,17},{2,18},{3,19},{4,20},{5,21},{6,22},{7,23},{8,24},{9,... | collective-permute-start | bytes 958472 | tf_op jit(solution)/shard_map/ppermute | solution.py:661
  144.4 18.7 %collective-permute-start.26 = (bf16[768,384]{1,0:T(8,128)(2,1)S(1)}, bf16[768,384]{1,0:T(8,128)(2,1)S(1)}, u32[]{:S(2)}, u32[]{:S(2)}) collective-permute-start(bf16[768,384]{1,0:T(8,128)(2,1)S(1)} %pad_maximum_fusion.3), channel_id=1, source_target_pairs={{0,8},{1,9},{2,10},{3,11},{4,12},{5,13},{6,14},{7,15},{8,0},{9,1},... | collective-permute-start | bytes 1769480 | tf_op jit(solution)/shard_map/ppermute | solution.py:661
  145.4 17.8 %collective-permute-start.27 = (bf16[768,384]{1,0:T(8,128)(2,1)S(1)}, bf16[768,384]{1,0:T(8,128)(2,1)S(1)}, u32[]{:S(2)}, u32[]{:S(2)}) collective-permute-start(bf16[768,384]{1,0:T(8,128)(2,1)S(1)} %pad_maximum_fusion.4), channel_id=1, source_target_pairs={{0,2},{1,3},{2,0},{3,1},{4,6},{5,7},{6,4},{7,5},{8,10},{9,11},{10,... | collective-permute-start | bytes 1769480 | tf_op jit(solution)/shard_map/ppermute | solution.py:661
  146.0 17.3 %collective-permute-start.28 = (bf16[8,64,384]{2,1,0:T(8,128)(2,1)S(1)}, bf16[8,64,384]{2,1,0:T(8,128)(2,1)S(1)}, u32[]{:S(2)}, u32[]{:S(2)}) collective-permute-start(bf16[8,64,384]{2,1,0:T(8,128)(2,1)S(1)} %bitcast.375), channel_id=1, source_target_pairs={{0,1},{1,0},{2,3},{3,2},{4,5},{5,4},{6,7},{7,6},{8,9},{9,8},{10,11... | collective-permute-start | bytes 1179656 | tf_op jit(solution)/shard_map/ppermute | solution.py:661
  178.2 13.2 %collective-permute-start.43 = (bf16[8,64,384]{2,1,0:T(8,128)(2,1)S(1)}, bf16[8,64,384]{2,1,0:T(8,128)(2,1)S(1)}, u32[]{:S(2)}, u32[]{:S(2)}) collective-permute-start(bf16[8,64,384]{2,1,0:T(8,128)(2,1)S(1)} %bitcast.397), channel_id=1, source_target_pairs={{0,1},{1,0},{2,3},{3,2},{4,5},{5,4},{6,7},{7,6},{8,9},{9,8},{10,11... | collective-permute-start | bytes 1179656 | tf_op jit(solution)/shard_map/ppermute | solution.py:661
  178.2 13.2 %collective-permute-start.44 = (bf16[8,64,384]{2,1,0:T(8,128)(2,1)S(1)}, bf16[8,64,384]{2,1,0:T(8,128)(2,1)S(1)}, u32[]{:S(2)}, u32[]{:S(2)}) collective-permute-start(bf16[8,64,384]{2,1,0:T(8,128)(2,1)S(1)} %bitcast.399), channel_id=1, source_target_pairs={{0,1},{1,0},{2,3},{3,2},{4,5},{5,4},{6,7},{7,6},{8,9},{9,8},{10,11... | collective-permute-start | bytes 1179656 | tf_op jit(solution)/shard_map/ppermute | solution.py:661
  178.7 12.7 %collective-permute-start.45 = (bf16[8,64,384]{2,1,0:T(8,128)(2,1)S(1)}, bf16[8,64,384]{2,1,0:T(8,128)(2,1)S(1)}, u32[]{:S(2)}, u32[]{:S(2)}) collective-permute-start(bf16[8,64,384]{2,1,0:T(8,128)(2,1)S(1)} %bitcast.395), channel_id=1, source_target_pairs={{0,1},{1,0},{2,3},{3,2},{4,5},{5,4},{6,7},{7,6},{8,9},{9,8},{10,11... | collective-permute-start | bytes 1179656 | tf_op jit(solution)/shard_map/ppermute | solution.py:661
  178.7 12.6 %collective-permute-start.41 = (bf16[2,2,64,384]{3,2,1,0:T(8,128)(2,1)S(1)}, bf16[2,2,64,384]{3,2,1,0:T(8,128)(2,1)S(1)}, u32[]{:S(2)}, u32[]{:S(2)}) collective-permute-start(bf16[2,2,64,384]{3,2,1,0:T(8,128)(2,1)S(1)} %get-tuple-element.359), channel_id=1, source_target_pairs={{0,8},{1,9},{2,10},{3,11},{4,12},{5,13},{6,14},{7,15},{8,0},{9,1},... | collective-permute-start | bytes 589832 | tf_op jit(solution)/shard_map/ppermute | solution.py:661
  (57 other events, 344.7 us)

commit v8 on v7

--- a/solution.py
+++ b/solution.py
@@ -522,7 +522,7 @@
             pltpu.VMEM((rows, width), f32), pltpu.VMEM((rows, 3 * width), bf16), pltpu.VMEM(wq.shape, bf16),
             pltpu.VMEM(wq.shape, bf16), pltpu.VMEM(wq.shape, bf16), pltpu.VMEM((rows, width), f32), dma((7,)), dma((2,)),
         ],
-        compiler_params=params(40),
+        compiler_params=params(42),
         cost_estimate=cost(5e9),
         name="dx",
     )(dh1, d, wq, wk, wv)
@@ -618,7 +618,7 @@
         out_shape=out_shape,
         scratch_shapes=[pltpu.VMEM(v.shape, v.dtype) for v in pieces]
         + [pltpu.VMEM(buf, f32), dma((len(pieces),)), dma((4,))],
-        compiler_params=params(22),
+        compiler_params=params(26),
         cost_estimate=cost(4e9),
         name="unpack_" + kind,
         input_output_aliases={len(pieces) + n: n for n in range(len(into))},

time: 213 us -> 213 us (level)
  no operation moved by 1% of the time
where the time goes in v8:
time: 213 us
  Pallas kernels  86.2 us (40%)
  waiting for transfers between devices  73.2 us (34%)
  starting transfers between devices  41 us (19%)
  other arithmetic  7.37 us (3%)
  local copies, waits for them, and re-layouts  2.79 us (1%)
  between operations  2.36 us (1%)
    ppermute x55, waiting for transfers between devices, swap(): return lax.ppermute(value, AXES, [(i, i ^ flip) for i in range(dp * seq)])  73.2 us
    ppermute x55, starting transfers between devices, swap(): return lax.ppermute(value, AXES, [(i, i ^ flip) for i in range(dp * seq)])  41 us
    pallas_call x1, Pallas kernels, forward(): pl.pallas_call(fwd_kernel, in_specs=[SMEM, SMEM] + [VMEM] * 9 + [HBM] * 8...  37.6 us
    pallas_call x4, Pallas kernels, unpack(): pl.pallas_call(functools.partial(unpack_kernel, kind, orders, halves), in...  19.2 us
    pallas_call x1, Pallas kernels, att_call(): pl.pallas_call(att_kernel, in_specs=[SMEM, SMEM, VMEM] + [HBM] * 8, out_s...  13.5 us
    pallas_call x1, Pallas kernels, mid_call(): pl.pallas_call(mid_kernel, in_specs=[VMEM, VMEM] + [HBM] * 6, out_specs=[...  9.22 us
    pallas_call x1, Pallas kernels, dx_call(): pl.pallas_call(dx_kernel, in_specs=[HBM] * 5, out_specs=HBM, out_shape=sd...  6 us
  transfers between devices with their start and end apart: 55, of which 24 were waited for; matrix products, arithmetic and copies ran while one was open for 2% of the time, Pallas kernels for 21%

profile of v8, /device:TPU:0, one launch (start us, length us, event | category | flops | bytes accessed | tf_op | source)
XLA Modules:
  0.0 212.9 jit_solution(12990966438650646054)
XLA Ops:
  1.9 37.6 %forward.1 = (f32[4,12,160]{2,1,0:T(8,128)}, f32[16,768]{1,0:T(8,128)}, bf16[640,768]{1,0:T(8,128)(2,1)}, bf16[640,768]{1,0:T(8,128)(2,1)}, bf16[640,768]{1,0:T(...) custom-call(s32[4]{0:T(128)} %refs_0_.5, ...), custom_call_target="tpu_custom_call" | custom-call | flops 28000000000 | bytes 1048576 | tf_op jit(solution)/shard_map/forward/pallas_call | solution.py:276
  40.2 4.3 %collective-permute-done = bf16[16,192,384]{2,1,0:T(8,128)(2,1)S(1)} collective-permute-done((bf16[16,192,384]{2,1,0:T(8,128)(2,1)}, bf16[16,192,384]{2,1,0:T(8,128)(2,1)S(1)}, u32[]{:S(2)}, u32[]{:S(2)}) %collective-permute-start) | collective-permute-done | bytes 2359328 | tf_op jit(solution)/shard_map/ppermute | solution.py:661
  46.8 2.9 %collective-permute-start.1 = (bf16[2,2,2,64,384]{4,3,2,1,0:T(8,128)(2,1)S(1)}, bf16[2,2,2,64,384]{4,3,2,1,0:T(8,128)(2,1)S(1)}, u32[]{:S(2)}, u32[]{:S(2)}) collective-permute-start(bf16[2,2,2,64,384]{4,3,2,1,0:T(8,128)(2,1)S(1)} %fusion.7), channel_id=1, source_target_pairs={{0,2},{1,3},{2,0},{3,1},{4,6},{5,7},{6,4},{7,5},{8,10},{9,11},{10,... | collective-permute-start | bytes 1179656 | tf_op jit(solution)/shard_map/ppermute | solution.py:661
  52.9 9.2 %mid_bwd.1 = (f32[16,768]{1,0:T(8,128)S(1)}, f32[640,768]{1,0:T(8,128)S(1)}, bf16[640,768]{1,0:T(8,128)(2,1)S(1)}, bf16[640,768]{1,0:T(8,128)(2,1)S(1)}) custom-call(f32[768]{0:T(1024)S(1)} %copy-done.5, f32[16,768]{1,0:T(8,128)S(1)} %copy-done.15, bf16[640,3072]{1,0:T(8,128)(2,1)} %get-tuple-element.240.refs_2_, bf16[768,3072]{1,0:T(8,128)(2,1)} %refs_3_.3, ...), custom_call_target="tpu_custom_call" | custom-call | flops 10000000000 | bytes 1048576 | tf_op jit(solution)/shard_map/mid_bwd/pallas_call | solution.py:403
  65.6 13.5 %att_bwd.1 = (f32[16,768]{1,0:T(8,128)S(1)}, bf16[640,3072]{1,0:T(8,128)(2,1)}, bf16[16,192,384]{2,1,0:T(8,128)(2,1)}, bf16[16,192,384]{2,1,0:T(8,128)(2,1)}) custom-call(s32[4]{0:T(128)S(1)} %copy-done.6, s32[3]{0:T(128)S(1)} %copy-done, f32[16,768]{1,0:T(8,128)S(1)} %get-tuple-element.257.refs_2_, bf16[640,768]{1,0:T(8,128)(2,1)S(1)} %copy-done.11, ...), custom_call_target="tpu_custom_call" | custom-call | flops 12000000000 | bytes 1048576 | tf_op jit(solution)/shard_map/att_bwd/pallas_call | solution.py:469
  84.3 6.0 %dx.1 = f32[640,768]{1,0:T(8,128)} custom-call(f32[640,768]{1,0:T(8,128)S(1)} %get-tuple-element.277.dh1_h, bf16[640,3072]{1,0:T(8,128)(2,1)S(1)} %copy-done.7, bf16[768,768]{1,0:T(8,128)(2,1)S(1)} %copy-done.2, bf16[768,768]{1,0:T(8,128)(2,1)S(1)} %copy-done.3, bf16[768,768]{1,0:T(8,128)(2,1)S(1)} %copy-done.4), custom_call_target="tpu_custom_call" | custom-call | flops 5000000000 | bytes 1048576 | tf_op jit(solution)/shard_map/dx/pallas_call | solution.py:516
  94.9 2.6 %collective-permute-start.16 = (bf16[2,192,384]{2,1,0:T(8,128)(2,1)S(1)}, bf16[2,192,384]{2,1,0:T(8,128)(2,1)S(1)}, u32[]{:S(2)}, u32[]{:S(2)}) collective-permute-start(bf16[2,192,384]{2,1,0:T(8,128)(2,1)S(1)} %pad_maximum_fusion.29), channel_id=1, source_target_pairs={{0,16},{1,17},{2,18},{3,19},{4,20},{5,21},{6,22},{7,23},{8,24},{9,... | collective-permute-start | bytes 884744 | tf_op jit(solution)/shard_map/ppermute | solution.py:661
  97.5 7.6 %collective-permute-done.13 = bf16[640,384]{1,0:T(8,128)(2,1)S(1)} collective-permute-done((bf16[640,384]{1,0:T(8,128)(2,1)S(1)}, bf16[640,384]{1,0:T(8,128)(2,1)S(1)}, u32[]{:S(2)}, u32[]{:S(2)}) %collective-permute-start.13) | collective-permute-done | bytes 491552 | tf_op jit(solution)/shard_map/ppermute | solution.py:661
  105.4 6.3 %collective-permute-done.15 = bf16[672,384]{1,0:T(8,128)(2,1)S(1)} collective-permute-done((bf16[672,384]{1,0:T(8,128)(2,1)S(1)}, bf16[672,384]{1,0:T(8,128)(2,1)S(1)}, u32[]{:S(2)}, u32[]{:S(2)}) %collective-permute-start.15) | collective-permute-done | bytes 516128 | tf_op jit(solution)/shard_map/ppermute | solution.py:661
  114.4 2.5 %collective-permute-start.18 = (bf16[384,384]{1,0:T(8,128)(2,1)S(1)}, bf16[384,384]{1,0:T(8,128)(2,1)S(1)}, u32[]{:S(2)}, u32[]{:S(2)}) collective-permute-start(bf16[384,384]{1,0:T(8,128)(2,1)S(1)} %pad_maximum_fusion.30), channel_id=1, source_target_pairs={{0,8},{1,9},{2,10},{3,11},{4,12},{5,13},{6,14},{7,15},{8,0},{9,1},... | collective-permute-start | bytes 884744 | tf_op jit(solution)/shard_map/ppermute | solution.py:661
  117.6 2.5 %collective-permute-done.17 = bf16[384,384]{1,0:T(8,128)(2,1)S(1)} collective-permute-done((bf16[384,384]{1,0:T(8,128)(2,1)S(1)}, bf16[384,384]{1,0:T(8,128)(2,1)S(1)}, u32[]{:S(2)}, u32[]{:S(2)}) %collective-permute-start.17) | collective-permute-done | bytes 294944 | tf_op jit(solution)/shard_map/ppermute | solution.py:661
  120.2 5.9 %collective-permute-done.18 = bf16[384,384]{1,0:T(8,128)(2,1)S(1)} collective-permute-done((bf16[384,384]{1,0:T(8,128)(2,1)S(1)}, bf16[384,384]{1,0:T(8,128)(2,1)S(1)}, u32[]{:S(2)}, u32[]{:S(2)}) %collective-permute-start.18) | collective-permute-done | bytes 294944 | tf_op jit(solution)/shard_map/ppermute | solution.py:661
  126.2 4.3 %collective-permute-done.20 = bf16[2,192,384]{2,1,0:T(8,128)(2,1)S(1)} collective-permute-done((bf16[2,192,384]{2,1,0:T(8,128)(2,1)S(1)}, bf16[2,192,384]{2,1,0:T(8,128)(2,1)S(1)}, u32[]{:S(2)}, u32[]{:S(2)}) %collective-permute-start.20) | collective-permute-done | bytes 294944 | tf_op jit(solution)/shard_map/ppermute | solution.py:661
  133.6 5.4 %collective-permute-done.21 = bf16[512,384]{1,0:T(8,128)(2,1)S(1)} collective-permute-done((bf16[512,384]{1,0:T(8,128)(2,1)S(1)}, bf16[512,384]{1,0:T(8,128)(2,1)S(1)}, u32[]{:S(2)}, u32[]{:S(2)}) %collective-permute-start.21) | collective-permute-done | bytes 393248 | tf_op jit(solution)/shard_map/ppermute | solution.py:661
  139.7 1.9 collective-permute-done.23
  146.0 11.4 %collective-permute-done.24 = bf16[416,384]{1,0:T(8,128)(2,1)S(1)} collective-permute-done((bf16[416,384]{1,0:T(8,128)(2,1)S(1)}, bf16[416,384]{1,0:T(8,128)(2,1)S(1)}, u32[]{:S(2)}, u32[]{:S(2)}) %collective-permute-start.24) | collective-permute-done | bytes 319520 | tf_op jit(solution)/shard_map/ppermute | solution.py:661
  158.0 5.1 %collective-permute-done.26 = bf16[768,384]{1,0:T(8,128)(2,1)S(1)} collective-permute-done((bf16[768,384]{1,0:T(8,128)(2,1)S(1)}, bf16[768,384]{1,0:T(8,128)(2,1)S(1)}, u32[]{:S(2)}, u32[]{:S(2)}) %collective-permute-start.26) | collective-permute-done | bytes 589856 | tf_op jit(solution)/shard_map/ppermute | solution.py:661
  168.8 5.6 %collective-permute-done.31 = bf16[640,384]{1,0:T(8,128)(2,1)S(1)} collective-permute-done((bf16[640,384]{1,0:T(8,128)(2,1)S(1)}, bf16[640,384]{1,0:T(8,128)(2,1)S(1)}, u32[]{:S(2)}, u32[]{:S(2)}) %collective-permute-start.31) | collective-permute-done | bytes 491552 | tf_op jit(solution)/shard_map/ppermute | solution.py:661
  179.9 4.5 %collective-permute-done.40 = bf16[2,2,64,384]{3,2,1,0:T(8,128)(2,1)S(1)} collective-permute-done((bf16[2,2,64,384]{3,2,1,0:T(8,128)(2,1)S(1)}, bf16[2,2,64,384]{3,2,1,0:T(8,128)(2,1)S(1)}, u32[]{:S(2)}, u32[]{:S(2)}) %collective-permute-start.40) | collective-permute-done | bytes 196640 | tf_op jit(solution)/shard_map/ppermute | solution.py:661
  185.3 6.1 %unpack_outer.1 = f32[3072,768]{1,0:T(8,128)} custom-call(bf16[8,64,384]{2,1,0:T(8,128)(2,1)S(1)} %bitcast.376, bf16[8,64,384]{2,1,0:T(8,128)(2,1)S(1)} %bitcast.394, bf16[8,64,384]{2,1,0:T(8,128)(2,1)S(1)} %collective-permute-done.28.refs_2_, bf16[8,64,384]{2,1,0:T(8,128)(2,1)S(1)} %collective-permute-done.37.refs_3_, bf16[8,64,384]{2,1,0:T(8,128)(2,1)S(1)} %bitcast.379, ...), custom_call_target="tpu_custom_call" | custom-call | flops 4000000000 | bytes 1048576 | tf_op jit(solution)/shard_map/unpack_outer/pallas_call | solution.py:614
  195.4 6.1 %unpack_inner.1 = f32[768,3072]{1,0:T(8,128)} custom-call(bf16[8,64,384]{2,1,0:T(8,128)(2,1)S(1)} %bitcast.385, bf16[8,64,384]{2,1,0:T(8,128)(2,1)S(1)} %bitcast.398, bf16[8,64,384]{2,1,0:T(8,128)(2,1)S(1)} %collective-permute-done.34.refs_2_, bf16[8,64,384]{2,1,0:T(8,128)(2,1)S(1)} %collective-permute-done.43.refs_3_, bf16[8,64,384]{2,1,0:T(8,128)(2,1)S(1)} %bitcast.388, ...), custom_call_target="tpu_custom_call" | custom-call | flops 4000000000 | bytes 1048576 | tf_op jit(solution)/shard_map/unpack_inner/pallas_call | solution.py:614
  201.5 2.2 %collective-permute-done.46.refs_1_ = bf16[8,64,384]{2,1,0:T(8,128)(2,1)S(1)} collective-permute-done((bf16[8,64,384]{2,1,0:T(8,128)(2,1)S(1)}, bf16[8,64,384]{2,1,0:T(8,128)(2,1)S(1)}, u32[]{:S(2)}, u32[]{:S(2)}) %collective-permute-start.46) | collective-permute-done | bytes 393248 | tf_op jit(solution)/shard_map/ppermute | solution.py:661
  205.6 3.5 %unpack_attn.2 = (f32[768,768]{1,0:T(8,128)}, f32[768,768]{1,0:T(8,128)}, f32[768,768]{1,0:T(8,128)}, f32[768,768]{1,0:T(8,128)}) custom-call(bf16[8,64,384]{2,1,0:T(8,128)(2,1)S(1)} %bitcast.406, bf16[8,64,384]{2,1,0:T(8,128)(2,1)S(1)} %collective-permute-done.46.refs_1_, bf16[8,64,384]{2,1,0:T(8,128)(2,1)S(1)} %bitcast.409, ...), custom_call_target="tpu_custom_call" | custom-call | flops 4000000000 | bytes 1048576 | tf_op jit(solution)/shard_map/unpack_attn/pallas_call | solution.py:614
  209.2 3.5 %unpack_attn.3 = (f32[768,768]{1,0:T(8,128)}, f32[768,768]{1,0:T(8,128)}, f32[768,768]{1,0:T(8,128)}, f32[768,768]{1,0:T(8,128)}) custom-call(bf16[8,64,384]{2,1,0:T(8,128)(2,1)S(1)} %collective-permute-done.49.refs_0_, ...), custom_call_target="tpu_custom_call", output_to_operand_aliasing={{0}: (6, {}), {1}: (7, {}), {2}: (8, {}), {3}: (9, {})} | custom-call | flops 4000000000 | bytes 1048576 | tf_op jit(solution)/shard_map/unpack_attn/pallas_call | solution.py:614
  (289 shorter events, 49.9 us)
Async XLA Ops:
  40.1 22.1 %collective-permute-start.4 = (bf16[16,192,384]{2,1,0:T(8,128)(2,1)}, bf16[16,192,384]{2,1,0:T(8,128)(2,1)S(1)}, u32[]{:S(2)}, u32[]{:S(2)}) collective-permute-start(bf16[16,192,384]{2,1,0:T(8,128)(2,1)} %get-tuple-element.246), channel_id=1, source_target_pairs={{0,1},{1,0},{2,3},{3,2},{4,5},{5,4},{6,7},{7,6},{8,9},{9,8},{10,11... | collective-permute-start | bytes 7077896 | tf_op jit(solution)/shard_map/ppermute | solution.py:661
  46.8 16.4 %collective-permute-start.1 = (bf16[2,2,2,64,384]{4,3,2,1,0:T(8,128)(2,1)S(1)}, bf16[2,2,2,64,384]{4,3,2,1,0:T(8,128)(2,1)S(1)}, u32[]{:S(2)}, u32[]{:S(2)}) collective-permute-start(bf16[2,2,2,64,384]{4,3,2,1,0:T(8,128)(2,1)S(1)} %fusion.7), channel_id=1, source_target_pairs={{0,2},{1,3},{2,0},{3,1},{4,6},{5,7},{6,4},{7,5},{8,10},{9,11},{10,... | collective-permute-start | bytes 1179656 | tf_op jit(solution)/shard_map/ppermute | solution.py:661
  49.6 13.6 %collective-permute-start.2 = (bf16[2,2,2,64,384]{4,3,2,1,0:T(8,128)(2,1)S(1)}, bf16[2,2,2,64,384]{4,3,2,1,0:T(8,128)(2,1)S(1)}, u32[]{:S(2)}, u32[]{:S(2)}) collective-permute-start(bf16[2,2,2,64,384]{4,3,2,1,0:T(8,128)(2,1)S(1)} %fusion.6), channel_id=1, source_target_pairs={{0,4},{1,5},{2,6},{3,7},{4,0},{5,1},{6,2},{7,3},{8,12},{9,13},{10,... | collective-permute-start | bytes 1179656 | tf_op jit(solution)/shard_map/ppermute | solution.py:661
  51.2 12.1 %collective-permute-start.3 = (bf16[2,2,2,64,384]{4,3,2,1,0:T(8,128)(2,1)S(1)}, bf16[2,2,2,64,384]{4,3,2,1,0:T(8,128)(2,1)S(1)}, u32[]{:S(2)}, u32[]{:S(2)}) collective-permute-start(bf16[2,2,2,64,384]{4,3,2,1,0:T(8,128)(2,1)S(1)} %get-tuple-element.237), channel_id=1, source_target_pairs={{0,8},{1,9},{2,10},{3,11},{4,12},{5,13},{6,14},{7,15},{8,0},{9,1},... | collective-permute-start | bytes 1179656 | tf_op jit(solution)/shard_map/ppermute | solution.py:661
  63.7 15.5 %collective-permute-start.5 = (bf16[768,384]{1,0:T(8,128)(2,1)S(1)}, bf16[768,384]{1,0:T(8,128)(2,1)S(1)}, u32[]{:S(2)}, u32[]{:S(2)}) collective-permute-start(bf16[768,384]{1,0:T(8,128)(2,1)S(1)} %pad_maximum_fusion.1), channel_id=1, source_target_pairs={{0,2},{1,3},{2,0},{3,1},{4,6},{5,7},{6,4},{7,5},{8,10},{9,11},{10,... | collective-permute-start | bytes 1769480 | tf_op jit(solution)/shard_map/ppermute | solution.py:661
  64.3 15.0 %collective-permute-start.6 = (bf16[768,384]{1,0:T(8,128)(2,1)S(1)}, bf16[768,384]{1,0:T(8,128)(2,1)S(1)}, u32[]{:S(2)}, u32[]{:S(2)}) collective-permute-start(bf16[768,384]{1,0:T(8,128)(2,1)S(1)} %pad_maximum_fusion.2), channel_id=1, source_target_pairs={{0,4},{1,5},{2,6},{3,7},{4,0},{5,1},{6,2},{7,3},{8,12},{9,13},{10,... | collective-permute-start | bytes 1769480 | tf_op jit(solution)/shard_map/ppermute | solution.py:661
  64.8 14.6 %collective-permute-start.7 = (bf16[768,384]{1,0:T(8,128)(2,1)S(1)}, bf16[768,384]{1,0:T(8,128)(2,1)S(1)}, u32[]{:S(2)}, u32[]{:S(2)}) collective-permute-start(bf16[768,384]{1,0:T(8,128)(2,1)S(1)} %pad_maximum_fusion), channel_id=1, source_target_pairs={{0,8},{1,9},{2,10},{3,11},{4,12},{5,13},{6,14},{7,15},{8,0},{9,1},... | collective-permute-start | bytes 1769480 | tf_op jit(solution)/shard_map/ppermute | solution.py:661
  79.9 11.7 %collective-permute-start.8 = (bf16[16,192,384]{2,1,0:T(8,128)(2,1)}, bf16[16,192,384]{2,1,0:T(8,128)(2,1)S(1)}, u32[]{:S(2)}, u32[]{:S(2)}) collective-permute-start(bf16[16,192,384]{2,1,0:T(8,128)(2,1)} %get-tuple-element.273), channel_id=1, source_target_pairs={{0,1},{1,0},{2,3},{3,2},{4,5},{5,4},{6,7},{7,6},{8,9},{9,8},{10,11... | collective-permute-start | bytes 7077896 | tf_op jit(solution)/shard_map/ppermute | solution.py:661
  92.3 19.4 %collective-permute-start.15 = (bf16[672,384]{1,0:T(8,128)(2,1)S(1)}, bf16[672,384]{1,0:T(8,128)(2,1)S(1)}, u32[]{:S(2)}, u32[]{:S(2)}) collective-permute-start(bf16[672,384]{1,0:T(8,128)(2,1)S(1)} %pad_maximum_fusion.6), channel_id=1, source_target_pairs={{0,8},{1,9},{2,10},{3,11},{4,12},{5,13},{6,14},{7,15},{8,0},{9,1},... | collective-permute-start | bytes 1548296 | tf_op jit(solution)/shard_map/ppermute | solution.py:661
  92.9 12.2 %collective-permute-start.13 = (bf16[640,384]{1,0:T(8,128)(2,1)S(1)}, bf16[640,384]{1,0:T(8,128)(2,1)S(1)}, u32[]{:S(2)}, u32[]{:S(2)}) collective-permute-start(bf16[640,384]{1,0:T(8,128)(2,1)S(1)} %pad_maximum_fusion.7), channel_id=1, source_target_pairs={{0,2},{1,3},{2,0},{3,1},{4,6},{5,7},{6,4},{7,5},{8,10},{9,11},{10,... | collective-permute-start | bytes 1474568 | tf_op jit(solution)/shard_map/ppermute | solution.py:661
  93.7 11.6 %collective-permute-start.14 = (bf16[640,384]{1,0:T(8,128)(2,1)S(1)}, bf16[640,384]{1,0:T(8,128)(2,1)S(1)}, u32[]{:S(2)}, u32[]{:S(2)}) collective-permute-start(bf16[640,384]{1,0:T(8,128)(2,1)S(1)} %pad_maximum_fusion.8), channel_id=1, source_target_pairs={{0,4},{1,5},{2,6},{3,7},{4,0},{5,1},{6,2},{7,3},{8,12},{9,13},{10,... | collective-permute-start | bytes 1474568 | tf_op jit(solution)/shard_map/ppermute | solution.py:661
  94.9 16.9 %collective-permute-start.16 = (bf16[2,192,384]{2,1,0:T(8,128)(2,1)S(1)}, bf16[2,192,384]{2,1,0:T(8,128)(2,1)S(1)}, u32[]{:S(2)}, u32[]{:S(2)}) collective-permute-start(bf16[2,192,384]{2,1,0:T(8,128)(2,1)S(1)} %pad_maximum_fusion.29), channel_id=1, source_target_pairs={{0,16},{1,17},{2,18},{3,19},{4,20},{5,21},{6,22},{7,23},{8,24},{9,... | collective-permute-start | bytes 884744 | tf_op jit(solution)/shard_map/ppermute | solution.py:661
  112.5 13.7 %collective-permute-start.19 = (bf16[416,384]{1,0:T(8,128)(2,1)S(1)}, bf16[416,384]{1,0:T(8,128)(2,1)S(1)}, u32[]{:S(2)}, u32[]{:S(2)}) collective-permute-start(bf16[416,384]{1,0:T(8,128)(2,1)S(1)} %pad_maximum_fusion.24), channel_id=1, source_target_pairs={{0,2},{1,3},{2,0},{3,1},{4,6},{5,7},{6,4},{7,5},{8,10},{9,11},{10,... | collective-permute-start | bytes 958472 | tf_op jit(solution)/shard_map/ppermute | solution.py:661
  114.4 11.7 %collective-permute-start.18 = (bf16[384,384]{1,0:T(8,128)(2,1)S(1)}, bf16[384,384]{1,0:T(8,128)(2,1)S(1)}, u32[]{:S(2)}, u32[]{:S(2)}) collective-permute-start(bf16[384,384]{1,0:T(8,128)(2,1)S(1)} %pad_maximum_fusion.30), channel_id=1, source_target_pairs={{0,8},{1,9},{2,10},{3,11},{4,12},{5,13},{6,14},{7,15},{8,0},{9,1},... | collective-permute-start | bytes 884744 | tf_op jit(solution)/shard_map/ppermute | solution.py:661
  116.9 13.7 %collective-permute-start.20 = (bf16[2,192,384]{2,1,0:T(8,128)(2,1)S(1)}, bf16[2,192,384]{2,1,0:T(8,128)(2,1)S(1)}, u32[]{:S(2)}, u32[]{:S(2)}) collective-permute-start(bf16[2,192,384]{2,1,0:T(8,128)(2,1)S(1)} %pad_maximum_fusion.31), channel_id=1, source_target_pairs={{0,16},{1,17},{2,18},{3,19},{4,20},{5,21},{6,22},{7,23},{8,24},{9,... | collective-permute-start | bytes 884744 | tf_op jit(solution)/shard_map/ppermute | solution.py:661
  142.3 15.1 %collective-permute-start.25 = (bf16[768,384]{1,0:T(8,128)(2,1)S(1)}, bf16[768,384]{1,0:T(8,128)(2,1)S(1)}, u32[]{:S(2)}, u32[]{:S(2)}) collective-permute-start(bf16[768,384]{1,0:T(8,128)(2,1)S(1)} %pad_maximum_fusion.5), channel_id=1, source_target_pairs={{0,4},{1,5},{2,6},{3,7},{4,0},{5,1},{6,2},{7,3},{8,12},{9,13},{10,... | collective-permute-start | bytes 1769480 | tf_op jit(solution)/shard_map/ppermute | solution.py:661
  143.6 13.8 %collective-permute-start.24 = (bf16[416,384]{1,0:T(8,128)(2,1)S(1)}, bf16[416,384]{1,0:T(8,128)(2,1)S(1)}, u32[]{:S(2)}, u32[]{:S(2)}) collective-permute-start(bf16[416,384]{1,0:T(8,128)(2,1)S(1)} %pad_maximum_fusion.25), channel_id=1, source_target_pairs={{0,16},{1,17},{2,18},{3,19},{4,20},{5,21},{6,22},{7,23},{8,24},{9,... | collective-permute-start | bytes 958472 | tf_op jit(solution)/shard_map/ppermute | solution.py:661
  144.4 18.7 %collective-permute-start.26 = (bf16[768,384]{1,0:T(8,128)(2,1)S(1)}, bf16[768,384]{1,0:T(8,128)(2,1)S(1)}, u32[]{:S(2)}, u32[]{:S(2)}) collective-permute-start(bf16[768,384]{1,0:T(8,128)(2,1)S(1)} %pad_maximum_fusion.3), channel_id=1, source_target_pairs={{0,8},{1,9},{2,10},{3,11},{4,12},{5,13},{6,14},{7,15},{8,0},{9,1},... | collective-permute-start | bytes 1769480 | tf_op jit(solution)/shard_map/ppermute | solution.py:661
  145.4 17.8 %collective-permute-start.27 = (bf16[768,384]{1,0:T(8,128)(2,1)S(1)}, bf16[768,384]{1,0:T(8,128)(2,1)S(1)}, u32[]{:S(2)}, u32[]{:S(2)}) collective-permute-start(bf16[768,384]{1,0:T(8,128)(2,1)S(1)} %pad_maximum_fusion.4), channel_id=1, source_target_pairs={{0,2},{1,3},{2,0},{3,1},{4,6},{5,7},{6,4},{7,5},{8,10},{9,11},{10,... | collective-permute-start | bytes 1769480 | tf_op jit(solution)/shard_map/ppermute | solution.py:661
  146.0 17.3 %collective-permute-start.28 = (bf16[8,64,384]{2,1,0:T(8,128)(2,1)S(1)}, bf16[8,64,384]{2,1,0:T(8,128)(2,1)S(1)}, u32[]{:S(2)}, u32[]{:S(2)}) collective-permute-start(bf16[8,64,384]{2,1,0:T(8,128)(2,1)S(1)} %bitcast.375), channel_id=1, source_target_pairs={{0,1},{1,0},{2,3},{3,2},{4,5},{5,4},{6,7},{7,6},{8,9},{9,8},{10,11... | collective-permute-start | bytes 1179656 | tf_op jit(solution)/shard_map/ppermute | solution.py:661
  178.2 13.2 %collective-permute-start.43 = (bf16[8,64,384]{2,1,0:T(8,128)(2,1)S(1)}, bf16[8,64,384]{2,1,0:T(8,128)(2,1)S(1)}, u32[]{:S(2)}, u32[]{:S(2)}) collective-permute-start(bf16[8,64,384]{2,1,0:T(8,128)(2,1)S(1)} %bitcast.397), channel_id=1, source_target_pairs={{0,1},{1,0},{2,3},{3,2},{4,5},{5,4},{6,7},{7,6},{8,9},{9,8},{10,11... | collective-permute-start | bytes 1179656 | tf_op jit(solution)/shard_map/ppermute | solution.py:661
  178.2 13.2 %collective-permute-start.44 = (bf16[8,64,384]{2,1,0:T(8,128)(2,1)S(1)}, bf16[8,64,384]{2,1,0:T(8,128)(2,1)S(1)}, u32[]{:S(2)}, u32[]{:S(2)}) collective-permute-start(bf16[8,64,384]{2,1,0:T(8,128)(2,1)S(1)} %bitcast.399), channel_id=1, source_target_pairs={{0,1},{1,0},{2,3},{3,2},{4,5},{5,4},{6,7},{7,6},{8,9},{9,8},{10,11... | collective-permute-start | bytes 1179656 | tf_op jit(solution)/shard_map/ppermute | solution.py:661
  178.8 12.7 %collective-permute-start.45 = (bf16[8,64,384]{2,1,0:T(8,128)(2,1)S(1)}, bf16[8,64,384]{2,1,0:T(8,128)(2,1)S(1)}, u32[]{:S(2)}, u32[]{:S(2)}) collective-permute-start(bf16[8,64,384]{2,1,0:T(8,128)(2,1)S(1)} %bitcast.395), channel_id=1, source_target_pairs={{0,1},{1,0},{2,3},{3,2},{4,5},{5,4},{6,7},{7,6},{8,9},{9,8},{10,11... | collective-permute-start | bytes 1179656 | tf_op jit(solution)/shard_map/ppermute | solution.py:661
  178.8 12.6 %collective-permute-start.41 = (bf16[2,2,64,384]{3,2,1,0:T(8,128)(2,1)S(1)}, bf16[2,2,64,384]{3,2,1,0:T(8,128)(2,1)S(1)}, u32[]{:S(2)}, u32[]{:S(2)}) collective-permute-start(bf16[2,2,64,384]{3,2,1,0:T(8,128)(2,1)S(1)} %get-tuple-element.359), channel_id=1, source_target_pairs={{0,8},{1,9},{2,10},{3,11},{4,12},{5,13},{6,14},{7,15},{8,0},{9,1},... | collective-permute-start | bytes 589832 | tf_op jit(solution)/shard_map/ppermute | solution.py:661
  (57 other events, 344.8 us)
